TPU v7x, 128 devices: a whole 4x4x4 slice. The times are simulated.
128 devices in a mesh: batch: 1, head: 16 (over z, y), seq: 8 (over x, core).
Axes of the slice: x: 4, y: 4, z: 4, core: 2. Of those that a mesh axis runs over, the one named last changes fastest.
Arguments:
- x_embed: bfloat16 [8192, 4096], P(('batch', 'seq'))
- positions: int32 [8192], P(('batch', 'seq'))
- w_q: bfloat16 [2, 4096, 16, 256], P(None, None, 'head')
- w_k: bfloat16 [2, 4096, 16, 256], P(None, None, 'head')
- w_v: bfloat16 [2, 4096, 16, 256], P(None, None, 'head')
- w_o: bfloat16 [2, 16, 256, 4096], P(None, 'head')
- w_gate: bfloat16 [2, 4096, 16384], P(None, None, 'head')
- w_up: bfloat16 [2, 4096, 16384], P(None, None, 'head')
- w_down: bfloat16 [2, 16384, 4096], P(None, 'head')
- norm_gain: bfloat16 [2, 4096], replicated
Outputs:
- output 1: bfloat16 [8192, 4096], P(('batch', 'seq'))
- output 2: bfloat16 [2, 8192, 16, 256], P(None, ('batch', 'seq'), 'head')
- output 3: bfloat16 [2, 8192, 16, 256], P(None, ('batch', 'seq'), 'head')
All inputs are finite; a program needn't handle non-finite values.
Results may differ from a plain program's by a relative error of at most 0.02.
Values are sent between devices in bfloat16 or wider.
A program may use at most 1 GiB of HBM per device.

v0:
```python
import math
import jax
import jax.numpy as jnp
from jax import lax
from jax.sharding import PartitionSpec as P

ROPE_BASE = 500000.0
EPS = 1e-5


def rms_norm(x_in, gain_row):
    x_f32 = x_in.astype(jnp.float32)
    inv_rms = lax.rsqrt(jnp.mean(x_f32 * x_f32, axis=-1, keepdims=True) + EPS)
    return (x_f32 * inv_rms * gain_row.astype(jnp.float32)).astype(jnp.bfloat16)


def rope_tables(positions, head_dim):
    half_dim = head_dim // 2
    inv_freq = ROPE_BASE ** (-(jnp.arange(half_dim, dtype=jnp.float32) * 2.0 / head_dim))
    angles = positions.astype(jnp.float32)[..., None] * inv_freq
    return jnp.cos(angles), jnp.sin(angles)


def apply_rope(heads_in, cos_t, sin_t):
    half_dim = heads_in.shape[-1] // 2
    heads_f32 = heads_in.astype(jnp.float32)
    first_half = heads_f32[..., :half_dim]
    second_half = heads_f32[..., half_dim:]
    cos_b = cos_t[..., None, :]
    sin_b = sin_t[..., None, :]
    rotated = jnp.concatenate([first_half * cos_b - second_half * sin_b, second_half * cos_b + first_half * sin_b], axis=-1)
    return rotated.astype(jnp.bfloat16)


def block_update(soft_state, q_rot, k_blk, v_blk, row_index, col_index, logit_scale):
    row_max, row_sum, accum_out = soft_state
    logits = jnp.einsum('qkgd,skd->qkgs', q_rot, k_blk, preferred_element_type=jnp.float32) * logit_scale
    allowed = (row_index[:, None] >= col_index[None, :])[:, None, None, :]
    logits = jnp.where(allowed, logits, -jnp.inf)
    new_max = jnp.maximum(row_max, jnp.max(logits, axis=-1))
    prob_f32 = jnp.exp(logits - new_max[..., None])
    rescale = jnp.exp(row_max - new_max)
    row_sum = row_sum * rescale + jnp.sum(prob_f32, axis=-1)
    pv_part = jnp.einsum('qkgs,skd->qkgd', prob_f32.astype(jnp.bfloat16), v_blk, preferred_element_type=jnp.float32)
    accum_out = accum_out * rescale[..., None] + pv_part
    return new_max, row_sum, accum_out


def passed_attention(q_rot, k_rot, v_heads, seq_count):
    tok_count, kv_local, group_size, head_dim = q_rot.shape
    my_index = lax.axis_index('seq')
    logit_scale = 1.0 / math.sqrt(head_dim)
    local_index = jnp.arange(tok_count)
    row_index = my_index * tok_count + local_index
    shift_pairs = [(sender, (sender + 1) % seq_count) for sender in range(seq_count)]
    stat_shape = (tok_count, kv_local, group_size)
    init_state = (jnp.full(stat_shape, -jnp.inf, jnp.float32), jnp.zeros(stat_shape, jnp.float32), jnp.zeros(stat_shape + (head_dim,), jnp.float32))
    first_state = block_update(init_state, q_rot, k_rot, v_heads, row_index, row_index, logit_scale)

    def pass_step(step_num, loop_carry):
        k_blk, v_blk, state_in = loop_carry
        k_blk = lax.ppermute(k_blk, 'seq', shift_pairs)
        v_blk = lax.ppermute(v_blk, 'seq', shift_pairs)
        src_index = (my_index - step_num) % seq_count
        col_index = src_index * tok_count + local_index
        return k_blk, v_blk, block_update(state_in, q_rot, k_blk, v_blk, row_index, col_index, logit_scale)

    final_carry = lax.fori_loop(1, seq_count, pass_step, (k_rot, v_heads, first_state))
    row_max, row_sum, accum_out = final_carry[2]
    attn_heads = (accum_out / row_sum[..., None]).astype(jnp.bfloat16)
    return attn_heads.reshape(tok_count, kv_local * group_size * head_dim)


def solution(mesh):
    seq_count = mesh.shape['seq']
    row_spec = P(('batch', 'seq'), None)
    pos_spec = P(('batch', 'seq'))
    head_spec = P(None, None, 'head', None)
    out_proj_spec = P(None, 'head', None, None)
    col_spec = P(None, None, 'head')
    down_spec = P(None, 'head', None)
    cache_spec = P(None, ('batch', 'seq'), 'head', None)

    def local_forward(x_loc, pos_loc, w_q, w_k, w_v, w_o, w_gate, w_up, w_down, norm_gain):
        tok_count, d_model = x_loc.shape
        layer_count = w_q.shape[0]
        q_local = w_q.shape[2]
        head_dim = w_q.shape[3]
        kv_local = w_k.shape[2]
        group_size = q_local // kv_local
        cos_t, sin_t = rope_tables(pos_loc, head_dim)
        x_cur = x_loc
        k_list = []
        v_list = []
        for layer in range(layer_count):
            normed = rms_norm(x_cur, norm_gain[layer])
            q_proj = jnp.dot(normed, w_q[layer].reshape(d_model, q_local * head_dim), preferred_element_type=jnp.float32).astype(jnp.bfloat16)
            k_proj = jnp.dot(normed, w_k[layer].reshape(d_model, kv_local * head_dim), preferred_element_type=jnp.float32).astype(jnp.bfloat16)
            v_proj = jnp.dot(normed, w_v[layer].reshape(d_model, kv_local * head_dim), preferred_element_type=jnp.float32).astype(jnp.bfloat16)
            q_rot = apply_rope(q_proj.reshape(tok_count, q_local, head_dim), cos_t, sin_t).reshape(tok_count, kv_local, group_size, head_dim)
            k_rot = apply_rope(k_proj.reshape(tok_count, kv_local, head_dim), cos_t, sin_t)
            v_heads = v_proj.reshape(tok_count, kv_local, head_dim)
            attn_heads = passed_attention(q_rot, k_rot, v_heads, seq_count)
            part_sum = jnp.dot(attn_heads, w_o[layer].reshape(q_local * head_dim, d_model), preferred_element_type=jnp.float32)
            gate_f32 = jnp.dot(normed, w_gate[layer], preferred_element_type=jnp.float32)
            up_f32 = jnp.dot(normed, w_up[layer], preferred_element_type=jnp.float32)
            hidden = (jax.nn.silu(gate_f32) * up_f32).astype(jnp.bfloat16)
            part_sum = part_sum + jnp.dot(hidden, w_down[layer], preferred_element_type=jnp.float32)
            update = lax.psum(part_sum, 'head').astype(jnp.bfloat16)
            x_cur = (x_cur.astype(jnp.float32) + update.astype(jnp.float32)).astype(jnp.bfloat16)
            k_list.append(k_rot)
            v_list.append(v_heads)
        return x_cur, jnp.stack(k_list), jnp.stack(v_list)

    return jax.shard_map(local_forward, mesh=mesh, in_specs=(row_spec, pos_spec, head_spec, head_spec, head_spec, out_proj_spec, col_spec, col_spec, down_spec, P(None, None)), out_specs=(row_spec, cache_spec, cache_spec), check_vma=False)
```

profile of v0, /device:TPU:6, one launch (start us, length us, event | category | flops | bytes accessed | tf_op | source)
XLA Modules:
  0.0 1155.3 jit_solution(2136107494929897462)
XLA Ops:
  1.4 5.1 fusion.46
  6.5 10.5 fusion.48
  17.0 6.5 fusion.133
  24.8 2.4 fusion.163
  27.2 2.4 fusion.169
  29.6 2.6 fusion.193
  34.3 12.6 %fusion.62 = f32[1024,1024]{1,0:T(8,128)S(1)} fusion(bf16[1024,4096]{1,0:T(8,128)(2,1)} %fusion.48, bf16[2,4096,1024]{2,1,0:T(8,128)(2,1)} %param.21), kind=kOutput, calls=%fused_computation.68 | convolution fusion | flops 8589934592 | bytes 20971520 | tf_op jit(solution)/shard_map/dot_general | solution.py:106
  46.9 15.3 %multiply_convert_fusion.1 = bf16[1024,1024]{1,0:T(8,128)(2,1)} fusion(f32[1024,1024]{1,0:T(8,128)S(1)} %fusion.62, bf16[1024,4096]{1,0:T(8,128)(2,1)} %fusion.48, bf16[2,4096,1024]{2,1,0:T(8,128)(2,1)} %param.20), kind=kOutput, calls=%fused_computation.82 | convolution fusion | flops 8596226048 | bytes 23068672 | tf_op jit(solution)/shard_map/dot_general | solution.py:105
  65.8 115.9 %while.48 = (s32[]{:T(128)}, bf16[1024,1,256]{2,0,1:T(8,128)(2,1)}, bf16[1024,1,256]{2,0,1:T(8,128)(2,1)}, f32[1024,1,1]{0,2,1:T(1,128)S(1)}, f32[1024,1,1]{0,2,...) while((s32[]{:T(128)}, bf16[1024,1,256]{2,0,1:T(8,128)(2,1)}, ...), condition=%wide.region_6.7_spmd.clone, body=%wide.region_3.6_spmd.clone.sunk | while | flops 1088950272 | bytes 22643040 | solution.py:68
  66.7 8.1 collective-permute-done
  78.6 1.9 collective-permute-done.1
  84.4 6.9 collective-permute-done
  95.1 1.9 collective-permute-done.1
  99.3 2.9 collective-permute-start.1
  102.2 5.7 collective-permute-done
  116.1 3.7 collective-permute-start.1
  119.9 4.5 collective-permute-done
  128.1 1.9 collective-permute-done.1
  133.9 3.7 collective-permute-start.1
  137.6 3.3 collective-permute-done
  148.8 2.8 collective-permute-start
  151.6 3.7 collective-permute-start.1
  155.3 2.1 collective-permute-done
  165.3 4.0 collective-permute-start
  169.3 3.7 collective-permute-start.1
  177.6 1.9 collective-permute-done.1
  181.8 16.1 %fusion.60 = f32[1024,4096]{1,0:T(8,128)} fusion(bf16[1024,1024]{1,0:T(8,128)(2,1)} %multiply_convert_fusion.1, bf16[2,1024,4096]{2,1,0:T(8,128)(2,1)} %param.22), kind=kOutput, calls=%fused_computation.66 | convolution fusion | flops 8589934592 | bytes 27262976 | tf_op jit(solution)/shard_map/dot_general | solution.py:108
  197.9 10.6 convolution_add_fusion.1
  208.5 362.5 %all-reduce.2 = bf16[1024,4096]{1,0:T(8,128)(2,1)} all-reduce(f32[1024,4096]{1,0:T(8,128)} %convolution_add_fusion.1), channel_id=1, replica_groups=mesh['batch'=1,'head'=16,'seq'=8] {'head'}, use_global_device_ids=true, to_apply=%region_7.8 | all-reduce | flops 4194304 | bytes 25165824 | tf_op jit(solution)/shard_map/psum | solution.py:109
  571.0 10.4 fusion.50
  581.4 10.3 fusion.52
  591.7 6.5 fusion.142
  600.1 2.4 fusion.151
  602.5 2.4 fusion.157
  605.0 2.6 fusion.201
  609.5 12.6 %fusion.56 = f32[1024,1024]{1,0:T(8,128)S(1)} fusion(bf16[1024,4096]{1,0:T(8,128)(2,1)} %fusion.52, bf16[2,4096,1024]{2,1,0:T(8,128)(2,1)} %param.21), kind=kOutput, calls=%fused_computation.62 | convolution fusion | flops 8589934592 | bytes 20971520 | tf_op jit(solution)/shard_map/dot_general | solution.py:106
  622.0 15.3 %multiply_convert_fusion = bf16[1024,1024]{1,0:T(8,128)(2,1)} fusion(f32[1024,1024]{1,0:T(8,128)S(1)} %fusion.56, bf16[1024,4096]{1,0:T(8,128)(2,1)} %fusion.52, bf16[2,4096,1024]{2,1,0:T(8,128)(2,1)} %param.20), kind=kOutput, calls=%fused_computation.80 | convolution fusion | flops 8596226048 | bytes 23068672 | tf_op jit(solution)/shard_map/dot_general | solution.py:105
  641.0 118.0 %while.49 = (s32[]{:T(128)}, bf16[1024,1,256]{2,0,1:T(8,128)(2,1)S(1)}, bf16[1024,1,256]{2,0,1:T(8,128)(2,1)}, f32[1024,1,1]{0,2,1:T(1,128)S(1)}, f32[1024,1,1]{...) while((s32[]{:T(128)}, ...), condition=%wide.region_14.15_spmd.clone, body=%wide.region_11.14_spmd.clone.sunk | while | flops 1088950272 | bytes 22643040 | solution.py:68
  641.3 3.9 collective-permute-start.2
  645.3 4.7 collective-permute-done.2
  651.8 3.7 collective-permute-done.3
  659.3 3.7 collective-permute-start.3
  663.0 3.5 collective-permute-done.2
  668.4 3.7 collective-permute-done.3
  674.4 2.6 collective-permute-start.2
  677.0 3.7 collective-permute-start.3
  680.8 2.3 collective-permute-done.2
  684.9 3.7 collective-permute-done.3
  691.0 3.8 collective-permute-start.2
  694.8 3.7 collective-permute-start.3
  701.5 3.7 collective-permute-done.3
  707.5 5.1 collective-permute-start.2
  712.6 3.7 collective-permute-start.3
  718.2 3.6 collective-permute-done.3
  724.1 6.3 collective-permute-start.2
  730.3 3.7 collective-permute-start.3
  735.9 3.0 collective-permute-done.3
  741.3 6.8 collective-permute-start.2
  748.1 3.7 collective-permute-start.3
  753.7 3.0 collective-permute-done.3
  759.0 16.1 %fusion.54 = f32[1024,4096]{1,0:T(8,128)} fusion(bf16[1024,1024]{1,0:T(8,128)(2,1)} %multiply_convert_fusion, bf16[2,1024,4096]{2,1,0:T(8,128)(2,1)} %param.22), kind=kOutput, calls=%fused_computation.60 | convolution fusion | flops 8589934592 | bytes 27262976 | tf_op jit(solution)/shard_map/dot_general | solution.py:108
  775.1 10.6 convolution_add_fusion
  785.7 359.0 %all-reduce.3 = bf16[1024,4096]{1,0:T(8,128)(2,1)} all-reduce(f32[1024,4096]{1,0:T(8,128)} %convolution_add_fusion), channel_id=1, replica_groups=mesh['batch'=1,'head'=16,'seq'=8] {'head'}, use_global_device_ids=true, to_apply=%region_15.16 | all-reduce | flops 4194304 | bytes 25165824 | tf_op jit(solution)/shard_map/psum | solution.py:109
  1144.7 10.1 fusion.53
  (195 shorter events, 98.7 us)
Async XLA Ops:
  1.4 5.1 copy-start.6
  17.0 7.3 copy-start.1
  17.0 7.7 copy-start.7
  24.7 2.4 copy-start.9
  66.3 8.6 collective-permute-start
  66.3 14.2 %collective-permute-start.1 = (bf16[1024,1,256]{2,0,1:T(8,128)(2,1)}, bf16[1024,1,256]{2,0,1:T(8,128)(2,1)S(1)}, u32[]{:S(2)}, u32[]{:S(2)}) collective-permute-start(bf16[1024,1,256]{2,0,1:T(8,128)(2,1)} %get-tuple-element.799), channel_id=1, source_target_pairs={{0,1},{1,2},{2,3},{3,4},{4,5},{5,6},{6,7},{7,0},{8,9},{9,10},{10,1... | collective-permute-start | bytes 1572872 | tf_op jit(solution)/shard_map/while/body/eval_jaxpr/ppermute | solution.py:63
  82.8 8.6 collective-permute-start
  82.8 14.2 %collective-permute-start.1 = (bf16[1024,1,256]{2,0,1:T(8,128)(2,1)}, bf16[1024,1,256]{2,0,1:T(8,128)(2,1)S(1)}, u32[]{:S(2)}, u32[]{:S(2)}) collective-permute-start(bf16[1024,1,256]{2,0,1:T(8,128)(2,1)} %get-tuple-element.799), channel_id=1, source_target_pairs={{0,1},{1,2},{2,3},{3,4},{4,5},{5,6},{6,7},{7,0},{8,9},{9,10},{10,1... | collective-permute-start | bytes 1572872 | tf_op jit(solution)/shard_map/while/body/eval_jaxpr/ppermute | solution.py:63
  99.3 8.6 collective-permute-start
  99.3 14.2 %collective-permute-start.1 = (bf16[1024,1,256]{2,0,1:T(8,128)(2,1)}, bf16[1024,1,256]{2,0,1:T(8,128)(2,1)S(1)}, u32[]{:S(2)}, u32[]{:S(2)}) collective-permute-start(bf16[1024,1,256]{2,0,1:T(8,128)(2,1)} %get-tuple-element.799), channel_id=1, source_target_pairs={{0,1},{1,2},{2,3},{3,4},{4,5},{5,6},{6,7},{7,0},{8,9},{9,10},{10,1... | collective-permute-start | bytes 1572872 | tf_op jit(solution)/shard_map/while/body/eval_jaxpr/ppermute | solution.py:63
  115.8 8.6 collective-permute-start
  116.1 13.9 %collective-permute-start.1 = (bf16[1024,1,256]{2,0,1:T(8,128)(2,1)}, bf16[1024,1,256]{2,0,1:T(8,128)(2,1)S(1)}, u32[]{:S(2)}, u32[]{:S(2)}) collective-permute-start(bf16[1024,1,256]{2,0,1:T(8,128)(2,1)} %get-tuple-element.799), channel_id=1, source_target_pairs={{0,1},{1,2},{2,3},{3,4},{4,5},{5,6},{6,7},{7,0},{8,9},{9,10},{10,1... | collective-permute-start | bytes 1572872 | tf_op jit(solution)/shard_map/while/body/eval_jaxpr/ppermute | solution.py:63
  132.3 8.6 collective-permute-start
  133.9 12.6 %collective-permute-start.1 = (bf16[1024,1,256]{2,0,1:T(8,128)(2,1)}, bf16[1024,1,256]{2,0,1:T(8,128)(2,1)S(1)}, u32[]{:S(2)}, u32[]{:S(2)}) collective-permute-start(bf16[1024,1,256]{2,0,1:T(8,128)(2,1)} %get-tuple-element.799), channel_id=1, source_target_pairs={{0,1},{1,2},{2,3},{3,4},{4,5},{5,6},{6,7},{7,0},{8,9},{9,10},{10,1... | collective-permute-start | bytes 1572872 | tf_op jit(solution)/shard_map/while/body/eval_jaxpr/ppermute | solution.py:63
  148.8 8.6 collective-permute-start
  151.6 11.4 collective-permute-start.1
  165.3 8.6 collective-permute-start
  169.3 10.2 collective-permute-start.1
  181.8 16.1 %copy-start.2 = (bf16[2,1,256,4096]{3,2,1,0:T(8,128)(2,1)S(1)}, bf16[2,1,256,4096]{3,2,1,0:T(8,128)(2,1)}, u32[]{:S(2)}) copy-start(bf16[2,1,256,4096]{3,2,1,0:T(8,128)(2,1)} %param.19) | copy-start | bytes 12582916
  591.7 8.4 copy-start
  591.7 8.4 copy-start.8
  598.2 0.8 copy-start.4
  600.1 2.4 copy-start.10
  638.2 1.1 copy-start.5
  641.3 8.6 collective-permute-start.2
  645.2 10.3 collective-permute-start.3
  657.9 8.6 collective-permute-start.2
  659.3 12.8 %collective-permute-start.3 = (bf16[1024,1,256]{2,0,1:T(8,128)(2,1)}, bf16[1024,1,256]{2,0,1:T(8,128)(2,1)S(1)}, u32[]{:S(2)}, u32[]{:S(2)}) collective-permute-start(bf16[1024,1,256]{2,0,1:T(8,128)(2,1)} %get-tuple-element.841), channel_id=1, source_target_pairs={{0,1},{1,2},{2,3},{3,4},{4,5},{5,6},{6,7},{7,0},{8,9},{9,10},{10,1... | collective-permute-start | bytes 1572872 | tf_op jit(solution)/shard_map/while/body/eval_jaxpr/ppermute | solution.py:63
  674.4 8.6 collective-permute-start.2
  677.0 11.6 %collective-permute-start.3 = (bf16[1024,1,256]{2,0,1:T(8,128)(2,1)}, bf16[1024,1,256]{2,0,1:T(8,128)(2,1)S(1)}, u32[]{:S(2)}, u32[]{:S(2)}) collective-permute-start(bf16[1024,1,256]{2,0,1:T(8,128)(2,1)} %get-tuple-element.841), channel_id=1, source_target_pairs={{0,1},{1,2},{2,3},{3,4},{4,5},{5,6},{6,7},{7,0},{8,9},{9,10},{10,1... | collective-permute-start | bytes 1572872 | tf_op jit(solution)/shard_map/while/body/eval_jaxpr/ppermute | solution.py:63
  691.0 8.6 collective-permute-start.2
  694.8 10.4 collective-permute-start.3
  707.5 8.8 collective-permute-start.2
  712.6 9.2 collective-permute-start.3
  724.1 10.0 collective-permute-start.2
  730.3 8.6 collective-permute-start.3
  741.3 10.6 collective-permute-start.2
  748.1 8.6 collective-permute-start.3
  759.0 16.1 %copy-start.3 = (bf16[2,1,256,4096]{3,2,1,0:T(8,128)(2,1)S(1)}, bf16[2,1,256,4096]{3,2,1,0:T(8,128)(2,1)}, u32[]{:S(2)}) copy-start(bf16[2,1,256,4096]{3,2,1,0:T(8,128)(2,1)} %param.19) | copy-start | bytes 12582916
where the time goes:
time: 1170 us; the launch traced here: 1160 us
  blocking collectives  722 us (62%)
  matrix products  174 us (15%)
  waiting for transfers between devices  81.1 us (7%)
  starting transfers between devices  80.9 us (7%)
  other arithmetic  70.7 us (6%)
  local copies, waits for them, and re-layouts  23.9 us (2%)
    psum x2, blocking collectives, local_forward(): update = lax.psum(part_sum, 'head').astype(jnp.bfloat16)  722 us
    ppermute x14, waiting for transfers between devices, pass_step(): k_blk = lax.ppermute(k_blk, 'seq', shift_pairs)  43.1 us
    ppermute x14, starting transfers between devices, pass_step(): v_blk = lax.ppermute(v_blk, 'seq', shift_pairs)  42.1 us
    ppermute x14, starting transfers between devices, pass_step(): k_blk = lax.ppermute(k_blk, 'seq', shift_pairs)  38.8 us
    ppermute x14, waiting for transfers between devices, pass_step(): v_blk = lax.ppermute(v_blk, 'seq', shift_pairs)  38 us
    dot_general x2, matrix products, local_forward(): jnp.dot(hidden, w_down[layer], preferred_element_type=jnp.float32)  32.2 us
    dot_general x2, matrix products, local_forward(): jnp.dot(normed, w_gate[layer], preferred_element_type=jnp.float32)  30.7 us
    dot_general x2, matrix products, local_forward(): up_f32 = jnp.dot(normed, w_up[layer], preferred_element_type=jnp.float32)  25.1 us
  transfers between devices with their start and end apart: 28, of which 25 were waited for; matrix products, arithmetic and copies ran while one was open for 3% of the time, Pallas kernels for 0%

commit v1 on v0

--- a/solution.py
+++ b/solution.py
@@ -106,8 +106,12 @@
             up_f32 = jnp.dot(normed, w_up[layer], preferred_element_type=jnp.float32)
             hidden = (jax.nn.silu(gate_f32) * up_f32).astype(jnp.bfloat16)
             part_sum = part_sum + jnp.dot(hidden, w_down[layer], preferred_element_type=jnp.float32)
-            update = lax.psum(part_sum, 'head').astype(jnp.bfloat16)
-            x_cur = (x_cur.astype(jnp.float32) + update.astype(jnp.float32)).astype(jnp.bfloat16)
+            head_count = lax.axis_size('head')
+            own_rows = tok_count // head_count
+            update = lax.psum_scatter(part_sum, 'head', scatter_dimension=0, tiled=True).astype(jnp.bfloat16)
+            x_own = lax.dynamic_slice_in_dim(x_cur, lax.axis_index('head') * own_rows, own_rows, axis=0)
+            x_own = (x_own.astype(jnp.float32) + update.astype(jnp.float32)).astype(jnp.bfloat16)
+            x_cur = lax.all_gather(x_own, 'head', axis=0, tiled=True)
             k_list.append(k_rot)
             v_list.append(v_heads)
         return x_cur, jnp.stack(k_list), jnp.stack(v_list)

time: 1170 us -> 824 us (0.70)
  blocking collectives: 722 us -> 0 us
  waiting for transfers between devices: 81.1 us -> 470 us
  starting transfers between devices: 80.9 us -> 59 us
  between operations: 1.4 us -> 14.6 us
    psum x2 -> x0, blocking collectives: 722 us -> none  [local_forward(): update = lax.psum(part_sum, 'head').astype(jnp.bfloat16)]
    reduce_scatter x0 -> x2, waiting for transfers between devices: none -> 236 us  [local_forward(): lax.psum_scatter(part_sum, 'head', scatter_dimension=0, tiled=True)]
    all_gather x0 -> x2, waiting for transfers between devices: none -> 138 us  [local_forward(): x_cur = lax.all_gather(x_own, 'head', axis=0, tiled=True)]
    ppermute x14, starting transfers between devices: 38.8 us -> 18.4 us  [pass_step(): k_blk = lax.ppermute(k_blk, 'seq', shift_pairs)]
    ppermute x14, waiting for transfers between devices: 43.1 us -> 61.9 us  [pass_step(): k_blk = lax.ppermute(k_blk, 'seq', shift_pairs)]
  transfers between devices with their start and end apart: 28 -> 32, of which waited for: 25 -> 32; matrix products, arithmetic and copies ran while one was open for 3% -> 6% of each run, Pallas kernels for 0% -> 0%
where the time goes in v1:
time: 824 us; the launch traced here: 814 us
  waiting for transfers between devices  470 us (57%)
  matrix products  177 us (21%)
  other arithmetic  59.8 us (7%)
  starting transfers between devices  59 us (7%)
  local copies, waits for them, and re-layouts  33.2 us (4%)
  between operations  14.6 us (2%)
    reduce_scatter x2, waiting for transfers between devices, local_forward(): lax.psum_scatter(part_sum, 'head', scatter_dimension=0, tiled=True)  236 us
    all_gather x2, waiting for transfers between devices, local_forward(): x_cur = lax.all_gather(x_own, 'head', axis=0, tiled=True)  138 us
    ppermute x14, waiting for transfers between devices, pass_step(): k_blk = lax.ppermute(k_blk, 'seq', shift_pairs)  61.9 us
    ppermute x14, starting transfers between devices, pass_step(): v_blk = lax.ppermute(v_blk, 'seq', shift_pairs)  40.2 us
    ppermute x14, waiting for transfers between devices, pass_step(): v_blk = lax.ppermute(v_blk, 'seq', shift_pairs)  34.3 us
    dot_general x2, matrix products, local_forward(): jnp.dot(hidden, w_down[layer], preferred_element_type=jnp.float32)  31 us
    dot_general x2, matrix products, local_forward(): jnp.dot(normed, w_gate[layer], preferred_element_type=jnp.float32)  30.8 us
    dot_general x2, matrix products, local_forward(): up_f32 = jnp.dot(normed, w_up[layer], preferred_element_type=jnp.float32)  27.8 us
  transfers between devices with their start and end apart: 32, of which 32 were waited for; matrix products, arithmetic and copies ran while one was open for 6% of the time, Pallas kernels for 0%

profile of v1, /device:TPU:6, one launch (start us, length us, event | category | flops | bytes accessed | tf_op | source)
XLA Modules:
  0.0 814.2 jit_solution(15337316500114594992)
XLA Ops:
  8.0 5.1 fusion.46
  13.1 10.5 %fusion.48 = bf16[1024,4096]{1,0:T(8,128)(2,1)} fusion(bf16[1024,4096]{1,0:T(8,128)(2,1)} %param.14, f32[4096]{0:T(1024)S(1)} %bitcast.397, f32[1024]{0:T(1024)S(1)} %add_rsqrt_fusion.1), kind=kLoop, calls=%fused_computation.50 | loop fusion | flops 16777216 | bytes 16797696 | tf_op jit(solution)/shard_map/convert_element_type | solution.py:14
  23.6 6.5 fusion.131
  31.4 2.4 fusion.161
  33.8 2.4 fusion.167
  36.2 2.6 fusion.191
  40.2 15.0 %fusion.60 = f32[1024,1024]{1,0:T(8,128)} fusion(bf16[1024,4096]{1,0:T(8,128)(2,1)} %fusion.48, bf16[2,4096,1024]{2,1,0:T(8,128)(2,1)} %param.21), kind=kOutput, calls=%fused_computation.64 | convolution fusion | flops 8589934592 | bytes 20971520 | tf_op jit(solution)/shard_map/dot_general | solution.py:106
  58.8 14.9 %multiply_convert_fusion.1 = bf16[1024,1024]{1,0:T(8,128)(2,1)S(1)} fusion(f32[1024,1024]{1,0:T(8,128)} %fusion.60, bf16[1024,4096]{1,0:T(8,128)(2,1)} %fusion.48, bf16[2,4096,1024]{2,1,0:T(8,128)(2,1)} %param.20), kind=kOutput, calls=%fused_computation.78 | convolution fusion | flops 8596226048 | bytes 23068672 | tf_op jit(solution)/shard_map/dot_general | solution.py:105
  73.7 14.8 %fusion.58 = f32[1024,4096]{1,0:T(8,128)} fusion(bf16[1024,1024]{1,0:T(8,128)(2,1)S(1)} %multiply_convert_fusion.1, bf16[2,1024,4096]{2,1,0:T(8,128)(2,1)} %param.22), kind=kOutput, calls=%fused_computation.62 | convolution fusion | flops 8589934592 | bytes 27262976 | tf_op jit(solution)/shard_map/dot_general | solution.py:108
  88.5 110.2 %while.48 = (s32[]{:T(128)}, bf16[1024,1,256]{2,0,1:T(8,128)(2,1)}, bf16[1024,1,256]{2,0,1:T(8,128)(2,1)S(1)}, f32[1024,1,1]{0,2,1:T(1,128)S(1)}, f32[1024,1,1]{...) while((s32[]{:T(128)}, bf16[1024,1,256]{2,0,1:T(8,128)(2,1)}, ...), condition=%wide.region_6.7_spmd.clone, body=%wide.region_3.6_spmd.clone.sunk | while | flops 1088950272 | bytes 22643040 | solution.py:68
  89.0 8.2 %collective-permute-done = bf16[1024,1,256]{2,0,1:T(8,128)(2,1)S(1)} collective-permute-done((bf16[1024,1,256]{2,0,1:T(8,128)(2,1)}, bf16[1024,1,256]{2,0,1:T(8,128)(2,1)S(1)}, u32[]{:S(2)}, u32[]{:S(2)}) %collective-permute-start) | collective-permute-done | bytes 524320 | tf_op jit(solution)/shard_map/while/body/eval_jaxpr/ppermute | solution.py:62
  99.8 3.0 collective-permute-done.1
  105.9 7.0 collective-permute-done
  115.5 3.0 collective-permute-done.1
  120.0 2.8 collective-permute-start.1
  122.9 5.7 collective-permute-done
  131.3 3.0 collective-permute-done.1
  136.1 3.7 collective-permute-start.1
  139.8 4.5 collective-permute-done
  147.0 3.0 collective-permute-done.1
  153.1 3.7 collective-permute-start.1
  156.8 3.3 collective-permute-done
  162.8 3.0 collective-permute-done.1
  167.3 2.8 collective-permute-start
  170.0 3.7 collective-permute-start.1
  173.8 2.1 collective-permute-done
  178.5 3.0 collective-permute-done.1
  183.0 4.0 collective-permute-start
  187.0 3.7 collective-permute-start.1
  194.3 3.0 collective-permute-done.1
  198.7 11.2 %convolution_add_fusion.1 = f32[1024,4096]{1,0:T(8,128)} fusion(f32[1024,4096]{1,0:T(8,128)} %fusion.58, bf16[2,1,256,4096]{3,2,1,0:T(8,128)(2,1)} %param.19, f32[1024,1,1,256]{3,0,2,1:T(8,128)S(1)} %get-tuple-element.491, f32[1024]{0:T(1024)S(1)} %bitcast.388), kind=kOutput, calls=%fused_computation.55 | convolution fusion | flops 2152202240 | bytes 36704256 | tf_op jit(solution)/shard_map/dot_general | solution.py:104
  210.0 119.3 %reduce-scatter.3.cloned.1.call-done = f32[64,4096]{1,0:T(8,128)} async-done(((f32[1024,4096]{1,0:T(8,128)}), f32[64,4096]{1,0:T(8,128)}) %reduce-scatter.3.cloned.1.call-update) | async-done | bytes 1048592 | tf_op jit(solution)/shard_map/reduce_scatter | solution.py:111
  329.2 2.2 add_convert_fusion.1
  331.7 70.2 %all-gather.3.cloned.1.call-done = bf16[1024,4096]{1,0:T(8,128)(2,1)} async-done(((bf16[64,4096]{1,0:T(8,128)(2,1)}), bf16[1024,4096]{1,0:T(8,128)(2,1)}) %all-gather.3.cloned.1.call-update) | async-done | bytes 8388624 | tf_op jit(solution)/shard_map/all_gather | solution.py:114
  402.0 5.1 fusion.49
  407.1 10.7 %fusion.51 = bf16[1024,4096]{1,0:T(8,128)(2,1)} fusion(bf16[1024,4096]{1,0:T(8,128)(2,1)} %all-gather.3.cloned.1.call-done, f32[4096]{0:T(1024)S(1)} %bitcast.396, f32[1024]{0:T(1024)S(1)} %add_rsqrt_fusion), kind=kLoop, calls=%fused_computation.53 | loop fusion | flops 16777216 | bytes 16797696 | tf_op jit(solution)/shard_map/convert_element_type | solution.py:14
  417.7 5.9 fusion.140
  424.7 2.4 fusion.149
  427.1 2.4 fusion.155
  429.5 12.8 %fusion.54 = f32[1024,1024]{1,0:T(8,128)} fusion(bf16[1024,4096]{1,0:T(8,128)(2,1)S(1)} %copy-done.1, bf16[2,4096,1024]{2,1,0:T(8,128)(2,1)} %param.21), kind=kOutput, calls=%fused_computation.58 | convolution fusion | flops 8589934592 | bytes 20971520 | tf_op jit(solution)/shard_map/dot_general | solution.py:106
  443.1 2.4 fusion.199
  447.6 15.9 %multiply_convert_fusion = bf16[1024,1024]{1,0:T(8,128)(2,1)} fusion(f32[1024,1024]{1,0:T(8,128)} %fusion.54, bf16[1024,4096]{1,0:T(8,128)(2,1)} %fusion.51, bf16[2,4096,1024]{2,1,0:T(8,128)(2,1)} %param.20), kind=kOutput, calls=%fused_computation.76 | convolution fusion | flops 8596226048 | bytes 23068672 | tf_op jit(solution)/shard_map/dot_general | solution.py:105
  467.1 16.2 %fusion.52 = f32[1024,4096]{1,0:T(8,128)} fusion(bf16[1024,1024]{1,0:T(8,128)(2,1)} %multiply_convert_fusion, bf16[2,1024,4096]{2,1,0:T(8,128)(2,1)} %param.22), kind=kOutput, calls=%fused_computation.56 | convolution fusion | flops 8589934592 | bytes 27262976 | tf_op jit(solution)/shard_map/dot_general | solution.py:108
  483.4 115.5 %while.49 = (s32[]{:T(128)}, bf16[1024,1,256]{2,0,1:T(8,128)(2,1)}, bf16[1024,1,256]{2,0,1:T(8,128)(2,1)}, f32[1024,1,1]{0,2,1:T(1,128)S(1)}, f32[1024,1,1]{0,2,...) while((s32[]{:T(128)}, bf16[1024,1,256]{2,0,1:T(8,128)(2,1)}, ...), condition=%wide.region_14.15_spmd.clone, body=%wide.region_11.14_spmd.clone.sunk | while | flops 1088950272 | bytes 22643040 | solution.py:68
  484.1 7.9 collective-permute-done.2
  501.8 6.7 collective-permute-done.2
  512.2 1.9 collective-permute-done.3
  516.4 3.1 collective-permute-start.3
  519.5 5.5 collective-permute-done.2
  533.5 3.7 collective-permute-start.3
  537.2 4.3 collective-permute-done.2
  545.2 1.9 collective-permute-done.3
  551.2 3.7 collective-permute-start.3
  554.9 3.1 collective-permute-done.2
  565.9 3.0 collective-permute-start.2
  568.9 3.7 collective-permute-start.3
  578.2 1.9 collective-permute-done.3
  582.4 4.2 collective-permute-start.2
  586.6 3.7 collective-permute-start.3
  598.9 11.2 %convolution_add_fusion = f32[1024,4096]{1,0:T(8,128)} fusion(f32[1024,4096]{1,0:T(8,128)} %fusion.52, bf16[2,1,256,4096]{3,2,1,0:T(8,128)(2,1)} %param.19, f32[1024,1,1,256]{3,0,2,1:T(8,128)S(1)} %get-tuple-element.493, f32[1024]{0:T(1024)S(1)} %bitcast.389), kind=kOutput, calls=%fused_computation.54 | convolution fusion | flops 2152202240 | bytes 36704256 | tf_op jit(solution)/shard_map/dot_general | solution.py:104
  610.1 116.6 %reduce-scatter.5.cloned.1.call-done = f32[64,4096]{1,0:T(8,128)} async-done(((f32[1024,4096]{1,0:T(8,128)}), f32[64,4096]{1,0:T(8,128)}) %reduce-scatter.5.cloned.1.call-update) | async-done | bytes 1048592 | tf_op jit(solution)/shard_map/reduce_scatter | solution.py:111
  726.7 2.2 add_convert_fusion
  731.4 67.8 %all-gather.5.cloned.1.call-done = bf16[1024,4096]{1,0:T(8,128)(2,1)} async-done(((bf16[64,4096]{1,0:T(8,128)(2,1)}), bf16[1024,4096]{1,0:T(8,128)(2,1)}) %all-gather.5.cloned.1.call-update) | async-done | bytes 8388624 | tf_op jit(solution)/shard_map/all_gather | solution.py:114
  799.3 7.9 copy.66
  (226 shorter events, 107.5 us)
Async XLA Ops:
  7.2 322.1 %reduce-scatter.3.cloned.1.call-start = ((), (), s32[]{:S(2)}) async-start(), calls=%async_computation.2 | async-start | bytes 17825792 | tf_op jit(solution)/shard_map/reduce_scatter | solution.py:111
  7.2 29.0 %copy-start.13 = (f32[128]{0:T(128)}, f32[128]{0:T(128)S(1)}, u32[]{:S(2)}) copy-start(f32[128]{0:T(128)S(1)} %negate_power_fusion) | copy-start | bytes 1540
  7.3 49.8 %copy-start.8 = (s32[1024]{0:T(1024)}, s32[1024]{0:T(1024)S(1)}, u32[]{:S(2)}) copy-start(s32[1024]{0:T(1024)S(1)} %iota_add_fusion.4) | copy-start | bytes 12292
  8.0 28.3 %copy-start.11 = (f32[1024]{0:T(1024)}, f32[1024]{0:T(1024)S(1)}, u32[]{:S(2)}) copy-start(f32[1024]{0:T(1024)S(1)} %convert_element_type.185) | copy-start | bytes 12292
  8.0 5.1 copy-start.10
  23.6 6.5 copy-start
  23.6 7.7 copy-start.16
  30.1 27.0 %copy-start.6 = (bf16[1024,256]{1,0:T(8,128)(2,1)}, bf16[1024,256]{1,0:T(8,128)(2,1)S(1)}, u32[]{:S(2)}) copy-start(bf16[1024,256]{1,0:T(8,128)(2,1)S(1)} %fusion.131) | copy-start | bytes 1572868
  31.4 2.4 copy-start.18
  38.9 16.3 %copy-start.2 = (bf16[1024,1,128]{0,2,1:T(8,128)(2,1)}, bf16[1024,1,128]{0,2,1:T(8,128)(2,1)S(1)}, u32[]{:S(2)}) copy-start(bf16[1024,1,128]{0,2,1:T(8,128)(2,1)S(1)} %get-tuple-element.641) | copy-start | bytes 786436
  38.9 16.3 %copy-start.4 = (bf16[1024,1,128]{0,2,1:T(8,128)(2,1)}, bf16[1024,1,128]{0,2,1:T(8,128)(2,1)S(1)}, u32[]{:S(2)}) copy-start(bf16[1024,1,128]{0,2,1:T(8,128)(2,1)S(1)} %get-tuple-element.642) | copy-start | bytes 786436
  88.5 8.6 %collective-permute-start = (bf16[1024,1,256]{2,0,1:T(8,128)(2,1)}, bf16[1024,1,256]{2,0,1:T(8,128)(2,1)S(1)}, u32[]{:S(2)}, u32[]{:S(2)}) collective-permute-start(bf16[1024,1,256]{2,0,1:T(8,128)(2,1)} %get-tuple-element.796), channel_id=1, source_target_pairs={{0,1},{1,2},{2,3},{3,4},{4,5},{5,6},{6,7},{7,0},{8,9},{9,10},{10,1... | collective-permute-start | bytes 1572872 | tf_op jit(solution)/shard_map/while/body/eval_jaxpr/ppermute | solution.py:62
  88.5 14.2 %collective-permute-start.1 = (bf16[1024,1,256]{2,0,1:T(8,128)(2,1)S(1)}, bf16[1024,1,256]{2,0,1:T(8,128)(2,1)S(1)}, u32[]{:S(2)}, u32[]{:S(2)}) collective-permute-start(bf16[1024,1,256]{2,0,1:T(8,128)(2,1)S(1)} %get-tuple-element.797), channel_id=1, source_target_pairs={{0,1},{1,2},{2,3},{3,4},{4,5},{5,6},{6,7},{7,0},{8,9},{9,10},{10,1... | collective-permute-start | bytes 1572872 | tf_op jit(solution)/shard_map/while/body/eval_jaxpr/ppermute | solution.py:63
  104.3 8.6 %collective-permute-start = (bf16[1024,1,256]{2,0,1:T(8,128)(2,1)}, bf16[1024,1,256]{2,0,1:T(8,128)(2,1)S(1)}, u32[]{:S(2)}, u32[]{:S(2)}) collective-permute-start(bf16[1024,1,256]{2,0,1:T(8,128)(2,1)} %get-tuple-element.796), channel_id=1, source_target_pairs={{0,1},{1,2},{2,3},{3,4},{4,5},{5,6},{6,7},{7,0},{8,9},{9,10},{10,1... | collective-permute-start | bytes 1572872 | tf_op jit(solution)/shard_map/while/body/eval_jaxpr/ppermute | solution.py:62
  104.3 14.2 %collective-permute-start.1 = (bf16[1024,1,256]{2,0,1:T(8,128)(2,1)S(1)}, bf16[1024,1,256]{2,0,1:T(8,128)(2,1)S(1)}, u32[]{:S(2)}, u32[]{:S(2)}) collective-permute-start(bf16[1024,1,256]{2,0,1:T(8,128)(2,1)S(1)} %get-tuple-element.797), channel_id=1, source_target_pairs={{0,1},{1,2},{2,3},{3,4},{4,5},{5,6},{6,7},{7,0},{8,9},{9,10},{10,1... | collective-permute-start | bytes 1572872 | tf_op jit(solution)/shard_map/while/body/eval_jaxpr/ppermute | solution.py:63
  120.0 8.6 %collective-permute-start = (bf16[1024,1,256]{2,0,1:T(8,128)(2,1)}, bf16[1024,1,256]{2,0,1:T(8,128)(2,1)S(1)}, u32[]{:S(2)}, u32[]{:S(2)}) collective-permute-start(bf16[1024,1,256]{2,0,1:T(8,128)(2,1)} %get-tuple-element.796), channel_id=1, source_target_pairs={{0,1},{1,2},{2,3},{3,4},{4,5},{5,6},{6,7},{7,0},{8,9},{9,10},{10,1... | collective-permute-start | bytes 1572872 | tf_op jit(solution)/shard_map/while/body/eval_jaxpr/ppermute | solution.py:62
  120.0 14.2 %collective-permute-start.1 = (bf16[1024,1,256]{2,0,1:T(8,128)(2,1)S(1)}, bf16[1024,1,256]{2,0,1:T(8,128)(2,1)S(1)}, u32[]{:S(2)}, u32[]{:S(2)}) collective-permute-start(bf16[1024,1,256]{2,0,1:T(8,128)(2,1)S(1)} %get-tuple-element.797), channel_id=1, source_target_pairs={{0,1},{1,2},{2,3},{3,4},{4,5},{5,6},{6,7},{7,0},{8,9},{9,10},{10,1... | collective-permute-start | bytes 1572872 | tf_op jit(solution)/shard_map/while/body/eval_jaxpr/ppermute | solution.py:63
  135.8 8.6 %collective-permute-start = (bf16[1024,1,256]{2,0,1:T(8,128)(2,1)}, bf16[1024,1,256]{2,0,1:T(8,128)(2,1)S(1)}, u32[]{:S(2)}, u32[]{:S(2)}) collective-permute-start(bf16[1024,1,256]{2,0,1:T(8,128)(2,1)} %get-tuple-element.796), channel_id=1, source_target_pairs={{0,1},{1,2},{2,3},{3,4},{4,5},{5,6},{6,7},{7,0},{8,9},{9,10},{10,1... | collective-permute-start | bytes 1572872 | tf_op jit(solution)/shard_map/while/body/eval_jaxpr/ppermute | solution.py:62
  136.1 13.9 %collective-permute-start.1 = (bf16[1024,1,256]{2,0,1:T(8,128)(2,1)S(1)}, bf16[1024,1,256]{2,0,1:T(8,128)(2,1)S(1)}, u32[]{:S(2)}, u32[]{:S(2)}) collective-permute-start(bf16[1024,1,256]{2,0,1:T(8,128)(2,1)S(1)} %get-tuple-element.797), channel_id=1, source_target_pairs={{0,1},{1,2},{2,3},{3,4},{4,5},{5,6},{6,7},{7,0},{8,9},{9,10},{10,1... | collective-permute-start | bytes 1572872 | tf_op jit(solution)/shard_map/while/body/eval_jaxpr/ppermute | solution.py:63
  151.5 8.6 %collective-permute-start = (bf16[1024,1,256]{2,0,1:T(8,128)(2,1)}, bf16[1024,1,256]{2,0,1:T(8,128)(2,1)S(1)}, u32[]{:S(2)}, u32[]{:S(2)}) collective-permute-start(bf16[1024,1,256]{2,0,1:T(8,128)(2,1)} %get-tuple-element.796), channel_id=1, source_target_pairs={{0,1},{1,2},{2,3},{3,4},{4,5},{5,6},{6,7},{7,0},{8,9},{9,10},{10,1... | collective-permute-start | bytes 1572872 | tf_op jit(solution)/shard_map/while/body/eval_jaxpr/ppermute | solution.py:62
  153.1 12.7 %collective-permute-start.1 = (bf16[1024,1,256]{2,0,1:T(8,128)(2,1)S(1)}, bf16[1024,1,256]{2,0,1:T(8,128)(2,1)S(1)}, u32[]{:S(2)}, u32[]{:S(2)}) collective-permute-start(bf16[1024,1,256]{2,0,1:T(8,128)(2,1)S(1)} %get-tuple-element.797), channel_id=1, source_target_pairs={{0,1},{1,2},{2,3},{3,4},{4,5},{5,6},{6,7},{7,0},{8,9},{9,10},{10,1... | collective-permute-start | bytes 1572872 | tf_op jit(solution)/shard_map/while/body/eval_jaxpr/ppermute | solution.py:63
  167.3 8.6 %collective-permute-start = (bf16[1024,1,256]{2,0,1:T(8,128)(2,1)}, bf16[1024,1,256]{2,0,1:T(8,128)(2,1)S(1)}, u32[]{:S(2)}, u32[]{:S(2)}) collective-permute-start(bf16[1024,1,256]{2,0,1:T(8,128)(2,1)} %get-tuple-element.796), channel_id=1, source_target_pairs={{0,1},{1,2},{2,3},{3,4},{4,5},{5,6},{6,7},{7,0},{8,9},{9,10},{10,1... | collective-permute-start | bytes 1572872 | tf_op jit(solution)/shard_map/while/body/eval_jaxpr/ppermute | solution.py:62
  170.0 11.4 %collective-permute-start.1 = (bf16[1024,1,256]{2,0,1:T(8,128)(2,1)S(1)}, bf16[1024,1,256]{2,0,1:T(8,128)(2,1)S(1)}, u32[]{:S(2)}, u32[]{:S(2)}) collective-permute-start(bf16[1024,1,256]{2,0,1:T(8,128)(2,1)S(1)} %get-tuple-element.797), channel_id=1, source_target_pairs={{0,1},{1,2},{2,3},{3,4},{4,5},{5,6},{6,7},{7,0},{8,9},{9,10},{10,1... | collective-permute-start | bytes 1572872 | tf_op jit(solution)/shard_map/while/body/eval_jaxpr/ppermute | solution.py:63
  183.0 8.6 %collective-permute-start = (bf16[1024,1,256]{2,0,1:T(8,128)(2,1)}, bf16[1024,1,256]{2,0,1:T(8,128)(2,1)S(1)}, u32[]{:S(2)}, u32[]{:S(2)}) collective-permute-start(bf16[1024,1,256]{2,0,1:T(8,128)(2,1)} %get-tuple-element.796), channel_id=1, source_target_pairs={{0,1},{1,2},{2,3},{3,4},{4,5},{5,6},{6,7},{7,0},{8,9},{9,10},{10,1... | collective-permute-start | bytes 1572872 | tf_op jit(solution)/shard_map/while/body/eval_jaxpr/ppermute | solution.py:62
  187.0 10.2 %collective-permute-start.1 = (bf16[1024,1,256]{2,0,1:T(8,128)(2,1)S(1)}, bf16[1024,1,256]{2,0,1:T(8,128)(2,1)S(1)}, u32[]{:S(2)}, u32[]{:S(2)}) collective-permute-start(bf16[1024,1,256]{2,0,1:T(8,128)(2,1)S(1)} %get-tuple-element.797), channel_id=1, source_target_pairs={{0,1},{1,2},{2,3},{3,4},{4,5},{5,6},{6,7},{7,0},{8,9},{9,10},{10,1... | collective-permute-start | bytes 1572872 | tf_op jit(solution)/shard_map/while/body/eval_jaxpr/ppermute | solution.py:63
  209.9 192.0 %all-gather.3.cloned.1.call-start = ((), (), s32[]{:S(2)}) async-start(), calls=%async_computation.3 | async-start | bytes 8912896 | tf_op jit(solution)/shard_map/all_gather | solution.py:114
  331.5 395.2 %reduce-scatter.5.cloned.1.call-start = ((), (), s32[]{:S(2)}) async-start(), calls=%async_computation.4 | async-start | bytes 17825792 | tf_op jit(solution)/shard_map/reduce_scatter | solution.py:111
  407.1 10.7 %copy-start.15 = (bf16[2,4096,1,256]{3,1,2,0:T(8,128)(2,1)S(1)}, bf16[2,4096,1,256]{3,1,2,0:T(8,128)(2,1)}, u32[]{:S(2)}) copy-start(bf16[2,4096,1,256]{3,1,2,0:T(8,128)(2,1)} %param.18) | copy-start | bytes 12582916
  417.7 5.9 copy-start.1
  417.7 7.0 copy-start.17
  424.7 2.4 copy-start.19
  429.5 13.6 %copy-start.12 = (f32[1024]{0:T(1024)S(1)}, f32[1024]{0:T(1024)}, u32[]{:S(2)}) copy-start(f32[1024]{0:T(1024)} %copy-done.11) | copy-start | bytes 12292
  429.5 13.6 %copy-start.14 = (f32[128]{0:T(128)S(1)}, f32[128]{0:T(128)}, u32[]{:S(2)}) copy-start(f32[128]{0:T(128)} %copy-done.13) | copy-start | bytes 1540
  447.6 15.9 %copy-start.9 = (s32[1024]{0:T(1024)S(1)}, s32[1024]{0:T(1024)}, u32[]{:S(2)}) copy-start(s32[1024]{0:T(1024)} %copy-done.8) | copy-start | bytes 12292
  483.4 8.6 %collective-permute-start.2 = (bf16[1024,1,256]{2,0,1:T(8,128)(2,1)}, bf16[1024,1,256]{2,0,1:T(8,128)(2,1)S(1)}, u32[]{:S(2)}, u32[]{:S(2)}) collective-permute-start(bf16[1024,1,256]{2,0,1:T(8,128)(2,1)} %get-tuple-element.838), channel_id=1, source_target_pairs={{0,1},{1,2},{2,3},{3,4},{4,5},{5,6},{6,7},{7,0},{8,9},{9,10},{10,1... | collective-permute-start | bytes 1572872 | tf_op jit(solution)/shard_map/while/body/eval_jaxpr/ppermute | solution.py:62
  483.4 14.2 %collective-permute-start.3 = (bf16[1024,1,256]{2,0,1:T(8,128)(2,1)}, bf16[1024,1,256]{2,0,1:T(8,128)(2,1)S(1)}, u32[]{:S(2)}, u32[]{:S(2)}) collective-permute-start(bf16[1024,1,256]{2,0,1:T(8,128)(2,1)} %get-tuple-element.839), channel_id=1, source_target_pairs={{0,1},{1,2},{2,3},{3,4},{4,5},{5,6},{6,7},{7,0},{8,9},{9,10},{10,1... | collective-permute-start | bytes 1572872 | tf_op jit(solution)/shard_map/while/body/eval_jaxpr/ppermute | solution.py:63
  499.9 8.6 %collective-permute-start.2 = (bf16[1024,1,256]{2,0,1:T(8,128)(2,1)}, bf16[1024,1,256]{2,0,1:T(8,128)(2,1)S(1)}, u32[]{:S(2)}, u32[]{:S(2)}) collective-permute-start(bf16[1024,1,256]{2,0,1:T(8,128)(2,1)} %get-tuple-element.838), channel_id=1, source_target_pairs={{0,1},{1,2},{2,3},{3,4},{4,5},{5,6},{6,7},{7,0},{8,9},{9,10},{10,1... | collective-permute-start | bytes 1572872 | tf_op jit(solution)/shard_map/while/body/eval_jaxpr/ppermute | solution.py:62
  499.9 14.2 %collective-permute-start.3 = (bf16[1024,1,256]{2,0,1:T(8,128)(2,1)}, bf16[1024,1,256]{2,0,1:T(8,128)(2,1)S(1)}, u32[]{:S(2)}, u32[]{:S(2)}) collective-permute-start(bf16[1024,1,256]{2,0,1:T(8,128)(2,1)} %get-tuple-element.839), channel_id=1, source_target_pairs={{0,1},{1,2},{2,3},{3,4},{4,5},{5,6},{6,7},{7,0},{8,9},{9,10},{10,1... | collective-permute-start | bytes 1572872 | tf_op jit(solution)/shard_map/while/body/eval_jaxpr/ppermute | solution.py:63
  516.4 8.6 %collective-permute-start.2 = (bf16[1024,1,256]{2,0,1:T(8,128)(2,1)}, bf16[1024,1,256]{2,0,1:T(8,128)(2,1)S(1)}, u32[]{:S(2)}, u32[]{:S(2)}) collective-permute-start(bf16[1024,1,256]{2,0,1:T(8,128)(2,1)} %get-tuple-element.838), channel_id=1, source_target_pairs={{0,1},{1,2},{2,3},{3,4},{4,5},{5,6},{6,7},{7,0},{8,9},{9,10},{10,1... | collective-permute-start | bytes 1572872 | tf_op jit(solution)/shard_map/while/body/eval_jaxpr/ppermute | solution.py:62
  516.4 14.2 %collective-permute-start.3 = (bf16[1024,1,256]{2,0,1:T(8,128)(2,1)}, bf16[1024,1,256]{2,0,1:T(8,128)(2,1)S(1)}, u32[]{:S(2)}, u32[]{:S(2)}) collective-permute-start(bf16[1024,1,256]{2,0,1:T(8,128)(2,1)} %get-tuple-element.839), channel_id=1, source_target_pairs={{0,1},{1,2},{2,3},{3,4},{4,5},{5,6},{6,7},{7,0},{8,9},{9,10},{10,1... | collective-permute-start | bytes 1572872 | tf_op jit(solution)/shard_map/while/body/eval_jaxpr/ppermute | solution.py:63
  532.9 8.6 %collective-permute-start.2 = (bf16[1024,1,256]{2,0,1:T(8,128)(2,1)}, bf16[1024,1,256]{2,0,1:T(8,128)(2,1)S(1)}, u32[]{:S(2)}, u32[]{:S(2)}) collective-permute-start(bf16[1024,1,256]{2,0,1:T(8,128)(2,1)} %get-tuple-element.838), channel_id=1, source_target_pairs={{0,1},{1,2},{2,3},{3,4},{4,5},{5,6},{6,7},{7,0},{8,9},{9,10},{10,1... | collective-permute-start | bytes 1572872 | tf_op jit(solution)/shard_map/while/body/eval_jaxpr/ppermute | solution.py:62
  533.5 13.6 %collective-permute-start.3 = (bf16[1024,1,256]{2,0,1:T(8,128)(2,1)}, bf16[1024,1,256]{2,0,1:T(8,128)(2,1)S(1)}, u32[]{:S(2)}, u32[]{:S(2)}) collective-permute-start(bf16[1024,1,256]{2,0,1:T(8,128)(2,1)} %get-tuple-element.839), channel_id=1, source_target_pairs={{0,1},{1,2},{2,3},{3,4},{4,5},{5,6},{6,7},{7,0},{8,9},{9,10},{10,1... | collective-permute-start | bytes 1572872 | tf_op jit(solution)/shard_map/while/body/eval_jaxpr/ppermute | solution.py:63
  549.4 8.6 %collective-permute-start.2 = (bf16[1024,1,256]{2,0,1:T(8,128)(2,1)}, bf16[1024,1,256]{2,0,1:T(8,128)(2,1)S(1)}, u32[]{:S(2)}, u32[]{:S(2)}) collective-permute-start(bf16[1024,1,256]{2,0,1:T(8,128)(2,1)} %get-tuple-element.838), channel_id=1, source_target_pairs={{0,1},{1,2},{2,3},{3,4},{4,5},{5,6},{6,7},{7,0},{8,9},{9,10},{10,1... | collective-permute-start | bytes 1572872 | tf_op jit(solution)/shard_map/while/body/eval_jaxpr/ppermute | solution.py:62
  551.2 12.4 %collective-permute-start.3 = (bf16[1024,1,256]{2,0,1:T(8,128)(2,1)}, bf16[1024,1,256]{2,0,1:T(8,128)(2,1)S(1)}, u32[]{:S(2)}, u32[]{:S(2)}) collective-permute-start(bf16[1024,1,256]{2,0,1:T(8,128)(2,1)} %get-tuple-element.839), channel_id=1, source_target_pairs={{0,1},{1,2},{2,3},{3,4},{4,5},{5,6},{6,7},{7,0},{8,9},{9,10},{10,1... | collective-permute-start | bytes 1572872 | tf_op jit(solution)/shard_map/while/body/eval_jaxpr/ppermute | solution.py:63
  565.9 8.6 %collective-permute-start.2 = (bf16[1024,1,256]{2,0,1:T(8,128)(2,1)}, bf16[1024,1,256]{2,0,1:T(8,128)(2,1)S(1)}, u32[]{:S(2)}, u32[]{:S(2)}) collective-permute-start(bf16[1024,1,256]{2,0,1:T(8,128)(2,1)} %get-tuple-element.838), channel_id=1, source_target_pairs={{0,1},{1,2},{2,3},{3,4},{4,5},{5,6},{6,7},{7,0},{8,9},{9,10},{10,1... | collective-permute-start | bytes 1572872 | tf_op jit(solution)/shard_map/while/body/eval_jaxpr/ppermute | solution.py:62
  568.9 11.2 %collective-permute-start.3 = (bf16[1024,1,256]{2,0,1:T(8,128)(2,1)}, bf16[1024,1,256]{2,0,1:T(8,128)(2,1)S(1)}, u32[]{:S(2)}, u32[]{:S(2)}) collective-permute-start(bf16[1024,1,256]{2,0,1:T(8,128)(2,1)} %get-tuple-element.839), channel_id=1, source_target_pairs={{0,1},{1,2},{2,3},{3,4},{4,5},{5,6},{6,7},{7,0},{8,9},{9,10},{10,1... | collective-permute-start | bytes 1572872 | tf_op jit(solution)/shard_map/while/body/eval_jaxpr/ppermute | solution.py:63
  582.4 8.6 %collective-permute-start.2 = (bf16[1024,1,256]{2,0,1:T(8,128)(2,1)}, bf16[1024,1,256]{2,0,1:T(8,128)(2,1)S(1)}, u32[]{:S(2)}, u32[]{:S(2)}) collective-permute-start(bf16[1024,1,256]{2,0,1:T(8,128)(2,1)} %get-tuple-element.838), channel_id=1, source_target_pairs={{0,1},{1,2},{2,3},{3,4},{4,5},{5,6},{6,7},{7,0},{8,9},{9,10},{10,1... | collective-permute-start | bytes 1572872 | tf_op jit(solution)/shard_map/while/body/eval_jaxpr/ppermute | solution.py:62
  586.6 10.0 %collective-permute-start.3 = (bf16[1024,1,256]{2,0,1:T(8,128)(2,1)}, bf16[1024,1,256]{2,0,1:T(8,128)(2,1)S(1)}, u32[]{:S(2)}, u32[]{:S(2)}) collective-permute-start(bf16[1024,1,256]{2,0,1:T(8,128)(2,1)} %get-tuple-element.839), channel_id=1, source_target_pairs={{0,1},{1,2},{2,3},{3,4},{4,5},{5,6},{6,7},{7,0},{8,9},{9,10},{10,1... | collective-permute-start | bytes 1572872 | tf_op jit(solution)/shard_map/while/body/eval_jaxpr/ppermute | solution.py:63
  610.0 118.9 %copy-start.3 = (bf16[1024,1,128]{0,2,1:T(8,128)(2,1)S(1)}, bf16[1024,1,128]{0,2,1:T(8,128)(2,1)}, u32[]{:S(2)}) copy-start(bf16[1024,1,128]{0,2,1:T(8,128)(2,1)} %copy-done.2) | copy-start | bytes 786436
  610.0 119.0 %copy-start.5 = (bf16[1024,1,128]{0,2,1:T(8,128)(2,1)S(1)}, bf16[1024,1,128]{0,2,1:T(8,128)(2,1)}, u32[]{:S(2)}) copy-start(bf16[1024,1,128]{0,2,1:T(8,128)(2,1)} %copy-done.4) | copy-start | bytes 786436
  610.1 120.3 %copy-start.7 = (bf16[1024,256]{1,0:T(8,128)(2,1)S(1)}, bf16[1024,256]{1,0:T(8,128)(2,1)}, u32[]{:S(2)}) copy-start(bf16[1024,256]{1,0:T(8,128)(2,1)} %copy-done.6) | copy-start | bytes 1572868
  610.1 189.2 %all-gather.5.cloned.1.call-start = ((), (), s32[]{:S(2)}) async-start(), calls=%async_computation.5 | async-start | bytes 8912896 | tf_op jit(solution)/shard_map/all_gather | solution.py:114
Sparse Core Ops, SparseCore 0:
  210.0 119.1 reduce-scatter.2
  332.0 69.9 all-gather.2
  610.2 116.4 reduce-scatter.4
  729.3 69.9 all-gather.4

commit v2 on v1

v2 whole, which is shorter than its diff:
```python
import functools
import math
import jax
import jax.numpy as jnp
from jax import lax
from jax.experimental import pallas as pl
from jax.experimental.pallas import tpu as pltpu
from jax.sharding import PartitionSpec as P

ROPE_BASE = 500000.0
EPS = 1e-5


def rms_norm(x_in, gain_row):
    x_f32 = x_in.astype(jnp.float32)
    inv_rms = lax.rsqrt(jnp.mean(x_f32 * x_f32, axis=-1, keepdims=True) + EPS)
    return (x_f32 * inv_rms * gain_row.astype(jnp.float32)).astype(jnp.bfloat16)


def rope_tables(positions, head_dim):
    half_dim = head_dim // 2
    inv_freq = ROPE_BASE ** (-(jnp.arange(half_dim, dtype=jnp.float32) * 2.0 / head_dim))
    angles = positions.astype(jnp.float32)[..., None] * inv_freq
    return jnp.cos(angles), jnp.sin(angles)


def apply_rope(heads_in, cos_t, sin_t):
    half_dim = heads_in.shape[-1] // 2
    heads_f32 = heads_in.astype(jnp.float32)
    first_half = heads_f32[..., :half_dim]
    second_half = heads_f32[..., half_dim:]
    cos_b = cos_t[..., None, :]
    sin_b = sin_t[..., None, :]
    rotated = jnp.concatenate([first_half * cos_b - second_half * sin_b, second_half * cos_b + first_half * sin_b], axis=-1)
    return rotated.astype(jnp.bfloat16)


LOG2E = 1.4426950408889634
KEY_BLOCK = 1024
ROW_BLOCK = 256


def flash_kernel(seq_tokens, q_ref, kv_ref, out_ref):
    rows, head_dim = q_ref.shape
    my_seq = lax.axis_index('seq')
    row_block = pl.program_id(0)
    scale = LOG2E / math.sqrt(head_dim)
    q_val = q_ref[...]

    def visit(state, key_start, key_count, masked):
        row_max, row_sum, accum = state
        keys = kv_ref[pl.ds(key_start, key_count), :head_dim]
        vals = kv_ref[pl.ds(key_start, key_count), head_dim:]
        logits = lax.dot_general(q_val, keys, (((1,), (1,)), ((), ())), preferred_element_type=jnp.float32) * scale
        if masked:
            row_iota = lax.broadcasted_iota(jnp.int32, logits.shape, 0)
            col_iota = lax.broadcasted_iota(jnp.int32, logits.shape, 1)
            logits = jnp.where(row_iota >= col_iota, logits, -jnp.inf)
        new_max = jnp.maximum(row_max, jnp.max(logits, axis=-1, keepdims=True))
        prob = jnp.exp2(logits - new_max)
        rescale = jnp.exp2(row_max - new_max)
        row_sum = row_sum * rescale + jnp.sum(prob, axis=-1, keepdims=True)
        accum = accum * rescale + jnp.dot(prob.astype(jnp.bfloat16), vals, preferred_element_type=jnp.float32)
        return new_max, row_sum, accum

    own_start = my_seq * seq_tokens
    state = (jnp.full((rows, 1), -jnp.inf, jnp.float32), jnp.zeros((rows, 1), jnp.float32), jnp.zeros((rows, head_dim), jnp.float32))
    diag_start = pl.multiple_of(own_start + row_block * rows, rows)
    state = visit(state, diag_start, rows, True)
    state = lax.fori_loop(0, row_block, lambda i, st: visit(st, pl.multiple_of(own_start + i * rows, rows), rows, False), state)
    past_blocks = own_start // KEY_BLOCK
    state = lax.fori_loop(0, past_blocks, lambda i, st: visit(st, pl.multiple_of(i * KEY_BLOCK, KEY_BLOCK), KEY_BLOCK, False), state)
    out_ref[...] = (state[2] / state[1]).astype(jnp.bfloat16)


def flash_attention(q_rot, kv_full):
    tok_count, head_dim = q_rot.shape
    return pl.pallas_call(
        functools.partial(flash_kernel, tok_count),
        out_shape=jax.ShapeDtypeStruct((tok_count, head_dim), jnp.bfloat16),
        grid=(tok_count // ROW_BLOCK,),
        in_specs=[pl.BlockSpec((ROW_BLOCK, head_dim), lambda i: (i, 0)), pl.BlockSpec(kv_full.shape, lambda i: (0, 0))],
        out_specs=pl.BlockSpec((ROW_BLOCK, head_dim), lambda i: (i, 0)),
        compiler_params=pltpu.CompilerParams(dimension_semantics=('arbitrary',), vmem_limit_bytes=48 * 1024 * 1024),
        cost_estimate=pl.CostEstimate(flops=4 * tok_count * kv_full.shape[0] * head_dim, bytes_accessed=kv_full.size * 2, transcendentals=tok_count * kv_full.shape[0]),
        name='flash',
    )(q_rot, kv_full)


def solution(mesh):
    row_spec = P(('batch', 'seq'), None)
    pos_spec = P(('batch', 'seq'))
    head_spec = P(None, None, 'head', None)
    out_proj_spec = P(None, 'head', None, None)
    col_spec = P(None, None, 'head')
    down_spec = P(None, 'head', None)
    cache_spec = P(None, ('batch', 'seq'), 'head', None)

    def local_forward(x_loc, pos_loc, w_q, w_k, w_v, w_o, w_gate, w_up, w_down, norm_gain):
        tok_count, d_model = x_loc.shape
        layer_count = w_q.shape[0]
        q_local = w_q.shape[2]
        head_dim = w_q.shape[3]
        kv_local = w_k.shape[2]
        cos_t, sin_t = rope_tables(pos_loc, head_dim)
        x_cur = x_loc
        k_list = []
        v_list = []
        for layer in range(layer_count):
            normed = rms_norm(x_cur, norm_gain[layer])
            q_proj = jnp.dot(normed, w_q[layer].reshape(d_model, q_local * head_dim), preferred_element_type=jnp.float32).astype(jnp.bfloat16)
            k_proj = jnp.dot(normed, w_k[layer].reshape(d_model, kv_local * head_dim), preferred_element_type=jnp.float32).astype(jnp.bfloat16)
            v_proj = jnp.dot(normed, w_v[layer].reshape(d_model, kv_local * head_dim), preferred_element_type=jnp.float32).astype(jnp.bfloat16)
            q_rot = apply_rope(q_proj.reshape(tok_count, q_local, head_dim), cos_t, sin_t)
            k_rot = apply_rope(k_proj.reshape(tok_count, kv_local, head_dim), cos_t, sin_t)
            v_heads = v_proj.reshape(tok_count, kv_local, head_dim)
            kv_own = jnp.concatenate([k_rot.reshape(tok_count, head_dim), v_proj], axis=1)
            kv_full = lax.all_gather(kv_own, 'seq', axis=0, tiled=True)
            attn_heads = flash_attention(q_rot.reshape(tok_count, head_dim), kv_full)
            gate_f32 = jnp.dot(normed, w_gate[layer], preferred_element_type=jnp.float32)
            up_f32 = jnp.dot(normed, w_up[layer], preferred_element_type=jnp.float32)
            hidden = (jax.nn.silu(gate_f32) * up_f32).astype(jnp.bfloat16)
            part_sum = jnp.dot(hidden, w_down[layer], preferred_element_type=jnp.float32)
            part_sum = part_sum + jnp.dot(attn_heads, w_o[layer].reshape(q_local * head_dim, d_model), preferred_element_type=jnp.float32)
            head_count = lax.axis_size('head')
            own_rows = tok_count // head_count
            update = lax.psum_scatter(part_sum, 'head', scatter_dimension=0, tiled=True).astype(jnp.bfloat16)
            x_own = lax.dynamic_slice_in_dim(x_cur, lax.axis_index('head') * own_rows, own_rows, axis=0)
            x_own = (x_own.astype(jnp.float32) + update.astype(jnp.float32)).astype(jnp.bfloat16)
            x_cur = lax.all_gather(x_own, 'head', axis=0, tiled=True)
            k_list.append(k_rot)
            v_list.append(v_heads)
        return x_cur, jnp.stack(k_list), jnp.stack(v_list)

    return jax.shard_map(local_forward, mesh=mesh, in_specs=(row_spec, pos_spec, head_spec, head_spec, head_spec, out_proj_spec, col_spec, col_spec, down_spec, P(None, None)), out_specs=(row_spec, cache_spec, cache_spec), check_vma=False)
```

time: 824 us -> 664 us (0.81)
  waiting for transfers between devices: 470 us -> 384 us
  Pallas kernels: 0 us -> 65.5 us
  starting transfers between devices: 59 us -> 0.98 us
  matrix products: 177 us -> 133 us
  local copies, waits for them, and re-layouts: 33.2 us -> 10.9 us
  other arithmetic: 59.8 us -> 45.1 us
    ppermute x28 -> x0, waiting for transfers between devices: 96.2 us -> none  [the longest x14 61.9 us: pass_step(): k_blk = lax.ppermute(k_blk, 'seq', shift_pairs)]
    pallas_call x0 -> x2, Pallas kernels: none -> 65.5 us  [flash_attention(): pl.pallas_call(functools.partial(flash_kernel, tok_count), out_shape=jax....]
    ppermute x28 -> x0, starting transfers between devices: 58.6 us -> none  [the longest x14 40.2 us: pass_step(): v_blk = lax.ppermute(v_blk, 'seq', shift_pairs)]
    dot_general x32 -> x0, matrix products: 42.6 us -> none  [the longest x16 23.1 us: block_update(): jnp.einsum('qkgs,skd->qkgd', prob_f32.astype(jnp.bfloat16), v_blk, prefer...]
    while x42 -> x0, local copies, waits for them, and re-layouts: 17 us -> none
    reduce_sum x16 -> x0, other arithmetic: 16.4 us -> none  [block_update(): row_sum = row_sum * rescale + jnp.sum(prob_f32, axis=-1)]
    all_gather x0 -> x2, waiting for transfers between devices: none -> 13 us  [local_forward(): kv_full = lax.all_gather(kv_own, 'seq', axis=0, tiled=True)]
  transfers between devices with their start and end apart: 32 -> 6, of which waited for: 32 -> 6; matrix products, arithmetic and copies ran while one was open for 6% -> 13% of each run, Pallas kernels for 0% -> 0%
where the time goes in v2:
time: 664 us; the launch traced here: 655 us
  waiting for transfers between devices  384 us (58%)
  matrix products  133 us (20%)
  Pallas kernels  65.5 us (10%)
  other arithmetic  45.1 us (7%)
  between operations  14.9 us (2%)
  local copies, waits for them, and re-layouts  10.9 us (2%)
    reduce_scatter x2, waiting for transfers between devices, local_forward(): lax.psum_scatter(part_sum, 'head', scatter_dimension=0, tiled=True)  232 us
    all_gather x2, waiting for transfers between devices, local_forward(): x_cur = lax.all_gather(x_own, 'head', axis=0, tiled=True)  139 us
    pallas_call x2, Pallas kernels, flash_attention(): pl.pallas_call(functools.partial(flash_kernel, tok_count), out_shape=jax....  65.5 us
    dot_general x2, matrix products, local_forward(): jnp.dot(normed, w_gate[layer], preferred_element_type=jnp.float32)  30.8 us
    dot_general x2, matrix products, local_forward(): jnp.dot(attn_heads, w_o[layer].reshape(q_local * head_dim, d_model), pref...  27.8 us
    dot_general x2, matrix products, local_forward(): jnp.dot(hidden, w_down[layer], preferred_element_type=jnp.float32)  27.3 us
    dot_general x2, matrix products, local_forward(): up_f32 = jnp.dot(normed, w_up[layer], preferred_element_type=jnp.float32)  25.4 us
    convert_element_type x2, other arithmetic, rms_norm(): return (x_f32 * inv_rms * gain_row.astype(jnp.float32)).astype(jnp.bfloat16)  21 us
  transfers between devices with their start and end apart: 6, of which 6 were waited for; matrix products, arithmetic and copies ran while one was open for 13% of the time, Pallas kernels for 0%

profile of v2, /device:TPU:6, one launch (start us, length us, event | category | flops | bytes accessed | tf_op | source)
XLA Modules:
  0.0 655.0 jit_solution(13744648900947491378)
XLA Ops:
  7.2 0.0 all-gather.5.cloned.1.call-start
  7.2 0.7 convert_element_type.128
  7.9 5.1 fusion
  13.0 0.0 copy-done.10
  13.1 10.5 %fusion.2 = bf16[1024,4096]{1,0:T(8,128)(2,1)} fusion(bf16[1024,4096]{1,0:T(8,128)(2,1)} %param.10, f32[4096]{0:T(1024)S(1)} %bitcast.139, f32[1024]{0:T(1024)S(1)} %add_rsqrt_fusion.1), kind=kLoop, calls=%fused_computation.6 | loop fusion | flops 16777216 | bytes 16797696 | tf_op jit(solution)/shard_map/convert_element_type | solution.py:17
  23.6 6.5 fusion.56
  30.0 1.1 copy-done.11
  31.1 2.3 fusion.83
  33.5 0.0 copy-done.13
  33.5 2.3 fusion.89
  35.8 2.5 fusion.113
  38.3 0.0 copy-start.4
  38.4 0.7 copy-done.4
  39.0 0.1 copy-done.6
  39.1 1.1 pad_maximum_fusion
  40.2 0.0 all-gather.5.cloned.1.call-update
  40.2 0.4 reduce-scatter.3.cloned.1.call-start
  40.6 0.1 pad_maximum_fusion.3.q_ref
  40.7 0.0 slice-start
  40.7 0.0 slice-start.1
  40.7 0.0 slice-start.2
  40.7 12.7 %fusion.14 = f32[1024,1024]{1,0:T(8,128)S(1)} fusion(bf16[1024,4096]{1,0:T(8,128)(2,1)} %fusion.2, bf16[2,4096,1024]{2,1,0:T(8,128)(2,1)} %param.17), kind=kOutput, calls=%fused_computation.20 | convolution fusion | flops 8589934592 | bytes 20971520 | tf_op jit(solution)/shard_map/dot_general | solution.py:121
  53.4 0.0 slice-start.3
  53.4 15.4 %multiply_convert_fusion.1 = bf16[1024,1024]{1,0:T(8,128)(2,1)} fusion(f32[1024,1024]{1,0:T(8,128)S(1)} %fusion.14, bf16[1024,4096]{1,0:T(8,128)(2,1)} %fusion.2, bf16[2,4096,1024]{2,1,0:T(8,128)(2,1)} %param.16), kind=kOutput, calls=%fused_computation.31 | convolution fusion | flops 8596226048 | bytes 23068672 | tf_op jit(solution)/shard_map/dot_general | solution.py:120
  68.8 13.6 %fusion.12 = f32[1024,4096]{1,0:T(8,128)} fusion(bf16[1024,1024]{1,0:T(8,128)(2,1)} %multiply_convert_fusion.1, bf16[2,1024,4096]{2,1,0:T(8,128)(2,1)S(1)} %bitcast.141), kind=kOutput, calls=%fused_computation.18 | convolution fusion | flops 8589934592 | bytes 27262976 | tf_op jit(solution)/shard_map/dot_general | solution.py:123
  82.5 7.8 %all-gather.5.cloned.1.call-done.kv_ref = bf16[8192,512]{1,0:T(8,128)(2,1)} async-done(((bf16[1024,512]{1,0:T(8,128)(2,1)}), bf16[8192,512]{1,0:T(8,128)(2,1)}) %all-gather.5.cloned.1.call-update) | async-done | bytes 8388624 | tf_op jit(solution)/shard_map/all_gather | solution.py:118
  90.3 32.6 %flash.2 = bf16[1024,256]{1,0:T(8,128)(2,1)S(1)} custom-call(bf16[1024,256]{1,0:T(8,128)(2,1)S(1)} %pad_maximum_fusion.3.q_ref, bf16[8192,512]{1,0:T(8,128)(2,1)} %all-gather.5.cloned.1.call-done.kv_ref), custom_call_target="tpu_custom_call" | custom-call | flops 8589934592 | bytes 8388608 | tf_op jit(solution)/shard_map/flash/pallas_call | solution.py:78
  122.9 13.9 %convolution_add_fusion.1 = f32[1024,4096]{1,0:T(8,128)} fusion(f32[1024,4096]{1,0:T(8,128)} %fusion.12, bf16[1024,256]{1,0:T(8,128)(2,1)S(1)} %flash.2, bf16[2,1,256,4096]{3,2,1,0:T(8,128)(2,1)S(1)} %copy-done.2), kind=kOutput, calls=%fused_computation.11 | convolution fusion | flops 2151677952 | bytes 36175872 | tf_op jit(solution)/shard_map/dot_general | solution.py:124
  136.8 0.0 reduce-scatter.3.cloned.1.call-update
  136.8 0.0 all-gather.7.cloned.1.call-start
  136.9 116.0 %reduce-scatter.3.cloned.1.call-done = f32[64,4096]{1,0:T(8,128)} async-done(((f32[1024,4096]{1,0:T(8,128)}), f32[64,4096]{1,0:T(8,128)}) %reduce-scatter.3.cloned.1.call-update) | async-done | bytes 1048592 | tf_op jit(solution)/shard_map/reduce_scatter | solution.py:127
  252.9 2.2 add_convert_fusion.1
  255.1 0.0 all-gather.7.cloned.1.call-update
  255.2 0.2 all-gather.9.cloned.1.call-start
  255.4 70.2 %all-gather.7.cloned.1.call-done = bf16[1024,4096]{1,0:T(8,128)(2,1)} async-done(((bf16[64,4096]{1,0:T(8,128)(2,1)}), bf16[1024,4096]{1,0:T(8,128)(2,1)}) %all-gather.7.cloned.1.call-update) | async-done | bytes 8388624 | tf_op jit(solution)/shard_map/all_gather | solution.py:130
  325.6 5.1 fusion.3
  330.7 10.5 %fusion.5 = bf16[1024,4096]{1,0:T(8,128)(2,1)} fusion(bf16[1024,4096]{1,0:T(8,128)(2,1)} %all-gather.7.cloned.1.call-done, f32[4096]{0:T(1024)S(1)} %bitcast.138, f32[1024]{0:T(1024)S(1)} %add_rsqrt_fusion), kind=kLoop, calls=%fused_computation.9 | loop fusion | flops 16777216 | bytes 16797696 | tf_op jit(solution)/shard_map/convert_element_type | solution.py:17
  341.2 6.5 fusion.65
  347.7 1.1 copy-done.12
  348.8 2.3 fusion.71
  351.1 2.3 fusion.77
  353.5 2.5 fusion.121
  356.0 1.1 pad_maximum_fusion.1
  357.0 0.0 all-gather.9.cloned.1.call-update
  357.1 0.3 reduce-scatter.5.cloned.1.call-start
  357.3 0.1 pad_maximum_fusion.4.q_ref
  357.4 0.0 slice-start.4
  357.4 0.0 slice-start.5
  357.4 0.0 slice-start.6
  357.4 12.7 %fusion.8 = f32[1024,1024]{1,0:T(8,128)S(1)} fusion(bf16[1024,4096]{1,0:T(8,128)(2,1)} %fusion.5, bf16[2,4096,1024]{2,1,0:T(8,128)(2,1)} %param.17), kind=kOutput, calls=%fused_computation.14 | convolution fusion | flops 8589934592 | bytes 20971520 | tf_op jit(solution)/shard_map/dot_general | solution.py:121
  370.1 0.0 slice-start.7
  370.1 15.4 %multiply_convert_fusion = bf16[1024,1024]{1,0:T(8,128)(2,1)} fusion(f32[1024,1024]{1,0:T(8,128)S(1)} %fusion.8, bf16[1024,4096]{1,0:T(8,128)(2,1)} %fusion.5, bf16[2,4096,1024]{2,1,0:T(8,128)(2,1)} %param.16), kind=kOutput, calls=%fused_computation.30 | convolution fusion | flops 8596226048 | bytes 23068672 | tf_op jit(solution)/shard_map/dot_general | solution.py:120
  385.6 13.6 %fusion.6 = f32[1024,4096]{1,0:T(8,128)} fusion(bf16[1024,1024]{1,0:T(8,128)(2,1)} %multiply_convert_fusion, bf16[2,1024,4096]{2,1,0:T(8,128)(2,1)S(1)} %bitcast.143), kind=kOutput, calls=%fused_computation.12 | convolution fusion | flops 8589934592 | bytes 27262976 | tf_op jit(solution)/shard_map/dot_general | solution.py:123
  399.2 5.2 all-gather.9.cloned.1.call-done.kv_ref
  404.4 32.9 %flash.3 = bf16[1024,256]{1,0:T(8,128)(2,1)S(1)} custom-call(bf16[1024,256]{1,0:T(8,128)(2,1)S(1)} %pad_maximum_fusion.4.q_ref, bf16[8192,512]{1,0:T(8,128)(2,1)} %all-gather.9.cloned.1.call-done.kv_ref), custom_call_target="tpu_custom_call" | custom-call | flops 8589934592 | bytes 8388608 | tf_op jit(solution)/shard_map/flash/pallas_call | solution.py:78
  437.3 13.9 %convolution_add_fusion = f32[1024,4096]{1,0:T(8,128)} fusion(f32[1024,4096]{1,0:T(8,128)} %fusion.6, bf16[1024,256]{1,0:T(8,128)(2,1)S(1)} %flash.3, bf16[2,1,256,4096]{3,2,1,0:T(8,128)(2,1)S(1)} %copy-done.3), kind=kOutput, calls=%fused_computation.10 | convolution fusion | flops 2151677952 | bytes 36175872 | tf_op jit(solution)/shard_map/dot_general | solution.py:124
  451.2 0.0 reduce-scatter.5.cloned.1.call-update
  451.2 0.0 all-gather.11.cloned.1.call-start
  451.3 116.0 %reduce-scatter.5.cloned.1.call-done = f32[64,4096]{1,0:T(8,128)} async-done(((f32[1024,4096]{1,0:T(8,128)}), f32[64,4096]{1,0:T(8,128)}) %reduce-scatter.5.cloned.1.call-update) | async-done | bytes 1048592 | tf_op jit(solution)/shard_map/reduce_scatter | solution.py:127
  567.3 2.2 add_convert_fusion
  569.5 0.0 all-gather.11.cloned.1.call-update
  569.6 1.5 maximum_maximum_fusion
  571.1 68.8 %all-gather.11.cloned.1.call-done = bf16[1024,4096]{1,0:T(8,128)(2,1)} async-done(((bf16[64,4096]{1,0:T(8,128)(2,1)}), bf16[1024,4096]{1,0:T(8,128)(2,1)}) %all-gather.11.cloned.1.call-update) | async-done | bytes 8388624 | tf_op jit(solution)/shard_map/all_gather | solution.py:130
  639.8 7.9 %copy.26 = bf16[1024,4096]{1,0:T(8,128)(2,1)} copy(bf16[1024,4096]{1,0:T(8,128)(2,1)} %all-gather.11.cloned.1.call-done) | data formatting | bytes 16777216
  (37 shorter events, 0.1 us)
Async XLA Ops:
  7.2 5.8 copy-start.10
  7.2 83.1 %all-gather.5.cloned.1.call-start = ((), (), s32[]{:S(2)}) async-start(), calls=%async_computation.2 | async-start | bytes 9437184 | tf_op jit(solution)/shard_map/all_gather | solution.py:118
  23.6 6.5 copy-start.1
  23.6 7.6 %copy-start.11 = (bf16[2,4096,1,256]{3,1,2,0:T(8,128)(2,1)S(1)}, bf16[2,4096,1,256]{3,1,2,0:T(8,128)(2,1)}, u32[]{:S(2)}) copy-start(bf16[2,4096,1,256]{3,1,2,0:T(8,128)(2,1)} %param.13) | copy-start | bytes 12582916
  31.1 7.2 %copy-start.8 = (bf16[1024,256]{1,0:T(8,128)(2,1)}, bf16[1024,256]{1,0:T(8,128)(2,1)S(1)}, u32[]{:S(2)}) copy-start(bf16[1024,256]{1,0:T(8,128)(2,1)S(1)} %fusion.56) | copy-start | bytes 1572868
  31.1 2.4 copy-start.13
  38.3 0.7 copy-start.4
  38.3 0.8 copy-start.6
  40.2 212.7 %reduce-scatter.3.cloned.1.call-start = ((), (), s32[]{:S(2)}) async-start(), calls=%async_computation.3 | async-start | bytes 17825792 | tf_op jit(solution)/shard_map/reduce_scatter | solution.py:127
  40.7 28.2 %slice-start = ((s8[16777216]{0:T(1024)(128)(4,1)}), s8[4194304]{0:T(1024)(128)(4,1)S(1)}, s32[]{:S(2)}) async-start(s8[16777216]{0:T(1024)(128)(4,1)} %bitcast.140), calls=%async_computation.8 | async-start | bytes 8388608
  40.7 28.1 %slice-start.1 = ((s8[16777216]{0:T(1024)(128)(4,1)}), s8[4194304]{0:T(1024)(128)(4,1)S(1)}, s32[]{:S(2)}) async-start(s8[16777216]{0:T(1024)(128)(4,1)} %bitcast.140), calls=%async_computation.9 | async-start | bytes 8388608
  40.7 28.1 %slice-start.2 = ((s8[16777216]{0:T(1024)(128)(4,1)}), s8[4194304]{0:T(1024)(128)(4,1)S(1)}, s32[]{:S(2)}) async-start(s8[16777216]{0:T(1024)(128)(4,1)} %bitcast.140), calls=%async_computation.10 | async-start | bytes 8388608
  53.4 15.4 %slice-start.3 = ((s8[16777216]{0:T(1024)(128)(4,1)}), s8[4194304]{0:T(1024)(128)(4,1)S(1)}, s32[]{:S(2)}) async-start(s8[16777216]{0:T(1024)(128)(4,1)} %bitcast.140), calls=%async_computation.11 | async-start | bytes 8388608
  90.3 32.6 %copy-start.2 = (bf16[2,1,256,4096]{3,2,1,0:T(8,128)(2,1)S(1)}, bf16[2,1,256,4096]{3,2,1,0:T(8,128)(2,1)}, u32[]{:S(2)}) copy-start(bf16[2,1,256,4096]{3,2,1,0:T(8,128)(2,1)} %param.15) | copy-start | bytes 12582916
  136.8 188.8 %all-gather.7.cloned.1.call-start = ((), (), s32[]{:S(2)}) async-start(), calls=%async_computation.4 | async-start | bytes 8912896 | tf_op jit(solution)/shard_map/all_gather | solution.py:130
  255.2 149.2 %all-gather.9.cloned.1.call-start = ((), (), s32[]{:S(2)}) async-start(), calls=%async_computation.5 | async-start | bytes 9437184 | tf_op jit(solution)/shard_map/all_gather | solution.py:118
  341.2 6.5 copy-start
  341.2 7.6 %copy-start.12 = (bf16[2,4096,1,256]{3,1,2,0:T(8,128)(2,1)S(1)}, bf16[2,4096,1,256]{3,1,2,0:T(8,128)(2,1)}, u32[]{:S(2)}) copy-start(bf16[2,4096,1,256]{3,1,2,0:T(8,128)(2,1)} %param.13) | copy-start | bytes 12582916
  348.8 2.3 copy-start.14
  357.1 210.2 %reduce-scatter.5.cloned.1.call-start = ((), (), s32[]{:S(2)}) async-start(), calls=%async_computation.6 | async-start | bytes 17825792 | tf_op jit(solution)/shard_map/reduce_scatter | solution.py:127
  357.4 28.2 %slice-start.4 = ((s8[16777216]{0:T(1024)(128)(4,1)}), s8[4194304]{0:T(1024)(128)(4,1)S(1)}, s32[]{:S(2)}) async-start(s8[16777216]{0:T(1024)(128)(4,1)} %bitcast.142), calls=%async_computation.12 | async-start | bytes 8388608
  357.4 28.2 %slice-start.5 = ((s8[16777216]{0:T(1024)(128)(4,1)}), s8[4194304]{0:T(1024)(128)(4,1)S(1)}, s32[]{:S(2)}) async-start(s8[16777216]{0:T(1024)(128)(4,1)} %bitcast.142), calls=%async_computation.13 | async-start | bytes 8388608
  357.4 28.2 %slice-start.6 = ((s8[16777216]{0:T(1024)(128)(4,1)}), s8[4194304]{0:T(1024)(128)(4,1)S(1)}, s32[]{:S(2)}) async-start(s8[16777216]{0:T(1024)(128)(4,1)} %bitcast.142), calls=%async_computation.14 | async-start | bytes 8388608
  370.1 15.4 %slice-start.7 = ((s8[16777216]{0:T(1024)(128)(4,1)}), s8[4194304]{0:T(1024)(128)(4,1)S(1)}, s32[]{:S(2)}) async-start(s8[16777216]{0:T(1024)(128)(4,1)} %bitcast.142), calls=%async_computation.15 | async-start | bytes 8388608
  404.4 32.9 %copy-start.3 = (bf16[2,1,256,4096]{3,2,1,0:T(8,128)(2,1)S(1)}, bf16[2,1,256,4096]{3,2,1,0:T(8,128)(2,1)}, u32[]{:S(2)}) copy-start(bf16[2,1,256,4096]{3,2,1,0:T(8,128)(2,1)} %param.15) | copy-start | bytes 12582916
  451.2 118.4 %copy-start.5 = (bf16[1024,1,128]{2,0,1:T(8,128)(2,1)S(1)}, bf16[1024,1,128]{2,0,1:T(8,128)(2,1)}, u32[]{:S(2)}) copy-start(bf16[1024,1,128]{2,0,1:T(8,128)(2,1)} %copy-done.4) | copy-start | bytes 786436
  451.2 118.4 %copy-start.7 = (bf16[1024,1,128]{2,0,1:T(8,128)(2,1)S(1)}, bf16[1024,1,128]{2,0,1:T(8,128)(2,1)}, u32[]{:S(2)}) copy-start(bf16[1024,1,128]{2,0,1:T(8,128)(2,1)} %copy-done.6) | copy-start | bytes 786436
  451.2 118.4 %copy-start.9 = (bf16[1024,256]{1,0:T(8,128)(2,1)S(1)}, bf16[1024,256]{1,0:T(8,128)(2,1)}, u32[]{:S(2)}) copy-start(bf16[1024,256]{1,0:T(8,128)(2,1)} %copy-done.8) | copy-start | bytes 1572868
  451.2 188.6 %all-gather.11.cloned.1.call-start = ((), (), s32[]{:S(2)}) async-start(), calls=%async_computation.7 | async-start | bytes 8912896 | tf_op jit(solution)/shard_map/all_gather | solution.py:130
Sparse Core Ops, SparseCore 0:
  40.3 49.9 all-gather.4
  137.0 115.8 reduce-scatter.2
  255.6 69.9 all-gather.6
  357.2 47.1 all-gather.8
  451.3 115.8 reduce-scatter.4
  569.9 69.9 all-gather.10

commit v3 on v2

--- a/solution.py
+++ b/solution.py
@@ -38,6 +38,7 @@
 LOG2E = 1.4426950408889634
 KEY_BLOCK = 1024
 ROW_BLOCK = 256
+CHUNK_ROWS = 128
 
 
 def flash_kernel(seq_tokens, q_ref, kv_ref, out_ref):
@@ -85,6 +86,177 @@
         cost_estimate=pl.CostEstimate(flops=4 * tok_count * kv_full.shape[0] * head_dim, bytes_accessed=kv_full.size * 2, transcendentals=tok_count * kv_full.shape[0]),
         name='flash',
     )(q_rot, kv_full)
+
+
+RING = 4
+HALVES = 2
+DIRS = 2
+STEPS = 8
+
+
+def tail_kernel(layer, chunk_rows, hid_ref, att_ref, x_ref, wd_ref, wo_ref, out_ref, part, xbuf, wbuf, recv_a, recv_b, load_sem, store_sem, send_sem, recv_sem):
+    tok_count, d_model = xbuf.shape
+    ff_local = hid_ref.shape[1]
+    chunk_count = tok_count // chunk_rows
+    quarter, eighth = chunk_rows // RING, chunk_rows // (2 * RING)
+    half_cols = d_model // HALVES
+    piece_cols = half_cols // RING
+    my_head = lax.axis_index('head')
+    pos_z, pos_y = my_head // RING, my_head % RING
+    sign = (1, -1)
+
+    def y_peer(d):
+        return pos_z * RING + (pos_y + sign[d] + RING) % RING
+
+    def z_peer(d):
+        return ((pos_z + sign[d] + RING) % RING) * RING + pos_y
+
+    first_pos, second_pos = (pos_y, pos_z), (pos_z, pos_y)
+    first_peer, second_peer = (y_peer, z_peer), (z_peer, y_peer)
+
+    loads = [
+        pltpu.make_async_copy(wd_ref.at[layer], wbuf.at[pl.ds(0, ff_local), :], load_sem.at[0]),
+        pltpu.make_async_copy(wo_ref.at[layer, 0], wbuf.at[pl.ds(ff_local, wo_ref.shape[2]), :], load_sem.at[1]),
+        pltpu.make_async_copy(x_ref, xbuf, load_sem.at[2]),
+    ]
+    for load in loads:
+        load.start()
+    barrier = pltpu.get_barrier_semaphore()
+    for peer in (y_peer, z_peer):
+        for d in range(DIRS):
+            pl.semaphore_signal(barrier, inc=1, device_id={'head': peer(d)}, device_id_type=pl.DeviceIdType.MESH)
+    pl.semaphore_wait(barrier, 2 * DIRS)
+    for load in loads:
+        load.wait()
+
+    def rows_of(chunk, piece, offset, count):
+        return pl.ds(pl.multiple_of(chunk * chunk_rows + piece * quarter + offset, eighth), count)
+
+    def cols_of(h, piece):
+        return pl.ds(pl.multiple_of(h * half_cols + piece * piece_cols, piece_cols), piece_cols)
+
+    def half_of(h):
+        return pl.ds(h * half_cols, half_cols)
+
+    def message(step, chunk, h, d):
+        p1, p2, s = first_pos[h], second_pos[h], sign[d]
+        far1, near1, behind1 = (p1 + 2) % RING, (p1 + s + RING) % RING, (p1 - s + RING) % RING
+        far2, near2, behind2 = (p2 + 2) % RING, (p2 + s + RING) % RING, (p2 - s + RING) % RING
+        if step == 0:
+            src, dst = part.at[rows_of(chunk, far1, d * eighth, eighth), half_of(h)], recv_a.at[chunk, h, d, pl.ds(quarter, eighth), :]
+        elif step == 1:
+            src, dst = part.at[rows_of(chunk, near1, 0, quarter), half_of(h)], recv_a.at[chunk, h, d, pl.ds(0, quarter), :]
+        elif step == 2:
+            src, dst = part.at[rows_of(chunk, p1, d * eighth, eighth), cols_of(h, far2)], recv_b.at[chunk, h, d, pl.ds(quarter, eighth), :]
+        elif step == 3:
+            src, dst = part.at[rows_of(chunk, p1, 0, quarter), cols_of(h, near2)], recv_b.at[chunk, h, d, pl.ds(0, quarter), :]
+        elif step == 4:
+            src = dst = xbuf.at[rows_of(chunk, p1, 0, quarter), cols_of(h, p2)]
+        elif step == 5:
+            src = dst = xbuf.at[rows_of(chunk, p1, d * eighth, eighth), cols_of(h, behind2)]
+        elif step == 6:
+            src = dst = xbuf.at[rows_of(chunk, p1, 0, quarter), half_of(h)]
+        else:
+            src = dst = xbuf.at[rows_of(chunk, behind1, d * eighth, eighth), half_of(h)]
+        peer = (first_peer if step in (0, 1, 6, 7) else second_peer)[h](d)
+        return pltpu.make_async_remote_copy(
+            src_ref=src, dst_ref=dst, send_sem=send_sem.at[chunk, step, h * DIRS + d], recv_sem=recv_sem.at[chunk, step, h * DIRS + d],
+            device_id={'head': peer}, device_id_type=pl.DeviceIdType.MESH)
+
+    def project(chunk):
+        rows = pl.ds(pl.multiple_of(chunk * chunk_rows, chunk_rows), chunk_rows)
+
+        def one_tile(i, carry):
+            cols = pl.ds(pl.multiple_of(i * piece_cols, piece_cols), piece_cols)
+            total = jnp.dot(hid_ref[rows, :], wbuf[:ff_local, cols], preferred_element_type=jnp.float32)
+            part[rows, cols] = total + jnp.dot(att_ref[rows, :], wbuf[ff_local:, cols], preferred_element_type=jnp.float32)
+            return carry
+
+        lax.fori_loop(0, d_model // piece_cols, one_tile, 0)
+
+    def store(chunk):
+        rows = pl.ds(pl.multiple_of(chunk * chunk_rows, chunk_rows), chunk_rows)
+        return pltpu.make_async_copy(xbuf.at[rows, :], out_ref.at[rows, :], store_sem.at[chunk])
+
+    def stage(number, chunk):
+        if number == 0:
+            project(chunk)
+        for h in range(HALVES):
+            p1, p2 = first_pos[h], second_pos[h]
+            if number:
+                for d in range(DIRS):
+                    message(number - 1, chunk, h, d).wait_recv()
+            if number in (1, 3):
+                for d in range(DIRS):
+                    if number == 1:
+                        rows, cols, arrived = rows_of(chunk, (p1 + sign[d] + RING) % RING, d * eighth, eighth), half_of(h), recv_a
+                    else:
+                        rows, cols, arrived = rows_of(chunk, p1, d * eighth, eighth), cols_of(h, (p2 + sign[d] + RING) % RING), recv_b
+                    part[rows, cols] = part[rows, cols] + arrived[chunk, h, d, pl.ds(quarter, eighth), :]
+            if number == 2:
+                rows = rows_of(chunk, p1, 0, quarter)
+                part[rows, half_of(h)] = part[rows, half_of(h)] + recv_a[chunk, h, 0, pl.ds(0, quarter), :] + recv_a[chunk, h, 1, pl.ds(0, quarter), :]
+            if number == 4:
+                rows, cols = rows_of(chunk, p1, 0, quarter), cols_of(h, p2)
+                total = part[rows, cols] + recv_b[chunk, h, 0, pl.ds(0, quarter), :] + recv_b[chunk, h, 1, pl.ds(0, quarter), :]
+                update = total.astype(jnp.bfloat16).astype(jnp.float32)
+                xbuf[rows, cols] = (xbuf[rows, cols].astype(jnp.float32) + update).astype(jnp.bfloat16)
+            if number < STEPS:
+                for d in range(DIRS):
+                    message(number, chunk, h, d).start()
+        if number == STEPS:
+            store(chunk).start()
+
+    def tick(t, carry):
+        for number in range(STEPS, -1, -1):
+            chunk = t - number
+
+            @pl.when(jnp.logical_and(chunk >= 0, chunk < chunk_count))
+            def _():
+                stage(number, chunk)
+        return carry
+
+    lax.fori_loop(0, chunk_count + STEPS, tick, 0)
+
+    def drain(chunk, carry):
+        for step in range(STEPS):
+            for h in range(HALVES):
+                for d in range(DIRS):
+                    message(step, chunk, h, d).wait_send()
+        store(chunk).wait()
+        return carry
+
+    lax.fori_loop(0, chunk_count, drain, 0)
+
+
+def layer_tail(layer, hidden, attn_heads, x_cur, w_down, w_o):
+    tok_count, d_model = x_cur.shape
+    chunk_rows = min(CHUNK_ROWS, tok_count)
+    chunk_count = tok_count // chunk_rows
+    depth = hidden.shape[1] + attn_heads.shape[1]
+    landed = 3 * chunk_rows // (2 * RING)
+    any_spec = pl.BlockSpec(memory_space=pl.ANY)
+    vmem_spec = pl.BlockSpec(memory_space=pltpu.VMEM)
+    return pl.pallas_call(
+        functools.partial(tail_kernel, layer, chunk_rows),
+        out_shape=jax.ShapeDtypeStruct((tok_count, d_model), jnp.bfloat16),
+        in_specs=[vmem_spec, vmem_spec, any_spec, any_spec, any_spec],
+        out_specs=any_spec,
+        scratch_shapes=[
+            pltpu.VMEM((tok_count, d_model), jnp.float32),
+            pltpu.VMEM((tok_count, d_model), jnp.bfloat16),
+            pltpu.VMEM((depth, d_model), jnp.bfloat16),
+            pltpu.VMEM((chunk_count, HALVES, DIRS, landed, d_model // HALVES), jnp.float32),
+            pltpu.VMEM((chunk_count, HALVES, DIRS, landed, d_model // HALVES // RING), jnp.float32),
+            pltpu.SemaphoreType.DMA((3,)),
+            pltpu.SemaphoreType.DMA((chunk_count,)),
+            pltpu.SemaphoreType.DMA((chunk_count, STEPS, HALVES * DIRS)),
+            pltpu.SemaphoreType.DMA((chunk_count, STEPS, HALVES * DIRS)),
+        ],
+        compiler_params=pltpu.CompilerParams(collective_id=layer, has_side_effects=True, vmem_limit_bytes=63 * 1024 * 1024),
+        cost_estimate=pl.CostEstimate(flops=2 * tok_count * depth * d_model, bytes_accessed=depth * d_model * 2, transcendentals=0),
+        name='tail',
+    )(hidden, attn_heads, x_cur, w_down, w_o)
 
 
 def solution(mesh):
@@ -120,14 +292,7 @@
             gate_f32 = jnp.dot(normed, w_gate[layer], preferred_element_type=jnp.float32)
             up_f32 = jnp.dot(normed, w_up[layer], preferred_element_type=jnp.float32)
             hidden = (jax.nn.silu(gate_f32) * up_f32).astype(jnp.bfloat16)
-            part_sum = jnp.dot(hidden, w_down[layer], preferred_element_type=jnp.float32)
-            part_sum = part_sum + jnp.dot(attn_heads, w_o[layer].reshape(q_local * head_dim, d_model), preferred_element_type=jnp.float32)
-            head_count = lax.axis_size('head')
-            own_rows = tok_count // head_count
-            update = lax.psum_scatter(part_sum, 'head', scatter_dimension=0, tiled=True).astype(jnp.bfloat16)
-            x_own = lax.dynamic_slice_in_dim(x_cur, lax.axis_index('head') * own_rows, own_rows, axis=0)
-            x_own = (x_own.astype(jnp.float32) + update.astype(jnp.float32)).astype(jnp.bfloat16)
-            x_cur = lax.all_gather(x_own, 'head', axis=0, tiled=True)
+            x_cur = layer_tail(layer, hidden, attn_heads, x_cur, w_down, w_o)
             k_list.append(k_rot)
             v_list.append(v_heads)
         return x_cur, jnp.stack(k_list), jnp.stack(v_list)

time: 664 us -> 570 us (0.86)
  waiting for transfers between devices: 384 us -> 41.1 us
  Pallas kernels: 65.5 us -> 377 us
  matrix products: 133 us -> 75.3 us
    pallas_call x0 -> x2, Pallas kernels: none -> 312 us  [layer_tail(): pl.pallas_call(functools.partial(tail_kernel, layer, chunk_rows), out_sha...]
    reduce_scatter x2 -> x0, waiting for transfers between devices: 232 us -> none  [local_forward(): lax.psum_scatter(part_sum, 'head', scatter_dimension=0, tiled=True)]
    all_gather x2 -> x0, waiting for transfers between devices: 139 us -> none  [local_forward(): x_cur = lax.all_gather(x_own, 'head', axis=0, tiled=True)]
    dot_general x4 -> x0, matrix products: 55 us -> none  [the longest x2 27.8 us: local_forward(): jnp.dot(attn_heads, w_o[layer].reshape(q_local * head_dim, d_model), pref...]
    all_gather x2, waiting for transfers between devices: 13 us -> 41.1 us  [local_forward(): kv_full = lax.all_gather(kv_own, 'seq', axis=0, tiled=True)]
    dot_general x2, matrix products: 12.9 us -> 4.66 us  [local_forward(): jnp.dot(normed, w_v[layer].reshape(d_model, kv_local * head_dim), preferr...]
    dot_general x2, matrix products: 4.66 us -> 12.3 us  [local_forward(): jnp.dot(normed, w_k[layer].reshape(d_model, kv_local * head_dim), preferr...]
  transfers between devices with their start and end apart: 6 -> 2, of which waited for: 6 -> 2; matrix products, arithmetic and copies ran while one was open for 13% -> 10% of each run, Pallas kernels for 0% -> 0%
where the time goes in v3:
time: 570 us; the launch traced here: 562 us
  Pallas kernels  377 us (66%)
  matrix products  75.3 us (13%)
  other arithmetic  41.2 us (7%)
  waiting for transfers between devices  41.1 us (7%)
  between operations  14.8 us (3%)
  local copies, waits for them, and re-layouts  11.7 us (2%)
    pallas_call x2, Pallas kernels, layer_tail(): pl.pallas_call(functools.partial(tail_kernel, layer, chunk_rows), out_sha...  312 us
    pallas_call x2, Pallas kernels, flash_attention(): pl.pallas_call(functools.partial(flash_kernel, tok_count), out_shape=jax....  64.9 us
    all_gather x2, waiting for transfers between devices, local_forward(): kv_full = lax.all_gather(kv_own, 'seq', axis=0, tiled=True)  41.1 us
    dot_general x2, matrix products, local_forward(): jnp.dot(normed, w_gate[layer], preferred_element_type=jnp.float32)  28 us
    dot_general x2, matrix products, local_forward(): up_f32 = jnp.dot(normed, w_up[layer], preferred_element_type=jnp.float32)  25.6 us
    convert_element_type x2, other arithmetic, rms_norm(): return (x_f32 * inv_rms * gain_row.astype(jnp.float32)).astype(jnp.bfloat16)  21.2 us
    dot_general x2, matrix products, local_forward(): jnp.dot(normed, w_k[layer].reshape(d_model, kv_local * head_dim), preferr...  12.3 us
    unnamed x29, local copies, waits for them, and re-layouts  11.7 us
  transfers between devices with their start and end apart: 2, of which 2 were waited for; matrix products, arithmetic and copies ran while one was open for 10% of the time, Pallas kernels for 0%

profile of v3, /device:TPU:6, one launch (start us, length us, event | category | flops | bytes accessed | tf_op | source)
XLA Modules:
  0.0 561.6 jit_solution(17799012170617451083)
XLA Ops:
  7.2 0.0 copy-start.6
  7.2 0.0 all-gather.3.cloned.1.call-start
  7.2 0.8 slice_convert_fusion
  8.1 5.1 fusion
  13.1 0.0 copy-done.6
  13.2 0.0 copy-start.7
  13.2 10.7 %fusion.2 = bf16[1024,4096]{1,0:T(8,128)(2,1)} fusion(bf16[1024,4096]{1,0:T(8,128)(2,1)} %x_ref.1, f32[4096]{0:T(1024)S(1)} %bitcast.125, f32[1024]{0:T(1024)S(1)} %add_rsqrt_fusion.1), kind=kLoop, calls=%fused_computation.6 | loop fusion | flops 16777216 | bytes 16797696 | tf_op jit(solution)/shard_map/convert_element_type | solution.py:17
  23.8 0.0 copy-done.7
  23.8 0.0 copy-start.3
  23.8 0.0 copy-start.8
  23.8 5.9 %fusion.73 = f32[1024,1,256]{2,0,1:T(8,128)S(1)} fusion(bf16[1024,4096]{1,0:T(8,128)(2,1)} %fusion.2, bf16[2,4096,1,256]{3,1,2,0:T(8,128)(2,1)S(1)} %copy-done.7), kind=kOutput, calls=%fused_computation.53 | convolution fusion | flops 2148007936 | bytes 11534336 | tf_op jit(solution)/shard_map/dot_general | solution.py:284
  29.7 0.0 copy-done.3
  29.7 1.1 copy-done.8
  30.8 0.0 copy-start.10
  30.8 2.3 fusion.79
  33.1 0.0 copy-done.10
  33.2 2.3 fusion.46
  35.5 0.0 copy-start.4
  35.5 2.5 fusion.103
  38.0 0.0 copy-done.4
  38.0 1.1 pad_maximum_fusion
  39.1 0.0 all-gather.3.cloned.1.call-update
  39.1 0.2 all-gather.5.cloned.1.call-start
  39.3 0.1 pad_maximum_fusion.3.q_ref
  39.4 12.6 %fusion.10 = f32[1024,1024]{1,0:T(8,128)S(1)} fusion(bf16[1024,4096]{1,0:T(8,128)(2,1)} %fusion.2, bf16[2,4096,1024]{2,1,0:T(8,128)(2,1)} %param.17), kind=kOutput, calls=%fused_computation.14 | convolution fusion | flops 8589934592 | bytes 20971520 | tf_op jit(solution)/shard_map/dot_general | solution.py:293
  52.0 15.3 %multiply_convert_fusion.1.hid_ref = bf16[1024,1024]{1,0:T(8,128)(2,1)} fusion(f32[1024,1024]{1,0:T(8,128)S(1)} %fusion.10, bf16[1024,4096]{1,0:T(8,128)(2,1)} %fusion.2, bf16[2,4096,1024]{2,1,0:T(8,128)(2,1)} %param.16), kind=kOutput, calls=%fused_computation.23 | convolution fusion | flops 8596226048 | bytes 23068672 | tf_op jit(solution)/shard_map/dot_general | solution.py:292
  67.2 22.0 %all-gather.3.cloned.1.call-done.kv_ref = bf16[8192,512]{1,0:T(8,128)(2,1)} async-done(((bf16[1024,512]{1,0:T(8,128)(2,1)}), bf16[8192,512]{1,0:T(8,128)(2,1)}) %all-gather.3.cloned.1.call-update) | async-done | bytes 8388624 | tf_op jit(solution)/shard_map/all_gather | solution.py:290
  89.2 32.5 %flash.2.att_ref = bf16[1024,256]{1,0:T(8,128)(2,1)S(1)} custom-call(bf16[1024,256]{1,0:T(8,128)(2,1)S(1)} %pad_maximum_fusion.3.q_ref, bf16[8192,512]{1,0:T(8,128)(2,1)} %all-gather.3.cloned.1.call-done.kv_ref), custom_call_target="tpu_custom_call" | custom-call | flops 8589934592 | bytes 8388608 | tf_op jit(solution)/shard_map/flash/pallas_call | solution.py:79
  121.7 0.0 copy-start.1
  121.7 0.8 copy-done.1
  122.5 156.4 %tail.2.x_ref = bf16[1024,4096]{1,0:T(8,128)(2,1)} custom-call(bf16[1024,1024]{1,0:T(8,128)(2,1)} %multiply_convert_fusion.1.hid_ref, bf16[1024,256]{1,0:T(8,128)(2,1)} %copy-done.1, bf16[1024,4096]{1,0:T(8,128)(2,1)} %x_ref.1, bf16[2,1024,4096]{2,1,0:T(8,128)(2,1)} %wd_ref.3, bf16[2,1,256,4096]{3,2,1,0:T(8,128)(2,1)} %wo_ref.3), custom_call_target="tpu_custom_call" | custom-call | flops 10737418240 | bytes 10485760 | tf_op jit(solution)/shard_map/tail/pallas_call | solution.py:240
  278.9 5.1 fusion.3
  283.9 10.5 %fusion.5 = bf16[1024,4096]{1,0:T(8,128)(2,1)} fusion(bf16[1024,4096]{1,0:T(8,128)(2,1)} %tail.2.x_ref, f32[4096]{0:T(1024)S(1)} %bitcast.124, f32[1024]{0:T(1024)S(1)} %add_rsqrt_fusion), kind=kLoop, calls=%fused_computation.9 | loop fusion | flops 16777216 | bytes 16797696 | tf_op jit(solution)/shard_map/convert_element_type | solution.py:17
  294.5 0.0 copy-start.2
  294.5 0.0 copy-start.9
  294.5 6.5 %fusion.61 = f32[1024,1,256]{2,0,1:T(8,128)S(1)} fusion(bf16[1024,4096]{1,0:T(8,128)(2,1)} %fusion.5, bf16[2,4096,1,256]{3,1,2,0:T(8,128)(2,1)} %param.13), kind=kOutput, calls=%fused_computation.49 | convolution fusion | flops 2148007936 | bytes 11534336 | tf_op jit(solution)/shard_map/dot_general | solution.py:284
  300.9 0.0 copy-done.2
  300.9 1.1 copy-done.9
  302.0 0.0 copy-start.11
  302.0 2.3 fusion.67
  304.4 0.0 copy-done.11
  304.4 0.0 copy-start.5
  304.4 2.3 fusion.55
  306.7 2.7 fusion.111
  309.5 1.1 pad_maximum_fusion.1
  310.5 0.0 all-gather.5.cloned.1.call-update
  310.6 0.1 pad_maximum_fusion.4.q_ref
  310.6 0.0 copy-done.5
  310.6 0.0 slice-start
  310.7 1.5 maximum_maximum_fusion
  312.2 0.0 slice-start.1
  312.2 13.1 %fusion.6 = f32[1024,1024]{1,0:T(8,128)S(1)} fusion(bf16[1024,4096]{1,0:T(8,128)(2,1)} %fusion.5, bf16[2,4096,1024]{2,1,0:T(8,128)(2,1)} %param.17), kind=kOutput, calls=%fused_computation.10 | convolution fusion | flops 8589934592 | bytes 20971520 | tf_op jit(solution)/shard_map/dot_general | solution.py:293
  325.2 0.0 slice-done
  325.2 0.0 slice-done.1
  325.3 12.8 %multiply_convert_fusion.hid_ref = bf16[1024,1024]{1,0:T(8,128)(2,1)} fusion(f32[1024,1024]{1,0:T(8,128)S(1)} %fusion.6, bf16[1024,4096]{1,0:T(8,128)(2,1)S(1)} %bitcast.113, bf16[2,4096,1024]{2,1,0:T(8,128)(2,1)} %param.16), kind=kOutput, calls=%fused_computation.22 | convolution fusion | flops 8596226048 | bytes 23068672 | tf_op jit(solution)/shard_map/dot_general | solution.py:292
  338.0 19.1 %all-gather.5.cloned.1.call-done.kv_ref = bf16[8192,512]{1,0:T(8,128)(2,1)} async-done(((bf16[1024,512]{1,0:T(8,128)(2,1)}), bf16[8192,512]{1,0:T(8,128)(2,1)}) %all-gather.5.cloned.1.call-update) | async-done | bytes 8388624 | tf_op jit(solution)/shard_map/all_gather | solution.py:290
  357.1 32.5 %flash.3.att_ref = bf16[1024,256]{1,0:T(8,128)(2,1)S(1)} custom-call(bf16[1024,256]{1,0:T(8,128)(2,1)S(1)} %pad_maximum_fusion.4.q_ref, bf16[8192,512]{1,0:T(8,128)(2,1)} %all-gather.5.cloned.1.call-done.kv_ref), custom_call_target="tpu_custom_call" | custom-call | flops 8589934592 | bytes 8388608 | tf_op jit(solution)/shard_map/flash/pallas_call | solution.py:79
  389.6 0.0 copy-start
  389.6 0.8 copy-done
  390.4 156.0 %tail.3 = bf16[1024,4096]{1,0:T(8,128)(2,1)} custom-call(bf16[1024,1024]{1,0:T(8,128)(2,1)} %multiply_convert_fusion.hid_ref, bf16[1024,256]{1,0:T(8,128)(2,1)} %copy-done, bf16[1024,4096]{1,0:T(8,128)(2,1)} %tail.2.x_ref, bf16[2,1024,4096]{2,1,0:T(8,128)(2,1)} %wd_ref.3, bf16[2,1,256,4096]{3,2,1,0:T(8,128)(2,1)} %wo_ref.3), custom_call_target="tpu_custom_call" | custom-call | flops 10737418240 | bytes 10485760 | tf_op jit(solution)/shard_map/tail/pallas_call | solution.py:240
  546.5 7.9 %copy.26 = bf16[1024,4096]{1,0:T(8,128)(2,1)} copy(bf16[1024,4096]{1,0:T(8,128)(2,1)} %tail.3) | data formatting | bytes 16777216
  (5 shorter events, 0.0 us)
Async XLA Ops:
  7.2 6.0 %copy-start.6 = (s32[1024]{0:T(1024)S(1)}, s32[1024]{0:T(1024)}, u32[]{:S(2)}) copy-start(s32[1024]{0:T(1024)} %param.11) | copy-start | bytes 12292
  7.2 82.0 %all-gather.3.cloned.1.call-start = ((), (), s32[]{:S(2)}) async-start(), calls=%async_computation | async-start | bytes 9437184 | tf_op jit(solution)/shard_map/all_gather | solution.py:290
  13.2 10.7 %copy-start.7 = (bf16[2,4096,1,256]{3,1,2,0:T(8,128)(2,1)S(1)}, bf16[2,4096,1,256]{3,1,2,0:T(8,128)(2,1)}, u32[]{:S(2)}) copy-start(bf16[2,4096,1,256]{3,1,2,0:T(8,128)(2,1)} %param.13) | copy-start | bytes 12582916
  23.8 5.9 %copy-start.3 = (bf16[1024,4096]{1,0:T(8,128)(2,1)S(1)}, bf16[1024,4096]{1,0:T(8,128)(2,1)}, u32[]{:S(2)}) copy-start(bf16[1024,4096]{1,0:T(8,128)(2,1)} %fusion.2) | copy-start | bytes 25165828
  23.8 7.0 %copy-start.8 = (bf16[2,4096,1,256]{3,1,2,0:T(8,128)(2,1)S(1)}, bf16[2,4096,1,256]{3,1,2,0:T(8,128)(2,1)}, u32[]{:S(2)}) copy-start(bf16[2,4096,1,256]{3,1,2,0:T(8,128)(2,1)} %param.12) | copy-start | bytes 12582916
  30.8 2.3 copy-start.10
  35.5 2.5 copy-start.4
  39.1 318.0 %all-gather.5.cloned.1.call-start = ((), (), s32[]{:S(2)}) async-start(), calls=%async_computation.1 | async-start | bytes 9437184 | tf_op jit(solution)/shard_map/all_gather | solution.py:290
  121.7 0.8 copy-start.1
  294.5 6.5 %copy-start.2 = (bf16[1024,4096]{1,0:T(8,128)(2,1)S(1)}, bf16[1024,4096]{1,0:T(8,128)(2,1)}, u32[]{:S(2)}) copy-start(bf16[1024,4096]{1,0:T(8,128)(2,1)} %fusion.5) | copy-start | bytes 25165828
  294.5 7.6 %copy-start.9 = (bf16[2,4096,1,256]{3,1,2,0:T(8,128)(2,1)S(1)}, bf16[2,4096,1,256]{3,1,2,0:T(8,128)(2,1)}, u32[]{:S(2)}) copy-start(bf16[2,4096,1,256]{3,1,2,0:T(8,128)(2,1)} %param.12) | copy-start | bytes 12582916
  302.0 2.3 copy-start.11
  304.4 6.3 %copy-start.5 = (bf16[1024,256]{1,0:T(8,128)(2,1)S(1)}, bf16[1024,256]{1,0:T(8,128)(2,1)}, u32[]{:S(2)}) copy-start(bf16[1024,256]{1,0:T(8,128)(2,1)} %copy-done.4) | copy-start | bytes 1572868
  310.6 14.6 %slice-start = ((s8[8388608]{0:T(1024)(128)(4,1)}), s8[4194304]{0:T(1024)(128)(4,1)S(1)}, s32[]{:S(2)}) async-start(s8[8388608]{0:T(1024)(128)(4,1)} %bitcast.112), calls=%async_computation.2 | async-start | bytes 8388608
  312.2 13.1 %slice-start.1 = ((s8[8388608]{0:T(1024)(128)(4,1)}), s8[4194304]{0:T(1024)(128)(4,1)S(1)}, s32[]{:S(2)}) async-start(s8[8388608]{0:T(1024)(128)(4,1)} %bitcast.112), calls=%async_computation.3 | async-start | bytes 8388608
  389.6 0.8 copy-start
Sparse Core Ops, SparseCore 0:
  39.2 49.9 all-gather.2
  310.7 46.4 all-gather.4

commit v4 on v3

--- a/solution.py
+++ b/solution.py
@@ -11,12 +11,6 @@
 EPS = 1e-5
 
 
-def rms_norm(x_in, gain_row):
-    x_f32 = x_in.astype(jnp.float32)
-    inv_rms = lax.rsqrt(jnp.mean(x_f32 * x_f32, axis=-1, keepdims=True) + EPS)
-    return (x_f32 * inv_rms * gain_row.astype(jnp.float32)).astype(jnp.bfloat16)
-
-
 def rope_tables(positions, head_dim):
     half_dim = head_dim // 2
     inv_freq = ROPE_BASE ** (-(jnp.arange(half_dim, dtype=jnp.float32) * 2.0 / head_dim))
@@ -24,68 +18,300 @@
     return jnp.cos(angles), jnp.sin(angles)
 
 
-def apply_rope(heads_in, cos_t, sin_t):
-    half_dim = heads_in.shape[-1] // 2
-    heads_f32 = heads_in.astype(jnp.float32)
-    first_half = heads_f32[..., :half_dim]
-    second_half = heads_f32[..., half_dim:]
-    cos_b = cos_t[..., None, :]
-    sin_b = sin_t[..., None, :]
-    rotated = jnp.concatenate([first_half * cos_b - second_half * sin_b, second_half * cos_b + first_half * sin_b], axis=-1)
-    return rotated.astype(jnp.bfloat16)
-
-
 LOG2E = 1.4426950408889634
-KEY_BLOCK = 1024
-ROW_BLOCK = 256
 CHUNK_ROWS = 128
 
 
-def flash_kernel(seq_tokens, q_ref, kv_ref, out_ref):
-    rows, head_dim = q_ref.shape
+CHIPS = 4
+KV_CHUNKS = 4
+W_TILE = 256
+NORM_ROWS = 64
+
+
+def head_kernel(layer, x_ref, cos_ref, sin_ref, gain_ref, wq_ref, wk_ref, wv_ref, wg_ref, wu_ref, hid_ref, att_ref, k_ref, v_ref,
+                hbuf, xs, wqkv, wtile, kv, qbuf, acc, row_max, row_sum, x_sem, w_sem, t_sem, out_sem, own_send, pass_send, ici_recv, core_recv):
+    tok_count, d_model = hbuf.shape
+    head_dim = qbuf.shape[1]
+    half_dim = head_dim // 2
+    rows_per = tok_count // KV_CHUNKS
+    half_rows = tok_count // 2
     my_seq = lax.axis_index('seq')
-    row_block = pl.program_id(0)
+    chip, core = my_seq // 2, my_seq % 2
+    other = chip * 2 + 1 - core
+    right = ((chip + 1) % CHIPS) * 2 + core
+    left = ((chip + CHIPS - 1) % CHIPS) * 2 + core
+
+    def x_load(i):
+        return pltpu.make_async_copy(x_ref.at[pl.ds(pl.multiple_of(i * rows_per, rows_per), rows_per), :], xs.at[i % 2], x_sem.at[i % 2])
+
+    def tile_load(i, which):
+        ref = (wg_ref, wu_ref)[which]
+        return pltpu.make_async_copy(ref.at[layer, :, pl.ds(pl.multiple_of(i * W_TILE, W_TILE), W_TILE)], wtile.at[i % 2, which], t_sem.at[i % 2, which])
+
+    x_load(0).start()
+    w_loads = [pltpu.make_async_copy(ref.at[layer], wqkv.at[n], w_sem.at[n]) for n, ref in enumerate((wk_ref, wv_ref, wq_ref))]
+    for load in w_loads:
+        load.start()
+    x_load(1).start()
+    for which in range(2):
+        tile_load(0, which).start()
+
+    barrier = pltpu.get_barrier_semaphore()
+    for peer in (left, right, other):
+        pl.semaphore_signal(barrier, inc=1, device_id={'seq': peer}, device_id_type=pl.DeviceIdType.MESH)
+    pl.semaphore_wait(barrier, 3)
+
+    def kv_copy(origin_chip, origin_core, i, to, send, recv):
+        rows = kv.at[pl.ds(pl.multiple_of((origin_chip * 2 + origin_core) * tok_count + i * rows_per, rows_per), rows_per), :]
+        return pltpu.make_async_remote_copy(src_ref=rows, dst_ref=rows, send_sem=send, recv_sem=recv, device_id={'seq': to}, device_id_type=pl.DeviceIdType.MESH)
+
+    def to_right(i):
+        return kv_copy(chip, core, i, right, own_send.at[0, i], ici_recv.at[0, i])
+
+    def to_wrap(i):
+        return kv_copy(chip, core, i, left, own_send.at[1, i], ici_recv.at[2, i])
+
+    def to_other(i):
+        return kv_copy(chip, core, i, other, own_send.at[2, i], core_recv.at[0, i])
+
+    def on_right(i):
+        return kv_copy(chip - 1, core, i, right, pass_send.at[0, i], ici_recv.at[1, i])
+
+    def on_other(back, i):
+        return kv_copy(chip - back, core, i, other, pass_send.at[back, i], core_recv.at[back, i])
+
+    def arrival(back, i):
+        return kv_copy(chip - back, core, i, other, pass_send.at[back, i], ici_recv.at[back - 1, i])
+
+    def serve(back, i):
+        @pl.when(chip >= back)
+        def _():
+            arrival(back, i).wait_recv()
+            on_other(back, i).start()
+        if back == 1:
+            @pl.when(jnp.logical_and(chip >= 1, chip < CHIPS - 1))
+            def _():
+                on_right(i).start()
+
+    def rope(values, rows):
+        cos_t, sin_t = cos_ref[rows, :], sin_ref[rows, :]
+        wide = values.astype(jnp.bfloat16).astype(jnp.float32)
+        first, second = wide[:, :half_dim], wide[:, half_dim:]
+        return jnp.concatenate([first * cos_t - second * sin_t, second * cos_t + first * sin_t], axis=1).astype(jnp.bfloat16)
+
+    gain = gain_ref[pl.ds(layer, 1), :].astype(jnp.float32)
+
+    def prepare(i, carry):
+        x_load(i).wait()
+        rows = pl.ds(pl.multiple_of(i * rows_per, rows_per), rows_per)
+
+        def norm(j, inner):
+            few = pl.ds(pl.multiple_of(j * NORM_ROWS, NORM_ROWS), NORM_ROWS)
+            x_f32 = xs[i % 2, few, :].astype(jnp.float32)
+            inv_rms = lax.rsqrt(jnp.mean(x_f32 * x_f32, axis=-1, keepdims=True) + EPS)
+            hbuf[pl.ds(pl.multiple_of(i * rows_per + j * NORM_ROWS, NORM_ROWS), NORM_ROWS), :] = (x_f32 * inv_rms * gain).astype(jnp.bfloat16)
+            return inner
+
+        lax.fori_loop(0, rows_per // NORM_ROWS, norm, 0)
+
+        @pl.when(i + 2 < KV_CHUNKS)
+        def _():
+            x_load(i + 2).start()
+
+        @pl.when(i == 0)
+        def _():
+            w_loads[0].wait()
+            w_loads[1].wait()
+
+        normed = hbuf[rows, :]
+        own = pl.ds(pl.multiple_of(my_seq * tok_count + i * rows_per, rows_per), rows_per)
+        kv[own, :head_dim] = rope(jnp.dot(normed, wqkv[0], preferred_element_type=jnp.float32), rows)
+        kv[own, head_dim:] = jnp.dot(normed, wqkv[1], preferred_element_type=jnp.float32).astype(jnp.bfloat16)
+
+        @pl.when(chip < CHIPS - 1)
+        def _():
+            to_right(i).start()
+
+        @pl.when(chip == 0)
+        def _():
+            to_wrap(i).start()
+
+        @pl.when(core == 0)
+        def _():
+            to_other(i).start()
+        return carry
+
+    lax.fori_loop(0, KV_CHUNKS, prepare, 0)
+    w_loads[2].wait()
+    own_rows = pl.ds(pl.multiple_of(my_seq * tok_count, tok_count), tok_count)
+    k_store = pltpu.make_async_copy(kv.at[own_rows, pl.ds(0, head_dim)], k_ref, out_sem.at[0])
+    v_store = pltpu.make_async_copy(kv.at[own_rows, pl.ds(head_dim, head_dim)], v_ref, out_sem.at[1])
+    k_store.start()
+    v_store.start()
+
+    def query(i, carry):
+        rows = pl.ds(pl.multiple_of(i * rows_per, rows_per), rows_per)
+        qbuf[rows, :] = rope(jnp.dot(hbuf[rows, :], wqkv[2], preferred_element_type=jnp.float32), rows)
+        return carry
+
+    lax.fori_loop(0, KV_CHUNKS, query, 0)
+
+    def gated(i, carry):
+        for which in range(2):
+            tile_load(i, which).wait()
+
+        @pl.when(i + 1 < wg_ref.shape[2] // W_TILE)
+        def _():
+            for which in range(2):
+                tile_load(i + 1, which).start()
+
+        def rows_step(j, inner):
+            rows = pl.ds(pl.multiple_of(j * rows_per, rows_per), rows_per)
+            normed = hbuf[rows, :]
+            gate = jnp.dot(normed, wtile[i % 2, 0], preferred_element_type=jnp.float32)
+            up = jnp.dot(normed, wtile[i % 2, 1], preferred_element_type=jnp.float32)
+            hid_ref[rows, pl.ds(pl.multiple_of(i * W_TILE, W_TILE), W_TILE)] = (gate * jax.nn.sigmoid(gate) * up).astype(jnp.bfloat16)
+            return inner
+
+        lax.fori_loop(0, KV_CHUNKS, rows_step, 0)
+        serve(1, i)
+        serve(3, i)
+        return carry
+
+    lax.fori_loop(0, KV_CHUNKS, gated, 0)
+
     scale = LOG2E / math.sqrt(head_dim)
-    q_val = q_ref[...]
-
-    def visit(state, key_start, key_count, masked):
-        row_max, row_sum, accum = state
-        keys = kv_ref[pl.ds(key_start, key_count), :head_dim]
-        vals = kv_ref[pl.ds(key_start, key_count), head_dim:]
-        logits = lax.dot_general(q_val, keys, (((1,), (1,)), ((), ())), preferred_element_type=jnp.float32) * scale
+    lanes = row_max.shape[1]
+
+    def attend(key_start, q_half, masked, first):
+        rows = pl.ds(q_half * half_rows, half_rows)
+        some = pl.ds(key_start, half_rows)
+        logits = lax.dot_general(qbuf[rows, :], kv[some, :head_dim], (((1,), (1,)), ((), ())), preferred_element_type=jnp.float32) * scale
         if masked:
-            row_iota = lax.broadcasted_iota(jnp.int32, logits.shape, 0)
-            col_iota = lax.broadcasted_iota(jnp.int32, logits.shape, 1)
-            logits = jnp.where(row_iota >= col_iota, logits, -jnp.inf)
-        new_max = jnp.maximum(row_max, jnp.max(logits, axis=-1, keepdims=True))
-        prob = jnp.exp2(logits - new_max)
-        rescale = jnp.exp2(row_max - new_max)
-        row_sum = row_sum * rescale + jnp.sum(prob, axis=-1, keepdims=True)
-        accum = accum * rescale + jnp.dot(prob.astype(jnp.bfloat16), vals, preferred_element_type=jnp.float32)
-        return new_max, row_sum, accum
-
-    own_start = my_seq * seq_tokens
-    state = (jnp.full((rows, 1), -jnp.inf, jnp.float32), jnp.zeros((rows, 1), jnp.float32), jnp.zeros((rows, head_dim), jnp.float32))
-    diag_start = pl.multiple_of(own_start + row_block * rows, rows)
-    state = visit(state, diag_start, rows, True)
-    state = lax.fori_loop(0, row_block, lambda i, st: visit(st, pl.multiple_of(own_start + i * rows, rows), rows, False), state)
-    past_blocks = own_start // KEY_BLOCK
-    state = lax.fori_loop(0, past_blocks, lambda i, st: visit(st, pl.multiple_of(i * KEY_BLOCK, KEY_BLOCK), KEY_BLOCK, False), state)
-    out_ref[...] = (state[2] / state[1]).astype(jnp.bfloat16)
-
-
-def flash_attention(q_rot, kv_full):
-    tok_count, head_dim = q_rot.shape
+            seen = lax.broadcasted_iota(jnp.int32, logits.shape, 0) >= lax.broadcasted_iota(jnp.int32, logits.shape, 1)
+            logits = jnp.where(seen, logits, -jnp.inf)
+        block_max = jnp.max(logits, axis=-1, keepdims=True)
+        if first:
+            new_max = jnp.broadcast_to(block_max, (half_rows, lanes))
+        else:
+            new_max = jnp.maximum(row_max[rows, :], block_max)
+        prob = jnp.exp2(logits - jnp.concatenate([new_max] * (half_rows // lanes), axis=1))
+        block_sum = jnp.sum(prob, axis=-1, keepdims=True)
+        block_out = jnp.dot(prob.astype(jnp.bfloat16), kv[some, head_dim:], preferred_element_type=jnp.float32)
+        if first:
+            row_sum[rows, :] = jnp.broadcast_to(block_sum, (half_rows, lanes))
+            acc[rows, :] = block_out
+        else:
+            rescale = jnp.exp2(row_max[rows, :] - new_max)
+            row_sum[rows, :] = row_sum[rows, :] * rescale + block_sum
+            acc[rows, :] = acc[rows, :] * jnp.concatenate([rescale] * (head_dim // lanes), axis=1) + block_out
+        row_max[rows, :] = new_max
+
+    own_start = pl.multiple_of(my_seq * tok_count, tok_count)
+    attend(own_start, 0, True, True)
+    attend(own_start, 1, False, True)
+    attend(pl.multiple_of(own_start + half_rows, half_rows), 1, True, False)
+
+    def past(block_chip, block_core):
+        def one(n, carry):
+            start = pl.multiple_of((block_chip * 2 + block_core) * tok_count + n * half_rows, half_rows)
+            attend(start, 0, False, False)
+            attend(start, 1, False, False)
+            return carry
+        lax.fori_loop(0, 2, one, 0)
+
+    def taken(back):
+        for i in range(KV_CHUNKS):
+            kv_copy(chip - back, 1 - core, i, other, pass_send.at[0, i], core_recv.at[back, i]).wait_recv()
+
+    @pl.when(core == 1)
+    def _():
+        taken(0)
+        past(chip, 0)
+
+    for back in (1, 3, 2):
+        if back == 2:
+            for i in range(KV_CHUNKS):
+                serve(2, i)
+
+        @pl.when(chip >= back)
+        def _():
+            past(chip - back, core)
+            taken(back)
+            past(chip - back, 1 - core)
+
+    def finish(i, carry):
+        rows = pl.ds(pl.multiple_of(i * rows_per, rows_per), rows_per)
+        att_ref[rows, :] = (acc[rows, :] / jnp.concatenate([row_sum[rows, :]] * (head_dim // lanes), axis=1)).astype(jnp.bfloat16)
+        return carry
+
+    lax.fori_loop(0, KV_CHUNKS, finish, 0)
+    k_store.wait()
+    v_store.wait()
+    for i in range(KV_CHUNKS):
+        @pl.when(chip < CHIPS - 1)
+        def _():
+            to_right(i).wait_send()
+
+        @pl.when(chip == 0)
+        def _():
+            to_wrap(i).wait_send()
+
+        @pl.when(core == 0)
+        def _():
+            to_other(i).wait_send()
+
+        @pl.when(jnp.logical_and(chip >= 1, chip < CHIPS - 1))
+        def _():
+            on_right(i).wait_send()
+
+        for back in (1, 2, 3):
+            @pl.when(chip >= back)
+            def _():
+                on_other(back, i).wait_send()
+
+
+def layer_head(layer, x_cur, cos_t, sin_t, norm_gain, w_q, w_k, w_v, w_gate, w_up):
+    tok_count, d_model = x_cur.shape
+    head_dim = w_q.shape[2]
+    ff_local = w_gate.shape[2]
+    rows_per = tok_count // KV_CHUNKS
+    any_spec = pl.BlockSpec(memory_space=pl.ANY)
+    vmem_spec = pl.BlockSpec(memory_space=pltpu.VMEM)
+    bf16 = jnp.bfloat16
     return pl.pallas_call(
-        functools.partial(flash_kernel, tok_count),
-        out_shape=jax.ShapeDtypeStruct((tok_count, head_dim), jnp.bfloat16),
-        grid=(tok_count // ROW_BLOCK,),
-        in_specs=[pl.BlockSpec((ROW_BLOCK, head_dim), lambda i: (i, 0)), pl.BlockSpec(kv_full.shape, lambda i: (0, 0))],
-        out_specs=pl.BlockSpec((ROW_BLOCK, head_dim), lambda i: (i, 0)),
-        compiler_params=pltpu.CompilerParams(dimension_semantics=('arbitrary',), vmem_limit_bytes=48 * 1024 * 1024),
-        cost_estimate=pl.CostEstimate(flops=4 * tok_count * kv_full.shape[0] * head_dim, bytes_accessed=kv_full.size * 2, transcendentals=tok_count * kv_full.shape[0]),
-        name='flash',
-    )(q_rot, kv_full)
+        functools.partial(head_kernel, layer),
+        out_shape=[
+            jax.ShapeDtypeStruct((tok_count, ff_local), bf16),
+            jax.ShapeDtypeStruct((tok_count, head_dim), bf16),
+            jax.ShapeDtypeStruct((tok_count, head_dim), bf16),
+            jax.ShapeDtypeStruct((tok_count, head_dim), bf16),
+        ],
+        in_specs=[any_spec, vmem_spec, vmem_spec, vmem_spec, any_spec, any_spec, any_spec, any_spec, any_spec],
+        out_specs=[vmem_spec, vmem_spec, any_spec, any_spec],
+        scratch_shapes=[
+            pltpu.VMEM((tok_count, d_model), bf16),
+            pltpu.VMEM((2, rows_per, d_model), bf16),
+            pltpu.VMEM((3, d_model, head_dim), bf16),
+            pltpu.VMEM((2, 2, d_model, W_TILE), bf16),
+            pltpu.VMEM((2 * CHIPS * tok_count, 2 * head_dim), bf16),
+            pltpu.VMEM((tok_count, head_dim), bf16),
+            pltpu.VMEM((tok_count, head_dim), jnp.float32),
+            pltpu.VMEM((tok_count, 128), jnp.float32),
+            pltpu.VMEM((tok_count, 128), jnp.float32),
+            pltpu.SemaphoreType.DMA((2,)),
+            pltpu.SemaphoreType.DMA((3,)),
+            pltpu.SemaphoreType.DMA((2, 2)),
+            pltpu.SemaphoreType.DMA((2,)),
+            pltpu.SemaphoreType.DMA((3, KV_CHUNKS)),
+            pltpu.SemaphoreType.DMA((4, KV_CHUNKS)),
+            pltpu.SemaphoreType.DMA((3, KV_CHUNKS)),
+            pltpu.SemaphoreType.DMA((4, KV_CHUNKS)),
+        ],
+        compiler_params=pltpu.CompilerParams(collective_id=2 + layer, has_side_effects=True, vmem_limit_bytes=63 * 1024 * 1024),
+        cost_estimate=pl.CostEstimate(flops=2 * tok_count * d_model * (3 * head_dim + 2 * ff_local), bytes_accessed=d_model * (3 * head_dim + 2 * ff_local) * 2, transcendentals=0),
+        name='head',
+    )(x_cur, cos_t, sin_t, norm_gain, w_q, w_k, w_v, w_gate, w_up)
 
 
 RING = 4
@@ -271,30 +497,17 @@
     def local_forward(x_loc, pos_loc, w_q, w_k, w_v, w_o, w_gate, w_up, w_down, norm_gain):
         tok_count, d_model = x_loc.shape
         layer_count = w_q.shape[0]
-        q_local = w_q.shape[2]
         head_dim = w_q.shape[3]
-        kv_local = w_k.shape[2]
+        flat_q, flat_k, flat_v = (w.reshape(layer_count, d_model, head_dim) for w in (w_q, w_k, w_v))
         cos_t, sin_t = rope_tables(pos_loc, head_dim)
         x_cur = x_loc
         k_list = []
         v_list = []
         for layer in range(layer_count):
-            normed = rms_norm(x_cur, norm_gain[layer])
-            q_proj = jnp.dot(normed, w_q[layer].reshape(d_model, q_local * head_dim), preferred_element_type=jnp.float32).astype(jnp.bfloat16)
-            k_proj = jnp.dot(normed, w_k[layer].reshape(d_model, kv_local * head_dim), preferred_element_type=jnp.float32).astype(jnp.bfloat16)
-            v_proj = jnp.dot(normed, w_v[layer].reshape(d_model, kv_local * head_dim), preferred_element_type=jnp.float32).astype(jnp.bfloat16)
-            q_rot = apply_rope(q_proj.reshape(tok_count, q_local, head_dim), cos_t, sin_t)
-            k_rot = apply_rope(k_proj.reshape(tok_count, kv_local, head_dim), cos_t, sin_t)
-            v_heads = v_proj.reshape(tok_count, kv_local, head_dim)
-            kv_own = jnp.concatenate([k_rot.reshape(tok_count, head_dim), v_proj], axis=1)
-            kv_full = lax.all_gather(kv_own, 'seq', axis=0, tiled=True)
-            attn_heads = flash_attention(q_rot.reshape(tok_count, head_dim), kv_full)
-            gate_f32 = jnp.dot(normed, w_gate[layer], preferred_element_type=jnp.float32)
-            up_f32 = jnp.dot(normed, w_up[layer], preferred_element_type=jnp.float32)
-            hidden = (jax.nn.silu(gate_f32) * up_f32).astype(jnp.bfloat16)
+            hidden, attn_heads, k_rot, v_heads = layer_head(layer, x_cur, cos_t, sin_t, norm_gain, flat_q, flat_k, flat_v, w_gate, w_up)
             x_cur = layer_tail(layer, hidden, attn_heads, x_cur, w_down, w_o)
-            k_list.append(k_rot)
-            v_list.append(v_heads)
+            k_list.append(k_rot.reshape(tok_count, 1, head_dim))
+            v_list.append(v_heads.reshape(tok_count, 1, head_dim))
         return x_cur, jnp.stack(k_list), jnp.stack(v_list)
 
     return jax.shard_map(local_forward, mesh=mesh, in_specs=(row_spec, pos_spec, head_spec, head_spec, head_spec, out_proj_spec, col_spec, col_spec, down_spec, P(None, None)), out_specs=(row_spec, cache_spec, cache_spec), check_vma=False)

time: 570 us -> 444 us (0.78); the launches traced: 562 us -> 443 us
  matrix products: 75.3 us -> 0 us
  Pallas kernels: 377 us -> 428 us
  waiting for transfers between devices: 41.1 us -> 0 us
  other arithmetic: 41.2 us -> 6.6 us
  between operations: 14.8 us -> 0.68 us
    dot_general x10 -> x0, matrix products: 75.3 us -> none  [the longest x2 28 us: local_forward(): jnp.dot(normed, w_gate[layer], preferred_element_type=jnp.float32)]
    pallas_call x2, Pallas kernels: 64.9 us -> 117 us  [layer_head(): pl.pallas_call(functools.partial(head_kernel, layer), out_shape=[jax.Shap...]
    all_gather x2 -> x0, waiting for transfers between devices: 41.1 us -> none  [local_forward(): kv_full = lax.all_gather(kv_own, 'seq', axis=0, tiled=True)]
    convert_element_type x2 -> x0, other arithmetic: 21.2 us -> none  [rms_norm(): return (x_f32 * inv_rms * gain_row.astype(jnp.float32)).astype(jnp.bfloat16)]
    reduce_sum x2 -> x0, other arithmetic: 10.1 us -> none  [rms_norm(): inv_rms = lax.rsqrt(jnp.mean(x_f32 * x_f32, axis=-1, keepdims=True) + EPS)]
    unnamed x29 -> x3, local copies, waits for them, and re-layouts: 11.7 us -> 7.89 us
  transfers between devices with their start and end apart: 2 -> 0, of which waited for: 2 -> 0; matrix products, arithmetic and copies ran while one was open for 10% -> 0% of each run, Pallas kernels for 0% -> 0%
where the time goes in v4:
time: 444 us; the launch traced here: 443 us
  Pallas kernels  428 us (96%)
  local copies, waits for them, and re-layouts  7.89 us (2%)
  other arithmetic  6.6 us (1%)
    pallas_call x2, Pallas kernels, layer_tail(): pl.pallas_call(functools.partial(tail_kernel, layer, chunk_rows), out_sha...  312 us
    pallas_call x2, Pallas kernels, layer_head(): pl.pallas_call(functools.partial(head_kernel, layer), out_shape=[jax.Shap...  117 us

profile of v4, /device:TPU:6, one launch (start us, length us, event | category | flops | bytes accessed | tf_op | source)
XLA Modules:
  0.0 443.4 jit_solution(4373273815320811571)
XLA Ops:
  0.6 0.7 convert_element_type.3
  1.3 3.0 multiply_sine_fusion
  4.4 59.5 %head.2 = (bf16[1024,1024]{1,0:T(8,128)(2,1)}, bf16[1024,256]{1,0:T(8,128)(2,1)}, bf16[1024,256]{1,0:T(8,128)(2,1)}, bf16[1024,256]{1,0:T(8,128)(2,1)}) custom-call(bf16[1024,4096]{1,0:T(8,128)(2,1)} %x_ref.3, f32[1024,128]{1,0:T(8,128)} %get-tuple-element.20.cos_ref, f32[1024,128]{1,0:T(8,128)} %get-tuple-element.19.sin_ref, bf16[2,4096]{1,0:T(2,128)(2,1)} %gain_ref.3, ...), custom_call_target="tpu_custom_call" | custom-call | flops 23622320128 | bytes 23068672 | tf_op jit(solution)/shard_map/head/pallas_call | solution.py:282
  63.9 157.8 %tail.2.x_ref = bf16[1024,4096]{1,0:T(8,128)(2,1)} custom-call(bf16[1024,1024]{1,0:T(8,128)(2,1)} %get-tuple-element.11.hid_ref, bf16[1024,256]{1,0:T(8,128)(2,1)} %get-tuple-element.12.att_ref, bf16[1024,4096]{1,0:T(8,128)(2,1)} %x_ref.3, bf16[2,1024,4096]{2,1,0:T(8,128)(2,1)} %wd_ref.3, bf16[2,1,256,4096]{3,2,1,0:T(8,128)(2,1)} %wo_ref.3), custom_call_target="tpu_custom_call" | custom-call | flops 10737418240 | bytes 10485760 | tf_op jit(solution)/shard_map/tail/pallas_call | solution.py:466
  221.6 57.1 %head.3 = (bf16[1024,1024]{1,0:T(8,128)(2,1)}, bf16[1024,256]{1,0:T(8,128)(2,1)}, bf16[1024,256]{1,0:T(8,128)(2,1)}, bf16[1024,256]{1,0:T(8,128)(2,1)}) custom-call(bf16[1024,4096]{1,0:T(8,128)(2,1)} %tail.2.x_ref, f32[1024,128]{1,0:T(8,128)} %get-tuple-element.20.cos_ref, f32[1024,128]{1,0:T(8,128)} %get-tuple-element.19.sin_ref, bf16[2,4096]{1,0:T(2,128)(2,1)} %gain_ref.3, ...), custom_call_target="tpu_custom_call" | custom-call | flops 23622320128 | bytes 23068672 | tf_op jit(solution)/shard_map/head/pallas_call | solution.py:282
  278.8 0.0 copy-start
  278.8 153.8 %tail.3 = bf16[1024,4096]{1,0:T(8,128)(2,1)} custom-call(bf16[1024,1024]{1,0:T(8,128)(2,1)} %get-tuple-element.13.hid_ref, bf16[1024,256]{1,0:T(8,128)(2,1)} %get-tuple-element.14.att_ref, bf16[1024,4096]{1,0:T(8,128)(2,1)} %tail.2.x_ref, bf16[2,1024,4096]{2,1,0:T(8,128)(2,1)} %wd_ref.3, bf16[2,1,256,4096]{3,2,1,0:T(8,128)(2,1)} %wo_ref.3), custom_call_target="tpu_custom_call" | custom-call | flops 10737418240 | bytes 10485760 | tf_op jit(solution)/shard_map/tail/pallas_call | solution.py:466
  432.7 0.0 copy-done
  432.7 2.9 pad_maximum_fusion
  435.5 7.9 %copy.14 = bf16[1024,4096]{1,0:T(8,128)(2,1)} copy(bf16[1024,4096]{1,0:T(8,128)(2,1)} %tail.3) | data formatting | bytes 16777216
  (1 shorter events, 0.0 us)
Async XLA Ops:
  278.8 153.9 %copy-start = (bf16[1024,256]{1,0:T(8,128)(2,1)S(1)}, bf16[1024,256]{1,0:T(8,128)(2,1)}, u32[]{:S(2)}) copy-start(bf16[1024,256]{1,0:T(8,128)(2,1)} %get-tuple-element.15) | copy-start | bytes 1572868

commit v5 on v4

--- a/solution.py
+++ b/solution.py
@@ -318,6 +318,8 @@
 HALVES = 2
 DIRS = 2
 STEPS = 8
+SKEW = 2
+W_GROUPS = 4
 
 
 def tail_kernel(layer, chunk_rows, hid_ref, att_ref, x_ref, wd_ref, wo_ref, out_ref, part, xbuf, wbuf, recv_a, recv_b, load_sem, store_sem, send_sem, recv_sem):
@@ -340,20 +342,23 @@
     first_pos, second_pos = (pos_y, pos_z), (pos_z, pos_y)
     first_peer, second_peer = (y_peer, z_peer), (z_peer, y_peer)
 
-    loads = [
-        pltpu.make_async_copy(wd_ref.at[layer], wbuf.at[pl.ds(0, ff_local), :], load_sem.at[0]),
-        pltpu.make_async_copy(wo_ref.at[layer, 0], wbuf.at[pl.ds(ff_local, wo_ref.shape[2]), :], load_sem.at[1]),
-        pltpu.make_async_copy(x_ref, xbuf, load_sem.at[2]),
-    ]
-    for load in loads:
-        load.start()
+    group_cols = d_model // W_GROUPS
+
+    def w_load(g):
+        cols = pl.ds(pl.multiple_of(g * group_cols, group_cols), group_cols)
+        return (pltpu.make_async_copy(wd_ref.at[layer, :, cols], wbuf.at[pl.ds(0, ff_local), cols], load_sem.at[g, 0]),
+                pltpu.make_async_copy(wo_ref.at[layer, 0, :, cols], wbuf.at[pl.ds(ff_local, wo_ref.shape[2]), cols], load_sem.at[g, 1]))
+
+    x_load = pltpu.make_async_copy(x_ref, xbuf, load_sem.at[W_GROUPS, 0])
+    for g in range(W_GROUPS):
+        for load in w_load(g):
+            load.start()
+    x_load.start()
     barrier = pltpu.get_barrier_semaphore()
     for peer in (y_peer, z_peer):
         for d in range(DIRS):
             pl.semaphore_signal(barrier, inc=1, device_id={'head': peer(d)}, device_id_type=pl.DeviceIdType.MESH)
     pl.semaphore_wait(barrier, 2 * DIRS)
-    for load in loads:
-        load.wait()
 
     def rows_of(chunk, piece, offset, count):
         return pl.ds(pl.multiple_of(chunk * chunk_rows + piece * quarter + offset, eighth), count)
@@ -394,6 +399,13 @@
 
         def one_tile(i, carry):
             cols = pl.ds(pl.multiple_of(i * piece_cols, piece_cols), piece_cols)
+            per_group = group_cols // piece_cols
+
+            @pl.when(jnp.logical_and(chunk == 0, i % per_group == 0))
+            def _():
+                for load in w_load(i // per_group):
+                    load.wait()
+
             total = jnp.dot(hid_ref[rows, :], wbuf[:ff_local, cols], preferred_element_type=jnp.float32)
             part[rows, cols] = total + jnp.dot(att_ref[rows, :], wbuf[ff_local:, cols], preferred_element_type=jnp.float32)
             return carry
@@ -407,6 +419,10 @@
     def stage(number, chunk):
         if number == 0:
             project(chunk)
+        if number == 1:
+            @pl.when(chunk == 0)
+            def _():
+                x_load.wait()
         for h in range(HALVES):
             p1, p2 = first_pos[h], second_pos[h]
             if number:
@@ -435,14 +451,14 @@
 
     def tick(t, carry):
         for number in range(STEPS, -1, -1):
-            chunk = t - number
+            chunk = t - SKEW * number
 
             @pl.when(jnp.logical_and(chunk >= 0, chunk < chunk_count))
             def _():
                 stage(number, chunk)
         return carry
 
-    lax.fori_loop(0, chunk_count + STEPS, tick, 0)
+    lax.fori_loop(0, chunk_count + SKEW * STEPS, tick, 0)
 
     def drain(chunk, carry):
         for step in range(STEPS):
@@ -474,7 +490,7 @@
             pltpu.VMEM((depth, d_model), jnp.bfloat16),
             pltpu.VMEM((chunk_count, HALVES, DIRS, landed, d_model // HALVES), jnp.float32),
             pltpu.VMEM((chunk_count, HALVES, DIRS, landed, d_model // HALVES // RING), jnp.float32),
-            pltpu.SemaphoreType.DMA((3,)),
+            pltpu.SemaphoreType.DMA((W_GROUPS + 1, 2)),
             pltpu.SemaphoreType.DMA((chunk_count,)),
             pltpu.SemaphoreType.DMA((chunk_count, STEPS, HALVES * DIRS)),
             pltpu.SemaphoreType.DMA((chunk_count, STEPS, HALVES * DIRS)),

time: 444 us -> 421 us (0.948)
  Pallas kernels: 428 us -> 405 us
    pallas_call x2, Pallas kernels: 312 us -> 288 us  [layer_tail(): pl.pallas_call(functools.partial(tail_kernel, layer, chunk_rows), out_sha...]
where the time goes in v5:
time: 421 us
  Pallas kernels  405 us (96%)
  local copies, waits for them, and re-layouts  7.89 us (2%)
  other arithmetic  6.6 us (2%)
    pallas_call x2, Pallas kernels, layer_tail(): pl.pallas_call(functools.partial(tail_kernel, layer, chunk_rows), out_sha...  288 us
    pallas_call x2, Pallas kernels, layer_head(): pl.pallas_call(functools.partial(head_kernel, layer), out_shape=[jax.Shap...  117 us

profile of v5, /device:TPU:6, one launch (start us, length us, event | category | flops | bytes accessed | tf_op | source)
XLA Modules:
  0.0 420.6 jit_solution(16214656223268465917)
XLA Ops:
  0.6 0.7 convert_element_type.3
  1.3 3.0 multiply_sine_fusion
  4.4 59.5 %head.2 = (bf16[1024,1024]{1,0:T(8,128)(2,1)}, bf16[1024,256]{1,0:T(8,128)(2,1)}, bf16[1024,256]{1,0:T(8,128)(2,1)}, bf16[1024,256]{1,0:T(8,128)(2,1)}) custom-call(bf16[1024,4096]{1,0:T(8,128)(2,1)} %x_ref.3, f32[1024,128]{1,0:T(8,128)} %get-tuple-element.20.cos_ref, f32[1024,128]{1,0:T(8,128)} %get-tuple-element.19.sin_ref, bf16[2,4096]{1,0:T(2,128)(2,1)} %gain_ref.3, ...), custom_call_target="tpu_custom_call" | custom-call | flops 23622320128 | bytes 23068672 | tf_op jit(solution)/shard_map/head/pallas_call | solution.py:282
  63.9 146.2 %tail.2.x_ref = bf16[1024,4096]{1,0:T(8,128)(2,1)} custom-call(bf16[1024,1024]{1,0:T(8,128)(2,1)} %get-tuple-element.11.hid_ref, bf16[1024,256]{1,0:T(8,128)(2,1)} %get-tuple-element.12.att_ref, bf16[1024,4096]{1,0:T(8,128)(2,1)} %x_ref.3, bf16[2,1024,4096]{2,1,0:T(8,128)(2,1)} %wd_ref.3, bf16[2,1,256,4096]{3,2,1,0:T(8,128)(2,1)} %wo_ref.3), custom_call_target="tpu_custom_call" | custom-call | flops 10737418240 | bytes 10485760 | tf_op jit(solution)/shard_map/tail/pallas_call | solution.py:482
  210.1 57.6 %head.3 = (bf16[1024,1024]{1,0:T(8,128)(2,1)}, bf16[1024,256]{1,0:T(8,128)(2,1)}, bf16[1024,256]{1,0:T(8,128)(2,1)}, bf16[1024,256]{1,0:T(8,128)(2,1)}) custom-call(bf16[1024,4096]{1,0:T(8,128)(2,1)} %tail.2.x_ref, f32[1024,128]{1,0:T(8,128)} %get-tuple-element.20.cos_ref, f32[1024,128]{1,0:T(8,128)} %get-tuple-element.19.sin_ref, bf16[2,4096]{1,0:T(2,128)(2,1)} %gain_ref.3, ...), custom_call_target="tpu_custom_call" | custom-call | flops 23622320128 | bytes 23068672 | tf_op jit(solution)/shard_map/head/pallas_call | solution.py:282
  267.7 0.0 copy-start
  267.7 142.1 %tail.3 = bf16[1024,4096]{1,0:T(8,128)(2,1)} custom-call(bf16[1024,1024]{1,0:T(8,128)(2,1)} %get-tuple-element.13.hid_ref, bf16[1024,256]{1,0:T(8,128)(2,1)} %get-tuple-element.14.att_ref, bf16[1024,4096]{1,0:T(8,128)(2,1)} %tail.2.x_ref, bf16[2,1024,4096]{2,1,0:T(8,128)(2,1)} %wd_ref.3, bf16[2,1,256,4096]{3,2,1,0:T(8,128)(2,1)} %wo_ref.3), custom_call_target="tpu_custom_call" | custom-call | flops 10737418240 | bytes 10485760 | tf_op jit(solution)/shard_map/tail/pallas_call | solution.py:482
  409.9 0.0 copy-done
  409.9 2.9 pad_maximum_fusion
  412.7 7.9 %copy.14 = bf16[1024,4096]{1,0:T(8,128)(2,1)} copy(bf16[1024,4096]{1,0:T(8,128)(2,1)} %tail.3) | data formatting | bytes 16777216
  (1 shorter events, 0.0 us)
Async XLA Ops:
  267.7 142.2 %copy-start = (bf16[1024,256]{1,0:T(8,128)(2,1)S(1)}, bf16[1024,256]{1,0:T(8,128)(2,1)}, u32[]{:S(2)}) copy-start(bf16[1024,256]{1,0:T(8,128)(2,1)} %get-tuple-element.15) | copy-start | bytes 1572868

commit v6 on v5

--- a/solution.py
+++ b/solution.py
@@ -19,17 +19,34 @@
 
 
 LOG2E = 1.4426950408889634
-CHUNK_ROWS = 128
+CHUNKS = 8
+NEAR_TICKS = (6, 9, 13)
+FAR_TICKS = (16, 19, 23)
 
 
 CHIPS = 4
+RING = 4
+HALVES = 2
+DIRS = 2
 KV_CHUNKS = 4
 W_TILE = 256
 NORM_ROWS = 64
 
 
-def head_kernel(layer, x_ref, cos_ref, sin_ref, gain_ref, wq_ref, wk_ref, wv_ref, wg_ref, wu_ref, hid_ref, att_ref, k_ref, v_ref,
-                hbuf, xs, wqkv, wtile, kv, qbuf, acc, row_max, row_sum, x_sem, w_sem, t_sem, out_sem, own_send, pass_send, ici_recv, core_recv):
+def head_kernel(layer, spread, *refs):
+    x_ref, cos_ref, sin_ref, gain_ref, wq_ref, wk_ref, wv_ref, wg_ref, wu_ref = refs[:9]
+    if spread:
+        hid_all_ref, att_all_ref, k_ref, v_ref, hid_ref, att_ref, give_send, give_recv, keep_sem = refs[9:18]
+    else:
+        wd_ref, wo_ref, hid_ref, att_ref, k_ref, v_ref, gd_ref, go_ref, give_send, give_recv = refs[9:19]
+    hbuf, xs, wqkv, wtile, kv, qbuf, acc, row_max, row_sum, x_sem, w_sem, t_sem, out_sem, own_send, pass_send, ici_recv, core_recv = refs[-17:]
+    my_head = lax.axis_index('head')
+    pos_z, pos_y = my_head // RING, my_head % RING
+    sign = (1, -1)
+
+    def z_device(z):
+        return (z + RING) % RING * RING + pos_y
+
     tok_count, d_model = hbuf.shape
     head_dim = qbuf.shape[1]
     half_dim = head_dim // 2
@@ -59,7 +76,51 @@
     barrier = pltpu.get_barrier_semaphore()
     for peer in (left, right, other):
         pl.semaphore_signal(barrier, inc=1, device_id={'seq': peer}, device_id_type=pl.DeviceIdType.MESH)
-    pl.semaphore_wait(barrier, 3)
+    for j in range(1, RING):
+        pl.semaphore_signal(barrier, inc=1, device_id={'head': z_device(pos_z + j)}, device_id_type=pl.DeviceIdType.MESH)
+    pl.semaphore_wait(barrier, 6)
+
+    def weight_part(step, d):
+        copies = []
+        for n, (own_ref, all_ref) in enumerate(((wd_ref, gd_ref), (wo_ref, go_ref))):
+            size = all_ref.shape[1] // (2 * CHIPS)
+            if step == 0:
+                rows = pl.ds(pl.multiple_of(my_seq * size, size), size)
+                src = own_ref.at[layer + 1, rows, :] if n == 0 else own_ref.at[layer + 1, 0, rows, :]
+                dst = all_ref.at[pos_z, rows, :]
+            else:
+                rows = pl.ds(pl.multiple_of(my_seq * size + d * (size // 2), size // 2), size // 2)
+                src = dst = all_ref.at[(pos_z - sign[d] + RING) % RING, rows, :]
+            copies.append(pltpu.make_async_remote_copy(
+                src_ref=src, dst_ref=dst, send_sem=give_send.at[step, d, n], recv_sem=give_recv.at[step, d, n],
+                device_id={'head': z_device(pos_z + sign[d])}, device_id_type=pl.DeviceIdType.MESH))
+        return copies
+
+    def give(src, dst, send, recv, z):
+        return pltpu.make_async_remote_copy(src_ref=src, dst_ref=dst, send_sem=send, recv_sem=recv, device_id={'head': z_device(z)}, device_id_type=pl.DeviceIdType.MESH)
+
+    def give_hidden(z, i, source):
+        rows = pl.ds(pl.multiple_of(z * rows_per, rows_per), rows_per)
+        cols = pl.ds(pl.multiple_of(i * W_TILE, W_TILE), W_TILE)
+        return give(hid_ref.at[rows, cols], hid_all_ref.at[source, :, cols], give_send.at[z, i], give_recv.at[source, i], z)
+
+    def keep_hidden(i):
+        rows = pl.ds(pl.multiple_of(pos_z * rows_per, rows_per), rows_per)
+        cols = pl.ds(pl.multiple_of(i * W_TILE, W_TILE), W_TILE)
+        return pltpu.make_async_copy(hid_ref.at[rows, cols], hid_all_ref.at[pos_z, :, cols], keep_sem.at[i])
+
+    def give_rows(z, source):
+        rows = pl.ds(pl.multiple_of(z * rows_per, rows_per), rows_per)
+        return give(att_ref.at[rows, :], att_all_ref.at[source], give_send.at[z, KV_CHUNKS], give_recv.at[source, KV_CHUNKS], z)
+
+    def keep_rows():
+        rows = pl.ds(pl.multiple_of(pos_z * rows_per, rows_per), rows_per)
+        return pltpu.make_async_copy(att_ref.at[rows, :], att_all_ref.at[pos_z], keep_sem.at[KV_CHUNKS])
+
+    if not spread:
+        for d in range(DIRS):
+            for copy in weight_part(0, d):
+                copy.start()
 
     def kv_copy(origin_chip, origin_core, i, to, send, recv):
         rows = kv.at[pl.ds(pl.multiple_of((origin_chip * 2 + origin_core) * tok_count + i * rows_per, rows_per), rows_per), :]
@@ -171,6 +232,14 @@
             gate = jnp.dot(normed, wtile[i % 2, 0], preferred_element_type=jnp.float32)
             up = jnp.dot(normed, wtile[i % 2, 1], preferred_element_type=jnp.float32)
             hid_ref[rows, pl.ds(pl.multiple_of(i * W_TILE, W_TILE), W_TILE)] = (gate * jax.nn.sigmoid(gate) * up).astype(jnp.bfloat16)
+            if spread:
+                @pl.when(j == pos_z)
+                def _():
+                    keep_hidden(i).start()
+
+                @pl.when(j != pos_z)
+                def _():
+                    give_hidden(j, i, pos_z).start()
             return inner
 
         lax.fori_loop(0, KV_CHUNKS, rows_step, 0)
@@ -179,6 +248,12 @@
         return carry
 
     lax.fori_loop(0, KV_CHUNKS, gated, 0)
+    if not spread:
+        for d in range(DIRS):
+            for copy in weight_part(0, d):
+                copy.wait_recv()
+            for copy in weight_part(1, d):
+                copy.start()
 
     scale = LOG2E / math.sqrt(head_dim)
     lanes = row_max.shape[1]
@@ -243,9 +318,35 @@
     def finish(i, carry):
         rows = pl.ds(pl.multiple_of(i * rows_per, rows_per), rows_per)
         att_ref[rows, :] = (acc[rows, :] / jnp.concatenate([row_sum[rows, :]] * (head_dim // lanes), axis=1)).astype(jnp.bfloat16)
+        if spread:
+            @pl.when(i == pos_z)
+            def _():
+                keep_rows().start()
+
+            @pl.when(i != pos_z)
+            def _():
+                give_rows(i, pos_z).start()
         return carry
 
     lax.fori_loop(0, KV_CHUNKS, finish, 0)
+    if spread:
+        for i in range(KV_CHUNKS):
+            keep_hidden(i).wait()
+        keep_rows().wait()
+        for j in range(1, RING):
+            z = (pos_z + j) % RING
+            for i in range(KV_CHUNKS):
+                give_hidden(z, i, z).wait_recv()
+                give_hidden(z, i, pos_z).wait_send()
+            give_rows(z, z).wait_recv()
+            give_rows(z, pos_z).wait_send()
+    else:
+        for d in range(DIRS):
+            for copy in weight_part(1, d):
+                copy.wait_recv()
+            for step in range(2):
+                for copy in weight_part(step, d):
+                    copy.wait_send()
     k_store.wait()
     v_store.wait()
     for i in range(KV_CHUNKS):
@@ -271,7 +372,7 @@
                 on_other(back, i).wait_send()
 
 
-def layer_head(layer, x_cur, cos_t, sin_t, norm_gain, w_q, w_k, w_v, w_gate, w_up):
+def layer_head(layer, x_cur, cos_t, sin_t, norm_gain, w_q, w_k, w_v, w_gate, w_up, w_down, w_o, spread):
     tok_count, d_model = x_cur.shape
     head_dim = w_q.shape[2]
     ff_local = w_gate.shape[2]
@@ -279,17 +380,27 @@
     any_spec = pl.BlockSpec(memory_space=pl.ANY)
     vmem_spec = pl.BlockSpec(memory_space=pltpu.VMEM)
     bf16 = jnp.bfloat16
+    rows_shape = jax.ShapeDtypeStruct((tok_count, head_dim), bf16)
+    args = (x_cur, cos_t, sin_t, norm_gain, w_q, w_k, w_v, w_gate, w_up)
+    in_specs = [any_spec, vmem_spec, vmem_spec, vmem_spec, any_spec, any_spec, any_spec, any_spec, any_spec]
+    if spread:
+        out_shape = [jax.ShapeDtypeStruct((RING, rows_per, ff_local), bf16), jax.ShapeDtypeStruct((RING, rows_per, head_dim), bf16), rows_shape, rows_shape]
+        out_specs = [any_spec] * 4
+        extra = [pltpu.VMEM((tok_count, ff_local), bf16), pltpu.VMEM((tok_count, head_dim), bf16), pltpu.SemaphoreType.DMA((RING, KV_CHUNKS + 1)),
+                 pltpu.SemaphoreType.DMA((RING, KV_CHUNKS + 1)), pltpu.SemaphoreType.DMA((KV_CHUNKS + 1,))]
+    else:
+        args += (w_down, w_o)
+        in_specs += [any_spec, any_spec]
+        out_shape = [jax.ShapeDtypeStruct((tok_count, ff_local), bf16), rows_shape, rows_shape, rows_shape,
+                     jax.ShapeDtypeStruct((RING, ff_local, d_model), bf16), jax.ShapeDtypeStruct((RING, head_dim, d_model), bf16)]
+        out_specs = [vmem_spec, vmem_spec] + [any_spec] * 4
+        extra = [pltpu.SemaphoreType.DMA((2, DIRS, 2)), pltpu.SemaphoreType.DMA((2, DIRS, 2))]
     return pl.pallas_call(
-        functools.partial(head_kernel, layer),
-        out_shape=[
-            jax.ShapeDtypeStruct((tok_count, ff_local), bf16),
-            jax.ShapeDtypeStruct((tok_count, head_dim), bf16),
-            jax.ShapeDtypeStruct((tok_count, head_dim), bf16),
-            jax.ShapeDtypeStruct((tok_count, head_dim), bf16),
-        ],
-        in_specs=[any_spec, vmem_spec, vmem_spec, vmem_spec, any_spec, any_spec, any_spec, any_spec, any_spec],
-        out_specs=[vmem_spec, vmem_spec, any_spec, any_spec],
-        scratch_shapes=[
+        functools.partial(head_kernel, layer, spread),
+        out_shape=out_shape,
+        in_specs=in_specs,
+        out_specs=out_specs,
+        scratch_shapes=extra + [
             pltpu.VMEM((tok_count, d_model), bf16),
             pltpu.VMEM((2, rows_per, d_model), bf16),
             pltpu.VMEM((3, d_model, head_dim), bf16),
@@ -311,21 +422,19 @@
         compiler_params=pltpu.CompilerParams(collective_id=2 + layer, has_side_effects=True, vmem_limit_bytes=63 * 1024 * 1024),
         cost_estimate=pl.CostEstimate(flops=2 * tok_count * d_model * (3 * head_dim + 2 * ff_local), bytes_accessed=d_model * (3 * head_dim + 2 * ff_local) * 2, transcendentals=0),
         name='head',
-    )(x_cur, cos_t, sin_t, norm_gain, w_q, w_k, w_v, w_gate, w_up)
-
-
-RING = 4
-HALVES = 2
-DIRS = 2
+    )(*args)
+
+
 STEPS = 8
 SKEW = 2
 W_GROUPS = 4
 
 
-def tail_kernel(layer, chunk_rows, hid_ref, att_ref, x_ref, wd_ref, wo_ref, out_ref, part, xbuf, wbuf, recv_a, recv_b, load_sem, store_sem, send_sem, recv_sem):
+def tail_kernel(layer, chunk_rows, hid_ref, att_ref, x_ref, wd_ref, wo_ref, gd_in_ref, go_in_ref, out_ref, gd_ref, go_ref,
+                part, xbuf, wbuf, recv_a, recv_b, load_sem, store_sem, send_sem, recv_sem, pass_send, pass_recv, side_send, side_recv):
     tok_count, d_model = xbuf.shape
     ff_local = hid_ref.shape[1]
-    chunk_count = tok_count // chunk_rows
+    chunk_count = CHUNKS
     quarter, eighth = chunk_rows // RING, chunk_rows // (2 * RING)
     half_cols = d_model // HALVES
     piece_cols = half_cols // RING
@@ -358,7 +467,59 @@
     for peer in (y_peer, z_peer):
         for d in range(DIRS):
             pl.semaphore_signal(barrier, inc=1, device_id={'head': peer(d)}, device_id_type=pl.DeviceIdType.MESH)
-    pl.semaphore_wait(barrier, 2 * DIRS)
+    my_seq = lax.axis_index('seq')
+    chip, core = my_seq // 2, my_seq % 2
+    other = chip * 2 + 1 - core
+
+    def x_chip(n):
+        return (chip + n + CHIPS) % CHIPS
+
+    for peer in (x_chip(1) * 2 + core, x_chip(-1) * 2 + core, other):
+        pl.semaphore_signal(barrier, inc=1, device_id={'seq': peer}, device_id_type=pl.DeviceIdType.MESH)
+    pl.semaphore_wait(barrier, 2 * DIRS + 3)
+
+    def weight_copies(j, part_chip, part_core, half, send, recv, to):
+        copies = []
+        for n, ref in enumerate((gd_ref, go_ref)):
+            size = ref.shape[1] // (2 * CHIPS)
+            start = (part_chip * 2 + part_core) * size
+            if half is None:
+                rows = pl.ds(pl.multiple_of(start, size), size)
+            else:
+                rows = pl.ds(pl.multiple_of(start + half * (size // 2), size // 2), size // 2)
+            place = ref.at[(pos_z + j) % RING, rows, :]
+            copies.append(pltpu.make_async_remote_copy(src_ref=place, dst_ref=place, send_sem=send.at[n], recv_sem=recv.at[n], device_id={'seq': to}, device_id_type=pl.DeviceIdType.MESH))
+        return copies
+
+    def own_pass(j, d):
+        return weight_copies(j, chip, core, None, pass_send.at[0, j - 1, d], pass_recv.at[0, j - 1, d], x_chip(sign[d]) * 2 + core)
+
+    def far_pass(j, d):
+        return weight_copies(j, x_chip(-sign[d]), core, d, pass_send.at[1, j - 1, d], pass_recv.at[1, j - 1, d], x_chip(sign[d]) * 2 + core)
+
+    def side_pass(j, n, side):
+        return weight_copies(j, x_chip(n), side, None, side_send.at[j - 1, n], side_recv.at[j - 1, n], other)
+
+    def serve_near(j):
+        for d in range(DIRS):
+            for copy in own_pass(j, d):
+                copy.wait_recv()
+            for copy in far_pass(j, d) + side_pass(j, 3 if d == 0 else 1, core):
+                copy.start()
+
+    def serve_far(j):
+        for d in range(DIRS):
+            for copy in far_pass(j, d):
+                copy.wait_recv()
+        for copy in side_pass(j, 2, core):
+            copy.start()
+
+    for j in range(1, RING):
+        for d in range(DIRS):
+            for copy in own_pass(j, d):
+                copy.start()
+        for copy in side_pass(j, 0, core):
+            copy.start()
 
     def rows_of(chunk, piece, offset, count):
         return pl.ds(pl.multiple_of(chunk * chunk_rows + piece * quarter + offset, eighth), count)
@@ -456,9 +617,17 @@
             @pl.when(jnp.logical_and(chunk >= 0, chunk < chunk_count))
             def _():
                 stage(number, chunk)
+        for j in range(1, RING):
+            @pl.when(t == NEAR_TICKS[j - 1])
+            def _():
+                serve_near(j)
+
+            @pl.when(t == FAR_TICKS[j - 1])
+            def _():
+                serve_far(j)
         return carry
 
-    lax.fori_loop(0, chunk_count + SKEW * STEPS, tick, 0)
+    lax.fori_loop(0, CHUNKS + SKEW * STEPS, tick, 0)
 
     def drain(chunk, carry):
         for step in range(STEPS):
@@ -469,36 +638,208 @@
         return carry
 
     lax.fori_loop(0, chunk_count, drain, 0)
-
-
-def layer_tail(layer, hidden, attn_heads, x_cur, w_down, w_o):
+    for j in range(1, RING):
+        for d in range(DIRS):
+            for copy in own_pass(j, d) + far_pass(j, d):
+                copy.wait_send()
+        for n in range(CHIPS):
+            for copy in side_pass(j, n, 1 - core):
+                copy.wait_recv()
+            for copy in side_pass(j, n, core):
+                copy.wait_send()
+
+
+def layer_tail(layer, hidden, attn_heads, x_cur, w_down, w_o, all_down, all_out):
     tok_count, d_model = x_cur.shape
-    chunk_rows = min(CHUNK_ROWS, tok_count)
-    chunk_count = tok_count // chunk_rows
+    chunk_rows = tok_count // CHUNKS
     depth = hidden.shape[1] + attn_heads.shape[1]
     landed = 3 * chunk_rows // (2 * RING)
     any_spec = pl.BlockSpec(memory_space=pl.ANY)
     vmem_spec = pl.BlockSpec(memory_space=pltpu.VMEM)
     return pl.pallas_call(
         functools.partial(tail_kernel, layer, chunk_rows),
-        out_shape=jax.ShapeDtypeStruct((tok_count, d_model), jnp.bfloat16),
-        in_specs=[vmem_spec, vmem_spec, any_spec, any_spec, any_spec],
-        out_specs=any_spec,
+        out_shape=[jax.ShapeDtypeStruct((tok_count, d_model), jnp.bfloat16), jax.ShapeDtypeStruct(all_down.shape, jnp.bfloat16), jax.ShapeDtypeStruct(all_out.shape, jnp.bfloat16)],
+        in_specs=[vmem_spec, vmem_spec] + [any_spec] * 5,
+        out_specs=[any_spec] * 3,
+        input_output_aliases={5: 1, 6: 2},
         scratch_shapes=[
             pltpu.VMEM((tok_count, d_model), jnp.float32),
             pltpu.VMEM((tok_count, d_model), jnp.bfloat16),
             pltpu.VMEM((depth, d_model), jnp.bfloat16),
-            pltpu.VMEM((chunk_count, HALVES, DIRS, landed, d_model // HALVES), jnp.float32),
-            pltpu.VMEM((chunk_count, HALVES, DIRS, landed, d_model // HALVES // RING), jnp.float32),
+            pltpu.VMEM((CHUNKS, HALVES, DIRS, landed, d_model // HALVES), jnp.float32),
+            pltpu.VMEM((CHUNKS, HALVES, DIRS, landed, d_model // HALVES // RING), jnp.float32),
             pltpu.SemaphoreType.DMA((W_GROUPS + 1, 2)),
-            pltpu.SemaphoreType.DMA((chunk_count,)),
-            pltpu.SemaphoreType.DMA((chunk_count, STEPS, HALVES * DIRS)),
-            pltpu.SemaphoreType.DMA((chunk_count, STEPS, HALVES * DIRS)),
+            pltpu.SemaphoreType.DMA((CHUNKS,)),
+            pltpu.SemaphoreType.DMA((CHUNKS, STEPS, HALVES * DIRS)),
+            pltpu.SemaphoreType.DMA((CHUNKS, STEPS, HALVES * DIRS)),
+            pltpu.SemaphoreType.DMA((2, RING - 1, DIRS, 2)),
+            pltpu.SemaphoreType.DMA((2, RING - 1, DIRS, 2)),
+            pltpu.SemaphoreType.DMA((RING - 1, CHIPS, 2)),
+            pltpu.SemaphoreType.DMA((RING - 1, CHIPS, 2)),
         ],
         compiler_params=pltpu.CompilerParams(collective_id=layer, has_side_effects=True, vmem_limit_bytes=63 * 1024 * 1024),
         cost_estimate=pl.CostEstimate(flops=2 * tok_count * depth * d_model, bytes_accessed=depth * d_model * 2, transcendentals=0),
         name='tail',
-    )(hidden, attn_heads, x_cur, w_down, w_o)
+    )(hidden, attn_heads, x_cur, w_down, w_o, all_down, all_out)
+
+
+LAST_STEPS = 6
+LAST_COLS = 256
+
+
+def last_kernel(layer, hid_ref, att_ref, x_ref, wd_ref, wo_ref, gd_ref, go_ref, out_ref, part, xres, xbuf, wtile, landed, w_sem, x_sem, store_sem, send_sem, recv_sem):
+    rows, d_model = part.shape
+    block = wtile.shape[3]
+    block_count = d_model // block
+    ff_local = hid_ref.shape[2]
+    quarter, eighth = rows // RING, rows // (2 * RING)
+    my_head = lax.axis_index('head')
+    pos_z, pos_y = my_head // RING, my_head % RING
+    sign = (1, -1)
+
+    def cols_of(c):
+        return pl.ds(pl.multiple_of(c * block, block), block)
+
+    def w_loads(c):
+        copies = []
+        for j in range(RING):
+            z = (pos_z + j) % RING
+            down = wd_ref.at[layer, :, cols_of(c)] if j == 0 else gd_ref.at[z, :, cols_of(c)]
+            out = wo_ref.at[layer, 0, :, cols_of(c)] if j == 0 else go_ref.at[z, :, cols_of(c)]
+            copies.append(pltpu.make_async_copy(down, wtile.at[c % 2, j, pl.ds(0, ff_local), :], w_sem.at[c % 2, j, 0]))
+            copies.append(pltpu.make_async_copy(out, wtile.at[c % 2, j, pl.ds(ff_local, wo_ref.shape[2]), :], w_sem.at[c % 2, j, 1]))
+        return copies
+
+    for copy in w_loads(0):
+        copy.start()
+    x_load = pltpu.make_async_copy(x_ref.at[pl.ds(pl.multiple_of(pos_z * rows + pos_y * quarter, quarter), quarter), :], xres, x_sem)
+    x_load.start()
+
+    def y_device(d):
+        return pos_z * RING + (pos_y + sign[d] + RING) % RING
+
+    def z_device(d):
+        return (pos_z + sign[d] + RING) % RING * RING + pos_y
+
+    barrier = pltpu.get_barrier_semaphore()
+    for device in (y_device, z_device):
+        for d in range(DIRS):
+            pl.semaphore_signal(barrier, inc=1, device_id={'head': device(d)}, device_id_type=pl.DeviceIdType.MESH)
+    pl.semaphore_wait(barrier, 2 * DIRS)
+    x_load.wait()
+
+    def rows_of(piece, offset, count):
+        return pl.ds(pl.multiple_of(piece * quarter + offset, eighth), count)
+
+    def message(step, c, d):
+        s = sign[d]
+        near, behind = (pos_y + s + RING) % RING, (pos_y - s + RING) % RING
+        if step == 0:
+            src, dst = part.at[rows_of((pos_y + 2) % RING, d * eighth, eighth), cols_of(c)], landed.at[c, d, pl.ds(quarter, eighth), :]
+        elif step == 1:
+            src, dst = part.at[rows_of(near, 0, quarter), cols_of(c)], landed.at[c, d, pl.ds(0, quarter), :]
+        elif step == 2:
+            src = dst = xbuf.at[pos_z, rows_of(pos_y, 0, quarter), cols_of(c)]
+        elif step == 3:
+            src = dst = xbuf.at[pos_z, rows_of(behind, d * eighth, eighth), cols_of(c)]
+        elif step == 4:
+            src = dst = xbuf.at[pos_z, :, cols_of(c)]
+        else:
+            src = dst = xbuf.at[(pos_z - s + RING) % RING, pl.ds(d * (rows // 2), rows // 2), cols_of(c)]
+        return pltpu.make_async_remote_copy(
+            src_ref=src, dst_ref=dst, send_sem=send_sem.at[c, step, d], recv_sem=recv_sem.at[c, step, d],
+            device_id={'head': (y_device if step < 4 else z_device)(d)}, device_id_type=pl.DeviceIdType.MESH)
+
+    def store(c):
+        return pltpu.make_async_copy(xbuf.at[:, :, cols_of(c)], out_ref.at[:, :, cols_of(c)], store_sem.at[c])
+
+    def project(c):
+        @pl.when(c + 1 < block_count)
+        def _():
+            for copy in w_loads(c + 1):
+                copy.start()
+
+        for copy in w_loads(c):
+            copy.wait()
+        total = None
+        for j in range(RING):
+            z = (pos_z + j) % RING
+            down = jnp.dot(hid_ref[z], wtile[c % 2, j, :ff_local, :], preferred_element_type=jnp.float32)
+            down = down + jnp.dot(att_ref[z], wtile[c % 2, j, ff_local:, :], preferred_element_type=jnp.float32)
+            total = down if total is None else total + down
+        part[:, cols_of(c)] = total
+
+    def stage(number, c):
+        if number == 0:
+            project(c)
+        else:
+            for d in range(DIRS):
+                message(number - 1, c, d).wait_recv()
+        if number == 1:
+            for d in range(DIRS):
+                piece = rows_of((pos_y + sign[d] + RING) % RING, d * eighth, eighth)
+                part[piece, cols_of(c)] = part[piece, cols_of(c)] + landed[c, d, pl.ds(quarter, eighth), :]
+        if number == 2:
+            own = rows_of(pos_y, 0, quarter)
+            total = part[own, cols_of(c)] + landed[c, 0, pl.ds(0, quarter), :] + landed[c, 1, pl.ds(0, quarter), :]
+            update = total.astype(jnp.bfloat16).astype(jnp.float32)
+            xbuf[pos_z, own, cols_of(c)] = (xres[:, cols_of(c)].astype(jnp.float32) + update).astype(jnp.bfloat16)
+        if number < LAST_STEPS:
+            for d in range(DIRS):
+                message(number, c, d).start()
+        else:
+            store(c).start()
+
+    def tick(t, carry):
+        for number in range(LAST_STEPS, -1, -1):
+            c = t - SKEW * number
+
+            @pl.when(jnp.logical_and(c >= 0, c < block_count))
+            def _():
+                stage(number, c)
+        return carry
+
+    lax.fori_loop(0, block_count + SKEW * LAST_STEPS, tick, 0)
+
+    def drain(c, carry):
+        for step in range(LAST_STEPS):
+            for d in range(DIRS):
+                message(step, c, d).wait_send()
+        store(c).wait()
+        return carry
+
+    lax.fori_loop(0, block_count, drain, 0)
+
+
+def layer_last(layer, hid_all, att_all, x_cur, w_down, w_o, all_down, all_out):
+    tok_count, d_model = x_cur.shape
+    rows = tok_count // RING
+    depth = hid_all.shape[2] + att_all.shape[2]
+    any_spec = pl.BlockSpec(memory_space=pl.ANY)
+    vmem_spec = pl.BlockSpec(memory_space=pltpu.VMEM)
+    blocks = d_model // LAST_COLS
+    out = pl.pallas_call(
+        functools.partial(last_kernel, layer),
+        out_shape=jax.ShapeDtypeStruct((RING, rows, d_model), jnp.bfloat16),
+        in_specs=[vmem_spec, vmem_spec] + [any_spec] * 5,
+        out_specs=any_spec,
+        scratch_shapes=[
+            pltpu.VMEM((rows, d_model), jnp.float32),
+            pltpu.VMEM((rows // RING, d_model), jnp.bfloat16),
+            pltpu.VMEM((RING, rows, d_model), jnp.bfloat16),
+            pltpu.VMEM((2, RING, depth, LAST_COLS), jnp.bfloat16),
+            pltpu.VMEM((blocks, DIRS, 3 * rows // (2 * RING), LAST_COLS), jnp.float32),
+            pltpu.SemaphoreType.DMA((2, RING, 2)),
+            pltpu.SemaphoreType.DMA,
+            pltpu.SemaphoreType.DMA((blocks,)),
+            pltpu.SemaphoreType.DMA((blocks, LAST_STEPS, DIRS)),
+            pltpu.SemaphoreType.DMA((blocks, LAST_STEPS, DIRS)),
+        ],
+        compiler_params=pltpu.CompilerParams(collective_id=layer, has_side_effects=True, vmem_limit_bytes=63 * 1024 * 1024),
+        cost_estimate=pl.CostEstimate(flops=2 * tok_count * depth * d_model, bytes_accessed=4 * depth * d_model * 2, transcendentals=0),
+        name='last',
+    )(hid_all, att_all, x_cur, w_down, w_o, all_down, all_out)
+    return out.reshape(tok_count, d_model)
 
 
 def solution(mesh):
@@ -516,14 +857,11 @@
         head_dim = w_q.shape[3]
         flat_q, flat_k, flat_v = (w.reshape(layer_count, d_model, head_dim) for w in (w_q, w_k, w_v))
         cos_t, sin_t = rope_tables(pos_loc, head_dim)
-        x_cur = x_loc
-        k_list = []
-        v_list = []
-        for layer in range(layer_count):
-            hidden, attn_heads, k_rot, v_heads = layer_head(layer, x_cur, cos_t, sin_t, norm_gain, flat_q, flat_k, flat_v, w_gate, w_up)
-            x_cur = layer_tail(layer, hidden, attn_heads, x_cur, w_down, w_o)
-            k_list.append(k_rot.reshape(tok_count, 1, head_dim))
-            v_list.append(v_heads.reshape(tok_count, 1, head_dim))
-        return x_cur, jnp.stack(k_list), jnp.stack(v_list)
+        hidden, attn_heads, k_first, v_first, all_down, all_out = layer_head(0, x_loc, cos_t, sin_t, norm_gain, flat_q, flat_k, flat_v, w_gate, w_up, w_down, w_o, False)
+        x_mid, all_down, all_out = layer_tail(0, hidden, attn_heads, x_loc, w_down, w_o, all_down, all_out)
+        hid_all, att_all, k_second, v_second = layer_head(1, x_mid, cos_t, sin_t, norm_gain, flat_q, flat_k, flat_v, w_gate, w_up, w_down, w_o, True)
+        x_out = layer_last(1, hid_all, att_all, x_mid, w_down, w_o, all_down, all_out)
+        caches = [jnp.stack([a.reshape(tok_count, 1, head_dim), b.reshape(tok_count, 1, head_dim)]) for a, b in ((k_first, k_second), (v_first, v_second))]
+        return x_out, caches[0], caches[1]
 
     return jax.shard_map(local_forward, mesh=mesh, in_specs=(row_spec, pos_spec, head_spec, head_spec, head_spec, out_proj_spec, col_spec, col_spec, down_spec, P(None, None)), out_specs=(row_spec, cache_spec, cache_spec), check_vma=False)

time: 421 us -> 389 us (0.924)
  Pallas kernels: 405 us -> 373 us
    pallas_call x2 -> x1, Pallas kernels: 288 us -> 147 us  [layer_tail(): pl.pallas_call(functools.partial(tail_kernel, layer, chunk_rows), out_sha...]
    pallas_call x2 -> x3, Pallas kernels: 117 us -> 226 us  [the longest x2 127 us: layer_head(): pl.pallas_call(functools.partial(head_kernel, layer, spread), out_shape=o...]
where the time goes in v6:
time: 389 us; the launch traced here: 388 us
  Pallas kernels  373 us (96%)
  local copies, waits for them, and re-layouts  7.89 us (2%)
  other arithmetic  6.6 us (2%)
    pallas_call x1, Pallas kernels, layer_tail(): pl.pallas_call(functools.partial(tail_kernel, layer, chunk_rows), out_sha...  147 us
    pallas_call x2, Pallas kernels, layer_head(): pl.pallas_call(functools.partial(head_kernel, layer, spread), out_shape=o...  127 us
    pallas_call x1, Pallas kernels, layer_last(): pl.pallas_call(functools.partial(last_kernel, layer), out_shape=jax.Shape...  98.6 us
    unnamed x3, local copies, waits for them, and re-layouts  7.89 us

profile of v6, /device:TPU:6, one launch (start us, length us, event | category | flops | bytes accessed | tf_op | source)
XLA Modules:
  0.0 388.2 jit_solution(223784747109580628)
XLA Ops:
  0.6 0.7 convert_element_type.3
  1.3 3.0 multiply_sine_fusion
  4.4 61.1 %head.2 = (bf16[1024,1024]{1,0:T(8,128)(2,1)}, bf16[1024,256]{1,0:T(8,128)(2,1)}, bf16[1024,256]{1,0:T(8,128)(2,1)}, bf16[1024,256]{1,0:T(8,128)(2,1)}, bf16[4,1...) custom-call(bf16[1024,4096]{1,0:T(8,128)(2,1)} %x_ref.1, f32[1024,128]{1,0:T(8,128)} %get-tuple-element.30.refs_1_, ...), custom_call_target="tpu_custom_call" | custom-call | flops 23622320128 | bytes 23068672 | tf_op jit(solution)/shard_map/head/pallas_call | solution.py:398
  65.5 147.2 %tail.1 = (bf16[1024,4096]{1,0:T(8,128)(2,1)}, bf16[4,1024,4096]{2,1,0:T(8,128)(2,1)}, bf16[4,256,4096]{2,1,0:T(8,128)(2,1)}) custom-call(bf16[1024,1024]{1,0:T(8,128)(2,1)} %get-tuple-element.16.hid_ref, bf16[1024,256]{1,0:T(8,128)(2,1)} %get-tuple-element.17.att_ref, bf16[1024,4096]{1,0:T(8,128)(2,1)} %x_ref.1, ...), custom_call_target="tpu_custom_call", output_to_operand_aliasing={{1}: (5, {}), {2}: (6, {})} | custom-call | flops 10737418240 | bytes 10485760 | tf_op jit(solution)/shard_map/tail/pallas_call | solution.py:659
  212.7 66.1 %head.3 = (bf16[4,256,1024]{2,1,0:T(8,128)(2,1)}, bf16[4,256,256]{2,1,0:T(8,128)(2,1)}, bf16[1024,256]{1,0:T(8,128)(2,1)}, bf16[1024,256]{1,0:T(8,128)(2,1)}) custom-call(bf16[1024,4096]{1,0:T(8,128)(2,1)} %get-tuple-element.20.refs_0_.x_ref, f32[1024,128]{1,0:T(8,128)} %get-tuple-element.30.refs_1_, f32[1024,128]{1,0:T(8,128)} %get-tuple-element.29.refs_2_, ...), custom_call_target="tpu_custom_call" | custom-call | flops 23622320128 | bytes 23068672 | tf_op jit(solution)/shard_map/head/pallas_call | solution.py:398
  278.8 0.0 copy-start
  278.8 98.6 %last.1 = bf16[4,256,4096]{2,1,0:T(8,128)(2,1)} custom-call(bf16[4,256,1024]{2,1,0:T(8,128)(2,1)} %get-tuple-element.21.hid_ref, bf16[4,256,256]{2,1,0:T(8,128)(2,1)} %get-tuple-element.22.att_ref, bf16[1024,4096]{1,0:T(8,128)(2,1)} %get-tuple-element.20.refs_0_.x_ref, bf16[2,1024,4096]{2,1,0:T(8,128)(2,1)} %wd_ref.3, bf16[2,1,256,4096]{3,2,1,0:T(8,128)(2,1)} %wo_ref.3, ...), custom_call_target="tpu_custom_call" | custom-call | flops 10737418240 | bytes 41943040 | tf_op jit(solution)/shard_map/last/pallas_call | solution.py:821
  377.5 0.0 copy-done
  377.5 2.9 pad_maximum_fusion
  380.3 7.9 %copy.18 = bf16[1024,4096]{1,0:T(8,128)(2,1)} copy(bf16[1024,4096]{1,0:T(8,128)(2,1)} %bitcast.8) | data formatting | bytes 16777216
  (1 shorter events, 0.0 us)
Async XLA Ops:
  278.8 98.7 %copy-start = (bf16[1024,256]{1,0:T(8,128)(2,1)S(1)}, bf16[1024,256]{1,0:T(8,128)(2,1)}, u32[]{:S(2)}) copy-start(bf16[1024,256]{1,0:T(8,128)(2,1)} %get-tuple-element.25) | copy-start | bytes 1572868

commit v7 on v6

--- a/solution.py
+++ b/solution.py
@@ -138,6 +138,21 @@
     def on_right(i):
         return kv_copy(chip - 1, core, i, right, pass_send.at[0, i], ici_recv.at[1, i])
 
+    def to_relay(i):
+        return kv_copy(chip, core, i, left, own_send.at[3, i], ici_recv.at[3, i])
+
+    def from_relay(i):
+        return kv_copy(1, core, i, left, pass_send.at[0, i], ici_recv.at[1, i])
+
+    def on_left(i):
+        return kv_copy(0, core, i, left, pass_send.at[0, i], ici_recv.at[1, i])
+
+    def relay(i):
+        @pl.when(chip == 0)
+        def _():
+            kv_copy(1, core, i, left, own_send.at[3, i], ici_recv.at[3, i]).wait_recv()
+            from_relay(i).start()
+
     def on_other(back, i):
         return kv_copy(chip - back, core, i, other, pass_send.at[back, i], core_recv.at[back, i])
 
@@ -150,9 +165,13 @@
             arrival(back, i).wait_recv()
             on_other(back, i).start()
         if back == 1:
-            @pl.when(jnp.logical_and(chip >= 1, chip < CHIPS - 1))
+            @pl.when(jnp.logical_and(i < KV_CHUNKS // 2, jnp.logical_and(chip >= 1, chip < CHIPS - 1)))
             def _():
                 on_right(i).start()
+        if back == 3:
+            @pl.when(jnp.logical_and(i >= KV_CHUNKS // 2, chip == CHIPS - 1))
+            def _():
+                on_left(i).start()
 
     def rope(values, rows):
         cos_t, sin_t = cos_ref[rows, :], sin_ref[rows, :]
@@ -196,6 +215,10 @@
         @pl.when(chip == 0)
         def _():
             to_wrap(i).start()
+
+        @pl.when(jnp.logical_and(i >= KV_CHUNKS // 2, chip == 1))
+        def _():
+            to_relay(i).start()
 
         @pl.when(core == 0)
         def _():
@@ -245,6 +268,10 @@
         lax.fori_loop(0, KV_CHUNKS, rows_step, 0)
         serve(1, i)
         serve(3, i)
+
+        @pl.when(i >= KV_CHUNKS // 2)
+        def _():
+            relay(i)
         return carry
 
     lax.fori_loop(0, KV_CHUNKS, gated, 0)
@@ -362,9 +389,22 @@
         def _():
             to_other(i).wait_send()
 
-        @pl.when(jnp.logical_and(chip >= 1, chip < CHIPS - 1))
-        def _():
-            on_right(i).wait_send()
+        if i < KV_CHUNKS // 2:
+            @pl.when(jnp.logical_and(chip >= 1, chip < CHIPS - 1))
+            def _():
+                on_right(i).wait_send()
+        else:
+            @pl.when(chip == 0)
+            def _():
+                from_relay(i).wait_send()
+
+            @pl.when(chip == 1)
+            def _():
+                to_relay(i).wait_send()
+
+            @pl.when(chip == CHIPS - 1)
+            def _():
+                on_left(i).wait_send()
 
         for back in (1, 2, 3):
             @pl.when(chip >= back)
@@ -414,9 +454,9 @@
             pltpu.SemaphoreType.DMA((3,)),
             pltpu.SemaphoreType.DMA((2, 2)),
             pltpu.SemaphoreType.DMA((2,)),
-            pltpu.SemaphoreType.DMA((3, KV_CHUNKS)),
             pltpu.SemaphoreType.DMA((4, KV_CHUNKS)),
-            pltpu.SemaphoreType.DMA((3, KV_CHUNKS)),
+            pltpu.SemaphoreType.DMA((4, KV_CHUNKS)),
+            pltpu.SemaphoreType.DMA((4, KV_CHUNKS)),
             pltpu.SemaphoreType.DMA((4, KV_CHUNKS)),
         ],
         compiler_params=pltpu.CompilerParams(collective_id=2 + layer, has_side_effects=True, vmem_limit_bytes=63 * 1024 * 1024),
@@ -731,24 +771,52 @@
     def rows_of(piece, offset, count):
         return pl.ds(pl.multiple_of(piece * quarter + offset, eighth), count)
 
-    def message(step, c, d):
+    def message(step, c, d, z_first):
         s = sign[d]
         near, behind = (pos_y + s + RING) % RING, (pos_y - s + RING) % RING
         if step == 0:
             src, dst = part.at[rows_of((pos_y + 2) % RING, d * eighth, eighth), cols_of(c)], landed.at[c, d, pl.ds(quarter, eighth), :]
         elif step == 1:
             src, dst = part.at[rows_of(near, 0, quarter), cols_of(c)], landed.at[c, d, pl.ds(0, quarter), :]
-        elif step == 2:
-            src = dst = xbuf.at[pos_z, rows_of(pos_y, 0, quarter), cols_of(c)]
-        elif step == 3:
-            src = dst = xbuf.at[pos_z, rows_of(behind, d * eighth, eighth), cols_of(c)]
-        elif step == 4:
-            src = dst = xbuf.at[pos_z, :, cols_of(c)]
+        elif z_first:
+            back = (pos_z - s + RING) % RING
+            if step == 2:
+                src = dst = xbuf.at[pos_z, rows_of(pos_y, 0, quarter), cols_of(c)]
+            elif step == 3:
+                src = dst = xbuf.at[back, rows_of(pos_y, d * eighth, eighth), cols_of(c)]
+            elif step == 4:
+                src = dst = xbuf.at[:, rows_of(pos_y, 0, quarter), cols_of(c)]
+            else:
+                src = dst = xbuf.at[:, rows_of(behind, d * eighth, eighth), cols_of(c)]
         else:
-            src = dst = xbuf.at[(pos_z - s + RING) % RING, pl.ds(d * (rows // 2), rows // 2), cols_of(c)]
+            if step == 2:
+                src = dst = xbuf.at[pos_z, rows_of(pos_y, 0, quarter), cols_of(c)]
+            elif step == 3:
+                src = dst = xbuf.at[pos_z, rows_of(behind, d * eighth, eighth), cols_of(c)]
+            elif step == 4:
+                src = dst = xbuf.at[pos_z, :, cols_of(c)]
+            else:
+                src = dst = xbuf.at[(pos_z - s + RING) % RING, pl.ds(d * (rows // 2), rows // 2), cols_of(c)]
+        along_y = step < 2 or (step < 4) != z_first
         return pltpu.make_async_remote_copy(
             src_ref=src, dst_ref=dst, send_sem=send_sem.at[c, step, d], recv_sem=recv_sem.at[c, step, d],
-            device_id={'head': (y_device if step < 4 else z_device)(d)}, device_id_type=pl.DeviceIdType.MESH)
+            device_id={'head': (y_device if along_y else z_device)(d)}, device_id_type=pl.DeviceIdType.MESH)
+
+    def on_messages(step, c, act):
+        if step < 2:
+            for d in range(DIRS):
+                act(message(step, c, d, False))
+            return
+
+        @pl.when(c % 4 == 3)
+        def _():
+            for d in range(DIRS):
+                act(message(step, c, d, True))
+
+        @pl.when(c % 4 != 3)
+        def _():
+            for d in range(DIRS):
+                act(message(step, c, d, False))
 
     def store(c):
         return pltpu.make_async_copy(xbuf.at[:, :, cols_of(c)], out_ref.at[:, :, cols_of(c)], store_sem.at[c])
@@ -773,8 +841,7 @@
         if number == 0:
             project(c)
         else:
-            for d in range(DIRS):
-                message(number - 1, c, d).wait_recv()
+            on_messages(number - 1, c, lambda copy: copy.wait_recv())
         if number == 1:
             for d in range(DIRS):
                 piece = rows_of((pos_y + sign[d] + RING) % RING, d * eighth, eighth)
@@ -785,8 +852,7 @@
             update = total.astype(jnp.bfloat16).astype(jnp.float32)
             xbuf[pos_z, own, cols_of(c)] = (xres[:, cols_of(c)].astype(jnp.float32) + update).astype(jnp.bfloat16)
         if number < LAST_STEPS:
-            for d in range(DIRS):
-                message(number, c, d).start()
+            on_messages(number, c, lambda copy: copy.start())
         else:
             store(c).start()
 
@@ -803,8 +869,7 @@
 
     def drain(c, carry):
         for step in range(LAST_STEPS):
-            for d in range(DIRS):
-                message(step, c, d).wait_send()
+            on_messages(step, c, lambda copy: copy.wait_send())
         store(c).wait()
         return carry
 
@@ -842,6 +907,47 @@
     return out.reshape(tok_count, d_model)
 
 
+EMIT_PARTS = 8
+
+
+def emit_kernel(x_ref, k_first, k_second, v_first, v_second, x_out, k_out, v_out, xbuf, rows, load_sem, store_sem):
+    size = x_ref.shape[0] // EMIT_PARTS
+    loads, stores = [], []
+    for n in range(EMIT_PARTS):
+        part = pl.ds(n * size, size)
+        loads.append(pltpu.make_async_copy(x_ref.at[part, :], xbuf.at[part, :], load_sem.at[n]))
+        stores.append(pltpu.make_async_copy(xbuf.at[part, :], x_out.at[part, :], store_sem.at[n]))
+    for n, (ref, out) in enumerate(((k_first, k_out.at[0]), (k_second, k_out.at[1]), (v_first, v_out.at[0]), (v_second, v_out.at[1]))):
+        loads.append(pltpu.make_async_copy(ref, rows.at[n], load_sem.at[EMIT_PARTS + n]))
+        stores.append(pltpu.make_async_copy(rows.at[n], out, store_sem.at[EMIT_PARTS + n]))
+    for copy in loads:
+        copy.start()
+    for load, store in zip(loads, stores):
+        load.wait()
+        store.start()
+    for copy in stores:
+        copy.wait()
+
+
+def emit(x_out, k_first, k_second, v_first, v_second):
+    any_spec = pl.BlockSpec(memory_space=pl.ANY)
+    cache = jax.ShapeDtypeStruct((2,) + k_first.shape, jnp.bfloat16)
+    return pl.pallas_call(
+        emit_kernel,
+        out_shape=[jax.ShapeDtypeStruct(x_out.shape, jnp.bfloat16), cache, cache],
+        in_specs=[any_spec] * 5,
+        out_specs=[any_spec] * 3,
+        scratch_shapes=[
+            pltpu.VMEM(x_out.shape, jnp.bfloat16),
+            pltpu.VMEM((4,) + k_first.shape, jnp.bfloat16),
+            pltpu.SemaphoreType.DMA((EMIT_PARTS + 4,)),
+            pltpu.SemaphoreType.DMA((EMIT_PARTS + 4,)),
+        ],
+        compiler_params=pltpu.CompilerParams(vmem_limit_bytes=63 * 1024 * 1024),
+        name='emit',
+    )(x_out, k_first, k_second, v_first, v_second)
+
+
 def solution(mesh):
     row_spec = P(('batch', 'seq'), None)
     pos_spec = P(('batch', 'seq'))
@@ -861,7 +967,8 @@
         x_mid, all_down, all_out = layer_tail(0, hidden, attn_heads, x_loc, w_down, w_o, all_down, all_out)
         hid_all, att_all, k_second, v_second = layer_head(1, x_mid, cos_t, sin_t, norm_gain, flat_q, flat_k, flat_v, w_gate, w_up, w_down, w_o, True)
         x_out = layer_last(1, hid_all, att_all, x_mid, w_down, w_o, all_down, all_out)
-        caches = [jnp.stack([a.reshape(tok_count, 1, head_dim), b.reshape(tok_count, 1, head_dim)]) for a, b in ((k_first, k_second), (v_first, v_second))]
-        return x_out, caches[0], caches[1]
+        x_out, k_all, v_all = emit(x_out, k_first, k_second, v_first, v_second)
+        cache_shape = (layer_count, tok_count, 1, head_dim)
+        return x_out, k_all.reshape(cache_shape), v_all.reshape(cache_shape)
 
     return jax.shard_map(local_forward, mesh=mesh, in_specs=(row_spec, pos_spec, head_spec, head_spec, head_spec, out_proj_spec, col_spec, col_spec, down_spec, P(None, None)), out_specs=(row_spec, cache_spec, cache_spec), check_vma=False)

time: 389 us -> 372 us (0.956)
  local copies, waits for them, and re-layouts: 7.89 us -> 0 us
  Pallas kernels: 373 us -> 367 us
    pallas_call x1, Pallas kernels: 98.6 us -> 88.3 us  [layer_last(): pl.pallas_call(functools.partial(last_kernel, layer), out_shape=jax.Shape...]
    pallas_call x0 -> x1, Pallas kernels: none -> 8.01 us  [emit(): pl.pallas_call(emit_kernel, out_shape=[jax.ShapeDtypeStruct(x_out.shape,...]
    unnamed x3 -> x0, local copies, waits for them, and re-layouts: 7.89 us -> none
    pallas_call x2, Pallas kernels: 127 us -> 123 us  [layer_head(): pl.pallas_call(functools.partial(head_kernel, layer, spread), out_shape=o...]
where the time goes in v7:
time: 372 us; the launch traced here: 371 us
  Pallas kernels  367 us (99%)
  other arithmetic  3.73 us (1%)
    pallas_call x1, Pallas kernels, layer_tail(): pl.pallas_call(functools.partial(tail_kernel, layer, chunk_rows), out_sha...  148 us
    pallas_call x2, Pallas kernels, layer_head(): pl.pallas_call(functools.partial(head_kernel, layer, spread), out_shape=o...  123 us
    pallas_call x1, Pallas kernels, layer_last(): pl.pallas_call(functools.partial(last_kernel, layer), out_shape=jax.Shape...  88.3 us
    pallas_call x1, Pallas kernels, emit(): pl.pallas_call(emit_kernel, out_shape=[jax.ShapeDtypeStruct(x_out.shape,...  8.01 us

profile of v7, /device:TPU:6, one launch (start us, length us, event | category | flops | bytes accessed | tf_op | source)
XLA Modules:
  0.0 371.5 jit_solution(11605642075114095241)
XLA Ops:
  0.6 0.7 convert_element_type.3
  1.3 3.0 multiply_sine_fusion
  4.4 58.4 %head.2 = (bf16[1024,1024]{1,0:T(8,128)(2,1)}, bf16[1024,256]{1,0:T(8,128)(2,1)}, bf16[1024,256]{1,0:T(8,128)(2,1)}, bf16[1024,256]{1,0:T(8,128)(2,1)}, bf16[4,1...) custom-call(bf16[1024,4096]{1,0:T(8,128)(2,1)} %x_ref.1, f32[1024,128]{1,0:T(8,128)} %get-tuple-element.39.refs_1_, ...), custom_call_target="tpu_custom_call" | custom-call | flops 23622320128 | bytes 23068672 | tf_op jit(solution)/shard_map/head/pallas_call | solution.py:438
  62.8 147.9 %tail.1 = (bf16[1024,4096]{1,0:T(8,128)(2,1)}, bf16[4,1024,4096]{2,1,0:T(8,128)(2,1)}, bf16[4,256,4096]{2,1,0:T(8,128)(2,1)}) custom-call(bf16[1024,1024]{1,0:T(8,128)(2,1)} %get-tuple-element.19.hid_ref, bf16[1024,256]{1,0:T(8,128)(2,1)} %get-tuple-element.20.att_ref, bf16[1024,4096]{1,0:T(8,128)(2,1)} %x_ref.1, ...), custom_call_target="tpu_custom_call", output_to_operand_aliasing={{1}: (5, {}), {2}: (6, {})} | custom-call | flops 10737418240 | bytes 10485760 | tf_op jit(solution)/shard_map/tail/pallas_call | solution.py:699
  210.7 64.3 %head.3 = (bf16[4,256,1024]{2,1,0:T(8,128)(2,1)}, bf16[4,256,256]{2,1,0:T(8,128)(2,1)}, bf16[1024,256]{1,0:T(8,128)(2,1)}, bf16[1024,256]{1,0:T(8,128)(2,1)}) custom-call(bf16[1024,4096]{1,0:T(8,128)(2,1)} %get-tuple-element.23.refs_0_.x_ref, f32[1024,128]{1,0:T(8,128)} %get-tuple-element.39.refs_1_, f32[1024,128]{1,0:T(8,128)} %get-tuple-element.38.refs_2_, ...), custom_call_target="tpu_custom_call" | custom-call | flops 23622320128 | bytes 23068672 | tf_op jit(solution)/shard_map/head/pallas_call | solution.py:438
  275.0 88.3 %last.1 = bf16[4,256,4096]{2,1,0:T(8,128)(2,1)} custom-call(bf16[4,256,1024]{2,1,0:T(8,128)(2,1)} %get-tuple-element.24.hid_ref, bf16[4,256,256]{2,1,0:T(8,128)(2,1)} %get-tuple-element.25.att_ref, bf16[1024,4096]{1,0:T(8,128)(2,1)} %get-tuple-element.23.refs_0_.x_ref, bf16[2,1024,4096]{2,1,0:T(8,128)(2,1)} %wd_ref.3, bf16[2,1,256,4096]{3,2,1,0:T(8,128)(2,1)} %wo_ref.3, ...), custom_call_target="tpu_custom_call" | custom-call | flops 10737418240 | bytes 41943040 | tf_op jit(solution)/shard_map/last/pallas_call | solution.py:886
  363.3 8.0 %emit.1 = (bf16[1024,4096]{1,0:T(8,128)(2,1)}, bf16[2,1024,256]{2,1,0:T(8,128)(2,1)}, bf16[2,1024,256]{2,1,0:T(8,128)(2,1)}) custom-call(bf16[1024,4096]{1,0:T(8,128)(2,1)} %bitcast.10, bf16[1024,256]{1,0:T(8,128)(2,1)} %get-tuple-element.28.k_first, bf16[1024,256]{1,0:T(8,128)(2,1)} %get-tuple-element.29.k_second, ...), custom_call_target="tpu_custom_call" | custom-call | tf_op jit(solution)/shard_map/emit/pallas_call | solution.py:935
  (1 shorter events, 0.0 us)

commit v8 on v7

--- a/solution.py
+++ b/solution.py
@@ -18,7 +18,6 @@
     return jnp.cos(angles), jnp.sin(angles)
 
 
-LOG2E = 1.4426950408889634
 CHUNKS = 8
 NEAR_TICKS = (6, 9, 13)
 FAR_TICKS = (16, 19, 23)
@@ -233,9 +232,12 @@
     k_store.start()
     v_store.start()
 
+    scale = 1.0 / math.sqrt(head_dim)
+
     def query(i, carry):
         rows = pl.ds(pl.multiple_of(i * rows_per, rows_per), rows_per)
-        qbuf[rows, :] = rope(jnp.dot(hbuf[rows, :], wqkv[2], preferred_element_type=jnp.float32), rows)
+        query_rows = rope(jnp.dot(hbuf[rows, :], wqkv[2], preferred_element_type=jnp.float32), rows)
+        qbuf[rows, :] = (query_rows.astype(jnp.float32) * scale).astype(jnp.bfloat16)
         return carry
 
     lax.fori_loop(0, KV_CHUNKS, query, 0)
@@ -272,23 +274,25 @@
         @pl.when(i >= KV_CHUNKS // 2)
         def _():
             relay(i)
+
+        if not spread:
+            @pl.when(i == 2)
+            def _():
+                for d in range(DIRS):
+                    for copy in weight_part(0, d):
+                        copy.wait_recv()
+                    for copy in weight_part(1, d):
+                        copy.start()
         return carry
 
     lax.fori_loop(0, KV_CHUNKS, gated, 0)
-    if not spread:
-        for d in range(DIRS):
-            for copy in weight_part(0, d):
-                copy.wait_recv()
-            for copy in weight_part(1, d):
-                copy.start()
-
-    scale = LOG2E / math.sqrt(head_dim)
-    lanes = row_max.shape[1]
-
-    def attend(key_start, q_half, masked, first):
+
+    lanes = row_max.shape[2]
+
+    def attend(key_start, q_half, side, masked, first):
         rows = pl.ds(q_half * half_rows, half_rows)
         some = pl.ds(key_start, half_rows)
-        logits = lax.dot_general(qbuf[rows, :], kv[some, :head_dim], (((1,), (1,)), ((), ())), preferred_element_type=jnp.float32) * scale
+        logits = lax.dot_general(qbuf[rows, :], kv[some, :head_dim], (((1,), (1,)), ((), ())), preferred_element_type=jnp.float32)
         if masked:
             seen = lax.broadcasted_iota(jnp.int32, logits.shape, 0) >= lax.broadcasted_iota(jnp.int32, logits.shape, 1)
             logits = jnp.where(seen, logits, -jnp.inf)
@@ -296,55 +300,30 @@
         if first:
             new_max = jnp.broadcast_to(block_max, (half_rows, lanes))
         else:
-            new_max = jnp.maximum(row_max[rows, :], block_max)
-        prob = jnp.exp2(logits - jnp.concatenate([new_max] * (half_rows // lanes), axis=1))
+            new_max = jnp.maximum(row_max[side, rows, :], block_max)
+        prob = jnp.exp(logits - jnp.concatenate([new_max] * (half_rows // lanes), axis=1))
         block_sum = jnp.sum(prob, axis=-1, keepdims=True)
         block_out = jnp.dot(prob.astype(jnp.bfloat16), kv[some, head_dim:], preferred_element_type=jnp.float32)
         if first:
-            row_sum[rows, :] = jnp.broadcast_to(block_sum, (half_rows, lanes))
-            acc[rows, :] = block_out
+            row_sum[side, rows, :] = jnp.broadcast_to(block_sum, (half_rows, lanes))
+            acc[side, rows, :] = block_out
         else:
-            rescale = jnp.exp2(row_max[rows, :] - new_max)
-            row_sum[rows, :] = row_sum[rows, :] * rescale + block_sum
-            acc[rows, :] = acc[rows, :] * jnp.concatenate([rescale] * (head_dim // lanes), axis=1) + block_out
-        row_max[rows, :] = new_max
-
-    own_start = pl.multiple_of(my_seq * tok_count, tok_count)
-    attend(own_start, 0, True, True)
-    attend(own_start, 1, False, True)
-    attend(pl.multiple_of(own_start + half_rows, half_rows), 1, True, False)
-
-    def past(block_chip, block_core):
-        def one(n, carry):
-            start = pl.multiple_of((block_chip * 2 + block_core) * tok_count + n * half_rows, half_rows)
-            attend(start, 0, False, False)
-            attend(start, 1, False, False)
-            return carry
-        lax.fori_loop(0, 2, one, 0)
+            rescale = jnp.exp(row_max[side, rows, :] - new_max)
+            row_sum[side, rows, :] = row_sum[side, rows, :] * rescale + block_sum
+            acc[side, rows, :] = acc[side, rows, :] * jnp.concatenate([rescale] * (head_dim // lanes), axis=1) + block_out
+        row_max[side, rows, :] = new_max
 
     def taken(back):
         for i in range(KV_CHUNKS):
             kv_copy(chip - back, 1 - core, i, other, pass_send.at[0, i], core_recv.at[back, i]).wait_recv()
 
-    @pl.when(core == 1)
-    def _():
-        taken(0)
-        past(chip, 0)
-
-    for back in (1, 3, 2):
-        if back == 2:
-            for i in range(KV_CHUNKS):
-                serve(2, i)
-
-        @pl.when(chip >= back)
-        def _():
-            past(chip - back, core)
-            taken(back)
-            past(chip - back, 1 - core)
-
-    def finish(i, carry):
-        rows = pl.ds(pl.multiple_of(i * rows_per, rows_per), rows_per)
-        att_ref[rows, :] = (acc[rows, :] / jnp.concatenate([row_sum[rows, :]] * (head_dim // lanes), axis=1)).astype(jnp.bfloat16)
+    def finish(i):
+        rows = pl.ds(i * rows_per, rows_per)
+        top = jnp.maximum(row_max[0, rows, :], row_max[1, rows, :])
+        weights = [jnp.exp(row_max[side, rows, :] - top) for side in range(2)]
+        total = weights[0] * row_sum[0, rows, :] + weights[1] * row_sum[1, rows, :]
+        wide = [jnp.concatenate([w] * (head_dim // lanes), axis=1) for w in weights + [total]]
+        att_ref[rows, :] = ((acc[0, rows, :] * wide[0] + acc[1, rows, :] * wide[1]) / wide[2]).astype(jnp.bfloat16)
         if spread:
             @pl.when(i == pos_z)
             def _():
@@ -353,9 +332,51 @@
             @pl.when(i != pos_z)
             def _():
                 give_rows(i, pos_z).start()
-        return carry
-
-    lax.fori_loop(0, KV_CHUNKS, finish, 0)
+
+    own_start = pl.multiple_of(my_seq * tok_count, tok_count)
+    second = pl.multiple_of(own_start + half_rows, half_rows)
+    attend(own_start, 0, 0, True, True)
+    attend(own_start, 1, 0, False, True)
+    attend(second, 1, 1, True, True)
+    top_rows = pl.ds(0, half_rows)
+    row_max[1, top_rows, :] = jnp.full((half_rows, lanes), -jnp.inf, jnp.float32)
+    row_sum[1, top_rows, :] = jnp.zeros((half_rows, lanes), jnp.float32)
+    acc[1, top_rows, :] = jnp.zeros((half_rows, head_dim), jnp.float32)
+
+    def past_block(n):
+        later = n - core
+        back = jnp.where(later < 2, 1, jnp.where(chip == CHIPS - 1, jnp.where(later < 4, 3, 2), 2))
+        block = (chip - back) * 2 + jnp.where(later % 2 == 0, core, 1 - core)
+        return jnp.where(jnp.logical_and(core == 1, n == 0), chip * 2, block)
+
+    for q_half in range(2):
+        def past(n, carry):
+            if q_half == 0:
+                @pl.when(jnp.logical_and(core == 1, n == 0))
+                def _():
+                    taken(0)
+
+                for back in (1, 3, 2):
+                    place = 0 if back == 1 else 2 if back == 3 else jnp.where(chip == CHIPS - 1, 4, 2)
+
+                    @pl.when(jnp.logical_and(chip >= back, n == core + place))
+                    def _():
+                        if back == 2:
+                            for i in range(KV_CHUNKS):
+                                serve(2, i)
+
+                    @pl.when(jnp.logical_and(chip >= back, n == core + place + 1))
+                    def _():
+                        taken(back)
+            start = past_block(n) * tok_count
+            attend(pl.multiple_of(start, half_rows), q_half, 0, False, False)
+            attend(pl.multiple_of(start + half_rows, half_rows), q_half, 1, False, False)
+            return carry
+
+        lax.fori_loop(0, my_seq, past, 0)
+        for i in range(q_half * KV_CHUNKS // 2, (q_half + 1) * KV_CHUNKS // 2):
+            finish(i)
+
     if spread:
         for i in range(KV_CHUNKS):
             keep_hidden(i).wait()
@@ -447,9 +468,9 @@
             pltpu.VMEM((2, 2, d_model, W_TILE), bf16),
             pltpu.VMEM((2 * CHIPS * tok_count, 2 * head_dim), bf16),
             pltpu.VMEM((tok_count, head_dim), bf16),
-            pltpu.VMEM((tok_count, head_dim), jnp.float32),
-            pltpu.VMEM((tok_count, 128), jnp.float32),
-            pltpu.VMEM((tok_count, 128), jnp.float32),
+            pltpu.VMEM((2, tok_count, head_dim), jnp.float32),
+            pltpu.VMEM((2, tok_count, 128), jnp.float32),
+            pltpu.VMEM((2, tok_count, 128), jnp.float32),
             pltpu.SemaphoreType.DMA((2,)),
             pltpu.SemaphoreType.DMA((3,)),
             pltpu.SemaphoreType.DMA((2, 2)),

time: 372 us -> 372 us (level)
  no operation moved by 1% of the time
where the time goes in v8:
time: 372 us
  Pallas kernels  367 us (99%)
  other arithmetic  3.73 us (1%)
    pallas_call x1, Pallas kernels, layer_tail(): pl.pallas_call(functools.partial(tail_kernel, layer, chunk_rows), out_sha...  147 us
    pallas_call x2, Pallas kernels, layer_head(): pl.pallas_call(functools.partial(head_kernel, layer, spread), out_shape=o...  123 us
    pallas_call x1, Pallas kernels, layer_last(): pl.pallas_call(functools.partial(last_kernel, layer), out_shape=jax.Shape...  89.3 us
    pallas_call x1, Pallas kernels, emit(): pl.pallas_call(emit_kernel, out_shape=[jax.ShapeDtypeStruct(x_out.shape,...  8.01 us

profile of v8, /device:TPU:6, one launch (start us, length us, event | category | flops | bytes accessed | tf_op | source)
XLA Modules:
  0.0 371.7 jit_solution(7826824524201081553)
XLA Ops:
  0.6 0.7 convert_element_type.3
  1.3 3.0 multiply_sine_fusion
  4.4 59.9 %head.2 = (bf16[1024,1024]{1,0:T(8,128)(2,1)}, bf16[1024,256]{1,0:T(8,128)(2,1)}, bf16[1024,256]{1,0:T(8,128)(2,1)}, bf16[1024,256]{1,0:T(8,128)(2,1)}, bf16[4,1...) custom-call(bf16[1024,4096]{1,0:T(8,128)(2,1)} %x_ref.1, f32[1024,128]{1,0:T(8,128)} %get-tuple-element.39.refs_1_, ...), custom_call_target="tpu_custom_call" | custom-call | flops 23622320128 | bytes 23068672 | tf_op jit(solution)/shard_map/head/pallas_call | solution.py:459
  64.3 147.1 %tail.1 = (bf16[1024,4096]{1,0:T(8,128)(2,1)}, bf16[4,1024,4096]{2,1,0:T(8,128)(2,1)}, bf16[4,256,4096]{2,1,0:T(8,128)(2,1)}) custom-call(bf16[1024,1024]{1,0:T(8,128)(2,1)} %get-tuple-element.19.hid_ref, bf16[1024,256]{1,0:T(8,128)(2,1)} %get-tuple-element.20.att_ref, bf16[1024,4096]{1,0:T(8,128)(2,1)} %x_ref.1, ...), custom_call_target="tpu_custom_call", output_to_operand_aliasing={{1}: (5, {}), {2}: (6, {})} | custom-call | flops 10737418240 | bytes 10485760 | tf_op jit(solution)/shard_map/tail/pallas_call | solution.py:720
  211.4 62.9 %head.3 = (bf16[4,256,1024]{2,1,0:T(8,128)(2,1)}, bf16[4,256,256]{2,1,0:T(8,128)(2,1)}, bf16[1024,256]{1,0:T(8,128)(2,1)}, bf16[1024,256]{1,0:T(8,128)(2,1)}) custom-call(bf16[1024,4096]{1,0:T(8,128)(2,1)} %get-tuple-element.23.refs_0_.x_ref, f32[1024,128]{1,0:T(8,128)} %get-tuple-element.39.refs_1_, f32[1024,128]{1,0:T(8,128)} %get-tuple-element.38.refs_2_, ...), custom_call_target="tpu_custom_call" | custom-call | flops 23622320128 | bytes 23068672 | tf_op jit(solution)/shard_map/head/pallas_call | solution.py:459
  274.2 89.3 %last.1 = bf16[4,256,4096]{2,1,0:T(8,128)(2,1)} custom-call(bf16[4,256,1024]{2,1,0:T(8,128)(2,1)} %get-tuple-element.24.hid_ref, bf16[4,256,256]{2,1,0:T(8,128)(2,1)} %get-tuple-element.25.att_ref, bf16[1024,4096]{1,0:T(8,128)(2,1)} %get-tuple-element.23.refs_0_.x_ref, bf16[2,1024,4096]{2,1,0:T(8,128)(2,1)} %wd_ref.3, bf16[2,1,256,4096]{3,2,1,0:T(8,128)(2,1)} %wo_ref.3, ...), custom_call_target="tpu_custom_call" | custom-call | flops 10737418240 | bytes 41943040 | tf_op jit(solution)/shard_map/last/pallas_call | solution.py:907
  363.5 8.0 %emit.1 = (bf16[1024,4096]{1,0:T(8,128)(2,1)}, bf16[2,1024,256]{2,1,0:T(8,128)(2,1)}, bf16[2,1024,256]{2,1,0:T(8,128)(2,1)}) custom-call(bf16[1024,4096]{1,0:T(8,128)(2,1)} %bitcast.10, bf16[1024,256]{1,0:T(8,128)(2,1)} %get-tuple-element.28.k_first, bf16[1024,256]{1,0:T(8,128)(2,1)} %get-tuple-element.29.k_second, ...), custom_call_target="tpu_custom_call" | custom-call | tf_op jit(solution)/shard_map/emit/pallas_call | solution.py:956
  (1 shorter events, 0.0 us)

commit v9 on v0

v9 whole, which is shorter than its diff:
```python
import functools
import math
import jax
import jax.numpy as jnp
from jax import lax
from jax.experimental import pallas as pl
from jax.experimental.pallas import tpu as pltpu
from jax.sharding import PartitionSpec as P

ROPE_BASE = 500000.0
EPS = 1e-5


def rope_tables(positions, head_dim):
    half_dim = head_dim // 2
    inv_freq = ROPE_BASE ** (-(jnp.arange(half_dim, dtype=jnp.float32) * 2.0 / head_dim))
    angles = positions.astype(jnp.float32)[..., None] * inv_freq
    return jnp.cos(angles), jnp.sin(angles)


CHIPS = 4
RING = 4
HALVES = 2
DIRS = 2
KV_CHUNKS = 4
W_TILE = 256
NORM_ROWS = 64
CHUNKS = 8
STEPS = 8
PART_SLOTS = 4
RECV_SLOTS = 5
DOWN_TILE = 512
START_GAP = 3
STAGE_GAP = 2
BLOCK_TICK = 19
BLOCK_GAP = 6
LAST_TICK = 43
NEAR_TICKS = ((9, 1), (15, 3))
FAR_TICKS = ((24, 1), (26, 3))
SERVE_TICKS = (31, 35, 39, 42)


def front_kernel(x_ref, cos_ref, sin_ref, gain_ref, wq_ref, wk_ref, wv_ref, wg_ref, wu_ref, wd_ref, wo_ref,
                 hid_all_ref, att_all_ref, k1_ref, v1_ref, k2_ref, v2_ref, gd_ref, go_ref, rest_ref,
                 xbuf, part, recv_a, recv_b, hid, att, wdo, wtile, kv, qbuf, acc, row_max, row_sum, xs, xres,
                 x_sem, res_sem, w_sem, down_sem, cache_sem, rest_sem, own_send, pass_send, ici_recv, core_recv, part_send, part_recv,
                 round_send, round_recv, side_send, side_recv, give_send, give_recv, keep_sem, ring_send, ring_recv, ready_sem):
    tok_count, d_model = xbuf.shape
    head_dim = qbuf.shape[1]
    half_dim = head_dim // 2
    ff_local = hid.shape[1]
    rows_per = tok_count // KV_CHUNKS
    half_rows = tok_count // 2
    lanes = row_max.shape[2]
    chunk_rows = tok_count // CHUNKS
    quarter, eighth = chunk_rows // RING, chunk_rows // (2 * RING)
    half_cols = d_model // HALVES
    piece_cols = half_cols // RING
    bf16, f32 = jnp.bfloat16, jnp.float32
    sign = (1, -1)
    mesh_id = pl.DeviceIdType.MESH

    my_head = lax.axis_index('head')
    pos_z, pos_y = my_head // RING, my_head % RING
    my_seq = lax.axis_index('seq')
    chip, core = my_seq // 2, my_seq % 2
    other = chip * 2 + 1 - core

    def wrap(n):
        return (n + RING) % RING

    def y_peer(d):
        return pos_z * RING + wrap(pos_y + sign[d])

    def z_device(z):
        return wrap(z) * RING + pos_y

    def z_peer(d):
        return z_device(pos_z + sign[d])

    def x_device(n):
        return wrap(chip + n) * 2 + core

    right, left = x_device(1), x_device(-1)

    def span(start, size, unit=None):
        return pl.ds(pl.multiple_of(start, unit or size), size)

    def remote(src, dst, send, recv, **to):
        return pltpu.make_async_remote_copy(src_ref=src, dst_ref=dst, send_sem=send, recv_sem=recv, device_id=to, device_id_type=mesh_id)

    def x_load(i):
        return pltpu.make_async_copy(x_ref.at[span(i * rows_per, rows_per), :], xs.at[i % 2], x_sem.at[i % 2])

    def weights(layer, piece):
        slot = piece % 2
        if isinstance(piece, int) and piece < 2:
            refs = ((wk_ref, wv_ref), (wq_ref,))[piece]
            return [pltpu.make_async_copy(ref.at[layer], wtile.at[slot, n], w_sem.at[slot, n]) for n, ref in enumerate(refs)]
        cols = span((piece - 2) * W_TILE, W_TILE)
        return [pltpu.make_async_copy(ref.at[layer, :, cols], wtile.at[slot, n], w_sem.at[slot, n]) for n, ref in enumerate((wg_ref, wu_ref))]

    def start(copies):
        for copy in copies:
            copy.start()

    def wait(copies):
        for copy in copies:
            copy.wait()

    down_tiles = d_model // DOWN_TILE

    def down_load(i):
        cols = span(i * DOWN_TILE, DOWN_TILE)
        return [pltpu.make_async_copy(wd_ref.at[0, :, cols], wdo.at[i % 2, pl.ds(0, ff_local), :], down_sem.at[i % 2, 0]),
                pltpu.make_async_copy(wo_ref.at[0, 0, :, cols], wdo.at[i % 2, pl.ds(ff_local, head_dim), :], down_sem.at[i % 2, 1])]

    def kv_copy(origin_chip, origin_core, i, to, send, recv):
        rows = kv.at[span((origin_chip * 2 + origin_core) * tok_count + i * rows_per, rows_per), :]
        return remote(rows, rows, send, recv, seq=to)

    def kv_routes(layer, i):
        late = i >= KV_CHUNKS // 2
        early = jnp.logical_not(late) if not isinstance(i, int) else not late

        def to(send, recv, origin_chip, origin_core, device):
            return kv_copy(origin_chip, origin_core, i, device, send, recv)
        own, passed, ici, side = own_send.at[layer], pass_send.at[layer], ici_recv.at[layer], core_recv.at[layer]
        return {
            'right': (chip < CHIPS - 1, lambda: to(own.at[0, i], ici.at[0, i], chip, core, right)),
            'wrap': (chip == 0, lambda: to(own.at[1, i], ici.at[2, i], chip, core, left)),
            'relay': (jnp.logical_and(late, chip == 1), lambda: to(own.at[3, i], ici.at[3, i], chip, core, left)),
            'other': (core == 0, lambda: to(own.at[2, i], side.at[0, i], chip, core, other)),
            'on_right': (jnp.logical_and(early, jnp.logical_and(chip >= 1, chip < CHIPS - 1)), lambda: to(passed.at[0, i], ici.at[1, i], chip - 1, core, right)),
            'from_relay': (jnp.logical_and(late, chip == 0), lambda: to(passed.at[0, i], ici.at[1, i], 1, core, left)),
            'on_left': (jnp.logical_and(late, chip == CHIPS - 1), lambda: to(passed.at[0, i], ici.at[1, i], 0, core, left)),
            'side1': (chip >= 1, lambda: to(passed.at[1, i], side.at[1, i], chip - 1, core, other)),
            'side2': (chip >= 2, lambda: to(passed.at[2, i], side.at[2, i], chip - 2, core, other)),
            'side3': (chip >= 3, lambda: to(passed.at[3, i], side.at[3, i], chip - 3, core, other)),
        }

    def start_route(layer, i, name):
        condition, copy = kv_routes(layer, i)[name]

        @pl.when(condition)
        def _():
            copy().start()

    def send_kv(layer, i):
        for name in ('right', 'wrap', 'relay', 'other'):
            start_route(layer, i, name)

    def kv_sent(layer):
        for i in range(KV_CHUNKS):
            for condition, copy in kv_routes(layer, i).values():
                @pl.when(condition)
                def _():
                    copy().wait_send()

    def serve(layer, back, i):
        @pl.when(chip >= back)
        def _():
            kv_copy(chip - back, core, i, other, pass_send.at[layer, back, i], ici_recv.at[layer, back - 1, i]).wait_recv()
        start_route(layer, i, 'side%d' % back)
        if back == 1:
            start_route(layer, i, 'on_right')
        if back == 3:
            start_route(layer, i, 'on_left')

    def relay(layer, i):
        condition, copy = kv_routes(layer, i)['from_relay']

        @pl.when(condition)
        def _():
            kv_copy(1, core, i, left, pass_send.at[layer, 0, i], ici_recv.at[layer, 3, i]).wait_recv()
            copy().start()

    def serve_all(layer, i):
        serve(layer, 1, i)
        serve(layer, 3, i)
        relay(layer, i)

    def taken(layer, back, chunks):
        for i in chunks:
            kv_copy(chip - back, 1 - core, i, other, pass_send.at[layer, 0, i], core_recv.at[layer, back, i]).wait_recv()

    def z_parts(step, d):
        copies = []
        for n, (own_ref, all_ref) in enumerate(((wd_ref, gd_ref), (wo_ref, go_ref))):
            size = all_ref.shape[1] // (2 * CHIPS)
            if step == 0:
                rows = span(my_seq * size, size)
                src = own_ref.at[1, rows, :] if n == 0 else own_ref.at[1, 0, rows, :]
                dst = all_ref.at[pos_z, rows, :]
            else:
                rows = span(my_seq * size + d * (size // 2), size // 2)
                src = dst = all_ref.at[wrap(pos_z - sign[d]), rows, :]
            copies.append(remote(src, dst, part_send.at[step, d, n], part_recv.at[step, d, n], head=z_peer(d)))
        return copies

    def part_copies(j, part_chip, part_core, half, send, recv, to):
        copies = []
        for n, ref in enumerate((gd_ref, go_ref)):
            size = ref.shape[1] // (2 * CHIPS)
            first = (part_chip * 2 + part_core) * size
            rows = span(first, size) if half is None else span(first + half * (size // 2), size // 2)
            place = ref.at[wrap(pos_z + j), rows, :]
            copies.append(remote(place, place, send.at[n], recv.at[n], seq=to))
        return copies

    def own_part(j, d):
        return part_copies(j, chip, core, None, round_send.at[0, j - 1, d], round_recv.at[0, j - 1, d], x_device(sign[d]))

    def far_part(j, d):
        return part_copies(j, wrap(chip - sign[d]), core, d, round_send.at[1, j - 1, d], round_recv.at[1, j - 1, d], x_device(sign[d]))

    def side_part(j, n, side):
        return part_copies(j, wrap(chip + n), side, None, side_send.at[j - 1, n], side_recv.at[j - 1, n], other)

    def round_start(j):
        for d in range(DIRS):
            start(own_part(j, d))
        start(side_part(j, 0, core))

    def near_parts(j):
        for d in range(DIRS):
            for copy in own_part(j, d):
                copy.wait_recv()
            start(far_part(j, d) + side_part(j, 3 if d == 0 else 1, core))

    def far_parts(j):
        for d in range(DIRS):
            for copy in far_part(j, d):
                copy.wait_recv()
        start(side_part(j, 2, core))

    def give_hidden(z, i, source):
        cols = span(i * W_TILE, W_TILE)
        return remote(hid.at[span(z * rows_per, rows_per), cols], hid_all_ref.at[source, :, cols], give_send.at[z, i], give_recv.at[source, i], head=z_device(z))

    def keep_hidden(i):
        cols = span(i * W_TILE, W_TILE)
        return pltpu.make_async_copy(hid.at[span(pos_z * rows_per, rows_per), cols], hid_all_ref.at[pos_z, :, cols], keep_sem.at[i])

    def give_rows(z, source):
        return remote(att.at[span(z * rows_per, rows_per), :], att_all_ref.at[source], give_send.at[z, KV_CHUNKS], give_recv.at[source, KV_CHUNKS], head=z_device(z))

    def keep_rows():
        return pltpu.make_async_copy(att.at[span(pos_z * rows_per, rows_per), :], att_all_ref.at[pos_z], keep_sem.at[KV_CHUNKS])

    def norm_rows(x_few, layer):
        x_f32 = x_few.astype(f32)
        inv_rms = lax.rsqrt(jnp.mean(x_f32 * x_f32, axis=-1, keepdims=True) + EPS)
        return (x_f32 * inv_rms * gain_ref[pl.ds(layer, 1), :].astype(f32)).astype(bf16)

    def rope(values, rows):
        cos_t, sin_t = cos_ref[rows, :], sin_ref[rows, :]
        wide = values.astype(bf16).astype(f32)
        first, second = wide[:, :half_dim], wide[:, half_dim:]
        return jnp.concatenate([first * cos_t - second * sin_t, second * cos_t + first * sin_t], axis=1).astype(bf16)

    def dot(a, b):
        return jnp.dot(a, b, preferred_element_type=f32)

    scale = 1.0 / math.sqrt(head_dim)

    def keys_values(normed, i):
        rows = span(i * rows_per, rows_per)
        own = span(my_seq * tok_count + i * rows_per, rows_per)
        kv[own, :head_dim] = rope(dot(normed, wtile[0, 0]), rows)
        kv[own, head_dim:] = dot(normed, wtile[0, 1]).astype(bf16)

    def queries(normed, i):
        rows = span(i * rows_per, rows_per)
        qbuf[rows, :] = (rope(dot(normed, wtile[1, 0]), rows).astype(f32) * scale).astype(bf16)

    def gated(normed, i, tile):
        gate = dot(normed, wtile[tile % 2, 0])
        up = dot(normed, wtile[tile % 2, 1])
        hid[span(i * rows_per, rows_per), span(tile * W_TILE, W_TILE)] = (gate * jax.nn.sigmoid(gate) * up).astype(bf16)

    def attend(key_start, q_half, side, masked, first):
        rows = pl.ds(q_half * half_rows, half_rows)
        some = span(key_start, half_rows)
        logits = lax.dot_general(qbuf[rows, :], kv[some, :head_dim], (((1,), (1,)), ((), ())), preferred_element_type=f32)
        if masked:
            seen = lax.broadcasted_iota(jnp.int32, logits.shape, 0) >= lax.broadcasted_iota(jnp.int32, logits.shape, 1)
            logits = jnp.where(seen, logits, -jnp.inf)
        block_max = jnp.max(logits, axis=-1, keepdims=True)
        if first:
            new_max = jnp.broadcast_to(block_max, (half_rows, lanes))
        else:
            new_max = jnp.maximum(row_max[side, rows, :], block_max)
        prob = jnp.exp(logits - jnp.concatenate([new_max] * (half_rows // lanes), axis=1))
        block_sum = jnp.sum(prob, axis=-1, keepdims=True)
        block_out = dot(prob.astype(bf16), kv[some, head_dim:])
        if first:
            row_sum[side, rows, :] = jnp.broadcast_to(block_sum, (half_rows, lanes))
            acc[side, rows, :] = block_out
        else:
            rescale = jnp.exp(row_max[side, rows, :] - new_max)
            row_sum[side, rows, :] = row_sum[side, rows, :] * rescale + block_sum
            acc[side, rows, :] = acc[side, rows, :] * jnp.concatenate([rescale] * (head_dim // lanes), axis=1) + block_out
        row_max[side, rows, :] = new_max

    def attend_own():
        own_start = my_seq * tok_count
        attend(own_start, 0, 0, True, True)
        attend(own_start, 1, 0, False, True)
        attend(own_start + half_rows, 1, 1, True, True)
        top_rows = pl.ds(0, half_rows)
        row_max[1, top_rows, :] = jnp.full((half_rows, lanes), -jnp.inf, f32)
        row_sum[1, top_rows, :] = jnp.zeros((half_rows, lanes), f32)
        acc[1, top_rows, :] = jnp.zeros((half_rows, head_dim), f32)

    def past_start(n):
        later = n - core
        back = jnp.where(later < 2, 1, jnp.where(chip == CHIPS - 1, jnp.where(later < 4, 3, 2), 2))
        block = (chip - back) * 2 + jnp.where(later % 2 == 0, core, 1 - core)
        return jnp.where(jnp.logical_and(core == 1, n == 0), chip * 2, block) * tok_count

    def attend_past(layer, chunks, visits):
        def past(n, carry):
            @pl.when(jnp.logical_and(core == 1, n == 0))
            def _():
                taken(layer, 0, chunks)

            for back in (1, 3, 2):
                place = 0 if back == 1 else 2 if back == 3 else jnp.where(chip == CHIPS - 1, 4, 2)
                if back == 2:
                    @pl.when(jnp.logical_and(chip >= back, n == core + place))
                    def _():
                        for i in chunks:
                            serve(layer, 2, i)

                @pl.when(jnp.logical_and(chip >= back, n == core + place + 1))
                def _():
                    taken(layer, back, chunks)
            for q_half, side in visits:
                attend(past_start(n) + side * half_rows, q_half, side, False, False)
            return carry

        lax.fori_loop(0, my_seq, past, 0)

    def finish(i, spread):
        rows = pl.ds(i * rows_per, rows_per)
        top = jnp.maximum(row_max[0, rows, :], row_max[1, rows, :])
        shares = [jnp.exp(row_max[side, rows, :] - top) for side in range(2)]
        total = shares[0] * row_sum[0, rows, :] + shares[1] * row_sum[1, rows, :]
        wide = [jnp.concatenate([w] * (head_dim // lanes), axis=1) for w in shares + [total]]
        att[rows, :] = ((acc[0, rows, :] * wide[0] + acc[1, rows, :] * wide[1]) / wide[2]).astype(bf16)
        if spread:
            @pl.when(i == pos_z)
            def _():
                keep_rows().start()

            @pl.when(i != pos_z)
            def _():
                give_rows(i, pos_z).start()

    first_pos, second_pos = (pos_y, pos_z), (pos_z, pos_y)
    first_peer, second_peer = (y_peer, z_peer), (z_peer, y_peer)

    def part_rows(chunk, piece, offset, count):
        return span((chunk % PART_SLOTS) * chunk_rows + piece * quarter + offset, count, eighth)

    def x_rows(chunk, piece, offset, count):
        return span(chunk * chunk_rows + piece * quarter + offset, count, eighth)

    def cols_of(h, piece):
        return span(h * half_cols + piece * piece_cols, piece_cols)

    def half_of(h):
        return pl.ds(h * half_cols, half_cols)

    def message(step, chunk, h, d):
        p1, p2, s = first_pos[h], second_pos[h], sign[d]
        slot = chunk % RECV_SLOTS
        if step == 0:
            src, dst = part.at[part_rows(chunk, wrap(p1 + 2), d * eighth, eighth), half_of(h)], recv_a.at[slot, h, d, pl.ds(quarter, eighth), :]
        elif step == 1:
            src, dst = part.at[part_rows(chunk, wrap(p1 + s), 0, quarter), half_of(h)], recv_a.at[slot, h, d, pl.ds(0, quarter), :]
        elif step == 2:
            src, dst = part.at[part_rows(chunk, p1, d * eighth, eighth), cols_of(h, wrap(p2 + 2))], recv_b.at[slot, h, d, pl.ds(quarter, eighth), :]
        elif step == 3:
            src, dst = part.at[part_rows(chunk, p1, 0, quarter), cols_of(h, wrap(p2 + s))], recv_b.at[slot, h, d, pl.ds(0, quarter), :]
        elif step == 4:
            src = dst = xbuf.at[x_rows(chunk, p1, 0, quarter), cols_of(h, p2)]
        elif step == 5:
            src = dst = xbuf.at[x_rows(chunk, p1, d * eighth, eighth), cols_of(h, wrap(p2 - s))]
        elif step == 6:
            src = dst = xbuf.at[x_rows(chunk, p1, 0, quarter), half_of(h)]
        else:
            src = dst = xbuf.at[x_rows(chunk, wrap(p1 - s), d * eighth, eighth), half_of(h)]
        peer = (first_peer if step in (0, 1, 6, 7) else second_peer)[h](d)
        return remote(src, dst, ring_send.at[chunk, step, h * DIRS + d], ring_recv.at[chunk, step, h * DIRS + d], head=peer)

    def each_message(chunk, steps, act):
        for step in steps:
            for h in range(HALVES):
                for d in range(DIRS):
                    act(message(step, chunk, h, d))

    def residual_load(chunk, h):
        return pltpu.make_async_copy(x_ref.at[x_rows(chunk, first_pos[h], 0, quarter), cols_of(h, second_pos[h])], xres.at[chunk, h], res_sem.at[chunk, h])

    def project(chunk):
        rows = span(chunk * chunk_rows, chunk_rows)
        slot_rows = span((chunk % PART_SLOTS) * chunk_rows, chunk_rows)

        def one_tile(i, carry):
            @pl.when(jnp.logical_or(chunk < CHUNKS - 1, i < down_tiles - 1))
            def _():
                start(down_load((i + 1) % down_tiles))

            wait(down_load(i))
            total = dot(hid[rows, :], wdo[i % 2, :ff_local, :])
            part[slot_rows, span(i * DOWN_TILE, DOWN_TILE)] = total + dot(att[rows, :], wdo[i % 2, ff_local:, :])
            return carry

        lax.fori_loop(0, down_tiles, one_tile, 0)

    def stage(number, chunk):
        slot = chunk % RECV_SLOTS
        if number == 0:
            @pl.when(chunk >= PART_SLOTS)
            def _():
                each_message(chunk - PART_SLOTS, range(4), lambda copy: copy.wait_send())
            project(chunk)
        for h in range(HALVES):
            p1, p2 = first_pos[h], second_pos[h]
            if number:
                for d in range(DIRS):
                    message(number - 1, chunk, h, d).wait_recv()
            if number in (1, 3):
                for d in range(DIRS):
                    if number == 1:
                        rows, cols, arrived = part_rows(chunk, wrap(p1 + sign[d]), d * eighth, eighth), half_of(h), recv_a
                    else:
                        rows, cols, arrived = part_rows(chunk, p1, d * eighth, eighth), cols_of(h, wrap(p2 + sign[d])), recv_b
                    part[rows, cols] = part[rows, cols] + arrived[slot, h, d, pl.ds(quarter, eighth), :]
            if number == 2:
                rows = part_rows(chunk, p1, 0, quarter)
                part[rows, half_of(h)] = part[rows, half_of(h)] + recv_a[slot, h, 0, pl.ds(0, quarter), :] + recv_a[slot, h, 1, pl.ds(0, quarter), :]
            if number == 4:
                residual_load(chunk, h).wait()
                rows, cols = part_rows(chunk, p1, 0, quarter), cols_of(h, p2)
                total = part[rows, cols] + recv_b[slot, h, 0, pl.ds(0, quarter), :] + recv_b[slot, h, 1, pl.ds(0, quarter), :]
                update = total.astype(bf16).astype(f32)
                xbuf[x_rows(chunk, p1, 0, quarter), cols] = (xres[chunk, h].astype(f32) + update).astype(bf16)
            if number < STEPS:
                for d in range(DIRS):
                    message(number, chunk, h, d).start()

    x_load(0).start()
    start(weights(0, 0))
    x_load(1).start()
    start(weights(0, 1))
    barrier = pltpu.get_barrier_semaphore()
    for peer in (left, right, other):
        pl.semaphore_signal(barrier, inc=1, device_id={'seq': peer}, device_id_type=mesh_id)
    for peer in [z_device(pos_z + j) for j in range(1, RING)] + [y_peer(d) for d in range(DIRS)]:
        pl.semaphore_signal(barrier, inc=1, device_id={'head': peer}, device_id_type=mesh_id)
    pl.semaphore_wait(barrier, 8)
    for d in range(DIRS):
        start(z_parts(0, d))

    def prepare(i, carry):
        x_load(i).wait()

        def few(n, inner):
            xbuf[span(i * rows_per + n * NORM_ROWS, NORM_ROWS), :] = norm_rows(xs[i % 2, span(n * NORM_ROWS, NORM_ROWS), :], 0)
            return inner

        lax.fori_loop(0, rows_per // NORM_ROWS, few, 0)

        @pl.when(i + 2 < KV_CHUNKS)
        def _():
            x_load(i + 2).start()

        @pl.when(i == 0)
        def _():
            wait(weights(0, 0))

        keys_values(xbuf[span(i * rows_per, rows_per), :], i)
        send_kv(0, i)
        return carry

    lax.fori_loop(0, KV_CHUNKS, prepare, 0)
    start(weights(0, 2))
    own_rows = span(my_seq * tok_count, tok_count)

    def cache_stores(layer):
        k_ref, v_ref = ((k1_ref, v1_ref), (k2_ref, v2_ref))[layer]
        return [pltpu.make_async_copy(kv.at[own_rows, pl.ds(0, head_dim)], k_ref, cache_sem.at[layer, 0]),
                pltpu.make_async_copy(kv.at[own_rows, pl.ds(head_dim, head_dim)], v_ref, cache_sem.at[layer, 1])]

    start(cache_stores(0))
    wait(weights(0, 1))

    def query(i, carry):
        queries(xbuf[span(i * rows_per, rows_per), :], i)
        return carry

    lax.fori_loop(0, KV_CHUNKS, query, 0)
    start(weights(0, 3))
    start(down_load(0))

    def residuals(n, carry):
        for h in range(HALVES):
            residual_load(n, h).start()
        return carry

    lax.fori_loop(0, CHUNKS, residuals, 0)

    def gate_tile(tile, carry):
        wait(weights(0, tile + 2))

        def rows_step(i, inner):
            gated(xbuf[span(i * rows_per, rows_per), :], i, tile)
            return inner

        lax.fori_loop(0, KV_CHUNKS, rows_step, 0)

        @pl.when(tile < 2)
        def _():
            start(weights(0, tile + 4))

        @pl.when(tile == 2)
        def _():
            start(weights(1, 0))
            for d in range(DIRS):
                for copy in z_parts(0, d):
                    copy.wait_recv()
                start(z_parts(1, d))

        @pl.when(tile == 3)
        def _():
            start(weights(1, 1))
        serve_all(0, tile)
        return carry

    lax.fori_loop(0, ff_local // W_TILE, gate_tile, 0)
    attend_own()
    attend_past(0, range(KV_CHUNKS), ((0, 0), (0, 1)))
    finish(0, False)
    finish(1, False)
    round_start(1)
    round_start(3)

    def block_work(j, phase):
        @pl.when(phase == 0)
        def _():
            @pl.when(j == 0)
            def _():
                for n in range(3):
                    pl.semaphore_wait(ready_sem.at[n], 1)

            def few(n, inner):
                xs[0, span(n * NORM_ROWS, NORM_ROWS), :] = norm_rows(xbuf[span(j * rows_per + n * NORM_ROWS, NORM_ROWS), :], 1)
                return inner

            lax.fori_loop(0, rows_per // NORM_ROWS, few, 0)
            wait(weights(1, 0))
            keys_values(xs[0], j)
            send_kv(1, j)
            start(weights(1, 2))

        @pl.when(phase == 1)
        def _():
            wait(weights(1, 1))
            queries(xs[0], j)
            start(weights(1, 3))

        @pl.when(jnp.logical_and(phase >= 1, phase <= 4))
        def _():
            tile = phase - 1
            wait(weights(1, tile + 2))
            gated(xs[0], j, tile)

            @pl.when(tile < 2)
            def _():
                start(weights(1, tile + 4))

            @pl.when(jnp.logical_and(tile == 2, j < KV_CHUNKS - 1))
            def _():
                start(weights(1, 0))

            @pl.when(jnp.logical_and(tile == 3, j < KV_CHUNKS - 1))
            def _():
                start(weights(1, 1))

            @pl.when(j == pos_z)
            def _():
                keep_hidden(tile).start()

            @pl.when(j != pos_z)
            def _():
                give_hidden(j, tile, pos_z).start()

    def tick(t, carry):
        for number in range(STEPS, -1, -1):
            place = t - STAGE_GAP * number
            chunk = place // START_GAP

            @pl.when(jnp.logical_and(place >= 0, jnp.logical_and(place % START_GAP == 0, chunk < CHUNKS)))
            def _():
                stage(number, chunk)

        @pl.when(jnp.logical_and(t >= 1, jnp.logical_and(t < 8, t <= my_seq)))
        def _():
            for side in range(2):
                attend(past_start(t - 1) + side * half_rows, 1, side, False, False)

        @pl.when(t == 2)
        def _():
            for d in range(DIRS):
                for copy in z_parts(1, d):
                    copy.wait_recv()
            round_start(2)

        @pl.when(t == 8)
        def _():
            finish(2, False)
            finish(3, False)
            kv_sent(0)
            wait(cache_stores(0))
            for n, peer in enumerate((left, right, other)):
                pl.semaphore_signal(ready_sem.at[n], inc=1, device_id={'seq': peer}, device_id_type=mesh_id)

        for when, j in NEAR_TICKS:
            @pl.when(t == when)
            def _():
                near_parts(j)

        for when, j in FAR_TICKS:
            @pl.when(t == when)
            def _():
                far_parts(j)

        late = t - BLOCK_TICK

        @pl.when(late >= 0)
        def _():
            block_work(late // BLOCK_GAP, late % BLOCK_GAP)

        for i, when in enumerate(SERVE_TICKS):
            @pl.when(t == when)
            def _():
                serve_all(1, i)
        return carry

    lax.fori_loop(0, LAST_TICK, tick, 0)

    start(cache_stores(1))
    rest_store = pltpu.make_async_copy(xbuf.at[span(pos_z * rows_per + pos_y * (rows_per // RING), rows_per // RING), :], rest_ref, rest_sem)
    rest_store.start()
    near_parts(2)
    attend_own()
    attend_past(1, (0, 1), ((0, 0), (1, 0)))
    attend_past(1, (2, 3), ((0, 1), (1, 1)))
    for i in range(KV_CHUNKS):
        finish(i, True)
    far_parts(2)

    wait(cache_stores(1))
    rest_store.wait()
    for i in range(KV_CHUNKS):
        keep_hidden(i).wait()
    keep_rows().wait()
    kv_sent(1)
    for d in range(DIRS):
        for step in range(2):
            for copy in z_parts(step, d):
                copy.wait_send()
    for j in range(1, RING):
        for d in range(DIRS):
            for copy in own_part(j, d) + far_part(j, d):
                copy.wait_send()
        for n in range(CHIPS):
            for copy in side_part(j, n, 1 - core):
                copy.wait_recv()
            for copy in side_part(j, n, core):
                copy.wait_send()
        z = wrap(pos_z + j)
        for i in range(KV_CHUNKS):
            give_hidden(z, i, z).wait_recv()
            give_hidden(z, i, pos_z).wait_send()
        give_rows(z, z).wait_recv()
        give_rows(z, pos_z).wait_send()

    def drain(chunk, carry):
        @pl.when(chunk >= CHUNKS - PART_SLOTS)
        def _():
            each_message(chunk, range(4), lambda copy: copy.wait_send())
        each_message(chunk, range(4, STEPS), lambda copy: copy.wait_send())
        return carry

    lax.fori_loop(0, CHUNKS, drain, 0)


def front(x_loc, cos_t, sin_t, norm_gain, w_q, w_k, w_v, w_gate, w_up, w_down, w_o):
    tok_count, d_model = x_loc.shape
    head_dim = w_q.shape[2]
    ff_local = w_gate.shape[2]
    rows_per = tok_count // KV_CHUNKS
    chunk_rows = tok_count // CHUNKS
    landed = 3 * chunk_rows // (2 * RING)
    half_cols = d_model // HALVES
    any_spec = pl.BlockSpec(memory_space=pl.ANY)
    vmem_spec = pl.BlockSpec(memory_space=pltpu.VMEM)
    bf16, f32 = jnp.bfloat16, jnp.float32
    dma = pltpu.SemaphoreType.DMA
    shape = jax.ShapeDtypeStruct
    return pl.pallas_call(
        front_kernel,
        out_shape=[shape((RING, rows_per, ff_local), bf16), shape((RING, rows_per, head_dim), bf16)] + [shape((tok_count, head_dim), bf16)] * 4
        + [shape((RING, ff_local, d_model), bf16), shape((RING, head_dim, d_model), bf16), shape((rows_per // RING, d_model), bf16)],
        in_specs=[any_spec, vmem_spec, vmem_spec, vmem_spec] + [any_spec] * 7,
        out_specs=[any_spec] * 9,
        scratch_shapes=[
            pltpu.VMEM((tok_count, d_model), bf16),
            pltpu.VMEM((PART_SLOTS * chunk_rows, d_model), f32),
            pltpu.VMEM((RECV_SLOTS, HALVES, DIRS, landed, half_cols), f32),
            pltpu.VMEM((RECV_SLOTS, HALVES, DIRS, landed, half_cols // RING), f32),
            pltpu.VMEM((tok_count, ff_local), bf16),
            pltpu.VMEM((tok_count, head_dim), bf16),
            pltpu.VMEM((2, ff_local + head_dim, DOWN_TILE), bf16),
            pltpu.VMEM((2, 2, d_model, W_TILE), bf16),
            pltpu.VMEM((2 * CHIPS * tok_count, 2 * head_dim), bf16),
            pltpu.VMEM((tok_count, head_dim), bf16),
            pltpu.VMEM((2, tok_count, head_dim), f32),
            pltpu.VMEM((2, tok_count, 128), f32),
            pltpu.VMEM((2, tok_count, 128), f32),
            pltpu.VMEM((2, rows_per, d_model), bf16),
            pltpu.VMEM((CHUNKS, HALVES, chunk_rows // RING, half_cols // RING), bf16),
            dma((2,)), dma((CHUNKS, HALVES)), dma((2, 2)), dma((2, 2)), dma((2, 2)), dma,
            dma((2, 4, KV_CHUNKS)), dma((2, 4, KV_CHUNKS)), dma((2, 4, KV_CHUNKS)), dma((2, 4, KV_CHUNKS)), dma((2, DIRS, 2)), dma((2, DIRS, 2)),
            dma((2, RING - 1, DIRS, 2)), dma((2, RING - 1, DIRS, 2)), dma((RING - 1, CHIPS, 2)), dma((RING - 1, CHIPS, 2)),
            dma((RING, KV_CHUNKS + 1)), dma((RING, KV_CHUNKS + 1)), dma((KV_CHUNKS + 1,)),
            dma((CHUNKS, STEPS, HALVES * DIRS)), dma((CHUNKS, STEPS, HALVES * DIRS)),
            pltpu.SemaphoreType.REGULAR((3,)),
        ],
        compiler_params=pltpu.CompilerParams(collective_id=0, has_side_effects=True, vmem_limit_bytes=67043328),
        name='front',
    )(x_loc, cos_t, sin_t, norm_gain, w_q, w_k, w_v, w_gate, w_up, w_down, w_o)


SKEW = 2
LAST_STEPS = 6
LAST_COLS = 256


def last_kernel(layer, hid_ref, att_ref, rest_ref, wd_ref, wo_ref, gd_ref, go_ref, out_ref, part, xres, xbuf, wtile, landed, w_sem, x_sem, store_sem, send_sem, recv_sem):
    rows, d_model = part.shape
    block = wtile.shape[3]
    block_count = d_model // block
    ff_local = hid_ref.shape[2]
    quarter, eighth = rows // RING, rows // (2 * RING)
    my_head = lax.axis_index('head')
    pos_z, pos_y = my_head // RING, my_head % RING
    sign = (1, -1)

    def cols_of(c):
        return pl.ds(pl.multiple_of(c * block, block), block)

    def w_loads(c):
        copies = []
        for j in range(RING):
            z = (pos_z + j) % RING
            down = wd_ref.at[layer, :, cols_of(c)] if j == 0 else gd_ref.at[z, :, cols_of(c)]
            out = wo_ref.at[layer, 0, :, cols_of(c)] if j == 0 else go_ref.at[z, :, cols_of(c)]
            copies.append(pltpu.make_async_copy(down, wtile.at[c % 2, j, pl.ds(0, ff_local), :], w_sem.at[c % 2, j, 0]))
            copies.append(pltpu.make_async_copy(out, wtile.at[c % 2, j, pl.ds(ff_local, wo_ref.shape[2]), :], w_sem.at[c % 2, j, 1]))
        return copies

    for copy in w_loads(0):
        copy.start()
    x_load = pltpu.make_async_copy(rest_ref, xres, x_sem)
    x_load.start()

    def y_device(d):
        return pos_z * RING + (pos_y + sign[d] + RING) % RING

    def z_device(d):
        return (pos_z + sign[d] + RING) % RING * RING + pos_y

    barrier = pltpu.get_barrier_semaphore()
    for device in (y_device, z_device):
        for d in range(DIRS):
            pl.semaphore_signal(barrier, inc=1, device_id={'head': device(d)}, device_id_type=pl.DeviceIdType.MESH)
    pl.semaphore_wait(barrier, 2 * DIRS)
    x_load.wait()

    def rows_of(piece, offset, count):
        return pl.ds(pl.multiple_of(piece * quarter + offset, eighth), count)

    def message(step, c, d, z_first):
        s = sign[d]
        near, behind = (pos_y + s + RING) % RING, (pos_y - s + RING) % RING
        if step == 0:
            src, dst = part.at[rows_of((pos_y + 2) % RING, d * eighth, eighth), cols_of(c)], landed.at[c, d, pl.ds(quarter, eighth), :]
        elif step == 1:
            src, dst = part.at[rows_of(near, 0, quarter), cols_of(c)], landed.at[c, d, pl.ds(0, quarter), :]
        elif z_first:
            back = (pos_z - s + RING) % RING
            if step == 2:
                src = dst = xbuf.at[pos_z, rows_of(pos_y, 0, quarter), cols_of(c)]
            elif step == 3:
                src = dst = xbuf.at[back, rows_of(pos_y, d * eighth, eighth), cols_of(c)]
            elif step == 4:
                src = dst = xbuf.at[:, rows_of(pos_y, 0, quarter), cols_of(c)]
            else:
                src = dst = xbuf.at[:, rows_of(behind, d * eighth, eighth), cols_of(c)]
        else:
            if step == 2:
                src = dst = xbuf.at[pos_z, rows_of(pos_y, 0, quarter), cols_of(c)]
            elif step == 3:
                src = dst = xbuf.at[pos_z, rows_of(behind, d * eighth, eighth), cols_of(c)]
            elif step == 4:
                src = dst = xbuf.at[pos_z, :, cols_of(c)]
            else:
                src = dst = xbuf.at[(pos_z - s + RING) % RING, pl.ds(d * (rows // 2), rows // 2), cols_of(c)]
        along_y = step < 2 or (step < 4) != z_first
        return pltpu.make_async_remote_copy(
            src_ref=src, dst_ref=dst, send_sem=send_sem.at[c, step, d], recv_sem=recv_sem.at[c, step, d],
            device_id={'head': (y_device if along_y else z_device)(d)}, device_id_type=pl.DeviceIdType.MESH)

    def on_messages(step, c, act):
        if step < 2:
            for d in range(DIRS):
                act(message(step, c, d, False))
            return

        @pl.when(c % 4 == 3)
        def _():
            for d in range(DIRS):
                act(message(step, c, d, True))

        @pl.when(c % 4 != 3)
        def _():
            for d in range(DIRS):
                act(message(step, c, d, False))

    def store(c):
        return pltpu.make_async_copy(xbuf.at[:, :, cols_of(c)], out_ref.at[:, :, cols_of(c)], store_sem.at[c])

    def project(c):
        @pl.when(c + 1 < block_count)
        def _():
            for copy in w_loads(c + 1):
                copy.start()

        for copy in w_loads(c):
            copy.wait()
        total = None
        for j in range(RING):
            z = (pos_z + j) % RING
            down = jnp.dot(hid_ref[z], wtile[c % 2, j, :ff_local, :], preferred_element_type=jnp.float32)
            down = down + jnp.dot(att_ref[z], wtile[c % 2, j, ff_local:, :], preferred_element_type=jnp.float32)
            total = down if total is None else total + down
        part[:, cols_of(c)] = total

    def stage(number, c):
        if number == 0:
            project(c)
        else:
            on_messages(number - 1, c, lambda copy: copy.wait_recv())
        if number == 1:
            for d in range(DIRS):
                piece = rows_of((pos_y + sign[d] + RING) % RING, d * eighth, eighth)
                part[piece, cols_of(c)] = part[piece, cols_of(c)] + landed[c, d, pl.ds(quarter, eighth), :]
        if number == 2:
            own = rows_of(pos_y, 0, quarter)
            total = part[own, cols_of(c)] + landed[c, 0, pl.ds(0, quarter), :] + landed[c, 1, pl.ds(0, quarter), :]
            update = total.astype(jnp.bfloat16).astype(jnp.float32)
            xbuf[pos_z, own, cols_of(c)] = (xres[:, cols_of(c)].astype(jnp.float32) + update).astype(jnp.bfloat16)
        if number < LAST_STEPS:
            on_messages(number, c, lambda copy: copy.start())
        else:
            store(c).start()

    def tick(t, carry):
        for number in range(LAST_STEPS, -1, -1):
            c = t - SKEW * number

            @pl.when(jnp.logical_and(c >= 0, c < block_count))
            def _():
                stage(number, c)
        return carry

    lax.fori_loop(0, block_count + SKEW * LAST_STEPS, tick, 0)

    def drain(c, carry):
        for step in range(LAST_STEPS):
            on_messages(step, c, lambda copy: copy.wait_send())
        store(c).wait()
        return carry

    lax.fori_loop(0, block_count, drain, 0)


def layer_last(layer, hid_all, att_all, rest, w_down, w_o, all_down, all_out):
    rows, d_model = hid_all.shape[1], rest.shape[1]
    tok_count = RING * rows
    depth = hid_all.shape[2] + att_all.shape[2]
    any_spec = pl.BlockSpec(memory_space=pl.ANY)
    vmem_spec = pl.BlockSpec(memory_space=pltpu.VMEM)
    blocks = d_model // LAST_COLS
    out = pl.pallas_call(
        functools.partial(last_kernel, layer),
        out_shape=jax.ShapeDtypeStruct((RING, rows, d_model), jnp.bfloat16),
        in_specs=[vmem_spec, vmem_spec] + [any_spec] * 5,
        out_specs=any_spec,
        scratch_shapes=[
            pltpu.VMEM((rows, d_model), jnp.float32),
            pltpu.VMEM((rows // RING, d_model), jnp.bfloat16),
            pltpu.VMEM((RING, rows, d_model), jnp.bfloat16),
            pltpu.VMEM((2, RING, depth, LAST_COLS), jnp.bfloat16),
            pltpu.VMEM((blocks, DIRS, 3 * rows // (2 * RING), LAST_COLS), jnp.float32),
            pltpu.SemaphoreType.DMA((2, RING, 2)),
            pltpu.SemaphoreType.DMA,
            pltpu.SemaphoreType.DMA((blocks,)),
            pltpu.SemaphoreType.DMA((blocks, LAST_STEPS, DIRS)),
            pltpu.SemaphoreType.DMA((blocks, LAST_STEPS, DIRS)),
        ],
        compiler_params=pltpu.CompilerParams(collective_id=layer, has_side_effects=True, vmem_limit_bytes=63 * 1024 * 1024),
        cost_estimate=pl.CostEstimate(flops=2 * tok_count * depth * d_model, bytes_accessed=4 * depth * d_model * 2, transcendentals=0),
        name='last',
    )(hid_all, att_all, rest, w_down, w_o, all_down, all_out)
    return out.reshape(tok_count, d_model)


EMIT_PARTS = 8


def emit_kernel(x_ref, k_first, k_second, v_first, v_second, x_out, k_out, v_out, xbuf, rows, load_sem, store_sem):
    size = x_ref.shape[0] // EMIT_PARTS
    loads, stores = [], []
    for n in range(EMIT_PARTS):
        part = pl.ds(n * size, size)
        loads.append(pltpu.make_async_copy(x_ref.at[part, :], xbuf.at[part, :], load_sem.at[n]))
        stores.append(pltpu.make_async_copy(xbuf.at[part, :], x_out.at[part, :], store_sem.at[n]))
    for n, (ref, out) in enumerate(((k_first, k_out.at[0]), (k_second, k_out.at[1]), (v_first, v_out.at[0]), (v_second, v_out.at[1]))):
        loads.append(pltpu.make_async_copy(ref, rows.at[n], load_sem.at[EMIT_PARTS + n]))
        stores.append(pltpu.make_async_copy(rows.at[n], out, store_sem.at[EMIT_PARTS + n]))
    for copy in loads:
        copy.start()
    for load, store in zip(loads, stores):
        load.wait()
        store.start()
    for copy in stores:
        copy.wait()


def emit(x_out, k_first, k_second, v_first, v_second):
    any_spec = pl.BlockSpec(memory_space=pl.ANY)
    cache = jax.ShapeDtypeStruct((2,) + k_first.shape, jnp.bfloat16)
    return pl.pallas_call(
        emit_kernel,
        out_shape=[jax.ShapeDtypeStruct(x_out.shape, jnp.bfloat16), cache, cache],
        in_specs=[any_spec] * 5,
        out_specs=[any_spec] * 3,
        scratch_shapes=[
            pltpu.VMEM(x_out.shape, jnp.bfloat16),
            pltpu.VMEM((4,) + k_first.shape, jnp.bfloat16),
            pltpu.SemaphoreType.DMA((EMIT_PARTS + 4,)),
            pltpu.SemaphoreType.DMA((EMIT_PARTS + 4,)),
        ],
        compiler_params=pltpu.CompilerParams(vmem_limit_bytes=63 * 1024 * 1024),
        name='emit',
    )(x_out, k_first, k_second, v_first, v_second)


def solution(mesh):
    row_spec = P(('batch', 'seq'), None)
    pos_spec = P(('batch', 'seq'))
    head_spec = P(None, None, 'head', None)
    out_proj_spec = P(None, 'head', None, None)
    col_spec = P(None, None, 'head')
    down_spec = P(None, 'head', None)
    cache_spec = P(None, ('batch', 'seq'), 'head', None)

    def local_forward(x_loc, pos_loc, w_q, w_k, w_v, w_o, w_gate, w_up, w_down, norm_gain):
        tok_count, d_model = x_loc.shape
        layer_count = w_q.shape[0]
        head_dim = w_q.shape[3]
        flat_q, flat_k, flat_v = (w.reshape(layer_count, d_model, head_dim) for w in (w_q, w_k, w_v))
        cos_t, sin_t = rope_tables(pos_loc, head_dim)
        hid_all, att_all, k_first, v_first, k_second, v_second, all_down, all_out, rest = front(x_loc, cos_t, sin_t, norm_gain, flat_q, flat_k, flat_v, w_gate, w_up, w_down, w_o)
        x_out = layer_last(1, hid_all, att_all, rest, w_down, w_o, all_down, all_out)
        x_out, k_all, v_all = emit(x_out, k_first, k_second, v_first, v_second)
        cache_shape = (layer_count, tok_count, 1, head_dim)
        return x_out, k_all.reshape(cache_shape), v_all.reshape(cache_shape)

    return jax.shard_map(local_forward, mesh=mesh, in_specs=(row_spec, pos_spec, head_spec, head_spec, head_spec, out_proj_spec, col_spec, col_spec, down_spec, P(None, None)), out_specs=(row_spec, cache_spec, cache_spec), check_vma=False)
```

time: 1170 us -> 398 us (0.34); the launches traced: 1160 us -> 397 us
  blocking collectives: 722 us -> 0 us
  Pallas kernels: 0 us -> 392 us
  matrix products: 174 us -> 0 us
  waiting for transfers between devices: 81.1 us -> 0 us
  starting transfers between devices: 80.9 us -> 0 us
  other arithmetic: 70.7 us -> 3.73 us
  local copies, waits for them, and re-layouts: 23.9 us -> 0 us
    psum x2 -> x0, blocking collectives: 722 us -> none  [local_forward(): update = lax.psum(part_sum, 'head').astype(jnp.bfloat16)]
    pallas_call x0 -> x3, Pallas kernels: none -> 392 us  [the longest x1 295 us: front(): pl.pallas_call(front_kernel, out_shape=[shape((RING, rows_per, ff_local),...]
    dot_general x46 -> x0, matrix products: 174 us -> none  [the longest x2 32.2 us: local_forward(): jnp.dot(hidden, w_down[layer], preferred_element_type=jnp.float32)]
    ppermute x28 -> x0, waiting for transfers between devices: 81.1 us -> none  [the longest x14 43.1 us: pass_step(): k_blk = lax.ppermute(k_blk, 'seq', shift_pairs)]
    ppermute x28 -> x0, starting transfers between devices: 80.9 us -> none  [the longest x14 42.1 us: pass_step(): v_blk = lax.ppermute(v_blk, 'seq', shift_pairs)]
    reduce_sum x18 -> x0, other arithmetic: 32 us -> none  [the longest x16 16.4 us: block_update(): row_sum = row_sum * rescale + jnp.sum(prob_f32, axis=-1)]
    convert_element_type x3 -> x0, other arithmetic: 31 us -> none  [the longest x2 20.8 us: rms_norm(): return (x_f32 * inv_rms * gain_row.astype(jnp.float32)).astype(jnp.bfloat16)]
    while x42 -> x0, local copies, waits for them, and re-layouts: 17.3 us -> none
  transfers between devices with their start and end apart: 28 -> 0, of which waited for: 25 -> 0; matrix products, arithmetic and copies ran while one was open for 3% -> 0% of each run, Pallas kernels for 0% -> 0%
where the time goes in v9:
time: 398 us; the launch traced here: 397 us
  Pallas kernels  392 us (98%)
    pallas_call x1, Pallas kernels, front(): pl.pallas_call(front_kernel, out_shape=[shape((RING, rows_per, ff_local),...  295 us
    pallas_call x1, Pallas kernels, layer_last(): pl.pallas_call(functools.partial(last_kernel, layer), out_shape=jax.Shape...  89.3 us
    pallas_call x1, Pallas kernels, emit(): pl.pallas_call(emit_kernel, out_shape=[jax.ShapeDtypeStruct(x_out.shape,...  8.01 us

profile of v9, /device:TPU:6, one launch (start us, length us, event | category | flops | bytes accessed | tf_op | source)
XLA Modules:
  0.0 397.0 jit_solution(10307462845950353260)
XLA Ops:
  0.6 0.7 convert_element_type.3
  1.3 3.0 multiply_sine_fusion
  4.4 295.1 %front.1 = (bf16[4,256,1024]{2,1,0:T(8,128)(2,1)}, bf16[4,256,256]{2,1,0:T(8,128)(2,1)}, bf16[1024,256]{1,0:T(8,128)(2,1)}, bf16[1024,256]{1,0:T(8,128)(2,1)}, b...) custom-call(bf16[1024,4096]{1,0:T(8,128)(2,1)} %x_ref.1, ...), custom_call_target="tpu_custom_call" | custom-call | tf_op jit(solution)/shard_map/front/pallas_call | solution.py:715
  299.5 89.3 %last.1 = bf16[4,256,4096]{2,1,0:T(8,128)(2,1)} custom-call(bf16[4,256,1024]{2,1,0:T(8,128)(2,1)} %get-tuple-element.15.hid_ref, bf16[4,256,256]{2,1,0:T(8,128)(2,1)} %get-tuple-element.16.att_ref, bf16[64,4096]{1,0:T(8,128)(2,1)} %get-tuple-element.17.rest_ref, bf16[2,1024,4096]{2,1,0:T(8,128)(2,1)} %wd_ref.3, bf16[2,1,256,4096]{3,2,1,0:T(8,128)(2,1)} %wo_ref.3, ...), custom_call_target="tpu_custom_call" | custom-call | flops 10737418240 | bytes 41943040 | tf_op jit(solution)/shard_map/last/pallas_call | solution.py:910
  388.8 8.0 %emit.1 = (bf16[1024,4096]{1,0:T(8,128)(2,1)}, bf16[2,1024,256]{2,1,0:T(8,128)(2,1)}, bf16[2,1024,256]{2,1,0:T(8,128)(2,1)}) custom-call(bf16[1024,4096]{1,0:T(8,128)(2,1)} %bitcast.10, bf16[1024,256]{1,0:T(8,128)(2,1)} %get-tuple-element.20.k_first, bf16[1024,256]{1,0:T(8,128)(2,1)} %get-tuple-element.21.k_second, ...), custom_call_target="tpu_custom_call" | custom-call | tf_op jit(solution)/shard_map/emit/pallas_call | solution.py:959
  (1 shorter events, 0.0 us)

commit v10 on v9

--- a/solution.py
+++ b/solution.py
@@ -37,14 +37,15 @@
 LAST_TICK = 43
 NEAR_TICKS = ((9, 1), (15, 3))
 FAR_TICKS = ((24, 1), (26, 3))
-SERVE_TICKS = (31, 35, 39, 42)
+SERVE_TICKS = (27, 31, 35, 42)
+GIVE_TICK = 37
 
 
 def front_kernel(x_ref, cos_ref, sin_ref, gain_ref, wq_ref, wk_ref, wv_ref, wg_ref, wu_ref, wd_ref, wo_ref,
                  hid_all_ref, att_all_ref, k1_ref, v1_ref, k2_ref, v2_ref, gd_ref, go_ref, rest_ref,
                  xbuf, part, recv_a, recv_b, hid, att, wdo, wtile, kv, qbuf, acc, row_max, row_sum, xs, xres,
                  x_sem, res_sem, w_sem, down_sem, cache_sem, rest_sem, own_send, pass_send, ici_recv, core_recv, part_send, part_recv,
-                 round_send, round_recv, side_send, side_recv, give_send, give_recv, keep_sem, ring_send, ring_recv, ready_sem):
+                 round_send, round_recv, side_send, side_recv, give_send, give_recv, keep_sem, relay_buf, relay_send, relay_recv, ring_send, ring_recv, ready_sem):
     tok_count, d_model = xbuf.shape
     head_dim = qbuf.shape[1]
     half_dim = head_dim // 2
@@ -241,6 +242,30 @@
     def keep_hidden(i):
         cols = span(i * W_TILE, W_TILE)
         return pltpu.make_async_copy(hid.at[span(pos_z * rows_per, rows_per), cols], hid_all_ref.at[pos_z, :, cols], keep_sem.at[i])
+
+    def via_neighbor(z, i):
+        step = jnp.where(i < KV_CHUNKS // 2, 1, -1)
+        return remote(hid.at[span(z * rows_per, rows_per), span(i * W_TILE, W_TILE)], relay_buf.at[i], give_send.at[z, i], relay_recv.at[i], head=z_device(pos_z + step))
+
+    def relay_hidden(i):
+        step = 1 if i < KV_CHUNKS // 2 else -1
+        source = wrap(pos_z - step)
+        return remote(relay_buf.at[i], hid_all_ref.at[source, :, span(i * W_TILE, W_TILE)], relay_send.at[i], give_recv.at[source, i], head=z_device(pos_z + step))
+
+    def send_hidden(z, i):
+        away = wrap(z - pos_z)
+
+        @pl.when(away == 2)
+        def _():
+            via_neighbor(z, i).start()
+
+        @pl.when(away % 2 == 1)
+        def _():
+            give_hidden(z, i, pos_z).start()
+
+        @pl.when(away == 0)
+        def _():
+            keep_hidden(i).start()
 
     def give_rows(z, source):
         return remote(att.at[span(z * rows_per, rows_per), :], att_all_ref.at[source], give_send.at[z, KV_CHUNKS], give_recv.at[source, KV_CHUNKS], head=z_device(z))
@@ -590,13 +615,9 @@
             def _():
                 start(weights(1, 1))
 
-            @pl.when(j == pos_z)
-            def _():
-                keep_hidden(tile).start()
-
-            @pl.when(j != pos_z)
-            def _():
-                give_hidden(j, tile, pos_z).start()
+            @pl.when(j == KV_CHUNKS - 1)
+            def _():
+                send_hidden(j, tile)
 
     def tick(t, carry):
         for number in range(STEPS, -1, -1):
@@ -638,6 +659,12 @@
             def _():
                 far_parts(j)
 
+        @pl.when(t == GIVE_TICK)
+        def _():
+            for i in range(KV_CHUNKS):
+                for z in range(KV_CHUNKS - 1):
+                    send_hidden(z, i)
+
         late = t - BLOCK_TICK
 
         @pl.when(late >= 0)
@@ -658,6 +685,9 @@
     near_parts(2)
     attend_own()
     attend_past(1, (0, 1), ((0, 0), (1, 0)))
+    for i in range(KV_CHUNKS):
+        via_neighbor(0, i).wait_recv()
+        relay_hidden(i).start()
     attend_past(1, (2, 3), ((0, 1), (1, 1)))
     for i in range(KV_CHUNKS):
         finish(i, True)
@@ -667,6 +697,7 @@
     rest_store.wait()
     for i in range(KV_CHUNKS):
         keep_hidden(i).wait()
+        relay_hidden(i).wait_send()
     keep_rows().wait()
     kv_sent(1)
     for d in range(DIRS):
@@ -738,6 +769,7 @@
             dma((2, 4, KV_CHUNKS)), dma((2, 4, KV_CHUNKS)), dma((2, 4, KV_CHUNKS)), dma((2, 4, KV_CHUNKS)), dma((2, DIRS, 2)), dma((2, DIRS, 2)),
             dma((2, RING - 1, DIRS, 2)), dma((2, RING - 1, DIRS, 2)), dma((RING - 1, CHIPS, 2)), dma((RING - 1, CHIPS, 2)),
             dma((RING, KV_CHUNKS + 1)), dma((RING, KV_CHUNKS + 1)), dma((KV_CHUNKS + 1,)),
+            pltpu.VMEM((KV_CHUNKS, rows_per, W_TILE), bf16), dma((KV_CHUNKS,)), dma((KV_CHUNKS,)),
             dma((CHUNKS, STEPS, HALVES * DIRS)), dma((CHUNKS, STEPS, HALVES * DIRS)),
             pltpu.SemaphoreType.REGULAR((3,)),
         ],

time: 398 us -> 356 us (0.89)
  Pallas kernels: 392 us -> 350 us
    pallas_call x1, Pallas kernels: 295 us -> 254 us  [front(): pl.pallas_call(front_kernel, out_shape=[shape((RING, rows_per, ff_local),...]
where the time goes in v10:
time: 356 us; the launch traced here: 355 us
  Pallas kernels  350 us (98%)
  other arithmetic  3.73 us (1%)
    pallas_call x1, Pallas kernels, front(): pl.pallas_call(front_kernel, out_shape=[shape((RING, rows_per, ff_local),...  254 us
    pallas_call x1, Pallas kernels, layer_last(): pl.pallas_call(functools.partial(last_kernel, layer), out_shape=jax.Shape...  88.7 us
    pallas_call x1, Pallas kernels, emit(): pl.pallas_call(emit_kernel, out_shape=[jax.ShapeDtypeStruct(x_out.shape,...  8.01 us

profile of v10, /device:TPU:6, one launch (start us, length us, event | category | flops | bytes accessed | tf_op | source)
XLA Modules:
  0.0 354.9 jit_solution(8885806506891651281)
XLA Ops:
  0.6 0.7 convert_element_type.3
  1.3 3.0 multiply_sine_fusion
  4.4 253.6 %front.1 = (bf16[4,256,1024]{2,1,0:T(8,128)(2,1)}, bf16[4,256,256]{2,1,0:T(8,128)(2,1)}, bf16[1024,256]{1,0:T(8,128)(2,1)}, bf16[1024,256]{1,0:T(8,128)(2,1)}, b...) custom-call(bf16[1024,4096]{1,0:T(8,128)(2,1)} %x_ref.1, ...), custom_call_target="tpu_custom_call" | custom-call | tf_op jit(solution)/shard_map/front/pallas_call | solution.py:746
  258.0 88.7 %last.1 = bf16[4,256,4096]{2,1,0:T(8,128)(2,1)} custom-call(bf16[4,256,1024]{2,1,0:T(8,128)(2,1)} %get-tuple-element.15.hid_ref, bf16[4,256,256]{2,1,0:T(8,128)(2,1)} %get-tuple-element.16.att_ref, bf16[64,4096]{1,0:T(8,128)(2,1)} %get-tuple-element.17.rest_ref, bf16[2,1024,4096]{2,1,0:T(8,128)(2,1)} %wd_ref.3, bf16[2,1,256,4096]{3,2,1,0:T(8,128)(2,1)} %wo_ref.3, ...), custom_call_target="tpu_custom_call" | custom-call | flops 10737418240 | bytes 41943040 | tf_op jit(solution)/shard_map/last/pallas_call | solution.py:942
  346.7 8.0 %emit.1 = (bf16[1024,4096]{1,0:T(8,128)(2,1)}, bf16[2,1024,256]{2,1,0:T(8,128)(2,1)}, bf16[2,1024,256]{2,1,0:T(8,128)(2,1)}) custom-call(bf16[1024,4096]{1,0:T(8,128)(2,1)} %bitcast.10, bf16[1024,256]{1,0:T(8,128)(2,1)} %get-tuple-element.20.k_first, bf16[1024,256]{1,0:T(8,128)(2,1)} %get-tuple-element.21.k_second, ...), custom_call_target="tpu_custom_call" | custom-call | tf_op jit(solution)/shard_map/emit/pallas_call | solution.py:991
  (1 shorter events, 0.0 us)

commit v11 on v10

--- a/solution.py
+++ b/solution.py
@@ -39,6 +39,9 @@
 FAR_TICKS = ((24, 1), (26, 3))
 SERVE_TICKS = (27, 31, 35, 42)
 GIVE_TICK = 37
+OWN_TICK = 3
+DONE_TICK = 11
+EARLY_TICK = 31
 
 
 def front_kernel(x_ref, cos_ref, sin_ref, gain_ref, wq_ref, wk_ref, wv_ref, wg_ref, wu_ref, wd_ref, wo_ref,
@@ -328,15 +331,17 @@
             acc[side, rows, :] = acc[side, rows, :] * jnp.concatenate([rescale] * (head_dim // lanes), axis=1) + block_out
         row_max[side, rows, :] = new_max
 
-    def attend_own():
+    def attend_own(layer_half):
         own_start = my_seq * tok_count
-        attend(own_start, 0, 0, True, True)
-        attend(own_start, 1, 0, False, True)
-        attend(own_start + half_rows, 1, 1, True, True)
-        top_rows = pl.ds(0, half_rows)
-        row_max[1, top_rows, :] = jnp.full((half_rows, lanes), -jnp.inf, f32)
-        row_sum[1, top_rows, :] = jnp.zeros((half_rows, lanes), f32)
-        acc[1, top_rows, :] = jnp.zeros((half_rows, head_dim), f32)
+        if layer_half == 0:
+            attend(own_start, 0, 0, True, True)
+            top_rows = pl.ds(0, half_rows)
+            row_max[1, top_rows, :] = jnp.full((half_rows, lanes), -jnp.inf, f32)
+            row_sum[1, top_rows, :] = jnp.zeros((half_rows, lanes), f32)
+            acc[1, top_rows, :] = jnp.zeros((half_rows, head_dim), f32)
+        else:
+            attend(own_start, 1, 0, False, True)
+            attend(own_start + half_rows, 1, 1, True, True)
 
     def past_start(n):
         later = n - core
@@ -344,28 +349,37 @@
         block = (chip - back) * 2 + jnp.where(later % 2 == 0, core, 1 - core)
         return jnp.where(jnp.logical_and(core == 1, n == 0), chip * 2, block) * tok_count
 
-    def attend_past(layer, chunks, visits):
+    def arrivals(layer, n, chunks):
+        @pl.when(jnp.logical_and(core == 1, n == 0))
+        def _():
+            taken(layer, 0, chunks)
+
+        for back in (1, 3, 2):
+            place = 0 if back == 1 else 2 if back == 3 else jnp.where(chip == CHIPS - 1, 4, 2)
+            if back == 2:
+                @pl.when(jnp.logical_and(chip >= back, n == core + place))
+                def _():
+                    for i in chunks:
+                        serve(layer, 2, i)
+
+            @pl.when(jnp.logical_and(chip >= back, n == core + place + 1))
+            def _():
+                taken(layer, back, chunks)
+
+    def visit(n, visits):
+        for q_half, side in visits:
+            attend(past_start(n) + side * half_rows, q_half, side, False, False)
+
+    def attend_past(layer, first_n, last_n, chunks, visits):
         def past(n, carry):
-            @pl.when(jnp.logical_and(core == 1, n == 0))
-            def _():
-                taken(layer, 0, chunks)
-
-            for back in (1, 3, 2):
-                place = 0 if back == 1 else 2 if back == 3 else jnp.where(chip == CHIPS - 1, 4, 2)
-                if back == 2:
-                    @pl.when(jnp.logical_and(chip >= back, n == core + place))
-                    def _():
-                        for i in chunks:
-                            serve(layer, 2, i)
-
-                @pl.when(jnp.logical_and(chip >= back, n == core + place + 1))
-                def _():
-                    taken(layer, back, chunks)
-            for q_half, side in visits:
-                attend(past_start(n) + side * half_rows, q_half, side, False, False)
+            if chunks:
+                arrivals(layer, n, chunks)
+            visit(n, visits)
             return carry
 
-        lax.fori_loop(0, my_seq, past, 0)
+        lax.fori_loop(first_n, last_n, past, 0)
+
+    near_count = my_seq - jnp.where(chip >= 2, 2, 0)
 
     def finish(i, spread):
         rows = pl.ds(i * rows_per, rows_per)
@@ -486,9 +500,6 @@
         pl.semaphore_signal(barrier, inc=1, device_id={'seq': peer}, device_id_type=mesh_id)
     for peer in [z_device(pos_z + j) for j in range(1, RING)] + [y_peer(d) for d in range(DIRS)]:
         pl.semaphore_signal(barrier, inc=1, device_id={'head': peer}, device_id_type=mesh_id)
-    pl.semaphore_wait(barrier, 8)
-    for d in range(DIRS):
-        start(z_parts(0, d))
 
     def prepare(i, carry):
         x_load(i).wait()
@@ -508,7 +519,17 @@
             wait(weights(0, 0))
 
         keys_values(xbuf[span(i * rows_per, rows_per), :], i)
+
+        @pl.when(i == 0)
+        def _():
+            pl.semaphore_wait(barrier, 8)
+
         send_kv(0, i)
+
+        @pl.when(i == 0)
+        def _():
+            for d in range(DIRS):
+                start(z_parts(0, d))
         return carry
 
     lax.fori_loop(0, KV_CHUNKS, prepare, 0)
@@ -538,36 +559,49 @@
 
     lax.fori_loop(0, CHUNKS, residuals, 0)
 
-    def gate_tile(tile, carry):
+    def gate_half(half, tile):
         wait(weights(0, tile + 2))
 
         def rows_step(i, inner):
             gated(xbuf[span(i * rows_per, rows_per), :], i, tile)
             return inner
 
-        lax.fori_loop(0, KV_CHUNKS, rows_step, 0)
+        lax.fori_loop(half * KV_CHUNKS // 2, (half + 1) * KV_CHUNKS // 2, rows_step, 0)
 
         @pl.when(tile < 2)
         def _():
             start(weights(0, tile + 4))
 
-        @pl.when(tile == 2)
-        def _():
-            start(weights(1, 0))
+        for last in (2, 3):
+            @pl.when(tile == last)
+            def _():
+                start(weights(1, last - 2) if half else weights(0, last))
+
+    def first_half(tile, carry):
+        gate_half(0, tile)
+
+        @pl.when(tile < 3)
+        def _():
+            serve_all(0, tile)
+        return carry
+
+    def second_half(tile, carry):
+        gate_half(1, tile)
+
+        @pl.when(tile == 0)
+        def _():
+            serve_all(0, 3)
+            attend_past(0, 0, near_count, range(KV_CHUNKS), ((0, 0), (0, 1)))
             for d in range(DIRS):
                 for copy in z_parts(0, d):
                     copy.wait_recv()
                 start(z_parts(1, d))
-
-        @pl.when(tile == 3)
-        def _():
-            start(weights(1, 1))
-        serve_all(0, tile)
         return carry
 
-    lax.fori_loop(0, ff_local // W_TILE, gate_tile, 0)
-    attend_own()
-    attend_past(0, range(KV_CHUNKS), ((0, 0), (0, 1)))
+    lax.fori_loop(0, ff_local // W_TILE, first_half, 0)
+    attend_own(0)
+    lax.fori_loop(0, 2, second_half, 0)
+    attend_past(0, near_count, my_seq, range(KV_CHUNKS), ((0, 0), (0, 1)))
     finish(0, False)
     finish(1, False)
     round_start(1)
@@ -628,10 +662,28 @@
             def _():
                 stage(number, chunk)
 
-        @pl.when(jnp.logical_and(t >= 1, jnp.logical_and(t < 8, t <= my_seq)))
-        def _():
-            for side in range(2):
-                attend(past_start(t - 1) + side * half_rows, 1, side, False, False)
+        @pl.when(jnp.logical_or(t == 1, t == 3))
+        def _():
+            gate_half(1, 2 + t // 2)
+
+        @pl.when(t == OWN_TICK)
+        def _():
+            attend_own(1)
+
+        @pl.when(jnp.logical_and(t > OWN_TICK, jnp.logical_and(t < DONE_TICK, t - OWN_TICK <= my_seq)))
+        def _():
+            visit(t - OWN_TICK - 1, ((1, 0), (1, 1)))
+
+        @pl.when(t == EARLY_TICK)
+        def _():
+            attend_own(0)
+
+        early = t - EARLY_TICK - 1
+
+        @pl.when(jnp.logical_and(early >= 0, jnp.logical_and(early < 7, early < my_seq)))
+        def _():
+            arrivals(1, early, (0, 1))
+            visit(early, ((0, 0),))
 
         @pl.when(t == 2)
         def _():
@@ -640,7 +692,7 @@
                     copy.wait_recv()
             round_start(2)
 
-        @pl.when(t == 8)
+        @pl.when(t == DONE_TICK)
         def _():
             finish(2, False)
             finish(3, False)
@@ -683,14 +735,18 @@
     rest_store = pltpu.make_async_copy(xbuf.at[span(pos_z * rows_per + pos_y * (rows_per // RING), rows_per // RING), :], rest_ref, rest_sem)
     rest_store.start()
     near_parts(2)
-    attend_own()
-    attend_past(1, (0, 1), ((0, 0), (1, 0)))
+    attend_own(1)
+    attend_past(1, 0, my_seq, (), ((1, 0),))
     for i in range(KV_CHUNKS):
         via_neighbor(0, i).wait_recv()
         relay_hidden(i).start()
-    attend_past(1, (2, 3), ((0, 1), (1, 1)))
-    for i in range(KV_CHUNKS):
-        finish(i, True)
+    attend_past(1, 0, near_count, (2, 3), ((0, 1), (1, 1)))
+    attend_past(1, near_count, my_seq, (2, 3), ((0, 1),))
+    finish(0, True)
+    finish(1, True)
+    attend_past(1, near_count, my_seq, (), ((1, 1),))
+    finish(2, True)
+    finish(3, True)
     far_parts(2)
 
     wait(cache_stores(1))

time: 356 us -> 352 us (0.989)
  Pallas kernels: 350 us -> 346 us
    pallas_call x1, Pallas kernels: 254 us -> 248 us  [front(): pl.pallas_call(front_kernel, out_shape=[shape((RING, rows_per, ff_local),...]
where the time goes in v11:
time: 352 us; the launch traced here: 351 us
  Pallas kernels  346 us (98%)
  other arithmetic  3.73 us (1%)
    pallas_call x1, Pallas kernels, front(): pl.pallas_call(front_kernel, out_shape=[shape((RING, rows_per, ff_local),...  248 us
    pallas_call x1, Pallas kernels, layer_last(): pl.pallas_call(functools.partial(last_kernel, layer), out_shape=jax.Shape...  89.9 us
    pallas_call x1, Pallas kernels, emit(): pl.pallas_call(emit_kernel, out_shape=[jax.ShapeDtypeStruct(x_out.shape,...  8.01 us

profile of v11, /device:TPU:6, one launch (start us, length us, event | category | flops | bytes accessed | tf_op | source)
XLA Modules:
  0.0 350.8 jit_solution(12759550979205196582)
XLA Ops:
  0.6 0.7 convert_element_type.3
  1.3 3.0 multiply_sine_fusion
  4.4 248.3 %front.1 = (bf16[4,256,1024]{2,1,0:T(8,128)(2,1)}, bf16[4,256,256]{2,1,0:T(8,128)(2,1)}, bf16[1024,256]{1,0:T(8,128)(2,1)}, bf16[1024,256]{1,0:T(8,128)(2,1)}, b...) custom-call(bf16[1024,4096]{1,0:T(8,128)(2,1)} %x_ref.1, ...), custom_call_target="tpu_custom_call" | custom-call | tf_op jit(solution)/shard_map/front/pallas_call | solution.py:802
  252.6 89.9 %last.1 = bf16[4,256,4096]{2,1,0:T(8,128)(2,1)} custom-call(bf16[4,256,1024]{2,1,0:T(8,128)(2,1)} %get-tuple-element.15.hid_ref, bf16[4,256,256]{2,1,0:T(8,128)(2,1)} %get-tuple-element.16.att_ref, bf16[64,4096]{1,0:T(8,128)(2,1)} %get-tuple-element.17.rest_ref, bf16[2,1024,4096]{2,1,0:T(8,128)(2,1)} %wd_ref.3, bf16[2,1,256,4096]{3,2,1,0:T(8,128)(2,1)} %wo_ref.3, ...), custom_call_target="tpu_custom_call" | custom-call | flops 10737418240 | bytes 41943040 | tf_op jit(solution)/shard_map/last/pallas_call | solution.py:998
  342.6 8.0 %emit.1 = (bf16[1024,4096]{1,0:T(8,128)(2,1)}, bf16[2,1024,256]{2,1,0:T(8,128)(2,1)}, bf16[2,1024,256]{2,1,0:T(8,128)(2,1)}) custom-call(bf16[1024,4096]{1,0:T(8,128)(2,1)} %bitcast.10, bf16[1024,256]{1,0:T(8,128)(2,1)} %get-tuple-element.20.k_first, bf16[1024,256]{1,0:T(8,128)(2,1)} %get-tuple-element.21.k_second, ...), custom_call_target="tpu_custom_call" | custom-call | tf_op jit(solution)/shard_map/emit/pallas_call | solution.py:1047
  (1 shorter events, 0.0 us)

commit v12 on v11

--- a/solution.py
+++ b/solution.py
@@ -42,13 +42,18 @@
 OWN_TICK = 3
 DONE_TICK = 11
 EARLY_TICK = 31
-
-
-def front_kernel(x_ref, cos_ref, sin_ref, gain_ref, wq_ref, wk_ref, wv_ref, wg_ref, wu_ref, wd_ref, wo_ref,
-                 hid_all_ref, att_all_ref, k1_ref, v1_ref, k2_ref, v2_ref, gd_ref, go_ref, rest_ref,
+LAST_STEPS = 6
+LAST_COLS = 256
+LAST_BLOCKS = 16
+LAST_GAP = 3
+
+
+def layers_kernel(x_ref, cos_ref, sin_ref, gain_ref, wq_ref, wk_ref, wv_ref, wg_ref, wu_ref, wd_ref, wo_ref,
+                 out_ref, k1_ref, v1_ref, k2_ref, v2_ref, gd_ref, go_ref,
                  xbuf, part, recv_a, recv_b, hid, att, wdo, wtile, kv, qbuf, acc, row_max, row_sum, xs, xres,
-                 x_sem, res_sem, w_sem, down_sem, cache_sem, rest_sem, own_send, pass_send, ici_recv, core_recv, part_send, part_recv,
-                 round_send, round_recv, side_send, side_recv, give_send, give_recv, keep_sem, relay_buf, relay_send, relay_recv, ring_send, ring_recv, ready_sem):
+                 x_sem, res_sem, w_sem, down_sem, cache_sem, store_sem, own_send, pass_send, ici_recv, core_recv, part_send, part_recv,
+                 round_send, round_recv, side_send, side_recv, give_send, give_recv, relay_buf, relay_send, relay_recv, att_all, ring_send, ring_recv,
+                 last_send, last_recv, tile_sem, ready_sem, drained_sem):
     tok_count, d_model = xbuf.shape
     head_dim = qbuf.shape[1]
     half_dim = head_dim // 2
@@ -240,11 +245,10 @@
 
     def give_hidden(z, i, source):
         cols = span(i * W_TILE, W_TILE)
-        return remote(hid.at[span(z * rows_per, rows_per), cols], hid_all_ref.at[source, :, cols], give_send.at[z, i], give_recv.at[source, i], head=z_device(z))
-
-    def keep_hidden(i):
-        cols = span(i * W_TILE, W_TILE)
-        return pltpu.make_async_copy(hid.at[span(pos_z * rows_per, rows_per), cols], hid_all_ref.at[pos_z, :, cols], keep_sem.at[i])
+        return remote(hid.at[span(z * rows_per, rows_per), cols], hidden_place(source, i), give_send.at[z, i], give_recv.at[source, i], head=z_device(z))
+
+    def hidden_place(source, i):
+        return xs.at[1, :, span(source * ff_local + i * W_TILE, W_TILE)]
 
     def via_neighbor(z, i):
         step = jnp.where(i < KV_CHUNKS // 2, 1, -1)
@@ -253,7 +257,7 @@
     def relay_hidden(i):
         step = 1 if i < KV_CHUNKS // 2 else -1
         source = wrap(pos_z - step)
-        return remote(relay_buf.at[i], hid_all_ref.at[source, :, span(i * W_TILE, W_TILE)], relay_send.at[i], give_recv.at[source, i], head=z_device(pos_z + step))
+        return remote(relay_buf.at[i], hidden_place(source, i), relay_send.at[i], give_recv.at[source, i], head=z_device(pos_z + step))
 
     def send_hidden(z, i):
         away = wrap(z - pos_z)
@@ -266,15 +270,8 @@
         def _():
             give_hidden(z, i, pos_z).start()
 
-        @pl.when(away == 0)
-        def _():
-            keep_hidden(i).start()
-
     def give_rows(z, source):
-        return remote(att.at[span(z * rows_per, rows_per), :], att_all_ref.at[source], give_send.at[z, KV_CHUNKS], give_recv.at[source, KV_CHUNKS], head=z_device(z))
-
-    def keep_rows():
-        return pltpu.make_async_copy(att.at[span(pos_z * rows_per, rows_per), :], att_all_ref.at[pos_z], keep_sem.at[KV_CHUNKS])
+        return remote(att.at[span(z * rows_per, rows_per), :], att_all.at[source], give_send.at[z, KV_CHUNKS], give_recv.at[source, KV_CHUNKS], head=z_device(z))
 
     def norm_rows(x_few, layer):
         x_f32 = x_few.astype(f32)
@@ -389,10 +386,6 @@
         wide = [jnp.concatenate([w] * (head_dim // lanes), axis=1) for w in shares + [total]]
         att[rows, :] = ((acc[0, rows, :] * wide[0] + acc[1, rows, :] * wide[1]) / wide[2]).astype(bf16)
         if spread:
-            @pl.when(i == pos_z)
-            def _():
-                keep_rows().start()
-
             @pl.when(i != pos_z)
             def _():
                 give_rows(i, pos_z).start()
@@ -731,9 +724,17 @@
 
     lax.fori_loop(0, LAST_TICK, tick, 0)
 
+    def drain(chunk, carry):
+        @pl.when(chunk >= CHUNKS - PART_SLOTS)
+        def _():
+            each_message(chunk, range(4), lambda copy: copy.wait_send())
+        each_message(chunk, range(4, STEPS), lambda copy: copy.wait_send())
+        return carry
+
+    lax.fori_loop(0, CHUNKS, drain, 0)
+    for d in range(DIRS):
+        pl.semaphore_signal(drained_sem.at[d], inc=1, device_id={'head': y_peer(d)}, device_id_type=mesh_id)
     start(cache_stores(1))
-    rest_store = pltpu.make_async_copy(xbuf.at[span(pos_z * rows_per + pos_y * (rows_per // RING), rows_per // RING), :], rest_ref, rest_sem)
-    rest_store.start()
     near_parts(2)
     attend_own(1)
     attend_past(1, 0, my_seq, (), ((1, 0),))
@@ -748,13 +749,143 @@
     finish(2, True)
     finish(3, True)
     far_parts(2)
+    for j in range(1, RING):
+        for n in range(CHIPS):
+            for copy in side_part(j, n, 1 - core):
+                copy.wait_recv()
+
+    quarter_rows = rows_per // RING
+    depth = ff_local + head_dim
+
+    def block_cols(c):
+        return span(c * LAST_COLS, LAST_COLS)
+
+    def tile_place(c, j, first, size):
+        return wtile.at[c % 2, j // 2, pl.ds((j % 2) * depth + first, size), :]
+
+    def tile_loads(c):
+        copies = []
+        for j in range(RING):
+            z = wrap(pos_z + j)
+            down = wd_ref.at[1, :, block_cols(c)] if j == 0 else gd_ref.at[z, :, block_cols(c)]
+            out = wo_ref.at[1, 0, :, block_cols(c)] if j == 0 else go_ref.at[z, :, block_cols(c)]
+            copies.append(pltpu.make_async_copy(down, tile_place(c, j, 0, ff_local), tile_sem.at[c % 2, j, 0]))
+            copies.append(pltpu.make_async_copy(out, tile_place(c, j, ff_local, head_dim), tile_sem.at[c % 2, j, 1]))
+        return copies
+
+    start(tile_loads(0))
+    for j in range(1, RING):
+        z = wrap(pos_z + j)
+        for i in range(KV_CHUNKS):
+            give_hidden(z, i, z).wait_recv()
+        give_rows(z, z).wait_recv()
+    for d in range(DIRS):
+        pl.semaphore_wait(drained_sem.at[d], 1)
+
+    def quarter_of(piece, offset, size):
+        return span(piece * quarter_rows + offset, size, quarter_rows // 2)
+
+    def landed(d, first, size):
+        return pl.ds(rows_per + d * (3 * quarter_rows // 2) + first, size)
+
+    def rows_at(z, piece, offset, size):
+        return span(z * rows_per + piece * quarter_rows + offset, size, quarter_rows // 2)
+
+    def last_messages(step, c, d, z_first):
+        s, cols, half = sign[d], block_cols(c), quarter_rows // 2
+        near, behind, back = wrap(pos_y + s), wrap(pos_y - s), wrap(pos_z - s)
+        along_y = step < 2 or (step < 4) != z_first
+        if step == 0:
+            pairs = [(part.at[quarter_of(wrap(pos_y + 2), d * half, half), cols], part.at[landed(d, quarter_rows, half), cols])]
+        elif step == 1:
+            pairs = [(part.at[quarter_of(near, 0, quarter_rows), cols], part.at[landed(d, 0, quarter_rows), cols])]
+        else:
+            if step == 2:
+                rows = [rows_at(pos_z, pos_y, 0, quarter_rows)]
+            elif step == 3:
+                rows = [rows_at(back, pos_y, d * half, half) if z_first else rows_at(pos_z, behind, d * half, half)]
+            elif step == 4:
+                rows = [rows_at(z, pos_y, 0, quarter_rows) for z in range(RING)] if z_first else [rows_at(pos_z, 0, 0, rows_per)]
+            else:
+                rows = [rows_at(z, behind, d * half, half) for z in range(RING)] if z_first else [rows_at(back, 0, d * (rows_per // 2), rows_per // 2)]
+            pairs = [(xbuf.at[r, cols], xbuf.at[r, cols]) for r in rows]
+        to = (y_peer if along_y else z_peer)(d)
+        return [remote(src, dst, last_send.at[c, step, d, n], last_recv.at[c, step, d, n], head=to) for n, (src, dst) in enumerate(pairs)]
+
+    def on_last(step, c, act):
+        def both(z_first):
+            for d in range(DIRS):
+                for copy in last_messages(step, c, d, z_first):
+                    act(copy)
+
+        if step < 2:
+            both(False)
+            return
+        z_first = jnp.logical_and(c >= 5, c % 2 == 1)
+
+        @pl.when(z_first)
+        def _():
+            both(True)
+
+        @pl.when(jnp.logical_not(z_first))
+        def _():
+            both(False)
+
+    def out_store(c):
+        return pltpu.make_async_copy(xbuf.at[:, block_cols(c)], out_ref.at[:, block_cols(c)], store_sem.at[c])
+
+    def last_project(c):
+        @pl.when(c + 1 < LAST_BLOCKS)
+        def _():
+            start(tile_loads(c + 1))
+
+        wait(tile_loads(c))
+        total = None
+        for j in range(RING):
+            z = wrap(pos_z + j)
+            own = span(pos_z * rows_per, rows_per)
+            hidden_rows = hid[own, :] if j == 0 else xs[1, :, span(z * ff_local, ff_local)]
+            out_rows = att[own, :] if j == 0 else att_all[z]
+            term = dot(hidden_rows, wtile[c % 2, j // 2, pl.ds((j % 2) * depth, ff_local), :])
+            term = term + dot(out_rows, wtile[c % 2, j // 2, pl.ds((j % 2) * depth + ff_local, head_dim), :])
+            total = term if total is None else total + term
+        part[pl.ds(0, rows_per), block_cols(c)] = total
+
+    def last_stage(number, c):
+        cols, half = block_cols(c), quarter_rows // 2
+        if number == 0:
+            last_project(c)
+        else:
+            on_last(number - 1, c, lambda copy: copy.wait_recv())
+        if number == 1:
+            for d in range(DIRS):
+                piece = quarter_of(wrap(pos_y + sign[d]), d * half, half)
+                part[piece, cols] = part[piece, cols] + part[landed(d, quarter_rows, half), cols]
+        if number == 2:
+            own = quarter_of(pos_y, 0, quarter_rows)
+            total = part[own, cols] + part[landed(0, 0, quarter_rows), cols] + part[landed(1, 0, quarter_rows), cols]
+            update = total.astype(bf16).astype(f32)
+            rows = rows_at(pos_z, pos_y, 0, quarter_rows)
+            xbuf[rows, cols] = (xbuf[rows, cols].astype(f32) + update).astype(bf16)
+        if number < LAST_STEPS:
+            on_last(number, c, lambda copy: copy.start())
+        else:
+            out_store(c).start()
+
+    def last_tick(t, carry):
+        for number in range(LAST_STEPS, -1, -1):
+            c = t - LAST_GAP * number
+
+            @pl.when(jnp.logical_and(c >= 0, c < LAST_BLOCKS))
+            def _():
+                last_stage(number, c)
+        return carry
+
+    lax.fori_loop(0, LAST_BLOCKS + LAST_GAP * LAST_STEPS, last_tick, 0)
 
     wait(cache_stores(1))
-    rest_store.wait()
     for i in range(KV_CHUNKS):
-        keep_hidden(i).wait()
         relay_hidden(i).wait_send()
-    keep_rows().wait()
     kv_sent(1)
     for d in range(DIRS):
         for step in range(2):
@@ -765,28 +896,23 @@
             for copy in own_part(j, d) + far_part(j, d):
                 copy.wait_send()
         for n in range(CHIPS):
-            for copy in side_part(j, n, 1 - core):
-                copy.wait_recv()
             for copy in side_part(j, n, core):
                 copy.wait_send()
         z = wrap(pos_z + j)
         for i in range(KV_CHUNKS):
-            give_hidden(z, i, z).wait_recv()
             give_hidden(z, i, pos_z).wait_send()
-        give_rows(z, z).wait_recv()
         give_rows(z, pos_z).wait_send()
 
-    def drain(chunk, carry):
-        @pl.when(chunk >= CHUNKS - PART_SLOTS)
-        def _():
-            each_message(chunk, range(4), lambda copy: copy.wait_send())
-        each_message(chunk, range(4, STEPS), lambda copy: copy.wait_send())
+    def last_drain(c, carry):
+        for step in range(LAST_STEPS):
+            on_last(step, c, lambda copy: copy.wait_send())
+        out_store(c).wait()
         return carry
 
-    lax.fori_loop(0, CHUNKS, drain, 0)
-
-
-def front(x_loc, cos_t, sin_t, norm_gain, w_q, w_k, w_v, w_gate, w_up, w_down, w_o):
+    lax.fori_loop(0, LAST_BLOCKS, last_drain, 0)
+
+
+def layers(x_loc, cos_t, sin_t, norm_gain, w_q, w_k, w_v, w_gate, w_up, w_down, w_o):
     tok_count, d_model = x_loc.shape
     head_dim = w_q.shape[2]
     ff_local = w_gate.shape[2]
@@ -800,11 +926,11 @@
     dma = pltpu.SemaphoreType.DMA
     shape = jax.ShapeDtypeStruct
     return pl.pallas_call(
-        front_kernel,
-        out_shape=[shape((RING, rows_per, ff_local), bf16), shape((RING, rows_per, head_dim), bf16)] + [shape((tok_count, head_dim), bf16)] * 4
-        + [shape((RING, ff_local, d_model), bf16), shape((RING, head_dim, d_model), bf16), shape((rows_per // RING, d_model), bf16)],
+        layers_kernel,
+        out_shape=[shape((tok_count, d_model), bf16)] + [shape((tok_count, head_dim), bf16)] * 4
+        + [shape((RING, ff_local, d_model), bf16), shape((RING, head_dim, d_model), bf16)],
         in_specs=[any_spec, vmem_spec, vmem_spec, vmem_spec] + [any_spec] * 7,
-        out_specs=[any_spec] * 9,
+        out_specs=[any_spec] * 7,
         scratch_shapes=[
             pltpu.VMEM((tok_count, d_model), bf16),
             pltpu.VMEM((PART_SLOTS * chunk_rows, d_model), f32),
@@ -821,202 +947,19 @@
             pltpu.VMEM((2, tok_count, 128), f32),
             pltpu.VMEM((2, rows_per, d_model), bf16),
             pltpu.VMEM((CHUNKS, HALVES, chunk_rows // RING, half_cols // RING), bf16),
-            dma((2,)), dma((CHUNKS, HALVES)), dma((2, 2)), dma((2, 2)), dma((2, 2)), dma,
+            dma((2,)), dma((CHUNKS, HALVES)), dma((2, 2)), dma((2, 2)), dma((2, 2)), dma((LAST_BLOCKS,)),
             dma((2, 4, KV_CHUNKS)), dma((2, 4, KV_CHUNKS)), dma((2, 4, KV_CHUNKS)), dma((2, 4, KV_CHUNKS)), dma((2, DIRS, 2)), dma((2, DIRS, 2)),
             dma((2, RING - 1, DIRS, 2)), dma((2, RING - 1, DIRS, 2)), dma((RING - 1, CHIPS, 2)), dma((RING - 1, CHIPS, 2)),
-            dma((RING, KV_CHUNKS + 1)), dma((RING, KV_CHUNKS + 1)), dma((KV_CHUNKS + 1,)),
+            dma((RING, KV_CHUNKS + 1)), dma((RING, KV_CHUNKS + 1)),
             pltpu.VMEM((KV_CHUNKS, rows_per, W_TILE), bf16), dma((KV_CHUNKS,)), dma((KV_CHUNKS,)),
+            pltpu.VMEM((RING, rows_per, head_dim), bf16),
             dma((CHUNKS, STEPS, HALVES * DIRS)), dma((CHUNKS, STEPS, HALVES * DIRS)),
-            pltpu.SemaphoreType.REGULAR((3,)),
+            dma((LAST_BLOCKS, LAST_STEPS, DIRS, RING)), dma((LAST_BLOCKS, LAST_STEPS, DIRS, RING)), dma((2, RING, 2)),
+            pltpu.SemaphoreType.REGULAR((3,)), pltpu.SemaphoreType.REGULAR((DIRS,)),
         ],
         compiler_params=pltpu.CompilerParams(collective_id=0, has_side_effects=True, vmem_limit_bytes=67043328),
-        name='front',
+        name='layers',
     )(x_loc, cos_t, sin_t, norm_gain, w_q, w_k, w_v, w_gate, w_up, w_down, w_o)
-
-
-SKEW = 2
-LAST_STEPS = 6
-LAST_COLS = 256
-
-
-def last_kernel(layer, hid_ref, att_ref, rest_ref, wd_ref, wo_ref, gd_ref, go_ref, out_ref, part, xres, xbuf, wtile, landed, w_sem, x_sem, store_sem, send_sem, recv_sem):
-    rows, d_model = part.shape
-    block = wtile.shape[3]
-    block_count = d_model // block
-    ff_local = hid_ref.shape[2]
-    quarter, eighth = rows // RING, rows // (2 * RING)
-    my_head = lax.axis_index('head')
-    pos_z, pos_y = my_head // RING, my_head % RING
-    sign = (1, -1)
-
-    def cols_of(c):
-        return pl.ds(pl.multiple_of(c * block, block), block)
-
-    def w_loads(c):
-        copies = []
-        for j in range(RING):
-            z = (pos_z + j) % RING
-            down = wd_ref.at[layer, :, cols_of(c)] if j == 0 else gd_ref.at[z, :, cols_of(c)]
-            out = wo_ref.at[layer, 0, :, cols_of(c)] if j == 0 else go_ref.at[z, :, cols_of(c)]
-            copies.append(pltpu.make_async_copy(down, wtile.at[c % 2, j, pl.ds(0, ff_local), :], w_sem.at[c % 2, j, 0]))
-            copies.append(pltpu.make_async_copy(out, wtile.at[c % 2, j, pl.ds(ff_local, wo_ref.shape[2]), :], w_sem.at[c % 2, j, 1]))
-        return copies
-
-    for copy in w_loads(0):
-        copy.start()
-    x_load = pltpu.make_async_copy(rest_ref, xres, x_sem)
-    x_load.start()
-
-    def y_device(d):
-        return pos_z * RING + (pos_y + sign[d] + RING) % RING
-
-    def z_device(d):
-        return (pos_z + sign[d] + RING) % RING * RING + pos_y
-
-    barrier = pltpu.get_barrier_semaphore()
-    for device in (y_device, z_device):
-        for d in range(DIRS):
-            pl.semaphore_signal(barrier, inc=1, device_id={'head': device(d)}, device_id_type=pl.DeviceIdType.MESH)
-    pl.semaphore_wait(barrier, 2 * DIRS)
-    x_load.wait()
-
-    def rows_of(piece, offset, count):
-        return pl.ds(pl.multiple_of(piece * quarter + offset, eighth), count)
-
-    def message(step, c, d, z_first):
-        s = sign[d]
-        near, behind = (pos_y + s + RING) % RING, (pos_y - s + RING) % RING
-        if step == 0:
-            src, dst = part.at[rows_of((pos_y + 2) % RING, d * eighth, eighth), cols_of(c)], landed.at[c, d, pl.ds(quarter, eighth), :]
-        elif step == 1:
-            src, dst = part.at[rows_of(near, 0, quarter), cols_of(c)], landed.at[c, d, pl.ds(0, quarter), :]
-        elif z_first:
-            back = (pos_z - s + RING) % RING
-            if step == 2:
-                src = dst = xbuf.at[pos_z, rows_of(pos_y, 0, quarter), cols_of(c)]
-            elif step == 3:
-                src = dst = xbuf.at[back, rows_of(pos_y, d * eighth, eighth), cols_of(c)]
-            elif step == 4:
-                src = dst = xbuf.at[:, rows_of(pos_y, 0, quarter), cols_of(c)]
-            else:
-                src = dst = xbuf.at[:, rows_of(behind, d * eighth, eighth), cols_of(c)]
-        else:
-            if step == 2:
-                src = dst = xbuf.at[pos_z, rows_of(pos_y, 0, quarter), cols_of(c)]
-            elif step == 3:
-                src = dst = xbuf.at[pos_z, rows_of(behind, d * eighth, eighth), cols_of(c)]
-            elif step == 4:
-                src = dst = xbuf.at[pos_z, :, cols_of(c)]
-            else:
-                src = dst = xbuf.at[(pos_z - s + RING) % RING, pl.ds(d * (rows // 2), rows // 2), cols_of(c)]
-        along_y = step < 2 or (step < 4) != z_first
-        return pltpu.make_async_remote_copy(
-            src_ref=src, dst_ref=dst, send_sem=send_sem.at[c, step, d], recv_sem=recv_sem.at[c, step, d],
-            device_id={'head': (y_device if along_y else z_device)(d)}, device_id_type=pl.DeviceIdType.MESH)
-
-    def on_messages(step, c, act):
-        if step < 2:
-            for d in range(DIRS):
-                act(message(step, c, d, False))
-            return
-
-        @pl.when(c % 4 == 3)
-        def _():
-            for d in range(DIRS):
-                act(message(step, c, d, True))
-
-        @pl.when(c % 4 != 3)
-        def _():
-            for d in range(DIRS):
-                act(message(step, c, d, False))
-
-    def store(c):
-        return pltpu.make_async_copy(xbuf.at[:, :, cols_of(c)], out_ref.at[:, :, cols_of(c)], store_sem.at[c])
-
-    def project(c):
-        @pl.when(c + 1 < block_count)
-        def _():
-            for copy in w_loads(c + 1):
-                copy.start()
-
-        for copy in w_loads(c):
-            copy.wait()
-        total = None
-        for j in range(RING):
-            z = (pos_z + j) % RING
-            down = jnp.dot(hid_ref[z], wtile[c % 2, j, :ff_local, :], preferred_element_type=jnp.float32)
-            down = down + jnp.dot(att_ref[z], wtile[c % 2, j, ff_local:, :], preferred_element_type=jnp.float32)
-            total = down if total is None else total + down
-        part[:, cols_of(c)] = total
-
-    def stage(number, c):
-        if number == 0:
-            project(c)
-        else:
-            on_messages(number - 1, c, lambda copy: copy.wait_recv())
-        if number == 1:
-            for d in range(DIRS):
-                piece = rows_of((pos_y + sign[d] + RING) % RING, d * eighth, eighth)
-                part[piece, cols_of(c)] = part[piece, cols_of(c)] + landed[c, d, pl.ds(quarter, eighth), :]
-        if number == 2:
-            own = rows_of(pos_y, 0, quarter)
-            total = part[own, cols_of(c)] + landed[c, 0, pl.ds(0, quarter), :] + landed[c, 1, pl.ds(0, quarter), :]
-            update = total.astype(jnp.bfloat16).astype(jnp.float32)
-            xbuf[pos_z, own, cols_of(c)] = (xres[:, cols_of(c)].astype(jnp.float32) + update).astype(jnp.bfloat16)
-        if number < LAST_STEPS:
-            on_messages(number, c, lambda copy: copy.start())
-        else:
-            store(c).start()
-
-    def tick(t, carry):
-        for number in range(LAST_STEPS, -1, -1):
-            c = t - SKEW * number
-
-            @pl.when(jnp.logical_and(c >= 0, c < block_count))
-            def _():
-                stage(number, c)
-        return carry
-
-    lax.fori_loop(0, block_count + SKEW * LAST_STEPS, tick, 0)
-
-    def drain(c, carry):
-        for step in range(LAST_STEPS):
-            on_messages(step, c, lambda copy: copy.wait_send())
-        store(c).wait()
-        return carry
-
-    lax.fori_loop(0, block_count, drain, 0)
-
-
-def layer_last(layer, hid_all, att_all, rest, w_down, w_o, all_down, all_out):
-    rows, d_model = hid_all.shape[1], rest.shape[1]
-    tok_count = RING * rows
-    depth = hid_all.shape[2] + att_all.shape[2]
-    any_spec = pl.BlockSpec(memory_space=pl.ANY)
-    vmem_spec = pl.BlockSpec(memory_space=pltpu.VMEM)
-    blocks = d_model // LAST_COLS
-    out = pl.pallas_call(
-        functools.partial(last_kernel, layer),
-        out_shape=jax.ShapeDtypeStruct((RING, rows, d_model), jnp.bfloat16),
-        in_specs=[vmem_spec, vmem_spec] + [any_spec] * 5,
-        out_specs=any_spec,
-        scratch_shapes=[
-            pltpu.VMEM((rows, d_model), jnp.float32),
-            pltpu.VMEM((rows // RING, d_model), jnp.bfloat16),
-            pltpu.VMEM((RING, rows, d_model), jnp.bfloat16),
-            pltpu.VMEM((2, RING, depth, LAST_COLS), jnp.bfloat16),
-            pltpu.VMEM((blocks, DIRS, 3 * rows // (2 * RING), LAST_COLS), jnp.float32),
-            pltpu.SemaphoreType.DMA((2, RING, 2)),
-            pltpu.SemaphoreType.DMA,
-            pltpu.SemaphoreType.DMA((blocks,)),
-            pltpu.SemaphoreType.DMA((blocks, LAST_STEPS, DIRS)),
-            pltpu.SemaphoreType.DMA((blocks, LAST_STEPS, DIRS)),
-        ],
-        compiler_params=pltpu.CompilerParams(collective_id=layer, has_side_effects=True, vmem_limit_bytes=63 * 1024 * 1024),
-        cost_estimate=pl.CostEstimate(flops=2 * tok_count * depth * d_model, bytes_accessed=4 * depth * d_model * 2, transcendentals=0),
-        name='last',
-    )(hid_all, att_all, rest, w_down, w_o, all_down, all_out)
-    return out.reshape(tok_count, d_model)
 
 
 EMIT_PARTS = 8
@@ -1075,8 +1018,7 @@
         head_dim = w_q.shape[3]
         flat_q, flat_k, flat_v = (w.reshape(layer_count, d_model, head_dim) for w in (w_q, w_k, w_v))
         cos_t, sin_t = rope_tables(pos_loc, head_dim)
-        hid_all, att_all, k_first, v_first, k_second, v_second, all_down, all_out, rest = front(x_loc, cos_t, sin_t, norm_gain, flat_q, flat_k, flat_v, w_gate, w_up, w_down, w_o)
-        x_out = layer_last(1, hid_all, att_all, rest, w_down, w_o, all_down, all_out)
+        x_out, k_first, v_first, k_second, v_second, _, _ = layers(x_loc, cos_t, sin_t, norm_gain, flat_q, flat_k, flat_v, w_gate, w_up, w_down, w_o)
         x_out, k_all, v_all = emit(x_out, k_first, k_second, v_first, v_second)
         cache_shape = (layer_count, tok_count, 1, head_dim)
         return x_out, k_all.reshape(cache_shape), v_all.reshape(cache_shape)

time: 352 us -> 356 us (1.011)
  Pallas kernels: 346 us -> 350 us
    pallas_call x2 -> x1, Pallas kernels: 338 us -> 342 us  [layers(): pl.pallas_call(layers_kernel, out_shape=[shape((tok_count, d_model), bf16...]
where the time goes in v12:
time: 356 us; the launch traced here: 354 us
  Pallas kernels  350 us (98%)
  other arithmetic  3.73 us (1%)
    pallas_call x1, Pallas kernels, layers(): pl.pallas_call(layers_kernel, out_shape=[shape((tok_count, d_model), bf16...  342 us
    pallas_call x1, Pallas kernels, emit(): pl.pallas_call(emit_kernel, out_shape=[jax.ShapeDtypeStruct(x_out.shape,...  8.01 us

profile of v12, /device:TPU:6, one launch (start us, length us, event | category | flops | bytes accessed | tf_op | source)
XLA Modules:
  0.0 354.3 jit_solution(4830935272946707400)
XLA Ops:
  0.6 0.7 convert_element_type.3
  1.3 3.0 multiply_sine_fusion
  4.4 341.8 %layers.1 = (bf16[1024,4096]{1,0:T(8,128)(2,1)}, bf16[1024,256]{1,0:T(8,128)(2,1)}, bf16[1024,256]{1,0:T(8,128)(2,1)}, bf16[1024,256]{1,0:T(8,128)(2,1)}, bf16[1...) custom-call(bf16[1024,4096]{1,0:T(8,128)(2,1)} %x_ref.1, ...), custom_call_target="tpu_custom_call" | custom-call | tf_op jit(solution)/shard_map/layers/pallas_call | solution.py:928
  346.1 8.0 %emit.1 = (bf16[1024,4096]{1,0:T(8,128)(2,1)}, bf16[2,1024,256]{2,1,0:T(8,128)(2,1)}, bf16[2,1024,256]{2,1,0:T(8,128)(2,1)}) custom-call(bf16[1024,4096]{1,0:T(8,128)(2,1)} %get-tuple-element.11.x_ref, bf16[1024,256]{1,0:T(8,128)(2,1)} %get-tuple-element.12.k_first, bf16[1024,256]{1,0:T(8,128)(2,1)} %get-tuple-element.13.k_second, ...), custom_call_target="tpu_custom_call" | custom-call | tf_op jit(solution)/shard_map/emit/pallas_call | solution.py:990
  (1 shorter events, 0.0 us)

commit v13 on v12

--- a/solution.py
+++ b/solution.py
@@ -45,7 +45,7 @@
 LAST_STEPS = 6
 LAST_COLS = 256
 LAST_BLOCKS = 16
-LAST_GAP = 3
+LAST_GAP = 2
 
 
 def layers_kernel(x_ref, cos_ref, sin_ref, gain_ref, wq_ref, wk_ref, wv_ref, wg_ref, wu_ref, wd_ref, wo_ref,
@@ -821,7 +821,7 @@
         if step < 2:
             both(False)
             return
-        z_first = jnp.logical_and(c >= 5, c % 2 == 1)
+        z_first = c % 4 == 3
 
         @pl.when(z_first)
         def _():

time: 356 us -> 359 us (level)
  no operation moved by 1% of the time
where the time goes in v13:
time: 359 us; the launch traced here: 358 us
  Pallas kernels  353 us (98%)
  other arithmetic  3.73 us (1%)
    pallas_call x1, Pallas kernels, layers(): pl.pallas_call(layers_kernel, out_shape=[shape((tok_count, d_model), bf16...  345 us
    pallas_call x1, Pallas kernels, emit(): pl.pallas_call(emit_kernel, out_shape=[jax.ShapeDtypeStruct(x_out.shape,...  8.01 us

profile of v13, /device:TPU:6, one launch (start us, length us, event | category | flops | bytes accessed | tf_op | source)
XLA Modules:
  0.0 357.7 jit_solution(11068266996492707909)
XLA Ops:
  0.6 0.7 convert_element_type.3
  1.3 3.0 multiply_sine_fusion
  4.4 345.2 %layers.1 = (bf16[1024,4096]{1,0:T(8,128)(2,1)}, bf16[1024,256]{1,0:T(8,128)(2,1)}, bf16[1024,256]{1,0:T(8,128)(2,1)}, bf16[1024,256]{1,0:T(8,128)(2,1)}, bf16[1...) custom-call(bf16[1024,4096]{1,0:T(8,128)(2,1)} %x_ref.1, ...), custom_call_target="tpu_custom_call" | custom-call | tf_op jit(solution)/shard_map/layers/pallas_call | solution.py:928
  349.5 8.0 %emit.1 = (bf16[1024,4096]{1,0:T(8,128)(2,1)}, bf16[2,1024,256]{2,1,0:T(8,128)(2,1)}, bf16[2,1024,256]{2,1,0:T(8,128)(2,1)}) custom-call(bf16[1024,4096]{1,0:T(8,128)(2,1)} %get-tuple-element.11.x_ref, bf16[1024,256]{1,0:T(8,128)(2,1)} %get-tuple-element.12.k_first, bf16[1024,256]{1,0:T(8,128)(2,1)} %get-tuple-element.13.k_second, ...), custom_call_target="tpu_custom_call" | custom-call | tf_op jit(solution)/shard_map/emit/pallas_call | solution.py:990
  (1 shorter events, 0.0 us)

commit v14 on v12

--- a/solution.py
+++ b/solution.py
@@ -51,13 +51,14 @@
 def layers_kernel(x_ref, cos_ref, sin_ref, gain_ref, wq_ref, wk_ref, wv_ref, wg_ref, wu_ref, wd_ref, wo_ref,
                  out_ref, k1_ref, v1_ref, k2_ref, v2_ref, gd_ref, go_ref,
                  xbuf, part, recv_a, recv_b, hid, att, wdo, wtile, kv, qbuf, acc, row_max, row_sum, xs, xres,
-                 x_sem, res_sem, w_sem, down_sem, cache_sem, store_sem, own_send, pass_send, ici_recv, core_recv, part_send, part_recv,
-                 round_send, round_recv, side_send, side_recv, give_send, give_recv, relay_buf, relay_send, relay_recv, att_all, ring_send, ring_recv,
+                 x_sem, res_sem, w_sem, down_sem, cache_sem, store_sem, kv_send, ici_recv, core_recv, part_send, part_recv,
+                 round_send, round_recv, side_send, side_recv, give_send, give_recv, relay_buf, relay_send, relay_recv, att_all, ring_send, gather_send, ring_recv,
                  last_send, last_recv, tile_sem, ready_sem, drained_sem):
     tok_count, d_model = xbuf.shape
     head_dim = qbuf.shape[1]
     half_dim = head_dim // 2
     ff_local = hid.shape[1]
+    depth = ff_local + head_dim
     rows_per = tok_count // KV_CHUNKS
     half_rows = tok_count // 2
     lanes = row_max.shape[2]
@@ -98,6 +99,9 @@
     def remote(src, dst, send, recv, **to):
         return pltpu.make_async_remote_copy(src_ref=src, dst_ref=dst, send_sem=send, recv_sem=recv, device_id=to, device_id_type=mesh_id)
 
+    def take(sem, ref):
+        remote(ref, ref, sem, sem, head=my_head).wait_recv()
+
     def x_load(i):
         return pltpu.make_async_copy(x_ref.at[span(i * rows_per, rows_per), :], xs.at[i % 2], x_sem.at[i % 2])
 
@@ -128,70 +132,76 @@
         rows = kv.at[span((origin_chip * 2 + origin_core) * tok_count + i * rows_per, rows_per), :]
         return remote(rows, rows, send, recv, seq=to)
 
-    def kv_routes(layer, i):
-        late = i >= KV_CHUNKS // 2
-        early = jnp.logical_not(late) if not isinstance(i, int) else not late
-
-        def to(send, recv, origin_chip, origin_core, device):
-            return kv_copy(origin_chip, origin_core, i, device, send, recv)
-        own, passed, ici, side = own_send.at[layer], pass_send.at[layer], ici_recv.at[layer], core_recv.at[layer]
+    def kv_routes(i):
+        def to(number, recv, origin_chip, origin_core, device):
+            return lambda: kv_copy(origin_chip, origin_core, i, device, kv_send.at[number], recv)
+        inner = jnp.logical_and(chip >= 1, chip < CHIPS - 1)
         return {
-            'right': (chip < CHIPS - 1, lambda: to(own.at[0, i], ici.at[0, i], chip, core, right)),
-            'wrap': (chip == 0, lambda: to(own.at[1, i], ici.at[2, i], chip, core, left)),
-            'relay': (jnp.logical_and(late, chip == 1), lambda: to(own.at[3, i], ici.at[3, i], chip, core, left)),
-            'other': (core == 0, lambda: to(own.at[2, i], side.at[0, i], chip, core, other)),
-            'on_right': (jnp.logical_and(early, jnp.logical_and(chip >= 1, chip < CHIPS - 1)), lambda: to(passed.at[0, i], ici.at[1, i], chip - 1, core, right)),
-            'from_relay': (jnp.logical_and(late, chip == 0), lambda: to(passed.at[0, i], ici.at[1, i], 1, core, left)),
-            'on_left': (jnp.logical_and(late, chip == CHIPS - 1), lambda: to(passed.at[0, i], ici.at[1, i], 0, core, left)),
-            'side1': (chip >= 1, lambda: to(passed.at[1, i], side.at[1, i], chip - 1, core, other)),
-            'side2': (chip >= 2, lambda: to(passed.at[2, i], side.at[2, i], chip - 2, core, other)),
-            'side3': (chip >= 3, lambda: to(passed.at[3, i], side.at[3, i], chip - 3, core, other)),
+            'right': (chip < CHIPS - 1, 'all', to(0, ici_recv.at[0, i], chip, core, right)),
+            'wrap': (chip == 0, 'all', to(1, ici_recv.at[2, i], chip, core, left)),
+            'relay': (chip == 1, 'late', to(2, ici_recv.at[3, i], chip, core, left)),
+            'other': (core == 0, 'all', to(3, core_recv.at[0, i], chip, core, other)),
+            'on_right': (inner, 'early', to(4, ici_recv.at[1, i], chip - 1, core, right)),
+            'from_relay': (chip == 0, 'late', to(5, ici_recv.at[1, i], 1, core, left)),
+            'on_left': (chip == CHIPS - 1, 'late', to(6, ici_recv.at[1, i], 0, core, left)),
+            'side1': (chip >= 1, 'all', to(7, core_recv.at[1, i], chip - 1, core, other)),
+            'side2': (chip >= 2, 'all', to(8, core_recv.at[2, i], chip - 2, core, other)),
+            'side3': (chip >= 3, 'all', to(9, core_recv.at[3, i], chip - 3, core, other)),
         }
 
-    def start_route(layer, i, name):
-        condition, copy = kv_routes(layer, i)[name]
+    def start_route(i, name):
+        condition, which, copy = kv_routes(i)[name]
+        if which != 'all':
+            late = i >= KV_CHUNKS // 2
+            if isinstance(i, int):
+                if late != (which == 'late'):
+                    return
+            else:
+                condition = jnp.logical_and(condition, late if which == 'late' else jnp.logical_not(late))
 
         @pl.when(condition)
         def _():
             copy().start()
 
-    def send_kv(layer, i):
+    def send_kv(i):
         for name in ('right', 'wrap', 'relay', 'other'):
-            start_route(layer, i, name)
-
-    def kv_sent(layer):
-        for i in range(KV_CHUNKS):
-            for condition, copy in kv_routes(layer, i).values():
-                @pl.when(condition)
-                def _():
-                    copy().wait_send()
-
-    def serve(layer, back, i):
+            start_route(i, name)
+
+    def kv_sent():
+        for number, (condition, which, _) in enumerate(kv_routes(0).values()):
+            @pl.when(condition)
+            def _():
+                take(kv_send.at[number], kv.at[pl.ds(0, tok_count if which == 'all' else half_rows), :])
+
+    def serve(back, i):
         @pl.when(chip >= back)
         def _():
-            kv_copy(chip - back, core, i, other, pass_send.at[layer, back, i], ici_recv.at[layer, back - 1, i]).wait_recv()
-        start_route(layer, i, 'side%d' % back)
+            kv_copy(chip - back, core, i, other, kv_send.at[0], ici_recv.at[back - 1, i]).wait_recv()
+        start_route(i, 'side%d' % back)
         if back == 1:
-            start_route(layer, i, 'on_right')
+            start_route(i, 'on_right')
         if back == 3:
-            start_route(layer, i, 'on_left')
-
-    def relay(layer, i):
-        condition, copy = kv_routes(layer, i)['from_relay']
-
-        @pl.when(condition)
-        def _():
-            kv_copy(1, core, i, left, pass_send.at[layer, 0, i], ici_recv.at[layer, 3, i]).wait_recv()
-            copy().start()
-
-    def serve_all(layer, i):
-        serve(layer, 1, i)
-        serve(layer, 3, i)
-        relay(layer, i)
-
-    def taken(layer, back, chunks):
+            start_route(i, 'on_left')
+
+    def relay(i):
+        def pass_on():
+            @pl.when(chip == 0)
+            def _():
+                kv_copy(1, core, i, left, kv_send.at[0], ici_recv.at[3, i]).wait_recv()
+            start_route(i, 'from_relay')
+        if not isinstance(i, int):
+            pl.when(i >= KV_CHUNKS // 2)(pass_on)
+        elif i >= KV_CHUNKS // 2:
+            pass_on()
+
+    def serve_all(i):
+        serve(1, i)
+        serve(3, i)
+        relay(i)
+
+    def taken(back, chunks):
         for i in chunks:
-            kv_copy(chip - back, 1 - core, i, other, pass_send.at[layer, 0, i], core_recv.at[layer, back, i]).wait_recv()
+            kv_copy(chip - back, 1 - core, i, other, kv_send.at[0], core_recv.at[back, i]).wait_recv()
 
     def z_parts(step, d):
         copies = []
@@ -204,7 +214,7 @@
             else:
                 rows = span(my_seq * size + d * (size // 2), size // 2)
                 src = dst = all_ref.at[wrap(pos_z - sign[d]), rows, :]
-            copies.append(remote(src, dst, part_send.at[step, d, n], part_recv.at[step, d, n], head=z_peer(d)))
+            copies.append(remote(src, dst, part_send, part_recv.at[step], head=z_peer(d)))
         return copies
 
     def part_copies(j, part_chip, part_core, half, send, recv, to):
@@ -214,17 +224,17 @@
             first = (part_chip * 2 + part_core) * size
             rows = span(first, size) if half is None else span(first + half * (size // 2), size // 2)
             place = ref.at[wrap(pos_z + j), rows, :]
-            copies.append(remote(place, place, send.at[n], recv.at[n], seq=to))
+            copies.append(remote(place, place, send, recv, seq=to))
         return copies
 
     def own_part(j, d):
-        return part_copies(j, chip, core, None, round_send.at[0, j - 1, d], round_recv.at[0, j - 1, d], x_device(sign[d]))
+        return part_copies(j, chip, core, None, round_send, round_recv.at[0, j - 1], x_device(sign[d]))
 
     def far_part(j, d):
-        return part_copies(j, wrap(chip - sign[d]), core, d, round_send.at[1, j - 1, d], round_recv.at[1, j - 1, d], x_device(sign[d]))
+        return part_copies(j, wrap(chip - sign[d]), core, d, round_send, round_recv.at[1, j - 1], x_device(sign[d]))
 
     def side_part(j, n, side):
-        return part_copies(j, wrap(chip + n), side, None, side_send.at[j - 1, n], side_recv.at[j - 1, n], other)
+        return part_copies(j, wrap(chip + n), side, None, side_send, side_recv, other)
 
     def round_start(j):
         for d in range(DIRS):
@@ -232,32 +242,29 @@
         start(side_part(j, 0, core))
 
     def near_parts(j):
+        take(round_recv.at[0, j - 1], xbuf.at[pl.ds(0, depth // CHIPS), :])
         for d in range(DIRS):
-            for copy in own_part(j, d):
-                copy.wait_recv()
             start(far_part(j, d) + side_part(j, 3 if d == 0 else 1, core))
 
     def far_parts(j):
-        for d in range(DIRS):
-            for copy in far_part(j, d):
-                copy.wait_recv()
+        take(round_recv.at[1, j - 1], xbuf.at[pl.ds(0, depth // (2 * CHIPS)), :])
         start(side_part(j, 2, core))
 
     def give_hidden(z, i, source):
         cols = span(i * W_TILE, W_TILE)
-        return remote(hid.at[span(z * rows_per, rows_per), cols], hidden_place(source, i), give_send.at[z, i], give_recv.at[source, i], head=z_device(z))
+        return remote(hid.at[span(z * rows_per, rows_per), cols], hidden_place(source, i), give_send, give_recv, head=z_device(z))
 
     def hidden_place(source, i):
         return xs.at[1, :, span(source * ff_local + i * W_TILE, W_TILE)]
 
     def via_neighbor(z, i):
         step = jnp.where(i < KV_CHUNKS // 2, 1, -1)
-        return remote(hid.at[span(z * rows_per, rows_per), span(i * W_TILE, W_TILE)], relay_buf.at[i], give_send.at[z, i], relay_recv.at[i], head=z_device(pos_z + step))
+        return remote(hid.at[span(z * rows_per, rows_per), span(i * W_TILE, W_TILE)], relay_buf.at[i], give_send, relay_recv, head=z_device(pos_z + step))
 
     def relay_hidden(i):
         step = 1 if i < KV_CHUNKS // 2 else -1
         source = wrap(pos_z - step)
-        return remote(relay_buf.at[i], hidden_place(source, i), relay_send.at[i], give_recv.at[source, i], head=z_device(pos_z + step))
+        return remote(relay_buf.at[i], hidden_place(source, i), relay_send, give_recv, head=z_device(pos_z + step))
 
     def send_hidden(z, i):
         away = wrap(z - pos_z)
@@ -271,7 +278,7 @@
             give_hidden(z, i, pos_z).start()
 
     def give_rows(z, source):
-        return remote(att.at[span(z * rows_per, rows_per), :], att_all.at[source], give_send.at[z, KV_CHUNKS], give_recv.at[source, KV_CHUNKS], head=z_device(z))
+        return remote(att.at[span(z * rows_per, rows_per), :], att_all.at[source], give_send, give_recv, head=z_device(z))
 
     def norm_rows(x_few, layer):
         x_f32 = x_few.astype(f32)
@@ -346,10 +353,10 @@
         block = (chip - back) * 2 + jnp.where(later % 2 == 0, core, 1 - core)
         return jnp.where(jnp.logical_and(core == 1, n == 0), chip * 2, block) * tok_count
 
-    def arrivals(layer, n, chunks):
+    def arrivals(n, chunks):
         @pl.when(jnp.logical_and(core == 1, n == 0))
         def _():
-            taken(layer, 0, chunks)
+            taken(0, chunks)
 
         for back in (1, 3, 2):
             place = 0 if back == 1 else 2 if back == 3 else jnp.where(chip == CHIPS - 1, 4, 2)
@@ -357,20 +364,20 @@
                 @pl.when(jnp.logical_and(chip >= back, n == core + place))
                 def _():
                     for i in chunks:
-                        serve(layer, 2, i)
+                        serve(2, i)
 
             @pl.when(jnp.logical_and(chip >= back, n == core + place + 1))
             def _():
-                taken(layer, back, chunks)
+                taken(back, chunks)
 
     def visit(n, visits):
         for q_half, side in visits:
             attend(past_start(n) + side * half_rows, q_half, side, False, False)
 
-    def attend_past(layer, first_n, last_n, chunks, visits):
+    def attend_past(first_n, last_n, chunks, visits):
         def past(n, carry):
             if chunks:
-                arrivals(layer, n, chunks)
+                arrivals(n, chunks)
             visit(n, visits)
             return carry
 
@@ -425,16 +432,17 @@
         else:
             src = dst = xbuf.at[x_rows(chunk, wrap(p1 - s), d * eighth, eighth), half_of(h)]
         peer = (first_peer if step in (0, 1, 6, 7) else second_peer)[h](d)
-        return remote(src, dst, ring_send.at[chunk, step, h * DIRS + d], ring_recv.at[chunk, step, h * DIRS + d], head=peer)
-
-    def each_message(chunk, steps, act):
-        for step in steps:
-            for h in range(HALVES):
-                for d in range(DIRS):
-                    act(message(step, chunk, h, d))
+        return remote(src, dst, ring_send.at[chunk % PART_SLOTS] if step < 4 else gather_send.at[step - 4], ring_recv.at[slot, step], head=peer)
+
+    def arrived_in(step, count=1):
+        rows = (2 * eighth, 2 * quarter, eighth // 2, quarter // 2, quarter // 2, quarter // 2, 2 * quarter, quarter)[step] * count
+        return (part if step < 4 else xbuf).at[pl.ds(0, rows), pl.ds(0, half_cols if step == 5 else d_model)]
+
+    def partials_sent(slot):
+        take(ring_send.at[slot], part.at[pl.ds(0, 2 * eighth + 2 * quarter + eighth // 2 + quarter // 2), :])
 
     def residual_load(chunk, h):
-        return pltpu.make_async_copy(x_ref.at[x_rows(chunk, first_pos[h], 0, quarter), cols_of(h, second_pos[h])], xres.at[chunk, h], res_sem.at[chunk, h])
+        return pltpu.make_async_copy(x_ref.at[x_rows(chunk, first_pos[h], 0, quarter), cols_of(h, second_pos[h])], xres.at[chunk, h], res_sem)
 
     def project(chunk):
         rows = span(chunk * chunk_rows, chunk_rows)
@@ -457,13 +465,16 @@
         if number == 0:
             @pl.when(chunk >= PART_SLOTS)
             def _():
-                each_message(chunk - PART_SLOTS, range(4), lambda copy: copy.wait_send())
+                partials_sent(chunk % PART_SLOTS)
             project(chunk)
+        else:
+            take(ring_recv.at[slot, number - 1], arrived_in(number - 1))
+        if number == 4:
+            @pl.when(chunk == 0)
+            def _():
+                take(res_sem, xres)
         for h in range(HALVES):
             p1, p2 = first_pos[h], second_pos[h]
-            if number:
-                for d in range(DIRS):
-                    message(number - 1, chunk, h, d).wait_recv()
             if number in (1, 3):
                 for d in range(DIRS):
                     if number == 1:
@@ -475,7 +486,6 @@
                 rows = part_rows(chunk, p1, 0, quarter)
                 part[rows, half_of(h)] = part[rows, half_of(h)] + recv_a[slot, h, 0, pl.ds(0, quarter), :] + recv_a[slot, h, 1, pl.ds(0, quarter), :]
             if number == 4:
-                residual_load(chunk, h).wait()
                 rows, cols = part_rows(chunk, p1, 0, quarter), cols_of(h, p2)
                 total = part[rows, cols] + recv_b[slot, h, 0, pl.ds(0, quarter), :] + recv_b[slot, h, 1, pl.ds(0, quarter), :]
                 update = total.astype(bf16).astype(f32)
@@ -517,7 +527,7 @@
         def _():
             pl.semaphore_wait(barrier, 8)
 
-        send_kv(0, i)
+        send_kv(i)
 
         @pl.when(i == 0)
         def _():
@@ -531,8 +541,8 @@
 
     def cache_stores(layer):
         k_ref, v_ref = ((k1_ref, v1_ref), (k2_ref, v2_ref))[layer]
-        return [pltpu.make_async_copy(kv.at[own_rows, pl.ds(0, head_dim)], k_ref, cache_sem.at[layer, 0]),
-                pltpu.make_async_copy(kv.at[own_rows, pl.ds(head_dim, head_dim)], v_ref, cache_sem.at[layer, 1])]
+        return [pltpu.make_async_copy(kv.at[own_rows, pl.ds(0, head_dim)], k_ref, cache_sem),
+                pltpu.make_async_copy(kv.at[own_rows, pl.ds(head_dim, head_dim)], v_ref, cache_sem)]
 
     start(cache_stores(0))
     wait(weights(0, 1))
@@ -575,7 +585,7 @@
 
         @pl.when(tile < 3)
         def _():
-            serve_all(0, tile)
+            serve_all(tile)
         return carry
 
     def second_half(tile, carry):
@@ -583,18 +593,17 @@
 
         @pl.when(tile == 0)
         def _():
-            serve_all(0, 3)
-            attend_past(0, 0, near_count, range(KV_CHUNKS), ((0, 0), (0, 1)))
+            serve_all(3)
+            attend_past(0, near_count, range(KV_CHUNKS), ((0, 0), (0, 1)))
+            take(part_recv.at[0], xbuf.at[pl.ds(0, depth // CHIPS), :])
             for d in range(DIRS):
-                for copy in z_parts(0, d):
-                    copy.wait_recv()
                 start(z_parts(1, d))
         return carry
 
     lax.fori_loop(0, ff_local // W_TILE, first_half, 0)
     attend_own(0)
     lax.fori_loop(0, 2, second_half, 0)
-    attend_past(0, near_count, my_seq, range(KV_CHUNKS), ((0, 0), (0, 1)))
+    attend_past(near_count, my_seq, range(KV_CHUNKS), ((0, 0), (0, 1)))
     finish(0, False)
     finish(1, False)
     round_start(1)
@@ -615,7 +624,7 @@
             lax.fori_loop(0, rows_per // NORM_ROWS, few, 0)
             wait(weights(1, 0))
             keys_values(xs[0], j)
-            send_kv(1, j)
+            send_kv(j)
             start(weights(1, 2))
 
         @pl.when(phase == 1)
@@ -675,22 +684,20 @@
 
         @pl.when(jnp.logical_and(early >= 0, jnp.logical_and(early < 7, early < my_seq)))
         def _():
-            arrivals(1, early, (0, 1))
+            arrivals(early, (0, 1))
             visit(early, ((0, 0),))
 
         @pl.when(t == 2)
         def _():
-            for d in range(DIRS):
-                for copy in z_parts(1, d):
-                    copy.wait_recv()
+            take(part_recv.at[1], xbuf.at[pl.ds(0, depth // (2 * CHIPS)), :])
             round_start(2)
 
         @pl.when(t == DONE_TICK)
         def _():
             finish(2, False)
             finish(3, False)
-            kv_sent(0)
-            wait(cache_stores(0))
+            kv_sent()
+            take(cache_sem, kv.at[own_rows, :])
             for n, peer in enumerate((left, right, other)):
                 pl.semaphore_signal(ready_sem.at[n], inc=1, device_id={'seq': peer}, device_id_type=mesh_id)
 
@@ -719,43 +726,36 @@
         for i, when in enumerate(SERVE_TICKS):
             @pl.when(t == when)
             def _():
-                serve_all(1, i)
+                serve_all(i)
         return carry
 
     lax.fori_loop(0, LAST_TICK, tick, 0)
 
-    def drain(chunk, carry):
-        @pl.when(chunk >= CHUNKS - PART_SLOTS)
-        def _():
-            each_message(chunk, range(4), lambda copy: copy.wait_send())
-        each_message(chunk, range(4, STEPS), lambda copy: copy.wait_send())
-        return carry
-
-    lax.fori_loop(0, CHUNKS, drain, 0)
+    for slot in range(PART_SLOTS):
+        partials_sent(slot)
+    for step in range(4, STEPS):
+        take(gather_send.at[step - 4], arrived_in(step, CHUNKS))
     for d in range(DIRS):
         pl.semaphore_signal(drained_sem.at[d], inc=1, device_id={'head': y_peer(d)}, device_id_type=mesh_id)
     start(cache_stores(1))
     near_parts(2)
     attend_own(1)
-    attend_past(1, 0, my_seq, (), ((1, 0),))
+    attend_past(0, my_seq, (), ((1, 0),))
+    take(relay_recv, relay_buf)
     for i in range(KV_CHUNKS):
-        via_neighbor(0, i).wait_recv()
         relay_hidden(i).start()
-    attend_past(1, 0, near_count, (2, 3), ((0, 1), (1, 1)))
-    attend_past(1, near_count, my_seq, (2, 3), ((0, 1),))
+    attend_past(0, near_count, (2, 3), ((0, 1), (1, 1)))
+    attend_past(near_count, my_seq, (2, 3), ((0, 1),))
     finish(0, True)
     finish(1, True)
-    attend_past(1, near_count, my_seq, (), ((1, 1),))
+    attend_past(near_count, my_seq, (), ((1, 1),))
     finish(2, True)
     finish(3, True)
     far_parts(2)
-    for j in range(1, RING):
-        for n in range(CHIPS):
-            for copy in side_part(j, n, 1 - core):
-                copy.wait_recv()
+    parts_ref = gd_ref.at[pl.ds(0, 2), pl.ds(0, 3 * depth // 4), :]
+    take(side_recv, parts_ref)
 
     quarter_rows = rows_per // RING
-    depth = ff_local + head_dim
 
     def block_cols(c):
         return span(c * LAST_COLS, LAST_COLS)
@@ -769,16 +769,13 @@
             z = wrap(pos_z + j)
             down = wd_ref.at[1, :, block_cols(c)] if j == 0 else gd_ref.at[z, :, block_cols(c)]
             out = wo_ref.at[1, 0, :, block_cols(c)] if j == 0 else go_ref.at[z, :, block_cols(c)]
-            copies.append(pltpu.make_async_copy(down, tile_place(c, j, 0, ff_local), tile_sem.at[c % 2, j, 0]))
-            copies.append(pltpu.make_async_copy(out, tile_place(c, j, ff_local, head_dim), tile_sem.at[c % 2, j, 1]))
+            copies.append(pltpu.make_async_copy(down, tile_place(c, j, 0, ff_local), tile_sem.at[c % 2]))
+            copies.append(pltpu.make_async_copy(out, tile_place(c, j, ff_local, head_dim), tile_sem.at[c % 2]))
         return copies
 
     start(tile_loads(0))
-    for j in range(1, RING):
-        z = wrap(pos_z + j)
-        for i in range(KV_CHUNKS):
-            give_hidden(z, i, z).wait_recv()
-        give_rows(z, z).wait_recv()
+    given = hid.at[pl.ds(0, (RING - 1) * rows_per * depth // ff_local), :]
+    take(give_recv, given)
     for d in range(DIRS):
         pl.semaphore_wait(drained_sem.at[d], 1)
 
@@ -810,13 +807,16 @@
                 rows = [rows_at(z, behind, d * half, half) for z in range(RING)] if z_first else [rows_at(back, 0, d * (rows_per // 2), rows_per // 2)]
             pairs = [(xbuf.at[r, cols], xbuf.at[r, cols]) for r in rows]
         to = (y_peer if along_y else z_peer)(d)
-        return [remote(src, dst, last_send.at[c, step, d, n], last_recv.at[c, step, d, n], head=to) for n, (src, dst) in enumerate(pairs)]
-
-    def on_last(step, c, act):
+        return [remote(src, dst, last_send.at[step], last_recv.at[c, step], head=to) for src, dst in pairs]
+
+    def last_arrived(step, cols):
+        rows = (quarter_rows, 2 * quarter_rows, 2 * quarter_rows, quarter_rows, 2 * rows_per, rows_per)[step]
+        return (part if step < 2 else xbuf).at[pl.ds(0, rows), cols]
+
+    def send_last(step, c):
         def both(z_first):
             for d in range(DIRS):
-                for copy in last_messages(step, c, d, z_first):
-                    act(copy)
+                start(last_messages(step, c, d, z_first))
 
         if step < 2:
             both(False)
@@ -832,14 +832,14 @@
             both(False)
 
     def out_store(c):
-        return pltpu.make_async_copy(xbuf.at[:, block_cols(c)], out_ref.at[:, block_cols(c)], store_sem.at[c])
+        return pltpu.make_async_copy(xbuf.at[:, block_cols(c)], out_ref.at[:, block_cols(c)], store_sem)
 
     def last_project(c):
         @pl.when(c + 1 < LAST_BLOCKS)
         def _():
             start(tile_loads(c + 1))
 
-        wait(tile_loads(c))
+        take(tile_sem.at[c % 2], wtile.at[c % 2, :, pl.ds(0, 2 * depth), :])
         total = None
         for j in range(RING):
             z = wrap(pos_z + j)
@@ -856,7 +856,7 @@
         if number == 0:
             last_project(c)
         else:
-            on_last(number - 1, c, lambda copy: copy.wait_recv())
+            take(last_recv.at[c, number - 1], last_arrived(number - 1, cols))
         if number == 1:
             for d in range(DIRS):
                 piece = quarter_of(wrap(pos_y + sign[d]), d * half, half)
@@ -868,7 +868,7 @@
             rows = rows_at(pos_z, pos_y, 0, quarter_rows)
             xbuf[rows, cols] = (xbuf[rows, cols].astype(f32) + update).astype(bf16)
         if number < LAST_STEPS:
-            on_last(number, c, lambda copy: copy.start())
+            send_last(number, c)
         else:
             out_store(c).start()
 
@@ -883,33 +883,16 @@
 
     lax.fori_loop(0, LAST_BLOCKS + LAST_GAP * LAST_STEPS, last_tick, 0)
 
-    wait(cache_stores(1))
-    for i in range(KV_CHUNKS):
-        relay_hidden(i).wait_send()
-    kv_sent(1)
-    for d in range(DIRS):
-        for step in range(2):
-            for copy in z_parts(step, d):
-                copy.wait_send()
-    for j in range(1, RING):
-        for d in range(DIRS):
-            for copy in own_part(j, d) + far_part(j, d):
-                copy.wait_send()
-        for n in range(CHIPS):
-            for copy in side_part(j, n, core):
-                copy.wait_send()
-        z = wrap(pos_z + j)
-        for i in range(KV_CHUNKS):
-            give_hidden(z, i, pos_z).wait_send()
-        give_rows(z, pos_z).wait_send()
-
-    def last_drain(c, carry):
-        for step in range(LAST_STEPS):
-            on_last(step, c, lambda copy: copy.wait_send())
-        out_store(c).wait()
-        return carry
-
-    lax.fori_loop(0, LAST_BLOCKS, last_drain, 0)
+    take(cache_sem, kv.at[own_rows, :])
+    take(relay_send, relay_buf)
+    kv_sent()
+    take(part_send, xbuf.at[pl.ds(0, 3 * depth // 8), :])
+    take(round_send, gd_ref.at[pl.ds(0, 2), pl.ds(0, 9 * depth // 16), :])
+    take(side_send, parts_ref)
+    take(give_send, given)
+    for step in range(LAST_STEPS):
+        take(last_send.at[step], last_arrived(step, pl.ds(0, d_model)))
+    take(store_sem, xbuf)
 
 
 def layers(x_loc, cos_t, sin_t, norm_gain, w_q, w_k, w_v, w_gate, w_up, w_down, w_o):
@@ -947,14 +930,14 @@
             pltpu.VMEM((2, tok_count, 128), f32),
             pltpu.VMEM((2, rows_per, d_model), bf16),
             pltpu.VMEM((CHUNKS, HALVES, chunk_rows // RING, half_cols // RING), bf16),
-            dma((2,)), dma((CHUNKS, HALVES)), dma((2, 2)), dma((2, 2)), dma((2, 2)), dma((LAST_BLOCKS,)),
-            dma((2, 4, KV_CHUNKS)), dma((2, 4, KV_CHUNKS)), dma((2, 4, KV_CHUNKS)), dma((2, 4, KV_CHUNKS)), dma((2, DIRS, 2)), dma((2, DIRS, 2)),
-            dma((2, RING - 1, DIRS, 2)), dma((2, RING - 1, DIRS, 2)), dma((RING - 1, CHIPS, 2)), dma((RING - 1, CHIPS, 2)),
-            dma((RING, KV_CHUNKS + 1)), dma((RING, KV_CHUNKS + 1)),
-            pltpu.VMEM((KV_CHUNKS, rows_per, W_TILE), bf16), dma((KV_CHUNKS,)), dma((KV_CHUNKS,)),
+            dma((2,)), dma, dma((2, 2)), dma((2, 2)), dma, dma,
+            dma((10,)), dma((4, KV_CHUNKS)), dma((4, KV_CHUNKS)), dma, dma((2,)),
+            dma, dma((2, RING - 1)), dma, dma,
+            dma, dma,
+            pltpu.VMEM((KV_CHUNKS, rows_per, W_TILE), bf16), dma, dma,
             pltpu.VMEM((RING, rows_per, head_dim), bf16),
-            dma((CHUNKS, STEPS, HALVES * DIRS)), dma((CHUNKS, STEPS, HALVES * DIRS)),
-            dma((LAST_BLOCKS, LAST_STEPS, DIRS, RING)), dma((LAST_BLOCKS, LAST_STEPS, DIRS, RING)), dma((2, RING, 2)),
+            dma((PART_SLOTS,)), dma((4,)), dma((RECV_SLOTS, STEPS)),
+            dma((LAST_STEPS,)), dma((LAST_BLOCKS, LAST_STEPS)), dma((2,)),
             pltpu.SemaphoreType.REGULAR((3,)), pltpu.SemaphoreType.REGULAR((DIRS,)),
         ],
         compiler_params=pltpu.CompilerParams(collective_id=0, has_side_effects=True, vmem_limit_bytes=67043328),

time: 356 us -> 336 us (0.944)
  Pallas kernels: 350 us -> 330 us
    pallas_call x1, Pallas kernels: 342 us -> 322 us  [layers(): pl.pallas_call(layers_kernel, out_shape=[shape((tok_count, d_model), bf16...]
where the time goes in v14:
time: 336 us; the launch traced here: 334 us
  Pallas kernels  330 us (98%)
  other arithmetic  3.73 us (1%)
    pallas_call x1, Pallas kernels, layers(): pl.pallas_call(layers_kernel, out_shape=[shape((tok_count, d_model), bf16...  322 us
    pallas_call x1, Pallas kernels, emit(): pl.pallas_call(emit_kernel, out_shape=[jax.ShapeDtypeStruct(x_out.shape,...  8.01 us

profile of v14, /device:TPU:6, one launch (start us, length us, event | category | flops | bytes accessed | tf_op | source)
XLA Modules:
  0.0 334.3 jit_solution(10844048117574801864)
XLA Ops:
  0.6 0.7 convert_element_type.3
  1.3 3.0 multiply_sine_fusion
  4.4 321.7 %layers.1 = (bf16[1024,4096]{1,0:T(8,128)(2,1)}, bf16[1024,256]{1,0:T(8,128)(2,1)}, bf16[1024,256]{1,0:T(8,128)(2,1)}, bf16[1024,256]{1,0:T(8,128)(2,1)}, bf16[1...) custom-call(bf16[1024,4096]{1,0:T(8,128)(2,1)} %x_ref.1, ...), custom_call_target="tpu_custom_call" | custom-call | tf_op jit(solution)/shard_map/layers/pallas_call | solution.py:911
  326.1 8.0 %emit.1 = (bf16[1024,4096]{1,0:T(8,128)(2,1)}, bf16[2,1024,256]{2,1,0:T(8,128)(2,1)}, bf16[2,1024,256]{2,1,0:T(8,128)(2,1)}) custom-call(bf16[1024,4096]{1,0:T(8,128)(2,1)} %get-tuple-element.11.x_ref, bf16[1024,256]{1,0:T(8,128)(2,1)} %get-tuple-element.12.k_first, bf16[1024,256]{1,0:T(8,128)(2,1)} %get-tuple-element.13.k_second, ...), custom_call_target="tpu_custom_call" | custom-call | tf_op jit(solution)/shard_map/emit/pallas_call | solution.py:973
  (1 shorter events, 0.0 us)

commit v15 on v14

--- a/solution.py
+++ b/solution.py
@@ -383,6 +383,7 @@
 
         lax.fori_loop(first_n, last_n, past, 0)
 
+    few_near = jnp.minimum(my_seq, 1)
     near_count = my_seq - jnp.where(chip >= 2, 2, 0)
 
     def finish(i, spread):
@@ -412,31 +413,28 @@
     def half_of(h):
         return pl.ds(h * half_cols, half_cols)
 
-    def message(step, chunk, h, d):
+    def ring_copies(step, chunk, h, d):
         p1, p2, s = first_pos[h], second_pos[h], sign[d]
-        slot = chunk % RECV_SLOTS
-        if step == 0:
-            src, dst = part.at[part_rows(chunk, wrap(p1 + 2), d * eighth, eighth), half_of(h)], recv_a.at[slot, h, d, pl.ds(quarter, eighth), :]
-        elif step == 1:
-            src, dst = part.at[part_rows(chunk, wrap(p1 + s), 0, quarter), half_of(h)], recv_a.at[slot, h, d, pl.ds(0, quarter), :]
-        elif step == 2:
-            src, dst = part.at[part_rows(chunk, p1, d * eighth, eighth), cols_of(h, wrap(p2 + 2))], recv_b.at[slot, h, d, pl.ds(quarter, eighth), :]
-        elif step == 3:
-            src, dst = part.at[part_rows(chunk, p1, 0, quarter), cols_of(h, wrap(p2 + s))], recv_b.at[slot, h, d, pl.ds(0, quarter), :]
-        elif step == 4:
-            src = dst = xbuf.at[x_rows(chunk, p1, 0, quarter), cols_of(h, p2)]
-        elif step == 5:
-            src = dst = xbuf.at[x_rows(chunk, p1, d * eighth, eighth), cols_of(h, wrap(p2 - s))]
-        elif step == 6:
-            src = dst = xbuf.at[x_rows(chunk, p1, 0, quarter), half_of(h)]
+        slot, mine, rest = chunk % RECV_SLOTS, d * eighth, (1 - d) * eighth
+        if step < 4:
+            box, piece_of, cols = (recv_a, wrap(p1 + s), half_of(h)) if step < 2 else (recv_b, p1, cols_of(h, wrap(p2 + s)))
+            far_piece, far_cols = (wrap(p1 + 2), half_of(h)) if step < 2 else (p1, cols_of(h, wrap(p2 + 2)))
+            if step % 2 == 0:
+                places = [(part.at[part_rows(chunk, far_piece, mine, eighth), far_cols], box.at[slot, h, d, pl.ds(quarter, eighth), :]),
+                          (part.at[part_rows(chunk, piece_of, rest, eighth), cols], box.at[slot, h, d, pl.ds(rest, eighth), :])]
+            else:
+                places = [(part.at[part_rows(chunk, piece_of, mine, eighth), cols], box.at[slot, h, d, pl.ds(mine, eighth), :])]
         else:
-            src = dst = xbuf.at[x_rows(chunk, wrap(p1 - s), d * eighth, eighth), half_of(h)]
+            piece_of, cols = (p1, cols_of(h, p2 if step == 4 else wrap(p2 - s))) if step < 6 else (p1 if step == 6 else wrap(p1 - s), half_of(h))
+            refs = [xbuf.at[x_rows(chunk, piece_of, offset, eighth), cols] for offset in ((mine, rest) if step % 2 == 0 else (mine,))]
+            places = [(ref, ref) for ref in refs]
         peer = (first_peer if step in (0, 1, 6, 7) else second_peer)[h](d)
-        return remote(src, dst, ring_send.at[chunk % PART_SLOTS] if step < 4 else gather_send.at[step - 4], ring_recv.at[slot, step], head=peer)
+        return [remote(src, dst, ring_send.at[chunk % PART_SLOTS] if step < 4 else gather_send.at[step + n - 4], ring_recv.at[slot, step + n], head=peer)
+                for n, (src, dst) in enumerate(places)]
 
     def arrived_in(step, count=1):
-        rows = (2 * eighth, 2 * quarter, eighth // 2, quarter // 2, quarter // 2, quarter // 2, 2 * quarter, quarter)[step] * count
-        return (part if step < 4 else xbuf).at[pl.ds(0, rows), pl.ds(0, half_cols if step == 5 else d_model)]
+        rows = (2 * eighth, 2 * quarter, eighth // 2, quarter // 2, quarter // 2, quarter // 2, quarter, 2 * quarter)[step] * count
+        return (part if step < 4 else xbuf).at[pl.ds(0, rows), pl.ds(0, half_cols if step == 4 else d_model)]
 
     def partials_sent(slot):
         take(ring_send.at[slot], part.at[pl.ds(0, 2 * eighth + 2 * quarter + eighth // 2 + quarter // 2), :])
@@ -490,9 +488,10 @@
                 total = part[rows, cols] + recv_b[slot, h, 0, pl.ds(0, quarter), :] + recv_b[slot, h, 1, pl.ds(0, quarter), :]
                 update = total.astype(bf16).astype(f32)
                 xbuf[x_rows(chunk, p1, 0, quarter), cols] = (xres[chunk, h].astype(f32) + update).astype(bf16)
-            if number < STEPS:
-                for d in range(DIRS):
-                    message(number, chunk, h, d).start()
+        if number < STEPS:
+            copies = [ring_copies(number, chunk, h, d) for h in range(HALVES) for d in range(DIRS)]
+            for n in range(len(copies[0])):
+                start([copy[n] for copy in copies])
 
     x_load(0).start()
     start(weights(0, 0))
@@ -503,6 +502,9 @@
         pl.semaphore_signal(barrier, inc=1, device_id={'seq': peer}, device_id_type=mesh_id)
     for peer in [z_device(pos_z + j) for j in range(1, RING)] + [y_peer(d) for d in range(DIRS)]:
         pl.semaphore_signal(barrier, inc=1, device_id={'head': peer}, device_id_type=mesh_id)
+    pl.semaphore_wait(barrier, 8)
+    for d in range(DIRS):
+        start(z_parts(0, d))
 
     def prepare(i, carry):
         x_load(i).wait()
@@ -522,17 +524,7 @@
             wait(weights(0, 0))
 
         keys_values(xbuf[span(i * rows_per, rows_per), :], i)
-
-        @pl.when(i == 0)
-        def _():
-            pl.semaphore_wait(barrier, 8)
-
         send_kv(i)
-
-        @pl.when(i == 0)
-        def _():
-            for d in range(DIRS):
-                start(z_parts(0, d))
         return carry
 
     lax.fori_loop(0, KV_CHUNKS, prepare, 0)
@@ -594,10 +586,11 @@
         @pl.when(tile == 0)
         def _():
             serve_all(3)
-            attend_past(0, near_count, range(KV_CHUNKS), ((0, 0), (0, 1)))
+            attend_past(0, few_near, range(KV_CHUNKS), ((0, 0), (0, 1)))
             take(part_recv.at[0], xbuf.at[pl.ds(0, depth // CHIPS), :])
             for d in range(DIRS):
                 start(z_parts(1, d))
+            attend_past(few_near, near_count, range(KV_CHUNKS), ((0, 0), (0, 1)))
         return carry
 
     lax.fori_loop(0, ff_local // W_TILE, first_half, 0)
@@ -791,32 +784,36 @@
     def last_messages(step, c, d, z_first):
         s, cols, half = sign[d], block_cols(c), quarter_rows // 2
         near, behind, back = wrap(pos_y + s), wrap(pos_y - s), wrap(pos_z - s)
+        mine, rest = d * half, (1 - d) * half
         along_y = step < 2 or (step < 4) != z_first
         if step == 0:
-            pairs = [(part.at[quarter_of(wrap(pos_y + 2), d * half, half), cols], part.at[landed(d, quarter_rows, half), cols])]
+            groups = [[(part.at[quarter_of(wrap(pos_y + 2), mine, half), cols], part.at[landed(d, quarter_rows, half), cols])],
+                      [(part.at[quarter_of(near, rest, half), cols], part.at[landed(d, rest, half), cols])]]
         elif step == 1:
-            pairs = [(part.at[quarter_of(near, 0, quarter_rows), cols], part.at[landed(d, 0, quarter_rows), cols])]
+            groups = [[(part.at[quarter_of(near, mine, half), cols], part.at[landed(d, mine, half), cols])]]
         else:
             if step == 2:
-                rows = [rows_at(pos_z, pos_y, 0, quarter_rows)]
+                rows = [[rows_at(pos_z, pos_y, offset, half)] for offset in (mine, rest)]
             elif step == 3:
-                rows = [rows_at(back, pos_y, d * half, half) if z_first else rows_at(pos_z, behind, d * half, half)]
+                rows = [[rows_at(back, pos_y, mine, half) if z_first else rows_at(pos_z, behind, mine, half)]]
             elif step == 4:
-                rows = [rows_at(z, pos_y, 0, quarter_rows) for z in range(RING)] if z_first else [rows_at(pos_z, 0, 0, rows_per)]
+                rows = [[rows_at(z, pos_y, offset, half) for z in range(RING)] if z_first else [rows_at(pos_z, 0, 4 * offset, 4 * half)] for offset in (mine, rest)]
             else:
-                rows = [rows_at(z, behind, d * half, half) for z in range(RING)] if z_first else [rows_at(back, 0, d * (rows_per // 2), rows_per // 2)]
-            pairs = [(xbuf.at[r, cols], xbuf.at[r, cols]) for r in rows]
+                rows = [[rows_at(z, behind, mine, half) for z in range(RING)] if z_first else [rows_at(back, 0, 4 * mine, 4 * half)]]
+            groups = [[(xbuf.at[r, cols], xbuf.at[r, cols]) for r in group] for group in rows]
         to = (y_peer if along_y else z_peer)(d)
-        return [remote(src, dst, last_send.at[step], last_recv.at[c, step], head=to) for src, dst in pairs]
+        return [[remote(src, dst, last_send.at[step + n], last_recv.at[c, step + n], head=to) for src, dst in group] for n, group in enumerate(groups)]
 
     def last_arrived(step, cols):
-        rows = (quarter_rows, 2 * quarter_rows, 2 * quarter_rows, quarter_rows, 2 * rows_per, rows_per)[step]
+        rows = (quarter_rows, 2 * quarter_rows, quarter_rows, 2 * quarter_rows, rows_per, 2 * rows_per)[step]
         return (part if step < 2 else xbuf).at[pl.ds(0, rows), cols]
 
     def send_last(step, c):
         def both(z_first):
-            for d in range(DIRS):
-                start(last_messages(step, c, d, z_first))
+            copies = [last_messages(step, c, d, z_first) for d in range(DIRS)]
+            for n in range(len(copies[0])):
+                for d in range(DIRS):
+                    start(copies[d][n])
 
         if step < 2:
             both(False)

time: 336 us -> 338 us (level)
  no operation moved by 1% of the time
where the time goes in v15:
time: 338 us; the launch traced here: 337 us
  Pallas kernels  332 us (98%)
  other arithmetic  3.73 us (1%)
    pallas_call x1, Pallas kernels, layers(): pl.pallas_call(layers_kernel, out_shape=[shape((tok_count, d_model), bf16...  324 us
    pallas_call x1, Pallas kernels, emit(): pl.pallas_call(emit_kernel, out_shape=[jax.ShapeDtypeStruct(x_out.shape,...  8.01 us

profile of v15, /device:TPU:6, one launch (start us, length us, event | category | flops | bytes accessed | tf_op | source)
XLA Modules:
  0.0 336.6 jit_solution(2730780243238765618)
XLA Ops:
  0.6 0.7 convert_element_type.3
  1.3 3.0 multiply_sine_fusion
  4.4 324.1 %layers.1 = (bf16[1024,4096]{1,0:T(8,128)(2,1)}, bf16[1024,256]{1,0:T(8,128)(2,1)}, bf16[1024,256]{1,0:T(8,128)(2,1)}, bf16[1024,256]{1,0:T(8,128)(2,1)}, bf16[1...) custom-call(bf16[1024,4096]{1,0:T(8,128)(2,1)} %x_ref.1, ...), custom_call_target="tpu_custom_call" | custom-call | tf_op jit(solution)/shard_map/layers/pallas_call | solution.py:908
  328.5 8.0 %emit.1 = (bf16[1024,4096]{1,0:T(8,128)(2,1)}, bf16[2,1024,256]{2,1,0:T(8,128)(2,1)}, bf16[2,1024,256]{2,1,0:T(8,128)(2,1)}) custom-call(bf16[1024,4096]{1,0:T(8,128)(2,1)} %get-tuple-element.11.x_ref, bf16[1024,256]{1,0:T(8,128)(2,1)} %get-tuple-element.12.k_first, bf16[1024,256]{1,0:T(8,128)(2,1)} %get-tuple-element.13.k_second, ...), custom_call_target="tpu_custom_call" | custom-call | tf_op jit(solution)/shard_map/emit/pallas_call | solution.py:970
  (1 shorter events, 0.0 us)

commit v16 on v14

--- a/solution.py
+++ b/solution.py
@@ -38,7 +38,7 @@
 NEAR_TICKS = ((9, 1), (15, 3))
 FAR_TICKS = ((24, 1), (26, 3))
 SERVE_TICKS = (27, 31, 35, 42)
-GIVE_TICK = 37
+GIVE_TICK = 38
 OWN_TICK = 3
 DONE_TICK = 11
 EARLY_TICK = 31
@@ -383,6 +383,7 @@
 
         lax.fori_loop(first_n, last_n, past, 0)
 
+    few_near = jnp.minimum(my_seq, 1)
     near_count = my_seq - jnp.where(chip >= 2, 2, 0)
 
     def finish(i, spread):
@@ -503,6 +504,9 @@
         pl.semaphore_signal(barrier, inc=1, device_id={'seq': peer}, device_id_type=mesh_id)
     for peer in [z_device(pos_z + j) for j in range(1, RING)] + [y_peer(d) for d in range(DIRS)]:
         pl.semaphore_signal(barrier, inc=1, device_id={'head': peer}, device_id_type=mesh_id)
+    pl.semaphore_wait(barrier, 8)
+    for d in range(DIRS):
+        start(z_parts(0, d))
 
     def prepare(i, carry):
         x_load(i).wait()
@@ -522,17 +526,7 @@
             wait(weights(0, 0))
 
         keys_values(xbuf[span(i * rows_per, rows_per), :], i)
-
-        @pl.when(i == 0)
-        def _():
-            pl.semaphore_wait(barrier, 8)
-
         send_kv(i)
-
-        @pl.when(i == 0)
-        def _():
-            for d in range(DIRS):
-                start(z_parts(0, d))
         return carry
 
     lax.fori_loop(0, KV_CHUNKS, prepare, 0)
@@ -594,10 +588,11 @@
         @pl.when(tile == 0)
         def _():
             serve_all(3)
-            attend_past(0, near_count, range(KV_CHUNKS), ((0, 0), (0, 1)))
+            attend_past(0, few_near, range(KV_CHUNKS), ((0, 0), (0, 1)))
             take(part_recv.at[0], xbuf.at[pl.ds(0, depth // CHIPS), :])
             for d in range(DIRS):
                 start(z_parts(1, d))
+            attend_past(few_near, near_count, range(KV_CHUNKS), ((0, 0), (0, 1)))
         return carry
 
     lax.fori_loop(0, ff_local // W_TILE, first_half, 0)
@@ -950,20 +945,22 @@
 
 def emit_kernel(x_ref, k_first, k_second, v_first, v_second, x_out, k_out, v_out, xbuf, rows, load_sem, store_sem):
     size = x_ref.shape[0] // EMIT_PARTS
-    loads, stores = [], []
-    for n in range(EMIT_PARTS):
-        part = pl.ds(n * size, size)
-        loads.append(pltpu.make_async_copy(x_ref.at[part, :], xbuf.at[part, :], load_sem.at[n]))
-        stores.append(pltpu.make_async_copy(xbuf.at[part, :], x_out.at[part, :], store_sem.at[n]))
-    for n, (ref, out) in enumerate(((k_first, k_out.at[0]), (k_second, k_out.at[1]), (v_first, v_out.at[0]), (v_second, v_out.at[1]))):
-        loads.append(pltpu.make_async_copy(ref, rows.at[n], load_sem.at[EMIT_PARTS + n]))
-        stores.append(pltpu.make_async_copy(rows.at[n], out, store_sem.at[EMIT_PARTS + n]))
-    for copy in loads:
+    parts = [pl.ds(n * size, size) for n in range(EMIT_PARTS)]
+    caches = ((k_first, k_out.at[0]), (k_second, k_out.at[1]), (v_first, v_out.at[0]), (v_second, v_out.at[1]))
+    loads = [pltpu.make_async_copy(x_ref.at[part, :], xbuf.at[part, :], load_sem.at[n]) for n, part in enumerate(parts)]
+    stores = [pltpu.make_async_copy(xbuf.at[part, :], x_out.at[part, :], store_sem.at[0]) for part in parts]
+    row_loads = [pltpu.make_async_copy(ref, rows.at[n], load_sem.at[EMIT_PARTS]) for n, (ref, _) in enumerate(caches)]
+    row_stores = [pltpu.make_async_copy(rows.at[n], out, store_sem.at[1]) for n, (_, out) in enumerate(caches)]
+    for copy in loads + row_loads:
         copy.start()
     for load, store in zip(loads, stores):
         load.wait()
         store.start()
-    for copy in stores:
+    for copy in row_loads:
+        copy.wait()
+    for copy in row_stores:
+        copy.start()
+    for copy in stores + row_stores:
         copy.wait()
 
 
@@ -978,8 +975,8 @@
         scratch_shapes=[
             pltpu.VMEM(x_out.shape, jnp.bfloat16),
             pltpu.VMEM((4,) + k_first.shape, jnp.bfloat16),
-            pltpu.SemaphoreType.DMA((EMIT_PARTS + 4,)),
-            pltpu.SemaphoreType.DMA((EMIT_PARTS + 4,)),
+            pltpu.SemaphoreType.DMA((EMIT_PARTS + 1,)),
+            pltpu.SemaphoreType.DMA((2,)),
         ],
         compiler_params=pltpu.CompilerParams(vmem_limit_bytes=63 * 1024 * 1024),
         name='emit',

time: 336 us -> 336 us (level)
  no operation moved by 1% of the time
where the time goes in v16:
time: 336 us; the launch traced here: 335 us
  Pallas kernels  330 us (98%)
  other arithmetic  3.73 us (1%)
    pallas_call x1, Pallas kernels, layers(): pl.pallas_call(layers_kernel, out_shape=[shape((tok_count, d_model), bf16...  322 us
    pallas_call x1, Pallas kernels, emit(): pl.pallas_call(emit_kernel, out_shape=[jax.ShapeDtypeStruct(x_out.shape,...  8.36 us

profile of v16, /device:TPU:6, one launch (start us, length us, event | category | flops | bytes accessed | tf_op | source)
XLA Modules:
  0.0 335.0 jit_solution(2491673218771813040)
XLA Ops:
  0.6 0.7 convert_element_type.3
  1.3 3.0 multiply_sine_fusion
  4.4 322.1 %layers.1 = (bf16[1024,4096]{1,0:T(8,128)(2,1)}, bf16[1024,256]{1,0:T(8,128)(2,1)}, bf16[1024,256]{1,0:T(8,128)(2,1)}, bf16[1024,256]{1,0:T(8,128)(2,1)}, bf16[1...) custom-call(bf16[1024,4096]{1,0:T(8,128)(2,1)} %x_ref.1, ...), custom_call_target="tpu_custom_call" | custom-call | tf_op jit(solution)/shard_map/layers/pallas_call | solution.py:906
  326.5 8.4 %emit.1 = (bf16[1024,4096]{1,0:T(8,128)(2,1)}, bf16[2,1024,256]{2,1,0:T(8,128)(2,1)}, bf16[2,1024,256]{2,1,0:T(8,128)(2,1)}) custom-call(bf16[1024,4096]{1,0:T(8,128)(2,1)} %get-tuple-element.11.x_ref, bf16[1024,256]{1,0:T(8,128)(2,1)} %get-tuple-element.12.k_first, bf16[1024,256]{1,0:T(8,128)(2,1)} %get-tuple-element.13.k_second, ...), custom_call_target="tpu_custom_call" | custom-call | tf_op jit(solution)/shard_map/emit/pallas_call | solution.py:970
  (1 shorter events, 0.0 us)

commit v17 on v14

--- a/solution.py
+++ b/solution.py
@@ -35,13 +35,14 @@
 BLOCK_TICK = 19
 BLOCK_GAP = 6
 LAST_TICK = 43
-NEAR_TICKS = ((9, 1), (15, 3))
-FAR_TICKS = ((24, 1), (26, 3))
-SERVE_TICKS = (27, 31, 35, 42)
+NEAR_TICKS = ((9, 1), (15, 3), (21, 2))
+FAR_TICKS = ((24, 1), (26, 3), (34, 2))
+SERVE_TICKS = (27, 32, 36, 42)
 GIVE_TICK = 37
 OWN_TICK = 3
 DONE_TICK = 11
-EARLY_TICK = 31
+EARLY_TICK = 32
+FAR_VISIT_TICK = 39
 LAST_STEPS = 6
 LAST_COLS = 256
 LAST_BLOCKS = 16
@@ -680,12 +681,15 @@
         def _():
             attend_own(0)
 
-        early = t - EARLY_TICK - 1
-
-        @pl.when(jnp.logical_and(early >= 0, jnp.logical_and(early < 7, early < my_seq)))
-        def _():
-            arrivals(early, (0, 1))
-            visit(early, ((0, 0),))
+        def early_visit(n, due, last_n):
+            @pl.when(jnp.logical_and(due, jnp.logical_and(n >= 0, n < last_n)))
+            def _():
+                arrivals(n, (0, 1))
+                visit(n, ((0, 0),))
+
+        for r in range(2):
+            early_visit(2 * (t - EARLY_TICK - 1) + r, t > EARLY_TICK, near_count)
+        early_visit(near_count + t - FAR_VISIT_TICK, t >= FAR_VISIT_TICK, my_seq)
 
         @pl.when(t == 2)
         def _():
@@ -738,7 +742,6 @@
     for d in range(DIRS):
         pl.semaphore_signal(drained_sem.at[d], inc=1, device_id={'head': y_peer(d)}, device_id_type=mesh_id)
     start(cache_stores(1))
-    near_parts(2)
     attend_own(1)
     attend_past(0, my_seq, (), ((1, 0),))
     take(relay_recv, relay_buf)
@@ -751,7 +754,6 @@
     attend_past(near_count, my_seq, (), ((1, 1),))
     finish(2, True)
     finish(3, True)
-    far_parts(2)
     parts_ref = gd_ref.at[pl.ds(0, 2), pl.ds(0, 3 * depth // 4), :]
     take(side_recv, parts_ref)
 

time: 336 us -> 338 us (level)
  no operation moved by 1% of the time
where the time goes in v17:
time: 338 us; the launch traced here: 336 us
  Pallas kernels  332 us (98%)
  other arithmetic  3.73 us (1%)
    pallas_call x1, Pallas kernels, layers(): pl.pallas_call(layers_kernel, out_shape=[shape((tok_count, d_model), bf16...  324 us
    pallas_call x1, Pallas kernels, emit(): pl.pallas_call(emit_kernel, out_shape=[jax.ShapeDtypeStruct(x_out.shape,...  8.01 us

profile of v17, /device:TPU:6, one launch (start us, length us, event | category | flops | bytes accessed | tf_op | source)
XLA Modules:
  0.0 336.5 jit_solution(2332064101338102785)
XLA Ops:
  0.6 0.7 convert_element_type.3
  1.3 3.0 multiply_sine_fusion
  4.4 323.9 %layers.1 = (bf16[1024,4096]{1,0:T(8,128)(2,1)}, bf16[1024,256]{1,0:T(8,128)(2,1)}, bf16[1024,256]{1,0:T(8,128)(2,1)}, bf16[1024,256]{1,0:T(8,128)(2,1)}, bf16[1...) custom-call(bf16[1024,4096]{1,0:T(8,128)(2,1)} %x_ref.1, ...), custom_call_target="tpu_custom_call" | custom-call | tf_op jit(solution)/shard_map/layers/pallas_call | solution.py:913
  328.3 8.0 %emit.1 = (bf16[1024,4096]{1,0:T(8,128)(2,1)}, bf16[2,1024,256]{2,1,0:T(8,128)(2,1)}, bf16[2,1024,256]{2,1,0:T(8,128)(2,1)}) custom-call(bf16[1024,4096]{1,0:T(8,128)(2,1)} %get-tuple-element.11.x_ref, bf16[1024,256]{1,0:T(8,128)(2,1)} %get-tuple-element.12.k_first, bf16[1024,256]{1,0:T(8,128)(2,1)} %get-tuple-element.13.k_second, ...), custom_call_target="tpu_custom_call" | custom-call | tf_op jit(solution)/shard_map/emit/pallas_call | solution.py:975
  (1 shorter events, 0.0 us)

commit v18 on v14

--- a/solution.py
+++ b/solution.py
@@ -35,9 +35,9 @@
 BLOCK_TICK = 19
 BLOCK_GAP = 6
 LAST_TICK = 43
-NEAR_TICKS = ((9, 1), (15, 3))
-FAR_TICKS = ((24, 1), (26, 3))
-SERVE_TICKS = (27, 31, 35, 42)
+NEAR_TICKS = ((9, 1), (15, 3), (28, 2))
+FAR_TICKS = ((24, 1), (26, 3), (41, 2))
+SERVE_TICKS = (27, 31, 36, 42)
 GIVE_TICK = 37
 OWN_TICK = 3
 DONE_TICK = 11
@@ -375,13 +375,22 @@
             attend(past_start(n) + side * half_rows, q_half, side, False, False)
 
     def attend_past(first_n, last_n, chunks, visits):
-        def past(n, carry):
-            if chunks:
-                arrivals(n, chunks)
-            visit(n, visits)
+        def past(n, count):
+            for r in range(count if chunks else 0):
+                arrivals(n + r, chunks)
+            for r in range(count):
+                visit(n + r, visits)
+
+        def two(p, carry):
+            past(first_n + 2 * p, 2)
             return carry
 
-        lax.fori_loop(first_n, last_n, past, 0)
+        count = last_n - first_n
+        lax.fori_loop(0, count // 2, two, 0)
+
+        @pl.when(count % 2 == 1)
+        def _():
+            past(last_n - 1, 1)
 
     near_count = my_seq - jnp.where(chip >= 2, 2, 0)
 
@@ -738,7 +747,6 @@
     for d in range(DIRS):
         pl.semaphore_signal(drained_sem.at[d], inc=1, device_id={'head': y_peer(d)}, device_id_type=mesh_id)
     start(cache_stores(1))
-    near_parts(2)
     attend_own(1)
     attend_past(0, my_seq, (), ((1, 0),))
     take(relay_recv, relay_buf)
@@ -751,7 +759,6 @@
     attend_past(near_count, my_seq, (), ((1, 1),))
     finish(2, True)
     finish(3, True)
-    far_parts(2)
     parts_ref = gd_ref.at[pl.ds(0, 2), pl.ds(0, 3 * depth // 4), :]
     take(side_recv, parts_ref)
 

time: 336 us -> 340 us (1.012)
  Pallas kernels: 330 us -> 334 us
    pallas_call x1, Pallas kernels: 322 us -> 326 us  [layers(): pl.pallas_call(layers_kernel, out_shape=[shape((tok_count, d_model), bf16...]
where the time goes in v18:
time: 340 us; the launch traced here: 339 us
  Pallas kernels  334 us (98%)
  other arithmetic  3.73 us (1%)
    pallas_call x1, Pallas kernels, layers(): pl.pallas_call(layers_kernel, out_shape=[shape((tok_count, d_model), bf16...  326 us
    pallas_call x1, Pallas kernels, emit(): pl.pallas_call(emit_kernel, out_shape=[jax.ShapeDtypeStruct(x_out.shape,...  8.01 us

profile of v18, /device:TPU:6, one launch (start us, length us, event | category | flops | bytes accessed | tf_op | source)
XLA Modules:
  0.0 338.6 jit_solution(5966669656933631770)
XLA Ops:
  0.6 0.7 convert_element_type.3
  1.3 3.0 multiply_sine_fusion
  4.4 326.0 %layers.1 = (bf16[1024,4096]{1,0:T(8,128)(2,1)}, bf16[1024,256]{1,0:T(8,128)(2,1)}, bf16[1024,256]{1,0:T(8,128)(2,1)}, bf16[1024,256]{1,0:T(8,128)(2,1)}, bf16[1...) custom-call(bf16[1024,4096]{1,0:T(8,128)(2,1)} %x_ref.1, ...), custom_call_target="tpu_custom_call" | custom-call | tf_op jit(solution)/shard_map/layers/pallas_call | solution.py:918
  330.4 8.0 %emit.1 = (bf16[1024,4096]{1,0:T(8,128)(2,1)}, bf16[2,1024,256]{2,1,0:T(8,128)(2,1)}, bf16[2,1024,256]{2,1,0:T(8,128)(2,1)}) custom-call(bf16[1024,4096]{1,0:T(8,128)(2,1)} %get-tuple-element.11.x_ref, bf16[1024,256]{1,0:T(8,128)(2,1)} %get-tuple-element.12.k_first, bf16[1024,256]{1,0:T(8,128)(2,1)} %get-tuple-element.13.k_second, ...), custom_call_target="tpu_custom_call" | custom-call | tf_op jit(solution)/shard_map/emit/pallas_call | solution.py:980
  (1 shorter events, 0.0 us)

commit v19 on v18

--- a/solution.py
+++ b/solution.py
@@ -35,8 +35,8 @@
 BLOCK_TICK = 19
 BLOCK_GAP = 6
 LAST_TICK = 43
-NEAR_TICKS = ((9, 1), (15, 3), (28, 2))
-FAR_TICKS = ((24, 1), (26, 3), (41, 2))
+NEAR_TICKS = ((9, 1), (15, 3), (20, 2))
+FAR_TICKS = ((24, 1), (26, 3), (36, 2))
 SERVE_TICKS = (27, 31, 36, 42)
 GIVE_TICK = 37
 OWN_TICK = 3
@@ -607,6 +607,8 @@
             take(part_recv.at[0], xbuf.at[pl.ds(0, depth // CHIPS), :])
             for d in range(DIRS):
                 start(z_parts(1, d))
+            round_start(1)
+            round_start(3)
         return carry
 
     lax.fori_loop(0, ff_local // W_TILE, first_half, 0)
@@ -615,8 +617,6 @@
     attend_past(near_count, my_seq, range(KV_CHUNKS), ((0, 0), (0, 1)))
     finish(0, False)
     finish(1, False)
-    round_start(1)
-    round_start(3)
 
     def block_work(j, phase):
         @pl.when(phase == 0)

time: 340 us -> 334 us (0.982)
  Pallas kernels: 334 us -> 328 us
    pallas_call x1, Pallas kernels: 326 us -> 320 us  [layers(): pl.pallas_call(layers_kernel, out_shape=[shape((tok_count, d_model), bf16...]
where the time goes in v19:
time: 334 us; the launch traced here: 333 us
  Pallas kernels  328 us (98%)
  other arithmetic  3.73 us (1%)
    pallas_call x1, Pallas kernels, layers(): pl.pallas_call(layers_kernel, out_shape=[shape((tok_count, d_model), bf16...  320 us
    pallas_call x1, Pallas kernels, emit(): pl.pallas_call(emit_kernel, out_shape=[jax.ShapeDtypeStruct(x_out.shape,...  8.01 us

profile of v19, /device:TPU:6, one launch (start us, length us, event | category | flops | bytes accessed | tf_op | source)
XLA Modules:
  0.0 332.6 jit_solution(7693375483370168422)
XLA Ops:
  0.6 0.7 convert_element_type.3
  1.3 3.0 multiply_sine_fusion
  4.4 320.0 %layers.1 = (bf16[1024,4096]{1,0:T(8,128)(2,1)}, bf16[1024,256]{1,0:T(8,128)(2,1)}, bf16[1024,256]{1,0:T(8,128)(2,1)}, bf16[1024,256]{1,0:T(8,128)(2,1)}, bf16[1...) custom-call(bf16[1024,4096]{1,0:T(8,128)(2,1)} %x_ref.1, ...), custom_call_target="tpu_custom_call" | custom-call | tf_op jit(solution)/shard_map/layers/pallas_call | solution.py:918
  324.4 8.0 %emit.1 = (bf16[1024,4096]{1,0:T(8,128)(2,1)}, bf16[2,1024,256]{2,1,0:T(8,128)(2,1)}, bf16[2,1024,256]{2,1,0:T(8,128)(2,1)}) custom-call(bf16[1024,4096]{1,0:T(8,128)(2,1)} %get-tuple-element.11.x_ref, bf16[1024,256]{1,0:T(8,128)(2,1)} %get-tuple-element.12.k_first, bf16[1024,256]{1,0:T(8,128)(2,1)} %get-tuple-element.13.k_second, ...), custom_call_target="tpu_custom_call" | custom-call | tf_op jit(solution)/shard_map/emit/pallas_call | solution.py:980
  (1 shorter events, 0.0 us)

commit v20 on v19

--- a/solution.py
+++ b/solution.py
@@ -37,7 +37,8 @@
 LAST_TICK = 43
 NEAR_TICKS = ((9, 1), (15, 3), (20, 2))
 FAR_TICKS = ((24, 1), (26, 3), (36, 2))
-SERVE_TICKS = (27, 31, 36, 42)
+SERVE_TICKS = ((27, 0), (31, 1), (36, 2), (38, 4), (41, 5))
+HALF_TICKS = (35, 37)
 GIVE_TICK = 37
 OWN_TICK = 3
 DONE_TICK = 11
@@ -128,8 +129,14 @@
         return [pltpu.make_async_copy(wd_ref.at[0, :, cols], wdo.at[i % 2, pl.ds(0, ff_local), :], down_sem.at[i % 2, 0]),
                 pltpu.make_async_copy(wo_ref.at[0, 0, :, cols], wdo.at[i % 2, pl.ds(ff_local, head_dim), :], down_sem.at[i % 2, 1])]
 
+    def kv_chunk(i):
+        if isinstance(i, int) and i >= KV_CHUNKS:
+            return (KV_CHUNKS - 1) * rows_per + (i - KV_CHUNKS) * (rows_per // 2), rows_per // 2
+        return i * rows_per, rows_per
+
     def kv_copy(origin_chip, origin_core, i, to, send, recv):
-        rows = kv.at[span((origin_chip * 2 + origin_core) * tok_count + i * rows_per, rows_per), :]
+        first, size = kv_chunk(i)
+        rows = kv.at[span((origin_chip * 2 + origin_core) * tok_count + first, size), :]
         return remote(rows, rows, send, recv, seq=to)
 
     def kv_routes(i):
@@ -297,8 +304,9 @@
     scale = 1.0 / math.sqrt(head_dim)
 
     def keys_values(normed, i):
-        rows = span(i * rows_per, rows_per)
-        own = span(my_seq * tok_count + i * rows_per, rows_per)
+        first, size = kv_chunk(i)
+        rows = span(first, size)
+        own = span(my_seq * tok_count + first, size)
         kv[own, :head_dim] = rope(dot(normed, wtile[0, 0]), rows)
         kv[own, head_dim:] = dot(normed, wtile[0, 1]).astype(bf16)
 
@@ -618,8 +626,24 @@
     finish(0, False)
     finish(1, False)
 
+    def last_half(r):
+        half = rows_per // 2
+        first = kv_chunk(KV_CHUNKS + r)[0]
+
+        def few(n, inner):
+            xs[0, span(r * half + n * NORM_ROWS, NORM_ROWS), :] = norm_rows(xbuf[span(first + n * NORM_ROWS, NORM_ROWS), :], 1)
+            return inner
+
+        lax.fori_loop(0, half // NORM_ROWS, few, 0)
+        if r == 0:
+            wait(weights(1, 0))
+        keys_values(xs[0, pl.ds(r * half, half), :], KV_CHUNKS + r)
+        send_kv(KV_CHUNKS + r)
+        if r == 1:
+            start(weights(1, 2))
+
     def block_work(j, phase):
-        @pl.when(phase == 0)
+        @pl.when(jnp.logical_and(phase == 0, j < KV_CHUNKS - 1))
         def _():
             @pl.when(j == 0)
             def _():
@@ -732,7 +756,12 @@
         def _():
             block_work(late // BLOCK_GAP, late % BLOCK_GAP)
 
-        for i, when in enumerate(SERVE_TICKS):
+        for r, when in enumerate(HALF_TICKS):
+            @pl.when(t == when)
+            def _():
+                last_half(r)
+
+        for when, i in SERVE_TICKS:
             @pl.when(t == when)
             def _():
                 serve_all(i)
@@ -752,8 +781,8 @@
     take(relay_recv, relay_buf)
     for i in range(KV_CHUNKS):
         relay_hidden(i).start()
-    attend_past(0, near_count, (2, 3), ((0, 1), (1, 1)))
-    attend_past(near_count, my_seq, (2, 3), ((0, 1),))
+    attend_past(0, near_count, (2, 4, 5), ((0, 1), (1, 1)))
+    attend_past(near_count, my_seq, (2, 4, 5), ((0, 1),))
     finish(0, True)
     finish(1, True)
     attend_past(near_count, my_seq, (), ((1, 1),))
@@ -938,7 +967,7 @@
             pltpu.VMEM((2, rows_per, d_model), bf16),
             pltpu.VMEM((CHUNKS, HALVES, chunk_rows // RING, half_cols // RING), bf16),
             dma((2,)), dma, dma((2, 2)), dma((2, 2)), dma, dma,
-            dma((10,)), dma((4, KV_CHUNKS)), dma((4, KV_CHUNKS)), dma, dma((2,)),
+            dma((10,)), dma((4, KV_CHUNKS + 2)), dma((4, KV_CHUNKS + 2)), dma, dma((2,)),
             dma, dma((2, RING - 1)), dma, dma,
             dma, dma,
             pltpu.VMEM((KV_CHUNKS, rows_per, W_TILE), bf16), dma, dma,

time: 334 us -> 336 us (level)
  no operation moved by 1% of the time
where the time goes in v20:
time: 336 us; the launch traced here: 335 us
  Pallas kernels  330 us (98%)
  other arithmetic  3.73 us (1%)
    pallas_call x1, Pallas kernels, layers(): pl.pallas_call(layers_kernel, out_shape=[shape((tok_count, d_model), bf16...  322 us
    pallas_call x1, Pallas kernels, emit(): pl.pallas_call(emit_kernel, out_shape=[jax.ShapeDtypeStruct(x_out.shape,...  8.01 us

profile of v20, /device:TPU:6, one launch (start us, length us, event | category | flops | bytes accessed | tf_op | source)
XLA Modules:
  0.0 334.5 jit_solution(5136901002547035617)
XLA Ops:
  0.6 0.7 convert_element_type.3
  1.3 3.0 multiply_sine_fusion
  4.4 321.9 %layers.1 = (bf16[1024,4096]{1,0:T(8,128)(2,1)}, bf16[1024,256]{1,0:T(8,128)(2,1)}, bf16[1024,256]{1,0:T(8,128)(2,1)}, bf16[1024,256]{1,0:T(8,128)(2,1)}, bf16[1...) custom-call(bf16[1024,4096]{1,0:T(8,128)(2,1)} %x_ref.1, ...), custom_call_target="tpu_custom_call" | custom-call | tf_op jit(solution)/shard_map/layers/pallas_call | solution.py:947
  326.3 8.0 %emit.1 = (bf16[1024,4096]{1,0:T(8,128)(2,1)}, bf16[2,1024,256]{2,1,0:T(8,128)(2,1)}, bf16[2,1024,256]{2,1,0:T(8,128)(2,1)}) custom-call(bf16[1024,4096]{1,0:T(8,128)(2,1)} %get-tuple-element.11.x_ref, bf16[1024,256]{1,0:T(8,128)(2,1)} %get-tuple-element.12.k_first, bf16[1024,256]{1,0:T(8,128)(2,1)} %get-tuple-element.13.k_second, ...), custom_call_target="tpu_custom_call" | custom-call | tf_op jit(solution)/shard_map/emit/pallas_call | solution.py:1009
  (1 shorter events, 0.0 us)

commit v21 on v19

--- a/solution.py
+++ b/solution.py
@@ -53,7 +53,7 @@
                  xbuf, part, recv_a, recv_b, hid, att, wdo, wtile, kv, qbuf, acc, row_max, row_sum, xs, xres,
                  x_sem, res_sem, w_sem, down_sem, cache_sem, store_sem, kv_send, ici_recv, core_recv, part_send, part_recv,
                  round_send, round_recv, side_send, side_recv, give_send, give_recv, relay_buf, relay_send, relay_recv, att_all, ring_send, gather_send, ring_recv,
-                 last_send, last_recv, tile_sem, ready_sem, drained_sem):
+                 last_send, last_recv, tile_sem, cos_buf, sin_buf, rope_sem, ready_sem, drained_sem):
     tok_count, d_model = xbuf.shape
     head_dim = qbuf.shape[1]
     half_dim = head_dim // 2
@@ -286,7 +286,7 @@
         return (x_f32 * inv_rms * gain_ref[pl.ds(layer, 1), :].astype(f32)).astype(bf16)
 
     def rope(values, rows):
-        cos_t, sin_t = cos_ref[rows, :], sin_ref[rows, :]
+        cos_t, sin_t = cos_buf[rows, :], sin_buf[rows, :]
         wide = values.astype(bf16).astype(f32)
         first, second = wide[:, :half_dim], wide[:, half_dim:]
         return jnp.concatenate([first * cos_t - second * sin_t, second * cos_t + first * sin_t], axis=1).astype(bf16)
@@ -503,10 +503,10 @@
                 for d in range(DIRS):
                     message(number, chunk, h, d).start()
 
+    rope_loads = [pltpu.make_async_copy(ref, buf, rope_sem.at[n]) for n, (ref, buf) in enumerate(((cos_ref, cos_buf), (sin_ref, sin_buf)))]
     x_load(0).start()
     start(weights(0, 0))
-    x_load(1).start()
-    start(weights(0, 1))
+    start(rope_loads)
     barrier = pltpu.get_barrier_semaphore()
     for peer in (left, right, other):
         pl.semaphore_signal(barrier, inc=1, device_id={'seq': peer}, device_id_type=mesh_id)
@@ -516,6 +516,11 @@
     def prepare(i, carry):
         x_load(i).wait()
 
+        @pl.when(i == 0)
+        def _():
+            x_load(1).start()
+            start(weights(0, 1))
+
         def few(n, inner):
             xbuf[span(i * rows_per + n * NORM_ROWS, NORM_ROWS), :] = norm_rows(xs[i % 2, span(n * NORM_ROWS, NORM_ROWS), :], 0)
             return inner
@@ -529,6 +534,7 @@
         @pl.when(i == 0)
         def _():
             wait(weights(0, 0))
+            wait(rope_loads)
 
         keys_values(xbuf[span(i * rows_per, rows_per), :], i)
 
@@ -919,7 +925,7 @@
         layers_kernel,
         out_shape=[shape((tok_count, d_model), bf16)] + [shape((tok_count, head_dim), bf16)] * 4
         + [shape((RING, ff_local, d_model), bf16), shape((RING, head_dim, d_model), bf16)],
-        in_specs=[any_spec, vmem_spec, vmem_spec, vmem_spec] + [any_spec] * 7,
+        in_specs=[any_spec, any_spec, any_spec, vmem_spec] + [any_spec] * 7,
         out_specs=[any_spec] * 7,
         scratch_shapes=[
             pltpu.VMEM((tok_count, d_model), bf16),
@@ -945,6 +951,7 @@
             pltpu.VMEM((RING, rows_per, head_dim), bf16),
             dma((PART_SLOTS,)), dma((4,)), dma((RECV_SLOTS, STEPS)),
             dma((LAST_STEPS,)), dma((LAST_BLOCKS, LAST_STEPS)), dma((2,)),
+            pltpu.VMEM((tok_count, head_dim // 2), f32), pltpu.VMEM((tok_count, head_dim // 2), f32), dma((2,)),
             pltpu.SemaphoreType.REGULAR((3,)), pltpu.SemaphoreType.REGULAR((DIRS,)),
         ],
         compiler_params=pltpu.CompilerParams(collective_id=0, has_side_effects=True, vmem_limit_bytes=67043328),

time: 334 us -> 333 us (level)
  no operation moved by 1% of the time
where the time goes in v21:
time: 333 us; the launch traced here: 332 us
  Pallas kernels  328 us (98%)
  other arithmetic  3.73 us (1%)
    pallas_call x1, Pallas kernels, layers(): pl.pallas_call(layers_kernel, out_shape=[shape((tok_count, d_model), bf16...  320 us
    pallas_call x1, Pallas kernels, emit(): pl.pallas_call(emit_kernel, out_shape=[jax.ShapeDtypeStruct(x_out.shape,...  8.01 us

profile of v21, /device:TPU:6, one launch (start us, length us, event | category | flops | bytes accessed | tf_op | source)
XLA Modules:
  0.0 332.2 jit_solution(16389744066736081127)
XLA Ops:
  0.6 0.7 convert_element_type.3
  1.3 3.0 multiply_sine_fusion
  4.4 319.6 %layers.1 = (bf16[1024,4096]{1,0:T(8,128)(2,1)}, bf16[1024,256]{1,0:T(8,128)(2,1)}, bf16[1024,256]{1,0:T(8,128)(2,1)}, bf16[1024,256]{1,0:T(8,128)(2,1)}, bf16[1...) custom-call(bf16[1024,4096]{1,0:T(8,128)(2,1)} %x_ref.1, ...), custom_call_target="tpu_custom_call" | custom-call | tf_op jit(solution)/shard_map/layers/pallas_call | solution.py:924
  324.0 8.0 %emit.1 = (bf16[1024,4096]{1,0:T(8,128)(2,1)}, bf16[2,1024,256]{2,1,0:T(8,128)(2,1)}, bf16[2,1024,256]{2,1,0:T(8,128)(2,1)}) custom-call(bf16[1024,4096]{1,0:T(8,128)(2,1)} %get-tuple-element.11.x_ref, bf16[1024,256]{1,0:T(8,128)(2,1)} %get-tuple-element.12.k_first, bf16[1024,256]{1,0:T(8,128)(2,1)} %get-tuple-element.13.k_second, ...), custom_call_target="tpu_custom_call" | custom-call | tf_op jit(solution)/shard_map/emit/pallas_call | solution.py:987
  (1 shorter events, 0.0 us)

commit v22 on v21

--- a/solution.py
+++ b/solution.py
@@ -453,7 +453,7 @@
     def residual_load(chunk, h):
         return pltpu.make_async_copy(x_ref.at[x_rows(chunk, first_pos[h], 0, quarter), cols_of(h, second_pos[h])], xres.at[chunk, h], res_sem)
 
-    def project(chunk):
+    def project(chunk, h):
         rows = span(chunk * chunk_rows, chunk_rows)
         slot_rows = span((chunk % PART_SLOTS) * chunk_rows, chunk_rows)
 
@@ -467,7 +467,8 @@
             part[slot_rows, span(i * DOWN_TILE, DOWN_TILE)] = total + dot(att[rows, :], wdo[i % 2, ff_local:, :])
             return carry
 
-        lax.fori_loop(0, down_tiles, one_tile, 0)
+        per_half = down_tiles // HALVES
+        lax.fori_loop(h * per_half, (h + 1) * per_half, one_tile, 0)
 
     def stage(number, chunk):
         slot = chunk % RECV_SLOTS
@@ -475,7 +476,6 @@
             @pl.when(chunk >= PART_SLOTS)
             def _():
                 partials_sent(chunk % PART_SLOTS)
-            project(chunk)
         else:
             take(ring_recv.at[slot, number - 1], arrived_in(number - 1))
         if number == 4:
@@ -484,6 +484,8 @@
                 take(res_sem, xres)
         for h in range(HALVES):
             p1, p2 = first_pos[h], second_pos[h]
+            if number == 0:
+                project(chunk, h)
             if number in (1, 3):
                 for d in range(DIRS):
                     if number == 1:

time: 333 us -> 333 us (level)
  no operation moved by 1% of the time
where the time goes in v22:
time: 333 us; the launch traced here: 332 us
  Pallas kernels  328 us (98%)
  other arithmetic  3.73 us (1%)
    pallas_call x1, Pallas kernels, layers(): pl.pallas_call(layers_kernel, out_shape=[shape((tok_count, d_model), bf16...  320 us
    pallas_call x1, Pallas kernels, emit(): pl.pallas_call(emit_kernel, out_shape=[jax.ShapeDtypeStruct(x_out.shape,...  8.01 us

profile of v22, /device:TPU:6, one launch (start us, length us, event | category | flops | bytes accessed | tf_op | source)
XLA Modules:
  0.0 332.1 jit_solution(9672168838280710550)
XLA Ops:
  0.6 0.7 convert_element_type.3
  1.3 3.0 multiply_sine_fusion
  4.4 319.5 %layers.1 = (bf16[1024,4096]{1,0:T(8,128)(2,1)}, bf16[1024,256]{1,0:T(8,128)(2,1)}, bf16[1024,256]{1,0:T(8,128)(2,1)}, bf16[1024,256]{1,0:T(8,128)(2,1)}, bf16[1...) custom-call(bf16[1024,4096]{1,0:T(8,128)(2,1)} %x_ref.1, ...), custom_call_target="tpu_custom_call" | custom-call | tf_op jit(solution)/shard_map/layers/pallas_call | solution.py:926
  323.9 8.0 %emit.1 = (bf16[1024,4096]{1,0:T(8,128)(2,1)}, bf16[2,1024,256]{2,1,0:T(8,128)(2,1)}, bf16[2,1024,256]{2,1,0:T(8,128)(2,1)}) custom-call(bf16[1024,4096]{1,0:T(8,128)(2,1)} %get-tuple-element.11.x_ref, bf16[1024,256]{1,0:T(8,128)(2,1)} %get-tuple-element.12.k_first, bf16[1024,256]{1,0:T(8,128)(2,1)} %get-tuple-element.13.k_second, ...), custom_call_target="tpu_custom_call" | custom-call | tf_op jit(solution)/shard_map/emit/pallas_call | solution.py:989
  (1 shorter events, 0.0 us)
